TPU v7x, 8 devices: a whole 2x2x1 slice. The times are simulated.
8 devices in a mesh: dp: 1 (over z), tx: 2 (over y), tyz: 4 (over x, core).
Axes of the slice: x: 2, y: 2, z: 1, core: 2. Of those that a mesh axis runs over, the one named last changes fastest.
Arguments:
- hidden: bfloat16 [64, 64, 2048], P('dp', None, ('tx', 'tyz'))
- lengths: int32 [64], P(('dp', 'tx', 'tyz'))
- k_cache: bfloat16 [64, 2048, 128], P(('dp', 'tx', 'tyz'))
- v_cache: bfloat16 [64, 2048, 128], P(('dp', 'tx', 'tyz'))
- ln_gain: float32 [2048], P(('tx', 'tyz'))
- w_query: bfloat16 [2048, 2048], P('tx', 'tyz')
- w_key: bfloat16 [2048, 128], P('tx')
- w_value: bfloat16 [2048, 128], P('tx')
- w_gate: bfloat16 [2048, 8192], P('tx', 'tyz')
- w_up: bfloat16 [2048, 8192], P('tx', 'tyz')
- w_down: bfloat16 [8192, 2048], P('tyz', 'tx')
- w_out: bfloat16 [2048, 2048], P('tyz', 'tx')
Outputs:
- output 1: bfloat16 [64, 64, 2048], P('dp', None, ('tx', 'tyz'))
- output 2: bfloat16 [64, 2048, 128], P(('dp', 'tx', 'tyz'))
- output 3: bfloat16 [64, 2048, 128], P(('dp', 'tx', 'tyz'))
All inputs are finite; a program needn't handle non-finite values.
Results may differ from a plain program's by a relative error of at most 0.00443472.
Values are sent between devices in bfloat16 or wider.
A program may use at most 1 GiB of HBM per device.

v0:
```python
import functools

import jax
import jax.numpy as jnp
from jax import lax
from jax.experimental import pallas as pl
from jax.experimental.pallas import tpu as pltpu
from jax.sharding import PartitionSpec as P

LN_EPS = 1e-6
ROPE_BASE = 10000.0
BF16 = jnp.bfloat16
F32 = jnp.float32


def swap(axis, pairs):
    return lambda a: lax.ppermute(a, axis, pairs)


swap_y = swap("tx", [(0, 1), (1, 0)])
swap_x = swap("tyz", [(0, 2), (2, 0), (1, 3), (3, 1)])
swap_c = swap("tyz", [(0, 1), (1, 0), (2, 3), (3, 2)])


def pick(arr, index):
    return lax.dynamic_index_in_dim(arr, index, axis=0, keepdims=False)


def norm_kernel(offs_ref, *refs):
    pieces, gain_ref, out_ref = refs[:8], refs[8], refs[9]
    width = pieces[0].shape[1]
    total = 8 * width
    xs = [p[...].astype(F32) for p in pieces]
    s1 = sum(jnp.sum(v, axis=-1, keepdims=True) for v in xs)
    s2 = sum(jnp.sum(v * v, axis=-1, keepdims=True) for v in xs)
    mean = s1 / total
    var = s2 / total - mean * mean
    inv = lax.rsqrt(var + LN_EPS)
    for i, v in enumerate(xs):
        off = pl.multiple_of(offs_ref[i], width)
        out_ref[:, pl.ds(off, width)] = ((v - mean) * inv * gain_ref[i : i + 1, :]).astype(BF16)


def layer_norm(pieces, gains, offs):
    tokens, width = pieces[0].shape
    blk = 256
    return pl.pallas_call(
        norm_kernel,
        grid_spec=pltpu.PrefetchScalarGridSpec(
            num_scalar_prefetch=1,
            grid=(tokens // blk,),
            in_specs=[pl.BlockSpec((blk, width), lambda i, o: (i, 0))] * 8 + [pl.BlockSpec((8, width), lambda i, o: (0, 0))],
            out_specs=pl.BlockSpec((blk, 8 * width), lambda i, o: (i, 0)),
        ),
        out_shape=jax.ShapeDtypeStruct((tokens, 8 * width), BF16),
        cost_estimate=pl.CostEstimate(flops=20 * tokens * 8 * width, bytes_accessed=32 * tokens * width, transcendentals=tokens),
        name="norm",
    )(offs, *pieces, gains)


def rope(t, cos_t, sin_t):
    t = t.astype(F32)
    return (t * cos_t + pltpu.roll(t, t.shape[-1] // 2, 1) * sin_t).astype(BF16)


def attn_kernel(len_ref, q0, q1, q2, q3, kv_ref, cos_ref, sin_ref, kc_ref, vc_ref, o0, o1, o2, o3, kn_ref, vn_ref, qs):
    new = kv_ref.shape[0]
    cache = kc_ref.shape[1]
    dim = kc_ref.shape[2]
    length = len_ref[pl.program_id(0)]
    cos_t, sin_t = cos_ref[...], sin_ref[...]
    win = new + 32
    kn_ref[...] = kc_ref[...]
    vn_ref[...] = vc_ref[...]
    base = pl.multiple_of(jnp.minimum((length // 16) * 16, cache - win), 16)
    rows = lax.broadcasted_iota(jnp.int32, (win, new), 0) + (base - length)
    hot = (rows == lax.broadcasted_iota(jnp.int32, (win, new), 1)).astype(BF16)
    key_rot = rope(kv_ref[:, :dim], cos_t, sin_t)
    r = lax.broadcasted_iota(jnp.int32, (win, dim), 0) + (base - length)
    fresh = (r >= 0) & (r < new)
    k_win = jnp.dot(hot, key_rot, preferred_element_type=F32)
    v_win = jnp.dot(hot, kv_ref[:, dim:], preferred_element_type=F32)
    sl = pl.ds(base, win)
    kn_ref[0, sl, :] = jnp.where(fresh, k_win, kc_ref[0, sl, :].astype(F32)).astype(BF16)
    vn_ref[0, sl, :] = jnp.where(fresh, v_win, vc_ref[0, sl, :].astype(F32)).astype(BF16)

    q_refs, o_refs = (q0, q1, q2, q3), (o0, o1, o2, o3)
    hpg = q0.shape[1] // dim
    for g in range(4):
        for h in range(hpg):
            qs[g * hpg * new + h * new : g * hpg * new + (h + 1) * new, :] = rope(q_refs[g][:, h * dim : (h + 1) * dim], cos_t, sin_t)

    def attend(keys):
        @pl.loop(0, 4)
        def _(g):
            group = pl.ds(pl.multiple_of(g * hpg * new, hpg * new), hpg * new)
            q = qs[group, :]
            s = lax.dot_general(q, kn_ref[0, :keys, :], (((1,), (1,)), ((), ())), preferred_element_type=F32)
            s = s * (dim ** -0.5)
            tok = lax.broadcasted_iota(jnp.int32, (hpg * new, keys), 0) % new
            pos = lax.broadcasted_iota(jnp.int32, (hpg * new, keys), 1)
            s = jnp.where(pos - tok <= length, s, -1e30)
            e = jnp.exp(s - jnp.max(s, axis=-1, keepdims=True))
            p = (e * (1.0 / jnp.sum(e, axis=-1, keepdims=True))).astype(BF16)
            qs[group, :] = jnp.dot(p, vn_ref[0, :keys, :], preferred_element_type=F32).astype(BF16)

    step = 256
    need = (length + new + step - 1) // step
    sizes = list(range(5, cache // step + 1))
    for n in sizes:
        cond = need <= n if n == sizes[0] else need == n
        pl.when(cond)(functools.partial(attend, n * step))
    for g in range(4):
        for h in range(hpg):
            o_refs[g][:, h * dim : (h + 1) * dim] = qs[(g * hpg + h) * new : (g * hpg + h + 1) * new, :]


def attention(lengths, qs, kv, cos_t, sin_t, k_cache, v_cache):
    rows, cache, dim = k_cache.shape
    new = kv.shape[0] // rows
    qw = qs[0].shape[1]
    tok = lambda w: pl.BlockSpec((new, w), lambda b, L: (b, 0))
    row = pl.BlockSpec((1, cache, dim), lambda b, L: (b, 0, 0))
    heads = 4 * qw // dim
    return pl.pallas_call(
        attn_kernel,
        grid_spec=pltpu.PrefetchScalarGridSpec(
            num_scalar_prefetch=1,
            grid=(rows,),
            in_specs=[tok(qw)] * 4 + [tok(2 * dim), tok(dim), tok(dim), row, row],
            out_specs=[tok(qw)] * 4 + [row, row],
            scratch_shapes=[pltpu.VMEM((heads * new, dim), BF16)],
        ),
        out_shape=[jax.ShapeDtypeStruct((rows * new, qw), BF16)] * 4 + [jax.ShapeDtypeStruct(k_cache.shape, BF16)] * 2,
        cost_estimate=pl.CostEstimate(
            flops=8 * rows * heads * new * cache * dim, bytes_accessed=8 * rows * cache * dim, transcendentals=rows * heads * new * cache
        ),
        name="attn",
    )(lengths, *qs, kv, cos_t, sin_t, k_cache, v_cache)


def glu_kernel(h_ref, near_w, far_w, a_ref):
    depth = near_w.shape[1]
    near, far = h_ref[:, :depth], h_ref[:, depth:]
    gate = jnp.dot(near, near_w[0], preferred_element_type=F32) + jnp.dot(far, far_w[0], preferred_element_type=F32)
    up = jnp.dot(near, near_w[1], preferred_element_type=F32) + jnp.dot(far, far_w[1], preferred_element_type=F32)
    a_ref[...] = (gate / (1.0 + jnp.exp(-gate)) * up).astype(BF16)


def glu(h, near_w, far_w):
    tokens, depth = h.shape
    cols = near_w.shape[2]
    blk = 512
    w = pl.BlockSpec(near_w.shape, lambda i: (0, 0, 0))
    return pl.pallas_call(
        glu_kernel,
        grid=(tokens // blk,),
        in_specs=[pl.BlockSpec((blk, depth), lambda i: (i, 0)), w, w],
        out_specs=pl.BlockSpec((blk, cols), lambda i: (i, 0)),
        out_shape=jax.ShapeDtypeStruct((tokens, cols), BF16),
        cost_estimate=pl.CostEstimate(flops=4 * tokens * depth * cols, bytes_accessed=2 * tokens * (depth + cols) + 4 * depth * cols, transcendentals=tokens * cols),
        name="glu",
    )(h, near_w, far_w)


def mix_kernel(n_lhs, n_w, n_add, *refs):
    lhs, ws, adds, out_ref = refs[:n_lhs], refs[n_lhs : n_lhs + n_w], refs[n_lhs + n_w : n_lhs + n_w + n_add], refs[-1]
    total = None
    i, row = 0, 0
    for l in lhs:
        k = l.shape[1]
        part = jnp.dot(l[...], ws[i][row : row + k, :], preferred_element_type=F32)
        total = part if total is None else total + part
        row += k
        if row == ws[i].shape[0]:
            i, row = i + 1, 0
    for t in adds:
        total = total + t[...].astype(F32)
    out_ref[...] = total.astype(out_ref.dtype)


def mix(lhs, ws, adds=(), dtype=F32, start=0, tokens=None):
    tokens = lhs[0].shape[0] if tokens is None else tokens
    cols = ws[0].shape[1]
    blk = 512
    first = start // blk
    tok = lambda w: pl.BlockSpec((blk, w), lambda i: (i + first, 0))
    depth = sum(l.shape[1] for l in lhs)
    add_specs = [tok(cols) if t.shape[0] != tokens else pl.BlockSpec((blk, cols), lambda i: (i, 0)) for t in adds]
    return pl.pallas_call(
        functools.partial(mix_kernel, len(lhs), len(ws), len(adds)),
        grid=(tokens // blk,),
        in_specs=[tok(l.shape[1]) for l in lhs] + [pl.BlockSpec(w.shape, lambda i: (0, 0)) for w in ws] + add_specs,
        out_specs=pl.BlockSpec((blk, cols), lambda i: (i, 0)),
        out_shape=jax.ShapeDtypeStruct((tokens, cols), dtype),
        cost_estimate=pl.CostEstimate(flops=2 * tokens * depth * cols, bytes_accessed=2 * depth * (tokens + cols), transcendentals=0),
        name="mix",
    )(*lhs, *ws, *adds)


BLOCK_ORDER = [(1, 1), (1, 0), (0, 1), (0, 0)]


def tie(value, *others):
    return lax.optimization_barrier((value, *others))[0]


def solution(mesh):
    def local_layer(hidden, lengths, k_cache, v_cache, ln_gain, w_query, w_key, w_value, w_gate, w_up, w_down, w_out):
        batch, new, width = hidden.shape
        rows_own, _, dim = k_cache.shape
        yi = lax.axis_index("tx")
        ti = lax.axis_index("tyz")
        xi, ci = ti // 2, ti % 2
        half = batch * new // 2
        own_tok = rows_own * new

        g = ln_gain.reshape(1, width)
        g = jnp.concatenate([g, swap_y(g)], 0)
        g = jnp.concatenate([g, swap_x(g)], 0)
        g = jnp.concatenate([g, swap_c(g)], 0)
        hid2 = hidden.reshape(2, half, width)
        mine, other = pick(hid2, yi), pick(hid2, 1 - yi)
        from_y = swap_y(other)
        mine_x = swap_x(mine)
        from_yx = swap_x(from_y)
        near = [mine, from_y, mine_x, from_yx]
        far = [swap_c(p) for p in near]
        offs = []
        for cr in range(2):
            for xr in range(2):
                for yr in range(2):
                    offs.append(width * (4 * yr + 2 * (xr ^ xi) + (cr ^ ci)))
        h = layer_norm(near + far, g, jnp.stack(offs).astype(jnp.int32))

        kv_rows = w_key.shape[0] // 2
        w_kv = jnp.concatenate([w_key, w_value], axis=1)
        kv_part = swap_y(lax.dynamic_slice_in_dim(w_kv, ci * kv_rows, kv_rows, 0))
        kv_pair = jnp.stack([kv_part, swap_c(kv_part)])
        kv_far = jnp.where(ci == 0, kv_pair, kv_pair[::-1]).reshape(w_kv.shape)
        q_far = swap_y(w_query)

        q = mix([h], [jnp.concatenate([w_query, q_far], 0)], dtype=BF16)
        h_own = lax.dynamic_slice_in_dim(h, ti * own_tok, own_tok, 0)
        kv = jnp.dot(h_own, jnp.concatenate([w_kv, kv_far], 0), preferred_element_type=F32).astype(BF16)

        q4 = q.reshape(2, 2, own_tok, q.shape[1])
        q_x = [pick(q4, xi), swap_x(pick(q4, 1 - xi))]
        q_c = [pick(v, ci) for v in q_x] + [swap_c(pick(v, 1 - ci)) for v in q_x]

        half_dim = dim // 2
        inv_freq = ROPE_BASE ** (-2.0 * jnp.arange(half_dim, dtype=F32) / dim)
        positions = (lengths[:, None] + jnp.arange(new, dtype=jnp.int32)[None, :]).reshape(own_tok)
        angles = positions.astype(F32)[:, None] * inv_freq
        cos_t, sin_t = jnp.cos(angles), jnp.sin(angles)
        cos_t = jnp.concatenate([cos_t, cos_t], -1)
        sin_t = jnp.concatenate([-sin_t, sin_t], -1)
        o0, o1, o2, o3, k_next, v_next = attention(lengths, q_c, kv, cos_t, sin_t, k_cache, v_cache)

        keep = [o0, swap_c(o2)]
        send = swap_x(jnp.stack([o1, swap_c(o3)]))
        flip = lambda pair, i: jnp.where(i == 0, jnp.stack(pair), jnp.stack(pair[::-1]))
        o_rows = flip([flip(keep, ci), jnp.where(ci == 0, send, send[::-1])], xi)
        o_own = o_rows.reshape(half, -1)
        o_far = swap_c(o_own)

        chunks = 4
        cw = w_gate.shape[1] // chunks
        a_own, a_far = [], []
        for j in range(chunks):
            near_w = jnp.stack([w[:, j * cw : (j + 1) * cw] for w in (w_gate, w_up)])
            far_w = swap_y(near_w)
            if j > 0:
                far_w = tie(far_w, a_own[-1], o0)
            a_own.append(glu(h, near_w, far_w))
            a_far.append(swap_c(a_own[-1]))
        lhs_near, lhs_far = a_own + [o_own], a_far + [swap_c(o_own)]

        def block(xr, cr):
            col = (2 * (xi ^ xr) + (ci ^ cr)) * width
            return jnp.concatenate([lax.dynamic_slice_in_dim(w, col, width, 1) for w in (w_down, w_out)], 0)

        blocks = [[block(xr, cr) for cr in range(2)] for xr in range(2)]
        other_y = [[None, None], [None, None]]
        for xr, cr in BLOCK_ORDER:
            other_y[xr][cr] = swap_y(blocks[xr][cr])

        def product(pair, adds=(), dtype=F32):
            return mix(lhs_near + lhs_far, [pair[0], swap_c(pair[1])], adds, dtype)

        p_own = product(blocks[1])
        r_own = swap_x(p_own)
        p_far = product([tie(w, p_own) for w in other_y[1]])
        r_far = swap_x(p_far)
        out_own = product([blocks[0][0], tie(blocks[0][1], p_far)], [mine, r_own], BF16)
        base = mix(lhs_far, [swap_c(tie(other_y[0][1], p_far))], [from_y, tie(r_far, out_own)])
        last = tie(other_y[0][0], base)
        parts = 2
        size = half // parts
        out_far = [swap_y(mix(lhs_near, [last], [base], BF16, i * size, size)) for i in range(parts)]
        out_far = jnp.concatenate(out_far, 0)
        out = jnp.where(yi == 0, jnp.stack([out_own, out_far]), jnp.stack([out_far, out_own]))
        return out.reshape(batch, new, width), k_next, v_next

    row_spec = P("dp", None, ("tx", "tyz"))
    batch_spec = P(("dp", "tx", "tyz"), None, None)
    in_specs = (row_spec, P(("dp", "tx", "tyz")), batch_spec, batch_spec, P(("tx", "tyz")), P("tx", "tyz"), P("tx", None), P("tx", None), P("tx", "tyz"), P("tx", "tyz"), P("tyz", "tx"), P("tyz", "tx"))
    out_specs = (row_spec, batch_spec, batch_spec)

    return jax.shard_map(local_layer, mesh=mesh, in_specs=in_specs, out_specs=out_specs, check_vma=False)
```

profile of v0, /device:TPU:0, one launch (start us, length us, event | category | flops | bytes accessed | tf_op | source)
XLA Modules:
  0.0 443.0 jit_solution(18280951403594618098)
XLA Ops:
  0.7 2.7 dynamic-slice_bitcast_fusion.1
  3.4 3.3 collective-permute-start
  11.2 4.7 %slice_bitcast_fusion = (bf16[1,1024,512]{2,1,0:T(8,128)(2,1)S(1)}, bf16[1,1024,512]{2,1,0:T(8,128)(2,1)S(1)}, bf16[1,1024,512]{2,1,0:T(8,128)(2,1)S(1)}, bf16[1...) fusion(bf16[1024,2048]{1,0:T(8,128)(2,1)} %param.21, ...), kind=kLoop, calls=%fused_computation.22 | loop fusion | bytes 16777216 | tf_op jit(solution)/shard_map/stack | solution.py:271
  18.9 12.1 %collective-permute-done.refs_1_.refs_6_ = bf16[2048,256]{1,0:T(8,128)(2,1)S(1)} collective-permute-done((bf16[2048,256]{1,0:T(8,128)(2,1)}, bf16[2048,256]{1,0:T(8,128)(2,1)S(1)}, u32[]{:S(2)}, u32[]{:S(2)}) %collective-permute-start) | collective-permute-done | bytes 1048608 | tf_op jit(solution)/shard_map/ppermute | solution.py:17
  37.9 16.7 %collective-permute-done.8 = f32[2,256]{1,0:T(2,128)S(1)} collective-permute-done((f32[2,256]{1,0:T(2,128)S(1)}, f32[2,256]{1,0:T(2,128)S(1)}, u32[]{:S(2)}, u32[]{:S(2)}) %collective-permute-start.8) | collective-permute-done | bytes 2080 | tf_op jit(solution)/shard_map/ppermute | solution.py:17
  56.5 4.0 constant_dynamic-slice_fusion.1
  63.8 3.0 pad_maximum_fusion.2.refs_1_
  70.3 13.0 %norm.1.h_ref.refs_0_ = bf16[2048,2048]{1,0:T(8,128)(2,1)} custom-call(s32[8]{0:T(128)} %stack.129.offs_ref, bf16[2048,256]{1,0:T(8,128)(2,1)} %copy-done.3, bf16[2048,256]{1,0:T(8,128)(2,1)} %copy-done.7, bf16[2048,256]{1,0:T(8,128)(2,1)} %collective-permute-done.1.refs_2_, bf16[2048,256]{1,0:T(8,128)(2,1)} %collective-permute-done.2.refs_3_, ...), custom_call_target="tpu_custom_call" | custom-call | flops 83886080 | bytes 16777216 | tf_op jit(solution)/shard_map/norm/pallas_call | solution.py:47
  83.4 8.7 %mix.7 = bf16[2048,512]{1,0:T(8,128)(2,1)} custom-call(bf16[2048,2048]{1,0:T(8,128)(2,1)} %norm.1.h_ref.refs_0_, bf16[2048,512]{1,0:T(8,128)(2,1)} %pad_maximum_fusion.2.refs_1_), custom_call_target="tpu_custom_call" | custom-call | flops 4294967296 | bytes 10485760 | tf_op jit(solution)/shard_map/mix/pallas_call | solution.py:190
  96.7 20.0 %collective-permute-done.16 = bf16[512,256]{1,0:T(8,128)(2,1)} collective-permute-done((bf16[512,256]{1,0:T(8,128)(2,1)}, bf16[512,256]{1,0:T(8,128)(2,1)}, u32[]{:S(2)}, u32[]{:S(2)}) %collective-permute-start.16) | collective-permute-done | bytes 262176 | tf_op jit(solution)/shard_map/ppermute | solution.py:17
  123.0 3.3 fusion.2.kv_ref
  129.7 13.2 %glu.4.refs_0_ = bf16[2048,512]{1,0:T(8,128)(2,1)} custom-call(bf16[2048,2048]{1,0:T(8,128)(2,1)} %norm.1.h_ref.refs_0_, bf16[2,1024,512]{2,1,0:T(8,128)(2,1)} %pad_maximum_fusion.near_w, bf16[2,1024,512]{2,1,0:T(8,128)(2,1)} %collective-permute-done.10.far_w), custom_call_target="tpu_custom_call" | custom-call | flops 8589934592 | bytes 14680064 | tf_op jit(solution)/shard_map/glu/pallas_call | solution.py:155
  143.9 46.2 %attn.1 = (bf16[512,512]{1,0:T(8,128)(2,1)}, bf16[512,512]{1,0:T(8,128)(2,1)}, bf16[512,512]{1,0:T(8,128)(2,1)}, bf16[512,512]{1,0:T(8,128)(2,1)}, bf16[8,2048,1...) custom-call(s32[8]{0:T(128)} %len_ref.1, bf16[512,512]{1,0:T(8,128)(2,1)} %get-tuple-element.46.q0, ...), custom_call_target="tpu_custom_call" | custom-call | flops 17179869184 | bytes 16777216 | tf_op jit(solution)/shard_map/attn/pallas_call | solution.py:125
  190.2 13.2 %glu.5.refs_1_ = bf16[2048,512]{1,0:T(8,128)(2,1)} custom-call(bf16[2048,2048]{1,0:T(8,128)(2,1)} %norm.1.h_ref.refs_0_, bf16[2,1024,512]{2,1,0:T(8,128)(2,1)} %pad_maximum_fusion.1.near_w, bf16[2,1024,512]{2,1,0:T(8,128)(2,1)} %collective-permute-done.11.far_w), custom_call_target="tpu_custom_call" | custom-call | flops 8589934592 | bytes 14680064 | tf_op jit(solution)/shard_map/glu/pallas_call | solution.py:155
  203.4 3.2 collective-permute-done.18.far_w
  208.2 13.2 %glu.6.refs_2_ = bf16[2048,512]{1,0:T(8,128)(2,1)} custom-call(bf16[2048,2048]{1,0:T(8,128)(2,1)} %norm.1.h_ref.refs_0_, bf16[2,1024,512]{2,1,0:T(8,128)(2,1)} %pad_maximum_fusion.3.near_w, bf16[2,1024,512]{2,1,0:T(8,128)(2,1)} %collective-permute-done.18.far_w), custom_call_target="tpu_custom_call" | custom-call | flops 8589934592 | bytes 14680064 | tf_op jit(solution)/shard_map/glu/pallas_call | solution.py:155
  221.4 29.6 %collective-permute-done.19.far_w = bf16[2,1024,512]{2,1,0:T(8,128)(2,1)} collective-permute-done((bf16[2,1024,512]{2,1,0:T(8,128)(2,1)}, bf16[2,1024,512]{2,1,0:T(8,128)(2,1)}, u32[]{:S(2)}, u32[]{:S(2)}) %collective-permute-start.19) | collective-permute-done | bytes 2097184 | tf_op jit(solution)/shard_map/ppermute | solution.py:17
  250.9 13.2 %glu.7.refs_3_ = bf16[2048,512]{1,0:T(8,128)(2,1)} custom-call(bf16[2048,2048]{1,0:T(8,128)(2,1)} %norm.1.h_ref.refs_0_, bf16[2,1024,512]{2,1,0:T(8,128)(2,1)} %pad_maximum_fusion.4.near_w, bf16[2,1024,512]{2,1,0:T(8,128)(2,1)} %collective-permute-done.19.far_w), custom_call_target="tpu_custom_call" | custom-call | flops 8589934592 | bytes 14680064 | tf_op jit(solution)/shard_map/glu/pallas_call | solution.py:155
  269.2 2.4 collective-permute-done.26.refs_8_.refs_3_
  274.8 12.3 %mix.8 = f32[2048,256]{1,0:T(8,128)} custom-call(bf16[2048,512]{1,0:T(8,128)(2,1)} %glu.4.refs_0_, bf16[2048,512]{1,0:T(8,128)(2,1)} %glu.5.refs_1_, bf16[2048,512]{1,0:T(8,128)(2,1)} %glu.6.refs_2_, bf16[2048,512]{1,0:T(8,128)(2,1)} %glu.7.refs_3_, bf16[2048,512]{1,0:T(8,128)(2,1)} %bitcast.56, bf16[2048,512]{1,0:T(8,128)(2,1)} %collective-permute-done.23.refs_5_.refs_0_, ...), custom_call_target="tpu_custom_call" | custom-call | flops 5368709120 | bytes 23592960 | tf_op jit(solution)/shard_map/mix/pallas_call | solution.py:190
  287.1 12.5 %collective-permute-done.30 = bf16[2560,256]{1,0:T(8,128)(2,1)} collective-permute-done((bf16[2560,256]{1,0:T(8,128)(2,1)}, bf16[2560,256]{1,0:T(8,128)(2,1)}, u32[]{:S(2)}, u32[]{:S(2)}) %collective-permute-start.30) | collective-permute-done | bytes 1310752 | tf_op jit(solution)/shard_map/ppermute | solution.py:17
  299.6 2.4 pad_maximum_fusion.6
  305.0 22.7 %collective-permute-done.28.refs_10_ = bf16[2560,256]{1,0:T(8,128)(2,1)} collective-permute-done((bf16[2560,256]{1,0:T(8,128)(2,1)S(1)}, bf16[2560,256]{1,0:T(8,128)(2,1)}, u32[]{:S(2)}, u32[]{:S(2)}) %collective-permute-start.28) | collective-permute-done | bytes 1310752 | tf_op jit(solution)/shard_map/ppermute | solution.py:17
  327.7 12.6 %mix.9 = f32[2048,256]{1,0:T(8,128)} custom-call(bf16[2048,512]{1,0:T(8,128)(2,1)} %glu.4.refs_0_, bf16[2048,512]{1,0:T(8,128)(2,1)} %glu.5.refs_1_, bf16[2048,512]{1,0:T(8,128)(2,1)} %glu.6.refs_2_, bf16[2048,512]{1,0:T(8,128)(2,1)} %glu.7.refs_3_, bf16[2048,512]{1,0:T(8,128)(2,1)} %bitcast.57, bf16[2048,512]{1,0:T(8,128)(2,1)} %collective-permute-done.23.refs_5_.refs_0_, ...), custom_call_target="tpu_custom_call" | custom-call | flops 5368709120 | bytes 23592960 | tf_op jit(solution)/shard_map/mix/pallas_call | solution.py:190
  341.7 13.4 %collective-permute-done.35 = bf16[2560,256]{1,0:T(8,128)(2,1)} collective-permute-done((bf16[2560,256]{1,0:T(8,128)(2,1)}, bf16[2560,256]{1,0:T(8,128)(2,1)}, u32[]{:S(2)}, u32[]{:S(2)}) %collective-permute-start.35) | collective-permute-done | bytes 1310752 | tf_op jit(solution)/shard_map/ppermute | solution.py:17
  356.8 13.0 %mix.10 = bf16[2048,256]{1,0:T(8,128)(2,1)} custom-call(bf16[2048,512]{1,0:T(8,128)(2,1)} %glu.4.refs_0_, bf16[2048,512]{1,0:T(8,128)(2,1)} %glu.5.refs_1_, bf16[2048,512]{1,0:T(8,128)(2,1)} %glu.6.refs_2_, bf16[2048,512]{1,0:T(8,128)(2,1)} %glu.7.refs_3_, bf16[2048,512]{1,0:T(8,128)(2,1)} %bitcast.58, ...), custom_call_target="tpu_custom_call" | custom-call | flops 5368709120 | bytes 23592960 | tf_op jit(solution)/shard_map/mix/pallas_call | solution.py:190
  369.8 26.7 %collective-permute-done.37.refs_7_ = f32[2048,256]{1,0:T(8,128)} collective-permute-done((f32[2048,256]{1,0:T(8,128)}, f32[2048,256]{1,0:T(8,128)}, u32[]{:S(2)}, u32[]{:S(2)}) %collective-permute-start.37) | collective-permute-done | bytes 2097184 | tf_op jit(solution)/shard_map/ppermute | solution.py:17
  396.5 8.9 %mix.11.refs_6_ = f32[2048,256]{1,0:T(8,128)} custom-call(bf16[2048,512]{1,0:T(8,128)(2,1)} %collective-permute-done.23.refs_5_.refs_0_, bf16[2048,512]{1,0:T(8,128)(2,1)} %collective-permute-done.24.refs_6_.refs_1_, bf16[2048,512]{1,0:T(8,128)(2,1)} %collective-permute-done.25.refs_7_.refs_2_, bf16[2048,512]{1,0:T(8,128)(2,1)} %copy-done.2, ...), custom_call_target="tpu_custom_call" | custom-call | flops 2684354560 | bytes 11796480 | tf_op jit(solution)/shard_map/mix/pallas_call | solution.py:190
  406.5 5.2 %mix.12 = bf16[1024,256]{1,0:T(8,128)(2,1)} custom-call(bf16[2048,512]{1,0:T(8,128)(2,1)} %glu.4.refs_0_, bf16[2048,512]{1,0:T(8,128)(2,1)} %glu.5.refs_1_, bf16[2048,512]{1,0:T(8,128)(2,1)} %glu.6.refs_2_, bf16[2048,512]{1,0:T(8,128)(2,1)} %glu.7.refs_3_, bf16[2048,512]{1,0:T(8,128)(2,1)} %bitcast.59, bf16[2560,256]{1,0:T(8,128)(2,1)} %copy-done.5, ...), custom_call_target="tpu_custom_call" | custom-call | flops 1342177280 | bytes 6553600 | tf_op jit(solution)/shard_map/mix/pallas_call | solution.py:190
  411.7 5.1 %mix.13 = bf16[1024,256]{1,0:T(8,128)(2,1)} custom-call(bf16[2048,512]{1,0:T(8,128)(2,1)} %glu.4.refs_0_, bf16[2048,512]{1,0:T(8,128)(2,1)} %glu.5.refs_1_, bf16[2048,512]{1,0:T(8,128)(2,1)} %glu.6.refs_2_, bf16[2048,512]{1,0:T(8,128)(2,1)} %glu.7.refs_3_, bf16[2048,512]{1,0:T(8,128)(2,1)} %bitcast.60, bf16[2560,256]{1,0:T(8,128)(2,1)} %copy-done.5, ...), custom_call_target="tpu_custom_call" | custom-call | flops 1342177280 | bytes 6553600 | tf_op jit(solution)/shard_map/mix/pallas_call | solution.py:190
  418.9 12.8 %collective-permute-done.38 = bf16[1024,256]{1,0:T(8,128)(2,1)S(1)} collective-permute-done((bf16[1024,256]{1,0:T(8,128)(2,1)S(1)}, bf16[1024,256]{1,0:T(8,128)(2,1)S(1)}, u32[]{:S(2)}, u32[]{:S(2)}) %collective-permute-start.38) | collective-permute-done | bytes 524320 | tf_op jit(solution)/shard_map/ppermute | solution.py:17
  431.6 9.6 %collective-permute-done.39 = bf16[1024,256]{1,0:T(8,128)(2,1)S(1)} collective-permute-done((bf16[1024,256]{1,0:T(8,128)(2,1)}, bf16[1024,256]{1,0:T(8,128)(2,1)S(1)}, u32[]{:S(2)}, u32[]{:S(2)}) %collective-permute-start.39) | collective-permute-done | bytes 524320 | tf_op jit(solution)/shard_map/ppermute | solution.py:17
  (152 shorter events, 59.0 us)
Async XLA Ops:
  3.4 27.6 %collective-permute-start = (bf16[2048,256]{1,0:T(8,128)(2,1)}, bf16[2048,256]{1,0:T(8,128)(2,1)S(1)}, u32[]{:S(2)}, u32[]{:S(2)}) collective-permute-start(bf16[2048,256]{1,0:T(8,128)(2,1)} %get-tuple-element.47), channel_id=1, source_target_pairs={{0,4},{4,0},{1,5},{5,1},{2,6},{6,2},{3,7},{7,3}} | collective-permute-start | bytes 3145736 | tf_op jit(solution)/shard_map/ppermute | solution.py:17
  6.7 49.3 %collective-permute-start.1 = (bf16[2048,256]{1,0:T(8,128)(2,1)S(1)}, bf16[2048,256]{1,0:T(8,128)(2,1)}, u32[]{:S(2)}, u32[]{:S(2)}) collective-permute-start(bf16[2048,256]{1,0:T(8,128)(2,1)S(1)} %get-tuple-element.48.refs_0_.refs_12_), channel_id=1, source_target_pairs={{0,2},{2,0},{1,3},{3,1},{4,6},{6,4},{5,7},{7,5}} | collective-permute-start | bytes 3145736 | tf_op jit(solution)/shard_map/ppermute | solution.py:17
  8.2 58.5 %collective-permute-start.3 = (bf16[2048,256]{1,0:T(8,128)(2,1)S(1)}, bf16[2048,256]{1,0:T(8,128)(2,1)}, u32[]{:S(2)}, u32[]{:S(2)}) collective-permute-start(bf16[2048,256]{1,0:T(8,128)(2,1)S(1)} %get-tuple-element.48.refs_0_.refs_12_), channel_id=1, source_target_pairs={{0,1},{1,0},{2,3},{3,2},{4,5},{5,4},{6,7},{7,6}} | collective-permute-start | bytes 3145736 | tf_op jit(solution)/shard_map/ppermute | solution.py:17
  8.2 27.9 %collective-permute-start.7 = (f32[1,256]{1,0:T(1,128)S(1)}, f32[1,256]{1,0:T(1,128)S(1)}, u32[]{:S(2)}, u32[]{:S(2)}) collective-permute-start(f32[1,256]{1,0:T(1,128)S(1)} %bitcast.71), channel_id=1, source_target_pairs={{0,4},{4,0},{1,5},{5,1},{2,6},{6,2},{3,7},{7,3}} | collective-permute-start | bytes 3080 | tf_op jit(solution)/shard_map/ppermute | solution.py:17
  8.7 53.6 %collective-permute-start.12 = (bf16[1024,512]{1,0:T(8,128)(2,1)}, bf16[1024,512]{1,0:T(8,128)(2,1)}, u32[]{:S(2)}, u32[]{:S(2)}) collective-permute-start(bf16[1024,512]{1,0:T(8,128)(2,1)} %param.17), channel_id=1, source_target_pairs={{0,4},{4,0},{1,5},{5,1},{2,6},{6,2},{3,7},{7,3}} | collective-permute-start | bytes 3145736 | tf_op jit(solution)/shard_map/ppermute | solution.py:17
  31.0 25.4 %collective-permute-start.2 = (bf16[2048,256]{1,0:T(8,128)(2,1)S(1)}, bf16[2048,256]{1,0:T(8,128)(2,1)}, u32[]{:S(2)}, u32[]{:S(2)}) collective-permute-start(bf16[2048,256]{1,0:T(8,128)(2,1)S(1)} %collective-permute-done.refs_1_.refs_6_), channel_id=1, source_target_pairs={{0,2},{2,0},{1,3},{3,1},{4,6},{6,4},{5,7},{7,5}} | collective-permute-start | bytes 3145736 | tf_op jit(solution)/shard_map/ppermute | solution.py:17
  36.1 18.5 %collective-permute-start.8 = (f32[2,256]{1,0:T(2,128)S(1)}, f32[2,256]{1,0:T(2,128)S(1)}, u32[]{:S(2)}, u32[]{:S(2)}) collective-permute-start(f32[2,256]{1,0:T(2,128)S(1)} %pad_maximum_fusion.15), channel_id=1, source_target_pairs={{0,2},{2,0},{1,3},{3,1},{4,6},{6,4},{5,7},{7,5}} | collective-permute-start | bytes 6152 | tf_op jit(solution)/shard_map/ppermute | solution.py:17
  56.4 14.0 %collective-permute-start.6 = (bf16[2048,256]{1,0:T(8,128)(2,1)}, bf16[2048,256]{1,0:T(8,128)(2,1)}, u32[]{:S(2)}, u32[]{:S(2)}) collective-permute-start(bf16[2048,256]{1,0:T(8,128)(2,1)} %collective-permute-done.2.refs_3_), channel_id=1, source_target_pairs={{0,1},{1,0},{2,3},{3,2},{4,5},{5,4},{6,7},{7,6}} | collective-permute-start | bytes 3145736 | tf_op jit(solution)/shard_map/ppermute | solution.py:17
  62.3 67.1 %collective-permute-start.10 = (bf16[2,1024,512]{2,1,0:T(8,128)(2,1)}, bf16[2,1024,512]{2,1,0:T(8,128)(2,1)}, u32[]{:S(2)}, u32[]{:S(2)}) collective-permute-start(bf16[2,1024,512]{2,1,0:T(8,128)(2,1)} %pad_maximum_fusion.near_w), channel_id=1, source_target_pairs={{0,4},{4,0},{1,5},{5,1},{2,6},{6,2},{3,7},{7,3}} | collective-permute-start | bytes 6291464 | tf_op jit(solution)/shard_map/ppermute | solution.py:17
  66.8 50.0 %collective-permute-start.16 = (bf16[512,256]{1,0:T(8,128)(2,1)}, bf16[512,256]{1,0:T(8,128)(2,1)}, u32[]{:S(2)}, u32[]{:S(2)}) collective-permute-start(bf16[512,256]{1,0:T(8,128)(2,1)} %constant_dynamic-slice_fusion.8), channel_id=1, source_target_pairs={{0,4},{4,0},{1,5},{5,1},{2,6},{6,2},{3,7},{7,3}} | collective-permute-start | bytes 786440 | tf_op jit(solution)/shard_map/ppermute | solution.py:17
  67.3 122.8 %collective-permute-start.11 = (bf16[2,1024,512]{2,1,0:T(8,128)(2,1)}, bf16[2,1024,512]{2,1,0:T(8,128)(2,1)}, u32[]{:S(2)}, u32[]{:S(2)}) collective-permute-start(bf16[2,1024,512]{2,1,0:T(8,128)(2,1)} %pad_maximum_fusion.1.near_w), channel_id=1, source_target_pairs={{0,4},{4,0},{1,5},{5,1},{2,6},{6,2},{3,7},{7,3}} | collective-permute-start | bytes 6291464 | tf_op jit(solution)/shard_map/ppermute | solution.py:17
  69.8 136.9 %collective-permute-start.18 = (bf16[2,1024,512]{2,1,0:T(8,128)(2,1)}, bf16[2,1024,512]{2,1,0:T(8,128)(2,1)}, u32[]{:S(2)}, u32[]{:S(2)}) collective-permute-start(bf16[2,1024,512]{2,1,0:T(8,128)(2,1)} %pad_maximum_fusion.3.near_w), channel_id=1, source_target_pairs={{0,4},{4,0},{1,5},{5,1},{2,6},{6,2},{3,7},{7,3}} | collective-permute-start | bytes 6291464 | tf_op jit(solution)/shard_map/ppermute | solution.py:17
  93.5 33.7 %collective-permute-start.13 = (bf16[2,512,512]{2,1,0:T(8,128)(2,1)S(1)}, bf16[2,512,512]{2,1,0:T(8,128)(2,1)}, u32[]{:S(2)}, u32[]{:S(2)}) collective-permute-start(bf16[2,512,512]{2,1,0:T(8,128)(2,1)S(1)} %dynamic-slice_bitcast_fusion), channel_id=1, source_target_pairs={{0,2},{2,0},{1,3},{3,1},{4,6},{6,4},{5,7},{7,5}} | collective-permute-start | bytes 3145736 | tf_op jit(solution)/shard_map/ppermute | solution.py:17
  120.4 130.5 %collective-permute-start.19 = (bf16[2,1024,512]{2,1,0:T(8,128)(2,1)}, bf16[2,1024,512]{2,1,0:T(8,128)(2,1)}, u32[]{:S(2)}, u32[]{:S(2)}) collective-permute-start(bf16[2,1024,512]{2,1,0:T(8,128)(2,1)} %pad_maximum_fusion.4.near_w), channel_id=1, source_target_pairs={{0,4},{4,0},{1,5},{5,1},{2,6},{6,2},{3,7},{7,3}} | collective-permute-start | bytes 6291464 | tf_op jit(solution)/shard_map/ppermute | solution.py:17
  127.1 15.8 %collective-permute-start.14 = (bf16[512,512]{1,0:T(8,128)(2,1)S(1)}, bf16[512,512]{1,0:T(8,128)(2,1)S(1)}, u32[]{:S(2)}, u32[]{:S(2)}) collective-permute-start(bf16[512,512]{1,0:T(8,128)(2,1)S(1)} %get-tuple-element.45), channel_id=1, source_target_pairs={{0,1},{1,0},{2,3},{3,2},{4,5},{5,4},{6,7},{7,6}} | collective-permute-start | bytes 1572872 | tf_op jit(solution)/shard_map/ppermute | solution.py:17
  142.9 124.6 %collective-permute-start.29 = (bf16[2560,256]{1,0:T(8,128)(2,1)}, bf16[2560,256]{1,0:T(8,128)(2,1)S(1)}, u32[]{:S(2)}, u32[]{:S(2)}) collective-permute-start(bf16[2560,256]{1,0:T(8,128)(2,1)} %pad_maximum_fusion.8), channel_id=1, source_target_pairs={{0,1},{1,0},{2,3},{3,2},{4,5},{5,4},{6,7},{7,6}} | collective-permute-start | bytes 3932168 | tf_op jit(solution)/shard_map/ppermute | solution.py:17
  143.1 124.5 %collective-permute-start.23 = (bf16[2048,512]{1,0:T(8,128)(2,1)}, bf16[2048,512]{1,0:T(8,128)(2,1)}, u32[]{:S(2)}, u32[]{:S(2)}) collective-permute-start(bf16[2048,512]{1,0:T(8,128)(2,1)} %glu.4.refs_0_), channel_id=1, source_target_pairs={{0,1},{1,0},{2,3},{3,2},{4,5},{5,4},{6,7},{7,6}} | collective-permute-start | bytes 6291464 | tf_op jit(solution)/shard_map/ppermute | solution.py:17
  190.1 16.5 %collective-permute-start.21 = (bf16[512,512]{1,0:T(8,128)(2,1)}, bf16[512,512]{1,0:T(8,128)(2,1)S(1)}, u32[]{:S(2)}, u32[]{:S(2)}) collective-permute-start(bf16[512,512]{1,0:T(8,128)(2,1)} %get-tuple-element.24), channel_id=1, source_target_pairs={{0,1},{1,0},{2,3},{3,2},{4,5},{5,4},{6,7},{7,6}} | collective-permute-start | bytes 1572872 | tf_op jit(solution)/shard_map/ppermute | solution.py:17
  206.6 57.5 %collective-permute-start.20 = (bf16[512,512]{1,0:T(8,128)(2,1)}, bf16[512,512]{1,0:T(8,128)(2,1)}, u32[]{:S(2)}, u32[]{:S(2)}) collective-permute-start(bf16[512,512]{1,0:T(8,128)(2,1)} %get-tuple-element.22), channel_id=1, source_target_pairs={{0,1},{1,0},{2,3},{3,2},{4,5},{5,4},{6,7},{7,6}} | collective-permute-start | bytes 1572872 | tf_op jit(solution)/shard_map/ppermute | solution.py:17
  206.7 59.7 %collective-permute-start.22 = (bf16[2,512,512]{2,1,0:T(8,128)(2,1)S(1)}, bf16[2,512,512]{2,1,0:T(8,128)(2,1)S(1)}, u32[]{:S(2)}, u32[]{:S(2)}) collective-permute-start(bf16[2,512,512]{2,1,0:T(8,128)(2,1)S(1)} %pad_maximum_fusion.9), channel_id=1, source_target_pairs={{0,2},{2,0},{1,3},{3,1},{4,6},{6,4},{5,7},{7,5}} | collective-permute-start | bytes 3145736 | tf_op jit(solution)/shard_map/ppermute | solution.py:17
  250.9 23.6 %collective-permute-start.25 = (bf16[2048,512]{1,0:T(8,128)(2,1)}, bf16[2048,512]{1,0:T(8,128)(2,1)}, u32[]{:S(2)}, u32[]{:S(2)}) collective-permute-start(bf16[2048,512]{1,0:T(8,128)(2,1)} %glu.6.refs_2_), channel_id=1, source_target_pairs={{0,1},{1,0},{2,3},{3,2},{4,5},{5,4},{6,7},{7,6}} | collective-permute-start | bytes 6291464 | tf_op jit(solution)/shard_map/ppermute | solution.py:17
  267.6 32.0 %collective-permute-start.30 = (bf16[2560,256]{1,0:T(8,128)(2,1)}, bf16[2560,256]{1,0:T(8,128)(2,1)}, u32[]{:S(2)}, u32[]{:S(2)}) collective-permute-start(bf16[2560,256]{1,0:T(8,128)(2,1)} %pad_maximum_fusion.8), channel_id=1, source_target_pairs={{0,4},{4,0},{1,5},{5,1},{2,6},{6,2},{3,7},{7,3}} | collective-permute-start | bytes 3932168 | tf_op jit(solution)/shard_map/ppermute | solution.py:17
  273.1 54.6 %collective-permute-start.28 = (bf16[2560,256]{1,0:T(8,128)(2,1)S(1)}, bf16[2560,256]{1,0:T(8,128)(2,1)}, u32[]{:S(2)}, u32[]{:S(2)}) collective-permute-start(bf16[2560,256]{1,0:T(8,128)(2,1)S(1)} %pad_maximum_fusion.7.refs_10_), channel_id=1, source_target_pairs={{0,4},{4,0},{1,5},{5,1},{2,6},{6,2},{3,7},{7,3}} | collective-permute-start | bytes 3932168 | tf_op jit(solution)/shard_map/ppermute | solution.py:17
  299.6 28.1 %collective-permute-start.31 = (bf16[2560,256]{1,0:T(8,128)(2,1)}, bf16[2560,256]{1,0:T(8,128)(2,1)}, u32[]{:S(2)}, u32[]{:S(2)}) collective-permute-start(bf16[2560,256]{1,0:T(8,128)(2,1)} %collective-permute-done.30), channel_id=1, source_target_pairs={{0,1},{1,0},{2,3},{3,2},{4,5},{5,4},{6,7},{7,6}} | collective-permute-start | bytes 3932168 | tf_op jit(solution)/shard_map/ppermute | solution.py:17
  302.0 53.1 %collective-permute-start.35 = (bf16[2560,256]{1,0:T(8,128)(2,1)}, bf16[2560,256]{1,0:T(8,128)(2,1)}, u32[]{:S(2)}, u32[]{:S(2)}) collective-permute-start(bf16[2560,256]{1,0:T(8,128)(2,1)} %pad_maximum_fusion.6), channel_id=1, source_target_pairs={{0,4},{4,0},{1,5},{5,1},{2,6},{6,2},{3,7},{7,3}} | collective-permute-start | bytes 3932168 | tf_op jit(solution)/shard_map/ppermute | solution.py:17
  303.5 53.3 %collective-permute-start.33 = (f32[2048,256]{1,0:T(8,128)}, f32[2048,256]{1,0:T(8,128)}, u32[]{:S(2)}, u32[]{:S(2)}) collective-permute-start(f32[2048,256]{1,0:T(8,128)} %mix.8), channel_id=1, source_target_pairs={{0,2},{2,0},{1,3},{3,1},{4,6},{6,4},{5,7},{7,5}} | collective-permute-start | bytes 6291464 | tf_op jit(solution)/shard_map/ppermute | solution.py:17
  340.3 56.3 %collective-permute-start.37 = (f32[2048,256]{1,0:T(8,128)}, f32[2048,256]{1,0:T(8,128)}, u32[]{:S(2)}, u32[]{:S(2)}) collective-permute-start(f32[2048,256]{1,0:T(8,128)} %mix.9), channel_id=1, source_target_pairs={{0,2},{2,0},{1,3},{3,1},{4,6},{6,4},{5,7},{7,5}} | collective-permute-start | bytes 6291464 | tf_op jit(solution)/shard_map/ppermute | solution.py:17
  341.7 15.1 %collective-permute-start.32 = (bf16[2560,256]{1,0:T(8,128)(2,1)}, bf16[2560,256]{1,0:T(8,128)(2,1)}, u32[]{:S(2)}, u32[]{:S(2)}) collective-permute-start(bf16[2560,256]{1,0:T(8,128)(2,1)} %pad_maximum_fusion.6), channel_id=1, source_target_pairs={{0,1},{1,0},{2,3},{3,2},{4,5},{5,4},{6,7},{7,6}} | collective-permute-start | bytes 3932168 | tf_op jit(solution)/shard_map/ppermute | solution.py:17
  355.2 41.4 %collective-permute-start.36 = (bf16[2560,256]{1,0:T(8,128)(2,1)}, bf16[2560,256]{1,0:T(8,128)(2,1)}, u32[]{:S(2)}, u32[]{:S(2)}) collective-permute-start(bf16[2560,256]{1,0:T(8,128)(2,1)} %collective-permute-done.35), channel_id=1, source_target_pairs={{0,1},{1,0},{2,3},{3,2},{4,5},{5,4},{6,7},{7,6}} | collective-permute-start | bytes 3932168 | tf_op jit(solution)/shard_map/ppermute | solution.py:17
  355.3 50.2 %collective-permute-start.34 = (bf16[2560,256]{1,0:T(8,128)(2,1)S(1)}, bf16[2560,256]{1,0:T(8,128)(2,1)S(1)}, u32[]{:S(2)}, u32[]{:S(2)}) collective-permute-start(bf16[2560,256]{1,0:T(8,128)(2,1)S(1)} %pad_maximum_fusion.5.refs_10_), channel_id=1, source_target_pairs={{0,4},{4,0},{1,5},{5,1},{2,6},{6,2},{3,7},{7,3}} | collective-permute-start | bytes 3932168 | tf_op jit(solution)/shard_map/ppermute | solution.py:17
  416.8 14.8 %collective-permute-start.38 = (bf16[1024,256]{1,0:T(8,128)(2,1)S(1)}, bf16[1024,256]{1,0:T(8,128)(2,1)S(1)}, u32[]{:S(2)}, u32[]{:S(2)}) collective-permute-start(bf16[1024,256]{1,0:T(8,128)(2,1)S(1)} %copy-done.19), channel_id=1, source_target_pairs={{0,4},{4,0},{1,5},{5,1},{2,6},{6,2},{3,7},{7,3}} | collective-permute-start | bytes 1572872 | tf_op jit(solution)/shard_map/ppermute | solution.py:17
  417.4 23.9 %collective-permute-start.39 = (bf16[1024,256]{1,0:T(8,128)(2,1)}, bf16[1024,256]{1,0:T(8,128)(2,1)S(1)}, u32[]{:S(2)}, u32[]{:S(2)}) collective-permute-start(bf16[1024,256]{1,0:T(8,128)(2,1)} %mix.13), channel_id=1, source_target_pairs={{0,4},{4,0},{1,5},{5,1},{2,6},{6,2},{3,7},{7,3}} | collective-permute-start | bytes 1572872 | tf_op jit(solution)/shard_map/ppermute | solution.py:17
  (35 other events, 352.2 us)
where the time goes:
time: 444 us; the launch traced here: 443 us
  waiting for transfers between devices  183 us (41%)
  Pallas kernels  178 us (40%)
  starting transfers between devices  31.2 us (7%)
  local copies, waits for them, and re-layouts  24.5 us (6%)
  other arithmetic  22.7 us (5%)
    ppermute x40, waiting for transfers between devices, swap(): return lambda a: lax.ppermute(a, axis, pairs)  183 us
    pallas_call x7, Pallas kernels, mix(): pl.pallas_call(functools.partial(mix_kernel, len(lhs), len(ws), len(adds)...  65.8 us
    pallas_call x4, Pallas kernels, glu(): pl.pallas_call(glu_kernel, grid=(tokens // blk,), in_specs=[pl.BlockSpec(...  52.7 us
    pallas_call x1, Pallas kernels, attention(): pl.pallas_call(attn_kernel, grid_spec=pltpu.PrefetchScalarGridSpec(num_sc...  46.2 us
    ppermute x40, starting transfers between devices, swap(): return lambda a: lax.ppermute(a, axis, pairs)  31.2 us
    pallas_call x1, Pallas kernels, layer_norm(): pl.pallas_call(norm_kernel, grid_spec=pltpu.PrefetchScalarGridSpec(num_sc...  13 us
  transfers between devices with their start and end apart: 40, of which 14 were waited for; matrix products, arithmetic and copies ran while one was open for 9% of the time, Pallas kernels for 38%

commit v1 on v0

--- a/solution.py
+++ b/solution.py
@@ -163,23 +163,25 @@
     )(h, near_w, far_w)
 
 
-def mix_kernel(n_lhs, n_w, n_add, *refs):
-    lhs, ws, adds, out_ref = refs[:n_lhs], refs[n_lhs : n_lhs + n_w], refs[n_lhs + n_w : n_lhs + n_w + n_add], refs[-1]
+def mix_kernel(plan, n_lhs, n_w, *refs):
+    lhs, ws, adds, out_ref = refs[:n_lhs], refs[n_lhs : n_lhs + n_w], refs[n_lhs + n_w : -1], refs[-1]
     total = None
-    i, row = 0, 0
-    for l in lhs:
-        k = l.shape[1]
-        part = jnp.dot(l[...], ws[i][row : row + k, :], preferred_element_type=F32)
+    for l, (w, row) in zip(lhs, plan):
+        part = jnp.dot(l[...], ws[w][row : row + l.shape[1], :], preferred_element_type=F32)
         total = part if total is None else total + part
-        row += k
-        if row == ws[i].shape[0]:
-            i, row = i + 1, 0
     for t in adds:
         total = total + t[...].astype(F32)
     out_ref[...] = total.astype(out_ref.dtype)
 
 
-def mix(lhs, ws, adds=(), dtype=F32, start=0, tokens=None):
+def mix(terms, adds=(), dtype=F32, start=0, tokens=None):
+    ws, plan = [], []
+    for _, w, row in terms:
+        found = [i for i, v in enumerate(ws) if v is w]
+        if not found:
+            ws.append(w)
+        plan.append((found[0] if found else len(ws) - 1, row))
+    lhs = [t[0] for t in terms]
     tokens = lhs[0].shape[0] if tokens is None else tokens
     cols = ws[0].shape[1]
     blk = 512
@@ -188,7 +190,7 @@
     depth = sum(l.shape[1] for l in lhs)
     add_specs = [tok(cols) if t.shape[0] != tokens else pl.BlockSpec((blk, cols), lambda i: (i, 0)) for t in adds]
     return pl.pallas_call(
-        functools.partial(mix_kernel, len(lhs), len(ws), len(adds)),
+        functools.partial(mix_kernel, plan, len(lhs), len(ws)),
         grid=(tokens // blk,),
         in_specs=[tok(l.shape[1]) for l in lhs] + [pl.BlockSpec(w.shape, lambda i: (0, 0)) for w in ws] + add_specs,
         out_specs=pl.BlockSpec((blk, cols), lambda i: (i, 0)),
@@ -240,7 +242,7 @@
         kv_far = jnp.where(ci == 0, kv_pair, kv_pair[::-1]).reshape(w_kv.shape)
         q_far = swap_y(w_query)
 
-        q = mix([h], [jnp.concatenate([w_query, q_far], 0)], dtype=BF16)
+        q = mix([(h, jnp.concatenate([w_query, q_far], 0), 0)], dtype=BF16)
         h_own = lax.dynamic_slice_in_dim(h, ti * own_tok, own_tok, 0)
         kv = jnp.dot(h_own, jnp.concatenate([w_kv, kv_far], 0), preferred_element_type=F32).astype(BF16)
 
@@ -270,11 +272,13 @@
         for j in range(chunks):
             near_w = jnp.stack([w[:, j * cw : (j + 1) * cw] for w in (w_gate, w_up)])
             far_w = swap_y(near_w)
+            if j == chunks - 1:
+                last_w = near_w, far_w
+                break
             if j > 0:
                 far_w = tie(far_w, a_own[-1], o0)
             a_own.append(glu(h, near_w, far_w))
             a_far.append(swap_c(a_own[-1]))
-        lhs_near, lhs_far = a_own + [o_own], a_far + [swap_c(o_own)]
 
         def block(xr, cr):
             col = (2 * (xi ^ xr) + (ci ^ cr)) * width
@@ -285,19 +289,38 @@
         for xr, cr in BLOCK_ORDER:
             other_y[xr][cr] = swap_y(blocks[xr][cr])
 
-        def product(pair, adds=(), dtype=F32):
-            return mix(lhs_near + lhs_far, [pair[0], swap_c(pair[1])], adds, dtype)
-
-        p_own = product(blocks[1])
-        r_own = swap_x(p_own)
-        p_far = product([tie(w, p_own) for w in other_y[1]])
-        r_far = swap_x(p_far)
-        out_own = product([blocks[0][0], tie(blocks[0][1], p_far)], [mine, r_own], BF16)
-        base = mix(lhs_far, [swap_c(tie(other_y[0][1], p_far))], [from_y, tie(r_far, out_own)])
-        last = tie(other_y[0][0], base)
+        o_far = swap_c(o_own)
+
+        def terms(near_w, far_w, which):
+            out = []
+            for a_part, o_part, w in ((a_own, o_own, near_w), (a_far, o_far, far_w)):
+                if w is not None:
+                    out += [(o_part, w, chunks * cw) if k == "o" else (a_part[k], w, k * cw) for k in which]
+            return out
+
+        early, late, every = [*range(chunks - 1), "o"], [chunks - 1], [*range(chunks), "o"]
         parts = 2
         size = half // parts
-        out_far = [swap_y(mix(lhs_near, [last], [base], BF16, i * size, size)) for i in range(parts)]
+
+        cross_far, same_far = swap_c(blocks[1][1]), swap_c(blocks[0][1])
+        pre_cross = mix(terms(blocks[1][0], cross_far, early))
+        pre_same = mix(terms(tie(blocks[0][0], pre_cross), same_far, early), [mine])
+        a_own.append(glu(h, last_w[0], tie(last_w[1], pre_same)))
+        a_far.append(swap_c(a_own[-1]))
+        p_own = mix(terms(blocks[1][0], cross_far, late), [pre_cross])
+        r_own = swap_x(p_own)
+
+        pre_far = mix(terms(None, swap_c(tie(other_y[1][1], p_own)), every))
+        near_w = tie(other_y[1][0], pre_far)
+        p_far = [mix(terms(near_w, None, every), [pre_far], F32, i * size, size) for i in range(parts)]
+        r_far = [swap_x(p) for p in p_far]
+        base = mix(terms(None, swap_c(tie(other_y[0][1], *p_far)), every), [from_y])
+        out_own = mix(terms(blocks[0][0], same_far, late), [pre_same, tie(r_own, base)], BF16)
+        last = tie(other_y[0][0], out_own)
+        out_far = []
+        for i in range(parts):
+            out_far.append(mix(terms(last, None, every), [base, r_far[i]], BF16, i * size, size))
+            out_far[i] = swap_y(out_far[i])
         out_far = jnp.concatenate(out_far, 0)
         out = jnp.where(yi == 0, jnp.stack([out_own, out_far]), jnp.stack([out_far, out_own]))
         return out.reshape(batch, new, width), k_next, v_next

time: 444 us -> 448 us (level)
  Pallas kernels: 178 us -> 193 us
  waiting for transfers between devices: 183 us -> 168 us
    pallas_call x7 -> x11, Pallas kernels: 65.8 us -> 81.3 us  [mix(): pl.pallas_call(functools.partial(mix_kernel, plan, len(lhs), len(ws)), gr...]
    ppermute x40 -> x41, waiting for transfers between devices: 183 us -> 168 us  [swap(): return lambda a: lax.ppermute(a, axis, pairs)]
    unnamed x55 -> x73, local copies, waits for them, and re-layouts: 4.74 us -> 9.19 us
    ppermute x40 -> x41, starting transfers between devices: 31.2 us -> 30.6 us  [swap(): return lambda a: lax.ppermute(a, axis, pairs)]
  transfers between devices with their start and end apart: 40 -> 41, of which waited for: 14 -> 13; matrix products, arithmetic and copies ran while one was open for 9% -> 9% of each run, Pallas kernels for 38% -> 40%
where the time goes in v1:
time: 448 us; the launch traced here: 447 us
  Pallas kernels  193 us (43%)
  waiting for transfers between devices  168 us (38%)
  starting transfers between devices  30.6 us (7%)
  local copies, waits for them, and re-layouts  26 us (6%)
  other arithmetic  25.3 us (6%)
    ppermute x41, waiting for transfers between devices, swap(): return lambda a: lax.ppermute(a, axis, pairs)  168 us
    pallas_call x11, Pallas kernels, mix(): pl.pallas_call(functools.partial(mix_kernel, plan, len(lhs), len(ws)), gr...  81.3 us
    pallas_call x4, Pallas kernels, glu(): pl.pallas_call(glu_kernel, grid=(tokens // blk,), in_specs=[pl.BlockSpec(...  52.9 us
    pallas_call x1, Pallas kernels, attention(): pl.pallas_call(attn_kernel, grid_spec=pltpu.PrefetchScalarGridSpec(num_sc...  46 us
    ppermute x41, starting transfers between devices, swap(): return lambda a: lax.ppermute(a, axis, pairs)  30.6 us
    pallas_call x1, Pallas kernels, layer_norm(): pl.pallas_call(norm_kernel, grid_spec=pltpu.PrefetchScalarGridSpec(num_sc...  13 us
    unnamed x73, local copies, waits for them, and re-layouts  9.19 us
  transfers between devices with their start and end apart: 41, of which 13 were waited for; matrix products, arithmetic and copies ran while one was open for 9% of the time, Pallas kernels for 40%

profile of v1, /device:TPU:0, one launch (start us, length us, event | category | flops | bytes accessed | tf_op | source)
XLA Modules:
  0.0 446.8 jit_solution(11020628471066495164)
XLA Ops:
  2.5 3.4 collective-permute-start
  9.4 20.5 %collective-permute-done.refs_1_.refs_6_ = bf16[2048,256]{1,0:T(8,128)(2,1)S(1)} collective-permute-done((bf16[2048,256]{1,0:T(8,128)(2,1)S(1)}, bf16[2048,256]{1,0:T(8,128)(2,1)S(1)}, u32[]{:S(2)}, u32[]{:S(2)}) %collective-permute-start) | collective-permute-done | bytes 1048608 | tf_op jit(solution)/shard_map/ppermute | solution.py:17
  31.9 3.8 slice_bitcast_fusion.6
  39.2 14.3 %collective-permute-done.8 = f32[2,256]{1,0:T(2,128)S(1)} collective-permute-done((f32[2,256]{1,0:T(2,128)S(1)}, f32[2,256]{1,0:T(2,128)S(1)}, u32[]{:S(2)}, u32[]{:S(2)}) %collective-permute-start.8) | collective-permute-done | bytes 2080 | tf_op jit(solution)/shard_map/ppermute | solution.py:17
  55.6 4.1 constant_dynamic-slice_fusion.1
  67.4 13.0 %norm.1.h_ref.refs_0_ = bf16[2048,2048]{1,0:T(8,128)(2,1)} custom-call(s32[8]{0:T(128)} %stack.129.offs_ref, bf16[2048,256]{1,0:T(8,128)(2,1)} %copy-done.6, bf16[2048,256]{1,0:T(8,128)(2,1)} %copy-done.11, bf16[2048,256]{1,0:T(8,128)(2,1)} %collective-permute-done.1.refs_2_, bf16[2048,256]{1,0:T(8,128)(2,1)} %collective-permute-done.2.refs_3_, ...), custom_call_target="tpu_custom_call" | custom-call | flops 83886080 | bytes 16777216 | tf_op jit(solution)/shard_map/norm/pallas_call | solution.py:47
  80.5 8.7 %mix.11 = bf16[2048,512]{1,0:T(8,128)(2,1)} custom-call(bf16[2048,2048]{1,0:T(8,128)(2,1)} %norm.1.h_ref.refs_0_, bf16[2048,512]{1,0:T(8,128)(2,1)} %pad_maximum_fusion.3.refs_1_), custom_call_target="tpu_custom_call" | custom-call | flops 4294967296 | bytes 10485760 | tf_op jit(solution)/shard_map/mix/pallas_call | solution.py:192
  99.2 17.3 %collective-permute-done.14 = bf16[2,512,512]{2,1,0:T(8,128)(2,1)} collective-permute-done((bf16[2,512,512]{2,1,0:T(8,128)(2,1)}, bf16[2,512,512]{2,1,0:T(8,128)(2,1)}, u32[]{:S(2)}, u32[]{:S(2)}) %collective-permute-start.14) | collective-permute-done | bytes 1048608 | tf_op jit(solution)/shard_map/ppermute | solution.py:17
  121.9 3.0 fusion.2.kv_ref
  125.8 46.0 %attn.1 = (bf16[512,512]{1,0:T(8,128)(2,1)}, bf16[512,512]{1,0:T(8,128)(2,1)}, bf16[512,512]{1,0:T(8,128)(2,1)}, bf16[512,512]{1,0:T(8,128)(2,1)}, bf16[8,2048,1...) custom-call(s32[8]{0:T(128)} %len_ref.1, bf16[512,512]{1,0:T(8,128)(2,1)} %get-tuple-element.46.q0, ...), custom_call_target="tpu_custom_call" | custom-call | flops 17179869184 | bytes 16777216 | tf_op jit(solution)/shard_map/attn/pallas_call | solution.py:125
  171.8 13.4 %glu.4.refs_0_ = bf16[2048,512]{1,0:T(8,128)(2,1)} custom-call(bf16[2048,2048]{1,0:T(8,128)(2,1)} %norm.1.h_ref.refs_0_, bf16[2,1024,512]{2,1,0:T(8,128)(2,1)} %pad_maximum_fusion.1.near_w, bf16[2,1024,512]{2,1,0:T(8,128)(2,1)} %collective-permute-done.11.far_w), custom_call_target="tpu_custom_call" | custom-call | flops 8589934592 | bytes 14680064 | tf_op jit(solution)/shard_map/glu/pallas_call | solution.py:155
  188.7 13.2 %glu.5.refs_1_ = bf16[2048,512]{1,0:T(8,128)(2,1)} custom-call(bf16[2048,2048]{1,0:T(8,128)(2,1)} %norm.1.h_ref.refs_0_, bf16[2,1024,512]{2,1,0:T(8,128)(2,1)} %pad_maximum_fusion.2.near_w, bf16[2,1024,512]{2,1,0:T(8,128)(2,1)} %collective-permute-done.12.far_w), custom_call_target="tpu_custom_call" | custom-call | flops 8589934592 | bytes 14680064 | tf_op jit(solution)/shard_map/glu/pallas_call | solution.py:155
  203.7 13.2 %glu.6.refs_2_ = bf16[2048,512]{1,0:T(8,128)(2,1)} custom-call(bf16[2048,2048]{1,0:T(8,128)(2,1)} %norm.1.h_ref.refs_0_, bf16[2,1024,512]{2,1,0:T(8,128)(2,1)} %pad_maximum_fusion.4.near_w, bf16[2,1024,512]{2,1,0:T(8,128)(2,1)} %collective-permute-done.19.far_w), custom_call_target="tpu_custom_call" | custom-call | flops 8589934592 | bytes 14680064 | tf_op jit(solution)/shard_map/glu/pallas_call | solution.py:155
  231.3 10.8 %mix.12.refs_4_ = f32[2048,256]{1,0:T(8,128)} custom-call(bf16[2048,512]{1,0:T(8,128)(2,1)} %glu.4.refs_0_, bf16[2048,512]{1,0:T(8,128)(2,1)} %glu.5.refs_1_, bf16[2048,512]{1,0:T(8,128)(2,1)} %glu.6.refs_2_, bf16[2048,512]{1,0:T(8,128)(2,1)} %bitcast.56, bf16[2048,512]{1,0:T(8,128)(2,1)} %copy-done.2, ...), custom_call_target="tpu_custom_call" | custom-call | flops 4294967296 | bytes 18874368 | tf_op jit(solution)/shard_map/mix/pallas_call | solution.py:192
  243.1 11.1 %mix.13.refs_4_ = f32[2048,256]{1,0:T(8,128)} custom-call(bf16[2048,512]{1,0:T(8,128)(2,1)} %glu.4.refs_0_, bf16[2048,512]{1,0:T(8,128)(2,1)} %glu.5.refs_1_, bf16[2048,512]{1,0:T(8,128)(2,1)} %glu.6.refs_2_, bf16[2048,512]{1,0:T(8,128)(2,1)} %bitcast.57, bf16[2048,512]{1,0:T(8,128)(2,1)} %copy-done.2, ...), custom_call_target="tpu_custom_call" | custom-call | flops 4294967296 | bytes 18874368 | tf_op jit(solution)/shard_map/mix/pallas_call | solution.py:192
  254.2 18.5 %collective-permute-done.10.far_w = bf16[2,1024,512]{2,1,0:T(8,128)(2,1)} collective-permute-done((bf16[2,1024,512]{2,1,0:T(8,128)(2,1)}, bf16[2,1024,512]{2,1,0:T(8,128)(2,1)}, u32[]{:S(2)}, u32[]{:S(2)}) %collective-permute-start.10) | collective-permute-done | bytes 2097184 | tf_op jit(solution)/shard_map/ppermute | solution.py:17
  272.7 13.2 %glu.7.refs_0_.refs_3_ = bf16[2048,512]{1,0:T(8,128)(2,1)} custom-call(bf16[2048,2048]{1,0:T(8,128)(2,1)} %norm.1.h_ref.refs_0_, bf16[2,1024,512]{2,1,0:T(8,128)(2,1)} %pad_maximum_fusion.near_w, bf16[2,1024,512]{2,1,0:T(8,128)(2,1)} %collective-permute-done.10.far_w), custom_call_target="tpu_custom_call" | custom-call | flops 8589934592 | bytes 14680064 | tf_op jit(solution)/shard_map/glu/pallas_call | solution.py:155
  287.3 2.9 collective-permute-done.29.refs_1_.refs_3_
  291.5 6.3 %mix.14 = f32[2048,256]{1,0:T(8,128)} custom-call(bf16[2048,512]{1,0:T(8,128)(2,1)} %glu.7.refs_0_.refs_3_, bf16[2048,512]{1,0:T(8,128)(2,1)} %copy-done.1, bf16[2560,256]{1,0:T(8,128)(2,1)} %pad_maximum_fusion.6.refs_8_.refs_2_, bf16[2560,256]{1,0:T(8,128)(2,1)} %copy-done.9, f32[2048,256]{1,0:T(8,128)} %mix.12.refs_4_), custom_call_target="tpu_custom_call" | custom-call | flops 1073741824 | bytes 4718592 | tf_op jit(solution)/shard_map/mix/pallas_call | solution.py:192
  297.9 19.5 %collective-permute-done.33 = bf16[2560,256]{1,0:T(8,128)(2,1)} collective-permute-done((bf16[2560,256]{1,0:T(8,128)(2,1)}, bf16[2560,256]{1,0:T(8,128)(2,1)}, u32[]{:S(2)}, u32[]{:S(2)}) %collective-permute-start.33) | collective-permute-done | bytes 1310752 | tf_op jit(solution)/shard_map/ppermute | solution.py:17
  320.8 8.0 %mix.15.refs_6_ = f32[2048,256]{1,0:T(8,128)} custom-call(bf16[2048,512]{1,0:T(8,128)(2,1)} %copy-done.2, bf16[2048,512]{1,0:T(8,128)(2,1)} %collective-permute-done.24.refs_5_.refs_1_, bf16[2048,512]{1,0:T(8,128)(2,1)} %copy-done.3, bf16[2048,512]{1,0:T(8,128)(2,1)} %copy-done.1, bf16[2048,512]{1,0:T(8,128)(2,1)} %collective-permute-done.26.refs_7_.refs_4_, ...), custom_call_target="tpu_custom_call" | custom-call | flops 2684354560 | bytes 11796480 | tf_op jit(solution)/shard_map/mix/pallas_call | solution.py:192
  328.8 20.2 %collective-permute-done.32.refs_5_ = bf16[2560,256]{1,0:T(8,128)(2,1)S(1)} collective-permute-done((bf16[2560,256]{1,0:T(8,128)(2,1)S(1)}, bf16[2560,256]{1,0:T(8,128)(2,1)S(1)}, u32[]{:S(2)}, u32[]{:S(2)}) %collective-permute-start.32) | collective-permute-done | bytes 1310752 | tf_op jit(solution)/shard_map/ppermute | solution.py:17
  350.1 5.1 %mix.17 = f32[1024,256]{1,0:T(8,128)} custom-call(bf16[2048,512]{1,0:T(8,128)(2,1)} %glu.4.refs_0_, bf16[2048,512]{1,0:T(8,128)(2,1)} %glu.5.refs_1_, bf16[2048,512]{1,0:T(8,128)(2,1)} %glu.6.refs_2_, bf16[2048,512]{1,0:T(8,128)(2,1)} %glu.7.refs_0_.refs_3_, bf16[2048,512]{1,0:T(8,128)(2,1)} %bitcast.58, bf16[2560,256]{1,0:T(8,128)(2,1)} %copy-done.7, ...), custom_call_target="tpu_custom_call" | custom-call | flops 1342177280 | bytes 6553600 | tf_op jit(solution)/shard_map/mix/pallas_call | solution.py:192
  355.2 5.6 %mix.16 = f32[1024,256]{1,0:T(8,128)} custom-call(bf16[2048,512]{1,0:T(8,128)(2,1)} %glu.4.refs_0_, bf16[2048,512]{1,0:T(8,128)(2,1)} %glu.5.refs_1_, bf16[2048,512]{1,0:T(8,128)(2,1)} %glu.6.refs_2_, bf16[2048,512]{1,0:T(8,128)(2,1)} %glu.7.refs_0_.refs_3_, bf16[2048,512]{1,0:T(8,128)(2,1)} %bitcast.59, bf16[2560,256]{1,0:T(8,128)(2,1)} %copy-done.7, ...), custom_call_target="tpu_custom_call" | custom-call | flops 1342177280 | bytes 6553600 | tf_op jit(solution)/shard_map/mix/pallas_call | solution.py:192
  360.8 15.9 %collective-permute-done.31 = bf16[2560,256]{1,0:T(8,128)(2,1)} collective-permute-done((bf16[2560,256]{1,0:T(8,128)(2,1)}, bf16[2560,256]{1,0:T(8,128)(2,1)}, u32[]{:S(2)}, u32[]{:S(2)}) %collective-permute-start.31) | collective-permute-done | bytes 1310752 | tf_op jit(solution)/shard_map/ppermute | solution.py:17
  380.3 8.4 %mix.18.refs_6_ = f32[2048,256]{1,0:T(8,128)} custom-call(bf16[2048,512]{1,0:T(8,128)(2,1)} %copy-done.2, bf16[2048,512]{1,0:T(8,128)(2,1)} %collective-permute-done.24.refs_5_.refs_1_, bf16[2048,512]{1,0:T(8,128)(2,1)} %copy-done.3, bf16[2048,512]{1,0:T(8,128)(2,1)} %copy-done.1, bf16[2048,512]{1,0:T(8,128)(2,1)} %collective-permute-done.26.refs_7_.refs_4_, ...), custom_call_target="tpu_custom_call" | custom-call | flops 2684354560 | bytes 11796480 | tf_op jit(solution)/shard_map/mix/pallas_call | solution.py:192
  388.6 6.6 %mix.19 = bf16[2048,256]{1,0:T(8,128)(2,1)} custom-call(bf16[2048,512]{1,0:T(8,128)(2,1)} %glu.7.refs_0_.refs_3_, bf16[2048,512]{1,0:T(8,128)(2,1)} %copy-done.1, bf16[2560,256]{1,0:T(8,128)(2,1)} %pad_maximum_fusion.5.refs_8_.refs_2_, bf16[2560,256]{1,0:T(8,128)(2,1)} %copy-done.8, f32[2048,256]{1,0:T(8,128)} %mix.13.refs_4_, ...), custom_call_target="tpu_custom_call" | custom-call | flops 1073741824 | bytes 4718592 | tf_op jit(solution)/shard_map/mix/pallas_call | solution.py:192
  395.2 12.8 %collective-permute-done.36.refs_5_ = bf16[2560,256]{1,0:T(8,128)(2,1)S(1)} collective-permute-done((bf16[2560,256]{1,0:T(8,128)(2,1)S(1)}, bf16[2560,256]{1,0:T(8,128)(2,1)S(1)}, u32[]{:S(2)}, u32[]{:S(2)}) %collective-permute-start.36) | collective-permute-done | bytes 1310752 | tf_op jit(solution)/shard_map/ppermute | solution.py:17
  409.0 5.4 %mix.20 = bf16[1024,256]{1,0:T(8,128)(2,1)} custom-call(bf16[2048,512]{1,0:T(8,128)(2,1)} %glu.4.refs_0_, bf16[2048,512]{1,0:T(8,128)(2,1)} %glu.5.refs_1_, bf16[2048,512]{1,0:T(8,128)(2,1)} %glu.6.refs_2_, bf16[2048,512]{1,0:T(8,128)(2,1)} %glu.7.refs_0_.refs_3_, bf16[2048,512]{1,0:T(8,128)(2,1)} %bitcast.60, bf16[2560,256]{1,0:T(8,128)(2,1)} %copy-done.10, ...), custom_call_target="tpu_custom_call" | custom-call | flops 1342177280 | bytes 6553600 | tf_op jit(solution)/shard_map/mix/pallas_call | solution.py:192
  415.8 10.5 %collective-permute-done.39.refs_7_ = f32[1024,256]{1,0:T(8,128)} collective-permute-done((f32[1024,256]{1,0:T(8,128)}, f32[1024,256]{1,0:T(8,128)}, u32[]{:S(2)}, u32[]{:S(2)}) %collective-permute-start.39) | collective-permute-done | bytes 1048608 | tf_op jit(solution)/shard_map/ppermute | solution.py:17
  426.3 5.4 %mix.21 = bf16[1024,256]{1,0:T(8,128)(2,1)} custom-call(bf16[2048,512]{1,0:T(8,128)(2,1)} %glu.4.refs_0_, bf16[2048,512]{1,0:T(8,128)(2,1)} %glu.5.refs_1_, bf16[2048,512]{1,0:T(8,128)(2,1)} %glu.6.refs_2_, bf16[2048,512]{1,0:T(8,128)(2,1)} %glu.7.refs_0_.refs_3_, bf16[2048,512]{1,0:T(8,128)(2,1)} %bitcast.61, bf16[2560,256]{1,0:T(8,128)(2,1)} %copy-done.10, ...), custom_call_target="tpu_custom_call" | custom-call | flops 1342177280 | bytes 6553600 | tf_op jit(solution)/shard_map/mix/pallas_call | solution.py:192
  432.2 12.8 %collective-permute-done.40 = bf16[1024,256]{1,0:T(8,128)(2,1)S(1)} collective-permute-done((bf16[1024,256]{1,0:T(8,128)(2,1)}, bf16[1024,256]{1,0:T(8,128)(2,1)S(1)}, u32[]{:S(2)}, u32[]{:S(2)}) %collective-permute-start.40) | collective-permute-done | bytes 524320 | tf_op jit(solution)/shard_map/ppermute | solution.py:17
  (176 shorter events, 73.1 us)
Async XLA Ops:
  2.5 27.4 %collective-permute-start = (bf16[2048,256]{1,0:T(8,128)(2,1)S(1)}, bf16[2048,256]{1,0:T(8,128)(2,1)S(1)}, u32[]{:S(2)}, u32[]{:S(2)}) collective-permute-start(bf16[2048,256]{1,0:T(8,128)(2,1)S(1)} %get-tuple-element.47), channel_id=1, source_target_pairs={{0,4},{4,0},{1,5},{5,1},{2,6},{6,2},{3,7},{7,3}} | collective-permute-start | bytes 3145736 | tf_op jit(solution)/shard_map/ppermute | solution.py:17
  5.9 49.1 %collective-permute-start.1 = (bf16[2048,256]{1,0:T(8,128)(2,1)S(1)}, bf16[2048,256]{1,0:T(8,128)(2,1)}, u32[]{:S(2)}, u32[]{:S(2)}) collective-permute-start(bf16[2048,256]{1,0:T(8,128)(2,1)S(1)} %get-tuple-element.48.refs_0_.refs_10_), channel_id=1, source_target_pairs={{0,2},{2,0},{1,3},{3,1},{4,6},{6,4},{5,7},{7,5}} | collective-permute-start | bytes 3145736 | tf_op jit(solution)/shard_map/ppermute | solution.py:17
  7.4 57.1 %collective-permute-start.3 = (bf16[2048,256]{1,0:T(8,128)(2,1)S(1)}, bf16[2048,256]{1,0:T(8,128)(2,1)}, u32[]{:S(2)}, u32[]{:S(2)}) collective-permute-start(bf16[2048,256]{1,0:T(8,128)(2,1)S(1)} %get-tuple-element.48.refs_0_.refs_10_), channel_id=1, source_target_pairs={{0,1},{1,0},{2,3},{3,2},{4,5},{5,4},{6,7},{7,6}} | collective-permute-start | bytes 3145736 | tf_op jit(solution)/shard_map/ppermute | solution.py:17
  7.4 31.4 %collective-permute-start.7 = (f32[1,256]{1,0:T(1,128)S(1)}, f32[1,256]{1,0:T(1,128)S(1)}, u32[]{:S(2)}, u32[]{:S(2)}) collective-permute-start(f32[1,256]{1,0:T(1,128)S(1)} %bitcast.71), channel_id=1, source_target_pairs={{0,4},{4,0},{1,5},{5,1},{2,6},{6,2},{3,7},{7,3}} | collective-permute-start | bytes 3080 | tf_op jit(solution)/shard_map/ppermute | solution.py:17
  7.9 52.4 %collective-permute-start.13 = (bf16[1024,512]{1,0:T(8,128)(2,1)}, bf16[1024,512]{1,0:T(8,128)(2,1)}, u32[]{:S(2)}, u32[]{:S(2)}) collective-permute-start(bf16[1024,512]{1,0:T(8,128)(2,1)} %param.17), channel_id=1, source_target_pairs={{0,4},{4,0},{1,5},{5,1},{2,6},{6,2},{3,7},{7,3}} | collective-permute-start | bytes 3145736 | tf_op jit(solution)/shard_map/ppermute | solution.py:17
  29.9 25.4 %collective-permute-start.2 = (bf16[2048,256]{1,0:T(8,128)(2,1)S(1)}, bf16[2048,256]{1,0:T(8,128)(2,1)}, u32[]{:S(2)}, u32[]{:S(2)}) collective-permute-start(bf16[2048,256]{1,0:T(8,128)(2,1)S(1)} %collective-permute-done.refs_1_.refs_6_), channel_id=1, source_target_pairs={{0,2},{2,0},{1,3},{3,1},{4,6},{6,4},{5,7},{7,5}} | collective-permute-start | bytes 3145736 | tf_op jit(solution)/shard_map/ppermute | solution.py:17
  38.8 14.8 %collective-permute-start.8 = (f32[2,256]{1,0:T(2,128)S(1)}, f32[2,256]{1,0:T(2,128)S(1)}, u32[]{:S(2)}, u32[]{:S(2)}) collective-permute-start(f32[2,256]{1,0:T(2,128)S(1)} %pad_maximum_fusion.15), channel_id=1, source_target_pairs={{0,2},{2,0},{1,3},{3,1},{4,6},{6,4},{5,7},{7,5}} | collective-permute-start | bytes 6152 | tf_op jit(solution)/shard_map/ppermute | solution.py:17
  60.3 37.5 %collective-permute-start.17 = (bf16[512,256]{1,0:T(8,128)(2,1)S(1)}, bf16[512,256]{1,0:T(8,128)(2,1)}, u32[]{:S(2)}, u32[]{:S(2)}) collective-permute-start(bf16[512,256]{1,0:T(8,128)(2,1)S(1)} %constant_dynamic-slice_fusion.8), channel_id=1, source_target_pairs={{0,4},{4,0},{1,5},{5,1},{2,6},{6,2},{3,7},{7,3}} | collective-permute-start | bytes 786440 | tf_op jit(solution)/shard_map/ppermute | solution.py:17
  64.4 107.4 %collective-permute-start.11 = (bf16[2,1024,512]{2,1,0:T(8,128)(2,1)}, bf16[2,1024,512]{2,1,0:T(8,128)(2,1)}, u32[]{:S(2)}, u32[]{:S(2)}) collective-permute-start(bf16[2,1024,512]{2,1,0:T(8,128)(2,1)} %pad_maximum_fusion.1.near_w), channel_id=1, source_target_pairs={{0,4},{4,0},{1,5},{5,1},{2,6},{6,2},{3,7},{7,3}} | collective-permute-start | bytes 6291464 | tf_op jit(solution)/shard_map/ppermute | solution.py:17
  65.0 120.5 %collective-permute-start.12 = (bf16[2,1024,512]{2,1,0:T(8,128)(2,1)}, bf16[2,1024,512]{2,1,0:T(8,128)(2,1)}, u32[]{:S(2)}, u32[]{:S(2)}) collective-permute-start(bf16[2,1024,512]{2,1,0:T(8,128)(2,1)} %pad_maximum_fusion.2.near_w), channel_id=1, source_target_pairs={{0,4},{4,0},{1,5},{5,1},{2,6},{6,2},{3,7},{7,3}} | collective-permute-start | bytes 6291464 | tf_op jit(solution)/shard_map/ppermute | solution.py:17
  91.6 24.9 %collective-permute-start.14 = (bf16[2,512,512]{2,1,0:T(8,128)(2,1)}, bf16[2,512,512]{2,1,0:T(8,128)(2,1)}, u32[]{:S(2)}, u32[]{:S(2)}) collective-permute-start(bf16[2,512,512]{2,1,0:T(8,128)(2,1)} %dynamic-slice_bitcast_fusion), channel_id=1, source_target_pairs={{0,2},{2,0},{1,3},{3,1},{4,6},{6,4},{5,7},{7,5}} | collective-permute-start | bytes 3145736 | tf_op jit(solution)/shard_map/ppermute | solution.py:17
  97.7 21.8 %collective-permute-start.18 = (bf16[512,256]{1,0:T(8,128)(2,1)}, bf16[512,256]{1,0:T(8,128)(2,1)S(1)}, u32[]{:S(2)}, u32[]{:S(2)}) collective-permute-start(bf16[512,256]{1,0:T(8,128)(2,1)} %collective-permute-done.17), channel_id=1, source_target_pairs={{0,1},{1,0},{2,3},{3,2},{4,5},{5,4},{6,7},{7,6}} | collective-permute-start | bytes 786440 | tf_op jit(solution)/shard_map/ppermute | solution.py:17
  98.7 26.3 %collective-permute-start.15 = (bf16[512,512]{1,0:T(8,128)(2,1)S(1)}, bf16[512,512]{1,0:T(8,128)(2,1)S(1)}, u32[]{:S(2)}, u32[]{:S(2)}) collective-permute-start(bf16[512,512]{1,0:T(8,128)(2,1)S(1)} %get-tuple-element.45), channel_id=1, source_target_pairs={{0,1},{1,0},{2,3},{3,2},{4,5},{5,4},{6,7},{7,6}} | collective-permute-start | bytes 1572872 | tf_op jit(solution)/shard_map/ppermute | solution.py:17
  119.6 84.2 %collective-permute-start.19 = (bf16[2,1024,512]{2,1,0:T(8,128)(2,1)}, bf16[2,1024,512]{2,1,0:T(8,128)(2,1)}, u32[]{:S(2)}, u32[]{:S(2)}) collective-permute-start(bf16[2,1024,512]{2,1,0:T(8,128)(2,1)} %pad_maximum_fusion.4.near_w), channel_id=1, source_target_pairs={{0,4},{4,0},{1,5},{5,1},{2,6},{6,2},{3,7},{7,3}} | collective-permute-start | bytes 6291464 | tf_op jit(solution)/shard_map/ppermute | solution.py:17
  125.0 99.8 %collective-permute-start.27 = (bf16[2560,256]{1,0:T(8,128)(2,1)}, bf16[2560,256]{1,0:T(8,128)(2,1)S(1)}, u32[]{:S(2)}, u32[]{:S(2)}) collective-permute-start(bf16[2560,256]{1,0:T(8,128)(2,1)} %pad_maximum_fusion.7), channel_id=1, source_target_pairs={{0,1},{1,0},{2,3},{3,2},{4,5},{5,4},{6,7},{7,6}} | collective-permute-start | bytes 3932168 | tf_op jit(solution)/shard_map/ppermute | solution.py:17
  171.8 13.9 %collective-permute-start.21 = (bf16[512,512]{1,0:T(8,128)(2,1)}, bf16[512,512]{1,0:T(8,128)(2,1)}, u32[]{:S(2)}, u32[]{:S(2)}) collective-permute-start(bf16[512,512]{1,0:T(8,128)(2,1)} %get-tuple-element.23), channel_id=1, source_target_pairs={{0,1},{1,0},{2,3},{3,2},{4,5},{5,4},{6,7},{7,6}} | collective-permute-start | bytes 1572872 | tf_op jit(solution)/shard_map/ppermute | solution.py:17
  185.2 42.2 %collective-permute-start.23 = (bf16[2048,512]{1,0:T(8,128)(2,1)}, bf16[2048,512]{1,0:T(8,128)(2,1)S(1)}, u32[]{:S(2)}, u32[]{:S(2)}) collective-permute-start(bf16[2048,512]{1,0:T(8,128)(2,1)} %glu.4.refs_0_), channel_id=1, source_target_pairs={{0,1},{1,0},{2,3},{3,2},{4,5},{5,4},{6,7},{7,6}} | collective-permute-start | bytes 6291464 | tf_op jit(solution)/shard_map/ppermute | solution.py:17
  185.5 31.4 %collective-permute-start.20 = (bf16[512,512]{1,0:T(8,128)(2,1)}, bf16[512,512]{1,0:T(8,128)(2,1)}, u32[]{:S(2)}, u32[]{:S(2)}) collective-permute-start(bf16[512,512]{1,0:T(8,128)(2,1)} %get-tuple-element.21), channel_id=1, source_target_pairs={{0,1},{1,0},{2,3},{3,2},{4,5},{5,4},{6,7},{7,6}} | collective-permute-start | bytes 1572872 | tf_op jit(solution)/shard_map/ppermute | solution.py:17
  188.0 31.2 %collective-permute-start.22 = (bf16[2,512,512]{2,1,0:T(8,128)(2,1)}, bf16[2,512,512]{2,1,0:T(8,128)(2,1)}, u32[]{:S(2)}, u32[]{:S(2)}) collective-permute-start(bf16[2,512,512]{2,1,0:T(8,128)(2,1)} %pad_maximum_fusion.9), channel_id=1, source_target_pairs={{0,2},{2,0},{1,3},{3,1},{4,6},{6,4},{5,7},{7,5}} | collective-permute-start | bytes 3145736 | tf_op jit(solution)/shard_map/ppermute | solution.py:17
  203.7 27.5 %collective-permute-start.24 = (bf16[2048,512]{1,0:T(8,128)(2,1)}, bf16[2048,512]{1,0:T(8,128)(2,1)}, u32[]{:S(2)}, u32[]{:S(2)}) collective-permute-start(bf16[2048,512]{1,0:T(8,128)(2,1)} %glu.5.refs_1_), channel_id=1, source_target_pairs={{0,1},{1,0},{2,3},{3,2},{4,5},{5,4},{6,7},{7,6}} | collective-permute-start | bytes 6291464 | tf_op jit(solution)/shard_map/ppermute | solution.py:17
  216.9 13.0 %collective-permute-start.25 = (bf16[2048,512]{1,0:T(8,128)(2,1)}, bf16[2048,512]{1,0:T(8,128)(2,1)S(1)}, u32[]{:S(2)}, u32[]{:S(2)}) collective-permute-start(bf16[2048,512]{1,0:T(8,128)(2,1)} %glu.6.refs_2_), channel_id=1, source_target_pairs={{0,1},{1,0},{2,3},{3,2},{4,5},{5,4},{6,7},{7,6}} | collective-permute-start | bytes 6291464 | tf_op jit(solution)/shard_map/ppermute | solution.py:17
  224.8 47.9 %collective-permute-start.10 = (bf16[2,1024,512]{2,1,0:T(8,128)(2,1)}, bf16[2,1024,512]{2,1,0:T(8,128)(2,1)}, u32[]{:S(2)}, u32[]{:S(2)}) collective-permute-start(bf16[2,1024,512]{2,1,0:T(8,128)(2,1)} %pad_maximum_fusion.near_w), channel_id=1, source_target_pairs={{0,4},{4,0},{1,5},{5,1},{2,6},{6,2},{3,7},{7,3}} | collective-permute-start | bytes 6291464 | tf_op jit(solution)/shard_map/ppermute | solution.py:17
  227.5 14.6 %collective-permute-start.28 = (bf16[2560,256]{1,0:T(8,128)(2,1)}, bf16[2560,256]{1,0:T(8,128)(2,1)S(1)}, u32[]{:S(2)}, u32[]{:S(2)}) collective-permute-start(bf16[2560,256]{1,0:T(8,128)(2,1)} %pad_maximum_fusion.8), channel_id=1, source_target_pairs={{0,1},{1,0},{2,3},{3,2},{4,5},{5,4},{6,7},{7,6}} | collective-permute-start | bytes 3932168 | tf_op jit(solution)/shard_map/ppermute | solution.py:17
  285.9 31.5 %collective-permute-start.33 = (bf16[2560,256]{1,0:T(8,128)(2,1)}, bf16[2560,256]{1,0:T(8,128)(2,1)}, u32[]{:S(2)}, u32[]{:S(2)}) collective-permute-start(bf16[2560,256]{1,0:T(8,128)(2,1)} %pad_maximum_fusion.7), channel_id=1, source_target_pairs={{0,4},{4,0},{1,5},{5,1},{2,6},{6,2},{3,7},{7,3}} | collective-permute-start | bytes 3932168 | tf_op jit(solution)/shard_map/ppermute | solution.py:17
  317.4 31.6 %collective-permute-start.32 = (bf16[2560,256]{1,0:T(8,128)(2,1)S(1)}, bf16[2560,256]{1,0:T(8,128)(2,1)S(1)}, u32[]{:S(2)}, u32[]{:S(2)}) collective-permute-start(bf16[2560,256]{1,0:T(8,128)(2,1)S(1)} %copy-done.5), channel_id=1, source_target_pairs={{0,4},{4,0},{1,5},{5,1},{2,6},{6,2},{3,7},{7,3}} | collective-permute-start | bytes 3932168 | tf_op jit(solution)/shard_map/ppermute | solution.py:17
  318.8 57.9 %collective-permute-start.31 = (bf16[2560,256]{1,0:T(8,128)(2,1)}, bf16[2560,256]{1,0:T(8,128)(2,1)}, u32[]{:S(2)}, u32[]{:S(2)}) collective-permute-start(bf16[2560,256]{1,0:T(8,128)(2,1)} %pad_maximum_fusion.8), channel_id=1, source_target_pairs={{0,4},{4,0},{1,5},{5,1},{2,6},{6,2},{3,7},{7,3}} | collective-permute-start | bytes 3932168 | tf_op jit(solution)/shard_map/ppermute | solution.py:17
  319.4 69.2 %collective-permute-start.30 = (f32[2048,256]{1,0:T(8,128)}, f32[2048,256]{1,0:T(8,128)}, u32[]{:S(2)}, u32[]{:S(2)}) collective-permute-start(f32[2048,256]{1,0:T(8,128)} %mix.14), channel_id=1, source_target_pairs={{0,2},{2,0},{1,3},{3,1},{4,6},{6,4},{5,7},{7,5}} | collective-permute-start | bytes 6291464 | tf_op jit(solution)/shard_map/ppermute | solution.py:17
  376.8 31.2 %collective-permute-start.36 = (bf16[2560,256]{1,0:T(8,128)(2,1)S(1)}, bf16[2560,256]{1,0:T(8,128)(2,1)S(1)}, u32[]{:S(2)}, u32[]{:S(2)}) collective-permute-start(bf16[2560,256]{1,0:T(8,128)(2,1)S(1)} %copy-done.4), channel_id=1, source_target_pairs={{0,4},{4,0},{1,5},{5,1},{2,6},{6,2},{3,7},{7,3}} | collective-permute-start | bytes 3932168 | tf_op jit(solution)/shard_map/ppermute | solution.py:17
  378.2 29.7 %collective-permute-start.37 = (f32[1024,256]{1,0:T(8,128)}, f32[1024,256]{1,0:T(8,128)}, u32[]{:S(2)}, u32[]{:S(2)}) collective-permute-start(f32[1024,256]{1,0:T(8,128)} %mix.16), channel_id=1, source_target_pairs={{0,2},{2,0},{1,3},{3,1},{4,6},{6,4},{5,7},{7,5}} | collective-permute-start | bytes 3145736 | tf_op jit(solution)/shard_map/ppermute | solution.py:17
  379.7 46.6 %collective-permute-start.39 = (f32[1024,256]{1,0:T(8,128)}, f32[1024,256]{1,0:T(8,128)}, u32[]{:S(2)}, u32[]{:S(2)}) collective-permute-start(f32[1024,256]{1,0:T(8,128)} %mix.17), channel_id=1, source_target_pairs={{0,2},{2,0},{1,3},{3,1},{4,6},{6,4},{5,7},{7,5}} | collective-permute-start | bytes 3145736 | tf_op jit(solution)/shard_map/ppermute | solution.py:17
  414.4 17.9 %collective-permute-start.38 = (bf16[1024,256]{1,0:T(8,128)(2,1)}, bf16[1024,256]{1,0:T(8,128)(2,1)S(1)}, u32[]{:S(2)}, u32[]{:S(2)}) collective-permute-start(bf16[1024,256]{1,0:T(8,128)(2,1)} %mix.20), channel_id=1, source_target_pairs={{0,4},{4,0},{1,5},{5,1},{2,6},{6,2},{3,7},{7,3}} | collective-permute-start | bytes 1572872 | tf_op jit(solution)/shard_map/ppermute | solution.py:17
  431.7 13.4 %collective-permute-start.40 = (bf16[1024,256]{1,0:T(8,128)(2,1)}, bf16[1024,256]{1,0:T(8,128)(2,1)S(1)}, u32[]{:S(2)}, u32[]{:S(2)}) collective-permute-start(bf16[1024,256]{1,0:T(8,128)(2,1)} %mix.21), channel_id=1, source_target_pairs={{0,4},{4,0},{1,5},{5,1},{2,6},{6,2},{3,7},{7,3}} | collective-permute-start | bytes 1572872 | tf_op jit(solution)/shard_map/ppermute | solution.py:17
  (45 other events, 327.2 us)

commit v2 on v1

--- a/solution.py
+++ b/solution.py
@@ -222,7 +222,8 @@
         g = jnp.concatenate([g, swap_x(g)], 0)
         g = jnp.concatenate([g, swap_c(g)], 0)
         hid2 = hidden.reshape(2, half, width)
-        mine, other = pick(hid2, yi), pick(hid2, 1 - yi)
+        other = pick(hid2, 1 - yi)
+        mine = pick(tie(hid2, other), yi)
         from_y = swap_y(other)
         mine_x = swap_x(mine)
         from_yx = swap_x(from_y)
@@ -250,6 +251,11 @@
         q_x = [pick(q4, xi), swap_x(pick(q4, 1 - xi))]
         q_c = [pick(v, ci) for v in q_x] + [swap_c(pick(v, 1 - ci)) for v in q_x]
 
+        chunks = 4
+        cw = w_gate.shape[1] // chunks
+        near_ws = [jnp.stack([w[:, j * cw : (j + 1) * cw] for w in (w_gate, w_up)]) for j in range(chunks)]
+        far_ws = [swap_y(w) for w in near_ws]
+        a_own = [glu(h, near_ws[0], far_ws[0])]
         half_dim = dim // 2
         inv_freq = ROPE_BASE ** (-2.0 * jnp.arange(half_dim, dtype=F32) / dim)
         positions = (lengths[:, None] + jnp.arange(new, dtype=jnp.int32)[None, :]).reshape(own_tok)
@@ -257,7 +263,7 @@
         cos_t, sin_t = jnp.cos(angles), jnp.sin(angles)
         cos_t = jnp.concatenate([cos_t, cos_t], -1)
         sin_t = jnp.concatenate([-sin_t, sin_t], -1)
-        o0, o1, o2, o3, k_next, v_next = attention(lengths, q_c, kv, cos_t, sin_t, k_cache, v_cache)
+        o0, o1, o2, o3, k_next, v_next = attention(lengths, [tie(q_c[0], a_own[0]), *q_c[1:]], kv, cos_t, sin_t, k_cache, v_cache)
 
         keep = [o0, swap_c(o2)]
         send = swap_x(jnp.stack([o1, swap_c(o3)]))
@@ -265,20 +271,11 @@
         o_rows = flip([flip(keep, ci), jnp.where(ci == 0, send, send[::-1])], xi)
         o_own = o_rows.reshape(half, -1)
         o_far = swap_c(o_own)
-
-        chunks = 4
-        cw = w_gate.shape[1] // chunks
-        a_own, a_far = [], []
-        for j in range(chunks):
-            near_w = jnp.stack([w[:, j * cw : (j + 1) * cw] for w in (w_gate, w_up)])
-            far_w = swap_y(near_w)
-            if j == chunks - 1:
-                last_w = near_w, far_w
-                break
-            if j > 0:
-                far_w = tie(far_w, a_own[-1], o0)
-            a_own.append(glu(h, near_w, far_w))
-            a_far.append(swap_c(a_own[-1]))
+        o_far = swap_c(o_own)
+
+        for j in range(1, chunks - 1):
+            a_own.append(glu(h, near_ws[j], tie(far_ws[j], a_own[-1], o0)))
+        a_far = [swap_c(v) for v in a_own]
 
         def block(xr, cr):
             col = (2 * (xi ^ xr) + (ci ^ cr)) * width
@@ -288,8 +285,6 @@
         other_y = [[None, None], [None, None]]
         for xr, cr in BLOCK_ORDER:
             other_y[xr][cr] = swap_y(blocks[xr][cr])
-
-        o_far = swap_c(o_own)
 
         def terms(near_w, far_w, which):
             out = []
@@ -305,18 +300,20 @@
         cross_far, same_far = swap_c(blocks[1][1]), swap_c(blocks[0][1])
         pre_cross = mix(terms(blocks[1][0], cross_far, early))
         pre_same = mix(terms(tie(blocks[0][0], pre_cross), same_far, early), [mine])
-        a_own.append(glu(h, last_w[0], tie(last_w[1], pre_same)))
+        a_own.append(glu(h, near_ws[-1], tie(far_ws[-1], pre_same)))
         a_far.append(swap_c(a_own[-1]))
         p_own = mix(terms(blocks[1][0], cross_far, late), [pre_cross])
         r_own = swap_x(p_own)
 
         pre_far = mix(terms(None, swap_c(tie(other_y[1][1], p_own)), every))
         near_w = tie(other_y[1][0], pre_far)
-        p_far = [mix(terms(near_w, None, every), [pre_far], F32, i * size, size) for i in range(parts)]
-        r_far = [swap_x(p) for p in p_far]
-        base = mix(terms(None, swap_c(tie(other_y[0][1], *p_far)), every), [from_y])
-        out_own = mix(terms(blocks[0][0], same_far, late), [pre_same, tie(r_own, base)], BF16)
-        last = tie(other_y[0][0], out_own)
+        p_far, r_far = [], []
+        for i in range(parts):
+            p_far.append(mix(terms(near_w, None, every), [pre_far], F32, i * size, size))
+            r_far.append(swap_x(p_far[i]))
+        out_own = mix(terms(blocks[0][0], same_far, late), [pre_same, tie(r_own, *p_far)], BF16)
+        base = mix(terms(None, swap_c(tie(other_y[0][1], out_own)), every), [from_y])
+        last = tie(other_y[0][0], base)
         out_far = []
         for i in range(parts):
             out_far.append(mix(terms(last, None, every), [base, r_far[i]], BF16, i * size, size))

time: 448 us -> 457 us (1.020)
  waiting for transfers between devices: 168 us -> 175 us
    ppermute x41, waiting for transfers between devices: 168 us -> 175 us  [swap(): return lambda a: lax.ppermute(a, axis, pairs)]
    unnamed x73 -> x67, local copies, waits for them, and re-layouts: 9.19 us -> 11.1 us
  transfers between devices with their start and end apart: 41 -> 41, of which waited for: 13 -> 15; matrix products, arithmetic and copies ran while one was open for 9% -> 10% of each run, Pallas kernels for 40% -> 39%
where the time goes in v2:
time: 457 us; the launch traced here: 456 us
  Pallas kernels  193 us (42%)
  waiting for transfers between devices  175 us (38%)
  local copies, waits for them, and re-layouts  29.9 us (7%)
  starting transfers between devices  28.8 us (6%)
  other arithmetic  25.1 us (5%)
    ppermute x41, waiting for transfers between devices, swap(): return lambda a: lax.ppermute(a, axis, pairs)  175 us
    pallas_call x11, Pallas kernels, mix(): pl.pallas_call(functools.partial(mix_kernel, plan, len(lhs), len(ws)), gr...  81.1 us
    pallas_call x4, Pallas kernels, glu(): pl.pallas_call(glu_kernel, grid=(tokens // blk,), in_specs=[pl.BlockSpec(...  52.8 us
    pallas_call x1, Pallas kernels, attention(): pl.pallas_call(attn_kernel, grid_spec=pltpu.PrefetchScalarGridSpec(num_sc...  46 us
    ppermute x41, starting transfers between devices, swap(): return lambda a: lax.ppermute(a, axis, pairs)  28.8 us
    pallas_call x1, Pallas kernels, layer_norm(): pl.pallas_call(norm_kernel, grid_spec=pltpu.PrefetchScalarGridSpec(num_sc...  13 us
    unnamed x67, local copies, waits for them, and re-layouts  11.1 us
  transfers between devices with their start and end apart: 41, of which 15 were waited for; matrix products, arithmetic and copies ran while one was open for 10% of the time, Pallas kernels for 39%

profile of v2, /device:TPU:0, one launch (start us, length us, event | category | flops | bytes accessed | tf_op | source)
XLA Modules:
  0.0 456.1 jit_solution(7134844982534021903)
XLA Ops:
  3.3 3.3 collective-permute-start
  8.2 21.9 %collective-permute-done.refs_1_.refs_6_ = bf16[2048,256]{1,0:T(8,128)(2,1)} collective-permute-done((bf16[2048,256]{1,0:T(8,128)(2,1)}, bf16[2048,256]{1,0:T(8,128)(2,1)}, u32[]{:S(2)}, u32[]{:S(2)}) %collective-permute-start) | collective-permute-done | bytes 1048608 | tf_op jit(solution)/shard_map/ppermute | solution.py:17
  35.7 6.0 %slice_bitcast_fusion.6 = (bf16[1,1024,512]{2,1,0:T(8,128)(2,1)}, bf16[1,1024,512]{2,1,0:T(8,128)(2,1)}, bf16[1,1024,512]{2,1,0:T(8,128)(2,1)S(1)}, bf16[1,1024,...) fusion(bf16[1024,2048]{1,0:T(8,128)(2,1)} %param.21, ...), kind=kLoop, calls=%fused_computation.29 | loop fusion | bytes 16777216 | tf_op jit(solution)/shard_map/stack | solution.py:256
  41.7 13.0 %collective-permute-done.8 = f32[2,256]{1,0:T(2,128)S(1)} collective-permute-done((f32[2,256]{1,0:T(2,128)S(1)}, f32[2,256]{1,0:T(2,128)S(1)}, u32[]{:S(2)}, u32[]{:S(2)}) %collective-permute-start.8) | collective-permute-done | bytes 2080 | tf_op jit(solution)/shard_map/ppermute | solution.py:17
  59.0 3.2 pad_maximum_fusion.1.near_w
  72.6 13.0 %norm.1.h_ref.refs_0_ = bf16[2048,2048]{1,0:T(8,128)(2,1)} custom-call(s32[8]{0:T(128)} %stack.129.offs_ref, bf16[2048,256]{1,0:T(8,128)(2,1)} %copy-done.6, bf16[2048,256]{1,0:T(8,128)(2,1)} %collective-permute-done.refs_1_.refs_6_, bf16[2048,256]{1,0:T(8,128)(2,1)} %collective-permute-done.1.refs_2_, bf16[2048,256]{1,0:T(8,128)(2,1)} %collective-permute-done.2.refs_3_, ...), custom_call_target="tpu_custom_call" | custom-call | flops 83886080 | bytes 16777216 | tf_op jit(solution)/shard_map/norm/pallas_call | solution.py:47
  85.7 8.7 %mix.11 = bf16[2048,512]{1,0:T(8,128)(2,1)} custom-call(bf16[2048,2048]{1,0:T(8,128)(2,1)} %norm.1.h_ref.refs_0_, bf16[2048,512]{1,0:T(8,128)(2,1)} %pad_maximum_fusion.3.refs_1_), custom_call_target="tpu_custom_call" | custom-call | flops 4294967296 | bytes 10485760 | tf_op jit(solution)/shard_map/mix/pallas_call | solution.py:192
  97.3 23.0 %collective-permute-done.17 = bf16[512,256]{1,0:T(8,128)(2,1)} collective-permute-done((bf16[512,256]{1,0:T(8,128)(2,1)S(1)}, bf16[512,256]{1,0:T(8,128)(2,1)}, u32[]{:S(2)}, u32[]{:S(2)}) %collective-permute-start.17) | collective-permute-done | bytes 262176 | tf_op jit(solution)/shard_map/ppermute | solution.py:17
  127.9 13.2 %glu.4.refs_0_ = bf16[2048,512]{1,0:T(8,128)(2,1)} custom-call(bf16[2048,2048]{1,0:T(8,128)(2,1)} %norm.1.h_ref.refs_0_, bf16[2,1024,512]{2,1,0:T(8,128)(2,1)} %pad_maximum_fusion.1.near_w, bf16[2,1024,512]{2,1,0:T(8,128)(2,1)} %collective-permute-done.11.far_w), custom_call_target="tpu_custom_call" | custom-call | flops 8589934592 | bytes 14680064 | tf_op jit(solution)/shard_map/glu/pallas_call | solution.py:155
  145.3 46.0 %attn.1 = (bf16[512,512]{1,0:T(8,128)(2,1)}, bf16[512,512]{1,0:T(8,128)(2,1)}, bf16[512,512]{1,0:T(8,128)(2,1)}, bf16[512,512]{1,0:T(8,128)(2,1)}, bf16[8,2048,1...) custom-call(s32[8]{0:T(128)} %len_ref.1, bf16[512,512]{1,0:T(8,128)(2,1)} %get-tuple-element.21.q0, ...), custom_call_target="tpu_custom_call" | custom-call | flops 17179869184 | bytes 16777216 | tf_op jit(solution)/shard_map/attn/pallas_call | solution.py:125
  191.4 4.0 constant_dynamic-slice_fusion.1
  201.1 13.2 %glu.5.refs_1_ = bf16[2048,512]{1,0:T(8,128)(2,1)} custom-call(bf16[2048,2048]{1,0:T(8,128)(2,1)} %norm.1.h_ref.refs_0_, bf16[2,1024,512]{2,1,0:T(8,128)(2,1)} %pad_maximum_fusion.2.near_w, bf16[2,1024,512]{2,1,0:T(8,128)(2,1)} %collective-permute-done.12.far_w), custom_call_target="tpu_custom_call" | custom-call | flops 8589934592 | bytes 14680064 | tf_op jit(solution)/shard_map/glu/pallas_call | solution.py:155
  214.3 13.2 %glu.6.refs_2_ = bf16[2048,512]{1,0:T(8,128)(2,1)} custom-call(bf16[2048,2048]{1,0:T(8,128)(2,1)} %norm.1.h_ref.refs_0_, bf16[2,1024,512]{2,1,0:T(8,128)(2,1)} %pad_maximum_fusion.4.near_w, bf16[2,1024,512]{2,1,0:T(8,128)(2,1)} %collective-permute-done.19.far_w), custom_call_target="tpu_custom_call" | custom-call | flops 8589934592 | bytes 14680064 | tf_op jit(solution)/shard_map/glu/pallas_call | solution.py:155
  238.3 10.8 %mix.12.refs_4_ = f32[2048,256]{1,0:T(8,128)} custom-call(bf16[2048,512]{1,0:T(8,128)(2,1)} %glu.4.refs_0_, bf16[2048,512]{1,0:T(8,128)(2,1)} %glu.5.refs_1_, bf16[2048,512]{1,0:T(8,128)(2,1)} %glu.6.refs_2_, bf16[2048,512]{1,0:T(8,128)(2,1)} %bitcast.58, bf16[2048,512]{1,0:T(8,128)(2,1)} %collective-permute-done.23.refs_4_.refs_0_, ...), custom_call_target="tpu_custom_call" | custom-call | flops 4294967296 | bytes 18874368 | tf_op jit(solution)/shard_map/mix/pallas_call | solution.py:192
  250.1 11.1 %mix.13.refs_4_ = f32[2048,256]{1,0:T(8,128)} custom-call(bf16[2048,512]{1,0:T(8,128)(2,1)} %glu.4.refs_0_, bf16[2048,512]{1,0:T(8,128)(2,1)} %glu.5.refs_1_, bf16[2048,512]{1,0:T(8,128)(2,1)} %glu.6.refs_2_, bf16[2048,512]{1,0:T(8,128)(2,1)} %bitcast.59, bf16[2048,512]{1,0:T(8,128)(2,1)} %collective-permute-done.23.refs_4_.refs_0_, ...), custom_call_target="tpu_custom_call" | custom-call | flops 4294967296 | bytes 18874368 | tf_op jit(solution)/shard_map/mix/pallas_call | solution.py:192
  261.2 20.4 %collective-permute-done.10.far_w = bf16[2,1024,512]{2,1,0:T(8,128)(2,1)} collective-permute-done((bf16[2,1024,512]{2,1,0:T(8,128)(2,1)}, bf16[2,1024,512]{2,1,0:T(8,128)(2,1)}, u32[]{:S(2)}, u32[]{:S(2)}) %collective-permute-start.10) | collective-permute-done | bytes 2097184 | tf_op jit(solution)/shard_map/ppermute | solution.py:17
  281.6 13.2 %glu.7.refs_0_.refs_3_ = bf16[2048,512]{1,0:T(8,128)(2,1)} custom-call(bf16[2048,2048]{1,0:T(8,128)(2,1)} %norm.1.h_ref.refs_0_, bf16[2,1024,512]{2,1,0:T(8,128)(2,1)} %pad_maximum_fusion.near_w, bf16[2,1024,512]{2,1,0:T(8,128)(2,1)} %collective-permute-done.10.far_w), custom_call_target="tpu_custom_call" | custom-call | flops 8589934592 | bytes 14680064 | tf_op jit(solution)/shard_map/glu/pallas_call | solution.py:155
  296.0 3.1 collective-permute-done.29.refs_1_.refs_3_
  300.5 6.4 %mix.14 = f32[2048,256]{1,0:T(8,128)} custom-call(bf16[2048,512]{1,0:T(8,128)(2,1)} %glu.7.refs_0_.refs_3_, bf16[2048,512]{1,0:T(8,128)(2,1)} %copy-done.3, bf16[2560,256]{1,0:T(8,128)(2,1)} %pad_maximum_fusion.6.refs_8_.refs_2_, bf16[2560,256]{1,0:T(8,128)(2,1)} %copy-done.9, f32[2048,256]{1,0:T(8,128)} %mix.12.refs_4_), custom_call_target="tpu_custom_call" | custom-call | flops 1073741824 | bytes 4718592 | tf_op jit(solution)/shard_map/mix/pallas_call | solution.py:192
  308.3 18.0 %collective-permute-done.32 = bf16[2560,256]{1,0:T(8,128)(2,1)} collective-permute-done((bf16[2560,256]{1,0:T(8,128)(2,1)}, bf16[2560,256]{1,0:T(8,128)(2,1)}, u32[]{:S(2)}, u32[]{:S(2)}) %collective-permute-start.32) | collective-permute-done | bytes 1310752 | tf_op jit(solution)/shard_map/ppermute | solution.py:17
  329.7 8.0 %mix.15.refs_6_ = f32[2048,256]{1,0:T(8,128)} custom-call(bf16[2048,512]{1,0:T(8,128)(2,1)} %collective-permute-done.23.refs_4_.refs_0_, bf16[2048,512]{1,0:T(8,128)(2,1)} %collective-permute-done.24.refs_5_.refs_1_, bf16[2048,512]{1,0:T(8,128)(2,1)} %collective-permute-done.25.refs_6_.refs_2_, bf16[2048,512]{1,0:T(8,128)(2,1)} %copy-done.3, ...), custom_call_target="tpu_custom_call" | custom-call | flops 2684354560 | bytes 11796480 | tf_op jit(solution)/shard_map/mix/pallas_call | solution.py:192
  337.6 20.3 %collective-permute-done.31.refs_5_ = bf16[2560,256]{1,0:T(8,128)(2,1)S(1)} collective-permute-done((bf16[2560,256]{1,0:T(8,128)(2,1)S(1)}, bf16[2560,256]{1,0:T(8,128)(2,1)S(1)}, u32[]{:S(2)}, u32[]{:S(2)}) %collective-permute-start.31) | collective-permute-done | bytes 1310752 | tf_op jit(solution)/shard_map/ppermute | solution.py:17
  359.0 5.2 %mix.17 = f32[1024,256]{1,0:T(8,128)} custom-call(bf16[2048,512]{1,0:T(8,128)(2,1)} %glu.4.refs_0_, bf16[2048,512]{1,0:T(8,128)(2,1)} %glu.5.refs_1_, bf16[2048,512]{1,0:T(8,128)(2,1)} %glu.6.refs_2_, bf16[2048,512]{1,0:T(8,128)(2,1)} %glu.7.refs_0_.refs_3_, bf16[2048,512]{1,0:T(8,128)(2,1)} %bitcast.60, bf16[2560,256]{1,0:T(8,128)(2,1)} %copy-done.7, ...), custom_call_target="tpu_custom_call" | custom-call | flops 1342177280 | bytes 6553600 | tf_op jit(solution)/shard_map/mix/pallas_call | solution.py:192
  364.2 5.3 %mix.16 = f32[1024,256]{1,0:T(8,128)} custom-call(bf16[2048,512]{1,0:T(8,128)(2,1)} %glu.4.refs_0_, bf16[2048,512]{1,0:T(8,128)(2,1)} %glu.5.refs_1_, bf16[2048,512]{1,0:T(8,128)(2,1)} %glu.6.refs_2_, bf16[2048,512]{1,0:T(8,128)(2,1)} %glu.7.refs_0_.refs_3_, bf16[2048,512]{1,0:T(8,128)(2,1)} %bitcast.61, bf16[2560,256]{1,0:T(8,128)(2,1)} %copy-done.7, ...), custom_call_target="tpu_custom_call" | custom-call | flops 1342177280 | bytes 6553600 | tf_op jit(solution)/shard_map/mix/pallas_call | solution.py:192
  369.5 6.7 %mix.18 = bf16[2048,256]{1,0:T(8,128)(2,1)} custom-call(bf16[2048,512]{1,0:T(8,128)(2,1)} %glu.7.refs_0_.refs_3_, bf16[2048,512]{1,0:T(8,128)(2,1)} %copy-done.3, bf16[2560,256]{1,0:T(8,128)(2,1)} %pad_maximum_fusion.5.refs_8_.refs_2_, bf16[2560,256]{1,0:T(8,128)(2,1)} %copy-done.8, f32[2048,256]{1,0:T(8,128)} %mix.13.refs_4_, ...), custom_call_target="tpu_custom_call" | custom-call | flops 1073741824 | bytes 4718592 | tf_op jit(solution)/shard_map/mix/pallas_call | solution.py:192
  376.2 9.5 %collective-permute-done.35 = bf16[2560,256]{1,0:T(8,128)(2,1)} collective-permute-done((bf16[2560,256]{1,0:T(8,128)(2,1)}, bf16[2560,256]{1,0:T(8,128)(2,1)}, u32[]{:S(2)}, u32[]{:S(2)}) %collective-permute-start.35) | collective-permute-done | bytes 1310752 | tf_op jit(solution)/shard_map/ppermute | solution.py:17
  389.1 8.3 %mix.19.refs_6_ = f32[2048,256]{1,0:T(8,128)} custom-call(bf16[2048,512]{1,0:T(8,128)(2,1)} %collective-permute-done.23.refs_4_.refs_0_, bf16[2048,512]{1,0:T(8,128)(2,1)} %collective-permute-done.24.refs_5_.refs_1_, bf16[2048,512]{1,0:T(8,128)(2,1)} %collective-permute-done.25.refs_6_.refs_2_, bf16[2048,512]{1,0:T(8,128)(2,1)} %copy-done.3, ...), custom_call_target="tpu_custom_call" | custom-call | flops 2684354560 | bytes 11796480 | tf_op jit(solution)/shard_map/mix/pallas_call | solution.py:192
  397.4 19.5 %collective-permute-done.34.refs_5_ = bf16[2560,256]{1,0:T(8,128)(2,1)S(1)} collective-permute-done((bf16[2560,256]{1,0:T(8,128)(2,1)S(1)}, bf16[2560,256]{1,0:T(8,128)(2,1)S(1)}, u32[]{:S(2)}, u32[]{:S(2)}) %collective-permute-start.34) | collective-permute-done | bytes 1310752 | tf_op jit(solution)/shard_map/ppermute | solution.py:17
  418.0 5.4 %mix.20 = bf16[1024,256]{1,0:T(8,128)(2,1)} custom-call(bf16[2048,512]{1,0:T(8,128)(2,1)} %glu.4.refs_0_, bf16[2048,512]{1,0:T(8,128)(2,1)} %glu.5.refs_1_, bf16[2048,512]{1,0:T(8,128)(2,1)} %glu.6.refs_2_, bf16[2048,512]{1,0:T(8,128)(2,1)} %glu.7.refs_0_.refs_3_, bf16[2048,512]{1,0:T(8,128)(2,1)} %bitcast.62, bf16[2560,256]{1,0:T(8,128)(2,1)} %copy-done.10, ...), custom_call_target="tpu_custom_call" | custom-call | flops 1342177280 | bytes 6553600 | tf_op jit(solution)/shard_map/mix/pallas_call | solution.py:192
  424.6 10.4 %collective-permute-done.39.refs_7_ = f32[1024,256]{1,0:T(8,128)} collective-permute-done((f32[1024,256]{1,0:T(8,128)}, f32[1024,256]{1,0:T(8,128)}, u32[]{:S(2)}, u32[]{:S(2)}) %collective-permute-start.39) | collective-permute-done | bytes 1048608 | tf_op jit(solution)/shard_map/ppermute | solution.py:17
  435.0 5.4 %mix.21 = bf16[1024,256]{1,0:T(8,128)(2,1)} custom-call(bf16[2048,512]{1,0:T(8,128)(2,1)} %glu.4.refs_0_, bf16[2048,512]{1,0:T(8,128)(2,1)} %glu.5.refs_1_, bf16[2048,512]{1,0:T(8,128)(2,1)} %glu.6.refs_2_, bf16[2048,512]{1,0:T(8,128)(2,1)} %glu.7.refs_0_.refs_3_, bf16[2048,512]{1,0:T(8,128)(2,1)} %bitcast.63, bf16[2560,256]{1,0:T(8,128)(2,1)} %copy-done.10, ...), custom_call_target="tpu_custom_call" | custom-call | flops 1342177280 | bytes 6553600 | tf_op jit(solution)/shard_map/mix/pallas_call | solution.py:192
  441.2 12.6 %collective-permute-done.40 = bf16[1024,256]{1,0:T(8,128)(2,1)S(1)} collective-permute-done((bf16[1024,256]{1,0:T(8,128)(2,1)}, bf16[1024,256]{1,0:T(8,128)(2,1)S(1)}, u32[]{:S(2)}, u32[]{:S(2)}) %collective-permute-start.40) | collective-permute-done | bytes 524320 | tf_op jit(solution)/shard_map/ppermute | solution.py:17
  (171 shorter events, 73.9 us)
Async XLA Ops:
  3.3 26.8 %collective-permute-start = (bf16[2048,256]{1,0:T(8,128)(2,1)}, bf16[2048,256]{1,0:T(8,128)(2,1)}, u32[]{:S(2)}, u32[]{:S(2)}) collective-permute-start(bf16[2048,256]{1,0:T(8,128)(2,1)} %dynamic-slice_bitcast_fusion.2), channel_id=1, source_target_pairs={{0,4},{4,0},{1,5},{5,1},{2,6},{6,2},{3,7},{7,3}} | collective-permute-start | bytes 3145736 | tf_op jit(solution)/shard_map/ppermute | solution.py:17
  6.7 49.4 %collective-permute-start.1 = (bf16[2048,256]{1,0:T(8,128)(2,1)S(1)}, bf16[2048,256]{1,0:T(8,128)(2,1)}, u32[]{:S(2)}, u32[]{:S(2)}) collective-permute-start(bf16[2048,256]{1,0:T(8,128)(2,1)S(1)} %dynamic-slice_bitcast_fusion.1.refs_0_.refs_10_), channel_id=1, source_target_pairs={{0,2},{2,0},{1,3},{3,1},{4,6},{6,4},{5,7},{7,5}} | collective-permute-start | bytes 3145736 | tf_op jit(solution)/shard_map/ppermute | solution.py:17
  30.1 26.4 %collective-permute-start.2 = (bf16[2048,256]{1,0:T(8,128)(2,1)}, bf16[2048,256]{1,0:T(8,128)(2,1)}, u32[]{:S(2)}, u32[]{:S(2)}) collective-permute-start(bf16[2048,256]{1,0:T(8,128)(2,1)} %collective-permute-done.refs_1_.refs_6_), channel_id=1, source_target_pairs={{0,2},{2,0},{1,3},{3,1},{4,6},{6,4},{5,7},{7,5}} | collective-permute-start | bytes 3145736 | tf_op jit(solution)/shard_map/ppermute | solution.py:17
  33.3 36.7 %collective-permute-start.3 = (bf16[2048,256]{1,0:T(8,128)(2,1)S(1)}, bf16[2048,256]{1,0:T(8,128)(2,1)}, u32[]{:S(2)}, u32[]{:S(2)}) collective-permute-start(bf16[2048,256]{1,0:T(8,128)(2,1)S(1)} %dynamic-slice_bitcast_fusion.1.refs_0_.refs_10_), channel_id=1, source_target_pairs={{0,1},{1,0},{2,3},{3,2},{4,5},{5,4},{6,7},{7,6}} | collective-permute-start | bytes 3145736 | tf_op jit(solution)/shard_map/ppermute | solution.py:17
  33.3 32.6 %collective-permute-start.13 = (bf16[1024,512]{1,0:T(8,128)(2,1)}, bf16[1024,512]{1,0:T(8,128)(2,1)}, u32[]{:S(2)}, u32[]{:S(2)}) collective-permute-start(bf16[1024,512]{1,0:T(8,128)(2,1)} %param.17), channel_id=1, source_target_pairs={{0,4},{4,0},{1,5},{5,1},{2,6},{6,2},{3,7},{7,3}} | collective-permute-start | bytes 3145736 | tf_op jit(solution)/shard_map/ppermute | solution.py:17
  35.4 19.3 %collective-permute-start.8 = (f32[2,256]{1,0:T(2,128)S(1)}, f32[2,256]{1,0:T(2,128)S(1)}, u32[]{:S(2)}, u32[]{:S(2)}) collective-permute-start(f32[2,256]{1,0:T(2,128)S(1)} %pad_maximum_fusion.15), channel_id=1, source_target_pairs={{0,2},{2,0},{1,3},{3,1},{4,6},{6,4},{5,7},{7,5}} | collective-permute-start | bytes 6152 | tf_op jit(solution)/shard_map/ppermute | solution.py:17
  55.9 16.1 %collective-permute-start.4 = (bf16[2048,256]{1,0:T(8,128)(2,1)}, bf16[2048,256]{1,0:T(8,128)(2,1)}, u32[]{:S(2)}, u32[]{:S(2)}) collective-permute-start(bf16[2048,256]{1,0:T(8,128)(2,1)} %collective-permute-done.refs_1_.refs_6_), channel_id=1, source_target_pairs={{0,1},{1,0},{2,3},{3,2},{4,5},{5,4},{6,7},{7,6}} | collective-permute-start | bytes 3145736 | tf_op jit(solution)/shard_map/ppermute | solution.py:17
  56.1 14.5 %collective-permute-start.5 = (bf16[2048,256]{1,0:T(8,128)(2,1)}, bf16[2048,256]{1,0:T(8,128)(2,1)}, u32[]{:S(2)}, u32[]{:S(2)}) collective-permute-start(bf16[2048,256]{1,0:T(8,128)(2,1)} %collective-permute-done.1.refs_2_), channel_id=1, source_target_pairs={{0,1},{1,0},{2,3},{3,2},{4,5},{5,4},{6,7},{7,6}} | collective-permute-start | bytes 3145736 | tf_op jit(solution)/shard_map/ppermute | solution.py:17
  56.5 16.2 %collective-permute-start.6 = (bf16[2048,256]{1,0:T(8,128)(2,1)}, bf16[2048,256]{1,0:T(8,128)(2,1)}, u32[]{:S(2)}, u32[]{:S(2)}) collective-permute-start(bf16[2048,256]{1,0:T(8,128)(2,1)} %collective-permute-done.2.refs_3_), channel_id=1, source_target_pairs={{0,1},{1,0},{2,3},{3,2},{4,5},{5,4},{6,7},{7,6}} | collective-permute-start | bytes 3145736 | tf_op jit(solution)/shard_map/ppermute | solution.py:17
  65.9 62.0 %collective-permute-start.11 = (bf16[2,1024,512]{2,1,0:T(8,128)(2,1)}, bf16[2,1024,512]{2,1,0:T(8,128)(2,1)}, u32[]{:S(2)}, u32[]{:S(2)}) collective-permute-start(bf16[2,1024,512]{2,1,0:T(8,128)(2,1)} %pad_maximum_fusion.1.near_w), channel_id=1, source_target_pairs={{0,4},{4,0},{1,5},{5,1},{2,6},{6,2},{3,7},{7,3}} | collective-permute-start | bytes 6291464 | tf_op jit(solution)/shard_map/ppermute | solution.py:17
  70.0 50.3 %collective-permute-start.17 = (bf16[512,256]{1,0:T(8,128)(2,1)S(1)}, bf16[512,256]{1,0:T(8,128)(2,1)}, u32[]{:S(2)}, u32[]{:S(2)}) collective-permute-start(bf16[512,256]{1,0:T(8,128)(2,1)S(1)} %constant_dynamic-slice_fusion.8), channel_id=1, source_target_pairs={{0,4},{4,0},{1,5},{5,1},{2,6},{6,2},{3,7},{7,3}} | collective-permute-start | bytes 786440 | tf_op jit(solution)/shard_map/ppermute | solution.py:17
  70.6 127.4 %collective-permute-start.12 = (bf16[2,1024,512]{2,1,0:T(8,128)(2,1)}, bf16[2,1024,512]{2,1,0:T(8,128)(2,1)}, u32[]{:S(2)}, u32[]{:S(2)}) collective-permute-start(bf16[2,1024,512]{2,1,0:T(8,128)(2,1)} %pad_maximum_fusion.2.near_w), channel_id=1, source_target_pairs={{0,4},{4,0},{1,5},{5,1},{2,6},{6,2},{3,7},{7,3}} | collective-permute-start | bytes 6291464 | tf_op jit(solution)/shard_map/ppermute | solution.py:17
  72.1 142.2 %collective-permute-start.19 = (bf16[2,1024,512]{2,1,0:T(8,128)(2,1)}, bf16[2,1024,512]{2,1,0:T(8,128)(2,1)}, u32[]{:S(2)}, u32[]{:S(2)}) collective-permute-start(bf16[2,1024,512]{2,1,0:T(8,128)(2,1)} %pad_maximum_fusion.4.near_w), channel_id=1, source_target_pairs={{0,4},{4,0},{1,5},{5,1},{2,6},{6,2},{3,7},{7,3}} | collective-permute-start | bytes 6291464 | tf_op jit(solution)/shard_map/ppermute | solution.py:17
  95.7 30.2 %collective-permute-start.14 = (bf16[2,512,512]{2,1,0:T(8,128)(2,1)S(1)}, bf16[2,512,512]{2,1,0:T(8,128)(2,1)}, u32[]{:S(2)}, u32[]{:S(2)}) collective-permute-start(bf16[2,512,512]{2,1,0:T(8,128)(2,1)S(1)} %dynamic-slice_bitcast_fusion), channel_id=1, source_target_pairs={{0,2},{2,0},{1,3},{3,1},{4,6},{6,4},{5,7},{7,5}} | collective-permute-start | bytes 3145736 | tf_op jit(solution)/shard_map/ppermute | solution.py:17
  125.3 18.9 %collective-permute-start.15 = (bf16[512,512]{1,0:T(8,128)(2,1)}, bf16[512,512]{1,0:T(8,128)(2,1)S(1)}, u32[]{:S(2)}, u32[]{:S(2)}) collective-permute-start(bf16[512,512]{1,0:T(8,128)(2,1)} %get-tuple-element.49), channel_id=1, source_target_pairs={{0,1},{1,0},{2,3},{3,2},{4,5},{5,4},{6,7},{7,6}} | collective-permute-start | bytes 1572872 | tf_op jit(solution)/shard_map/ppermute | solution.py:17
  127.9 16.4 %collective-permute-start.16 = (bf16[512,512]{1,0:T(8,128)(2,1)S(1)}, bf16[512,512]{1,0:T(8,128)(2,1)S(1)}, u32[]{:S(2)}, u32[]{:S(2)}) collective-permute-start(bf16[512,512]{1,0:T(8,128)(2,1)S(1)} %get-tuple-element.55), channel_id=1, source_target_pairs={{0,1},{1,0},{2,3},{3,2},{4,5},{5,4},{6,7},{7,6}} | collective-permute-start | bytes 1572872 | tf_op jit(solution)/shard_map/ppermute | solution.py:17
  197.5 36.2 %collective-permute-start.27 = (bf16[2560,256]{1,0:T(8,128)(2,1)}, bf16[2560,256]{1,0:T(8,128)(2,1)S(1)}, u32[]{:S(2)}, u32[]{:S(2)}) collective-permute-start(bf16[2560,256]{1,0:T(8,128)(2,1)} %pad_maximum_fusion.7), channel_id=1, source_target_pairs={{0,1},{1,0},{2,3},{3,2},{4,5},{5,4},{6,7},{7,6}} | collective-permute-start | bytes 3932168 | tf_op jit(solution)/shard_map/ppermute | solution.py:17
  197.9 38.1 %collective-permute-start.23 = (bf16[2048,512]{1,0:T(8,128)(2,1)}, bf16[2048,512]{1,0:T(8,128)(2,1)}, u32[]{:S(2)}, u32[]{:S(2)}) collective-permute-start(bf16[2048,512]{1,0:T(8,128)(2,1)} %glu.4.refs_0_), channel_id=1, source_target_pairs={{0,1},{1,0},{2,3},{3,2},{4,5},{5,4},{6,7},{7,6}} | collective-permute-start | bytes 6291464 | tf_op jit(solution)/shard_map/ppermute | solution.py:17
  198.0 29.5 %collective-permute-start.20 = (bf16[512,512]{1,0:T(8,128)(2,1)}, bf16[512,512]{1,0:T(8,128)(2,1)}, u32[]{:S(2)}, u32[]{:S(2)}) collective-permute-start(bf16[512,512]{1,0:T(8,128)(2,1)} %get-tuple-element.25), channel_id=1, source_target_pairs={{0,1},{1,0},{2,3},{3,2},{4,5},{5,4},{6,7},{7,6}} | collective-permute-start | bytes 1572872 | tf_op jit(solution)/shard_map/ppermute | solution.py:17
  200.5 29.2 %collective-permute-start.22 = (bf16[2,512,512]{2,1,0:T(8,128)(2,1)S(1)}, bf16[2,512,512]{2,1,0:T(8,128)(2,1)S(1)}, u32[]{:S(2)}, u32[]{:S(2)}) collective-permute-start(bf16[2,512,512]{2,1,0:T(8,128)(2,1)S(1)} %pad_maximum_fusion.9), channel_id=1, source_target_pairs={{0,2},{2,0},{1,3},{3,1},{4,6},{6,4},{5,7},{7,5}} | collective-permute-start | bytes 3145736 | tf_op jit(solution)/shard_map/ppermute | solution.py:17
  214.3 24.1 %collective-permute-start.24 = (bf16[2048,512]{1,0:T(8,128)(2,1)}, bf16[2048,512]{1,0:T(8,128)(2,1)}, u32[]{:S(2)}, u32[]{:S(2)}) collective-permute-start(bf16[2048,512]{1,0:T(8,128)(2,1)} %glu.5.refs_1_), channel_id=1, source_target_pairs={{0,1},{1,0},{2,3},{3,2},{4,5},{5,4},{6,7},{7,6}} | collective-permute-start | bytes 6291464 | tf_op jit(solution)/shard_map/ppermute | solution.py:17
  233.7 47.9 %collective-permute-start.10 = (bf16[2,1024,512]{2,1,0:T(8,128)(2,1)}, bf16[2,1024,512]{2,1,0:T(8,128)(2,1)}, u32[]{:S(2)}, u32[]{:S(2)}) collective-permute-start(bf16[2,1024,512]{2,1,0:T(8,128)(2,1)} %pad_maximum_fusion.near_w), channel_id=1, source_target_pairs={{0,4},{4,0},{1,5},{5,1},{2,6},{6,2},{3,7},{7,3}} | collective-permute-start | bytes 6291464 | tf_op jit(solution)/shard_map/ppermute | solution.py:17
  236.0 13.1 %collective-permute-start.28 = (bf16[2560,256]{1,0:T(8,128)(2,1)}, bf16[2560,256]{1,0:T(8,128)(2,1)S(1)}, u32[]{:S(2)}, u32[]{:S(2)}) collective-permute-start(bf16[2560,256]{1,0:T(8,128)(2,1)} %pad_maximum_fusion.8), channel_id=1, source_target_pairs={{0,1},{1,0},{2,3},{3,2},{4,5},{5,4},{6,7},{7,6}} | collective-permute-start | bytes 3932168 | tf_op jit(solution)/shard_map/ppermute | solution.py:17
  294.8 31.5 %collective-permute-start.32 = (bf16[2560,256]{1,0:T(8,128)(2,1)}, bf16[2560,256]{1,0:T(8,128)(2,1)}, u32[]{:S(2)}, u32[]{:S(2)}) collective-permute-start(bf16[2560,256]{1,0:T(8,128)(2,1)} %pad_maximum_fusion.7), channel_id=1, source_target_pairs={{0,4},{4,0},{1,5},{5,1},{2,6},{6,2},{3,7},{7,3}} | collective-permute-start | bytes 3932168 | tf_op jit(solution)/shard_map/ppermute | solution.py:17
  306.8 62.7 %collective-permute-start.30 = (f32[2048,256]{1,0:T(8,128)}, f32[2048,256]{1,0:T(8,128)}, u32[]{:S(2)}, u32[]{:S(2)}) collective-permute-start(f32[2048,256]{1,0:T(8,128)} %mix.14), channel_id=1, source_target_pairs={{0,2},{2,0},{1,3},{3,1},{4,6},{6,4},{5,7},{7,5}} | collective-permute-start | bytes 6291464 | tf_op jit(solution)/shard_map/ppermute | solution.py:17
  326.3 31.6 %collective-permute-start.31 = (bf16[2560,256]{1,0:T(8,128)(2,1)S(1)}, bf16[2560,256]{1,0:T(8,128)(2,1)S(1)}, u32[]{:S(2)}, u32[]{:S(2)}) collective-permute-start(bf16[2560,256]{1,0:T(8,128)(2,1)S(1)} %copy-done.5), channel_id=1, source_target_pairs={{0,4},{4,0},{1,5},{5,1},{2,6},{6,2},{3,7},{7,3}} | collective-permute-start | bytes 3932168 | tf_op jit(solution)/shard_map/ppermute | solution.py:17
  327.5 58.2 %collective-permute-start.35 = (bf16[2560,256]{1,0:T(8,128)(2,1)}, bf16[2560,256]{1,0:T(8,128)(2,1)}, u32[]{:S(2)}, u32[]{:S(2)}) collective-permute-start(bf16[2560,256]{1,0:T(8,128)(2,1)} %pad_maximum_fusion.8), channel_id=1, source_target_pairs={{0,4},{4,0},{1,5},{5,1},{2,6},{6,2},{3,7},{7,3}} | collective-permute-start | bytes 3932168 | tf_op jit(solution)/shard_map/ppermute | solution.py:17
  385.7 31.2 %collective-permute-start.34 = (bf16[2560,256]{1,0:T(8,128)(2,1)S(1)}, bf16[2560,256]{1,0:T(8,128)(2,1)S(1)}, u32[]{:S(2)}, u32[]{:S(2)}) collective-permute-start(bf16[2560,256]{1,0:T(8,128)(2,1)S(1)} %copy-done.4), channel_id=1, source_target_pairs={{0,4},{4,0},{1,5},{5,1},{2,6},{6,2},{3,7},{7,3}} | collective-permute-start | bytes 3932168 | tf_op jit(solution)/shard_map/ppermute | solution.py:17
  386.9 30.0 %collective-permute-start.37 = (f32[1024,256]{1,0:T(8,128)}, f32[1024,256]{1,0:T(8,128)}, u32[]{:S(2)}, u32[]{:S(2)}) collective-permute-start(f32[1024,256]{1,0:T(8,128)} %mix.16), channel_id=1, source_target_pairs={{0,2},{2,0},{1,3},{3,1},{4,6},{6,4},{5,7},{7,5}} | collective-permute-start | bytes 3145736 | tf_op jit(solution)/shard_map/ppermute | solution.py:17
  388.6 46.4 %collective-permute-start.39 = (f32[1024,256]{1,0:T(8,128)}, f32[1024,256]{1,0:T(8,128)}, u32[]{:S(2)}, u32[]{:S(2)}) collective-permute-start(f32[1024,256]{1,0:T(8,128)} %mix.17), channel_id=1, source_target_pairs={{0,2},{2,0},{1,3},{3,1},{4,6},{6,4},{5,7},{7,5}} | collective-permute-start | bytes 3145736 | tf_op jit(solution)/shard_map/ppermute | solution.py:17
  423.4 17.8 %collective-permute-start.38 = (bf16[1024,256]{1,0:T(8,128)(2,1)}, bf16[1024,256]{1,0:T(8,128)(2,1)S(1)}, u32[]{:S(2)}, u32[]{:S(2)}) collective-permute-start(bf16[1024,256]{1,0:T(8,128)(2,1)} %mix.20), channel_id=1, source_target_pairs={{0,4},{4,0},{1,5},{5,1},{2,6},{6,2},{3,7},{7,3}} | collective-permute-start | bytes 1572872 | tf_op jit(solution)/shard_map/ppermute | solution.py:17
  440.4 13.4 %collective-permute-start.40 = (bf16[1024,256]{1,0:T(8,128)(2,1)}, bf16[1024,256]{1,0:T(8,128)(2,1)S(1)}, u32[]{:S(2)}, u32[]{:S(2)}) collective-permute-start(bf16[1024,256]{1,0:T(8,128)(2,1)} %mix.21), channel_id=1, source_target_pairs={{0,4},{4,0},{1,5},{5,1},{2,6},{6,2},{3,7},{7,3}} | collective-permute-start | bytes 1572872 | tf_op jit(solution)/shard_map/ppermute | solution.py:17
  (42 other events, 302.4 us)

commit v3 on v2

--- a/solution.py
+++ b/solution.py
@@ -174,7 +174,7 @@
     out_ref[...] = total.astype(out_ref.dtype)
 
 
-def mix(terms, adds=(), dtype=F32, start=0, tokens=None):
+def mix(terms, adds=(), dtype=F32, start=0, tokens=None, col=0):
     ws, plan = [], []
     for _, w, row in terms:
         found = [i for i, v in enumerate(ws) if v is w]
@@ -188,7 +188,7 @@
     first = start // blk
     tok = lambda w: pl.BlockSpec((blk, w), lambda i: (i + first, 0))
     depth = sum(l.shape[1] for l in lhs)
-    add_specs = [tok(cols) if t.shape[0] != tokens else pl.BlockSpec((blk, cols), lambda i: (i, 0)) for t in adds]
+    add_specs = [pl.BlockSpec((blk, cols), lambda i, f=first * (t.shape[0] != tokens), c=col * (t.shape[1] != cols): (i + f, c)) for t in adds]
     return pl.pallas_call(
         functools.partial(mix_kernel, plan, len(lhs), len(ws)),
         grid=(tokens // blk,),
@@ -200,7 +200,7 @@
     )(*lhs, *ws, *adds)
 
 
-BLOCK_ORDER = [(1, 1), (1, 0), (0, 1), (0, 0)]
+BLOCK_ORDER = ["11", "10A", "10B", "01", "00A", "00B"]
 
 
 def tie(value, *others):
@@ -282,9 +282,14 @@
             return jnp.concatenate([lax.dynamic_slice_in_dim(w, col, width, 1) for w in (w_down, w_out)], 0)
 
         blocks = [[block(xr, cr) for cr in range(2)] for xr in range(2)]
-        other_y = [[None, None], [None, None]]
-        for xr, cr in BLOCK_ORDER:
-            other_y[xr][cr] = swap_y(blocks[xr][cr])
+        narrow = width // 2
+        other_y = {}
+        for name in BLOCK_ORDER:
+            b = blocks[int(name[0])][int(name[1])]
+            if name[2:]:
+                col = "AB".index(name[2]) * narrow
+                b = b[:, col : col + narrow]
+            other_y[name] = swap_y(b)
 
         def terms(near_w, far_w, which):
             out = []
@@ -294,32 +299,42 @@
             return out
 
         early, late, every = [*range(chunks - 1), "o"], [chunks - 1], [*range(chunks), "o"]
-        parts = 2
-        size = half // parts
+        split = (0, 3 * half // 4), (3 * half // 4, half // 4)
 
         cross_far, same_far = swap_c(blocks[1][1]), swap_c(blocks[0][1])
         pre_cross = mix(terms(blocks[1][0], cross_far, early))
         pre_same = mix(terms(tie(blocks[0][0], pre_cross), same_far, early), [mine])
         a_own.append(glu(h, near_ws[-1], tie(far_ws[-1], pre_same)))
         a_far.append(swap_c(a_own[-1]))
-        p_own = mix(terms(blocks[1][0], cross_far, late), [pre_cross])
-        r_own = swap_x(p_own)
-
-        pre_far = mix(terms(None, swap_c(tie(other_y[1][1], p_own)), every))
-        near_w = tie(other_y[1][0], pre_far)
-        p_far, r_far = [], []
-        for i in range(parts):
-            p_far.append(mix(terms(near_w, None, every), [pre_far], F32, i * size, size))
-            r_far.append(swap_x(p_far[i]))
-        out_own = mix(terms(blocks[0][0], same_far, late), [pre_same, tie(r_own, *p_far)], BF16)
-        base = mix(terms(None, swap_c(tie(other_y[0][1], out_own)), every), [from_y])
-        last = tie(other_y[0][0], base)
+        p_own, r_own = [], []
+        for i, span in enumerate(split):
+            p_own.append(mix(terms(blocks[1][0], cross_far, late), [pre_cross], F32, *span))
+            r_own.append(swap_x(p_own[i]))
+
+        pre_far = mix(terms(None, swap_c(tie(other_y["11"], *p_own)), every))
+        r_far = []
+        held = pre_far
+        for i, side in enumerate("AB"):
+            held = mix(terms(tie(other_y["10" + side], held), None, every), [pre_far], col=i)
+            r_far.append(swap_x(held))
+
+        def finish_own(i):
+            return mix(terms(blocks[0][0], same_far, late), [pre_same, r_own[i]], BF16, *split[i])
+
+        out = jnp.zeros((2, half, width), BF16)
+        r_own[0] = tie(r_own[0], held)
+        held = finish_own(0)
+        out = lax.dynamic_update_slice(out, held[None], (yi, 0, 0))
+        base = held = mix(terms(None, swap_c(tie(other_y["01"], held)), every), [from_y])
         out_far = []
-        for i in range(parts):
-            out_far.append(mix(terms(last, None, every), [base, r_far[i]], BF16, i * size, size))
-            out_far[i] = swap_y(out_far[i])
-        out_far = jnp.concatenate(out_far, 0)
-        out = jnp.where(yi == 0, jnp.stack([out_own, out_far]), jnp.stack([out_far, out_own]))
+        for i, side in enumerate("AB"):
+            held = mix(terms(tie(other_y["00" + side], held), None, every), [base, r_far[i]], BF16, col=i)
+            out_far.append(swap_y(held))
+        r_own[1] = tie(r_own[1], held)
+        held = finish_own(1)
+        out = lax.dynamic_update_slice(out, held[None], (yi, split[1][0], 0))
+        for i, part in enumerate(out_far):
+            out = lax.dynamic_update_slice(out, part[None], (1 - yi, 0, i * narrow))
         return out.reshape(batch, new, width), k_next, v_next
 
     row_spec = P("dp", None, ("tx", "tyz"))

time: 457 us -> 474 us (1.037)
  Pallas kernels: 193 us -> 209 us
  waiting for transfers between devices: 175 us -> 166 us
  local copies, waits for them, and re-layouts: 29.9 us -> 35.3 us
    pallas_call x11 -> x13, Pallas kernels: 81.1 us -> 97.3 us  [mix(): pl.pallas_call(functools.partial(mix_kernel, plan, len(lhs), len(ws)), gr...]
    ppermute x41 -> x44, waiting for transfers between devices: 175 us -> 166 us  [swap(): return lambda a: lax.ppermute(a, axis, pairs)]
    ppermute x41 -> x44, starting transfers between devices: 28.8 us -> 32.8 us  [swap(): return lambda a: lax.ppermute(a, axis, pairs)]
    unnamed x67 -> x77, local copies, waits for them, and re-layouts: 11.1 us -> 13 us
  transfers between devices with their start and end apart: 41 -> 44, of which waited for: 15 -> 15; matrix products, arithmetic and copies ran while one was open for 10% -> 11% of each run, Pallas kernels for 39% -> 41%
where the time goes in v3:
time: 474 us; the launch traced here: 473 us
  Pallas kernels  209 us (44%)
  waiting for transfers between devices  166 us (35%)
  local copies, waits for them, and re-layouts  35.3 us (7%)
  starting transfers between devices  32.8 us (7%)
  other arithmetic  26.3 us (6%)
    ppermute x44, waiting for transfers between devices, swap(): return lambda a: lax.ppermute(a, axis, pairs)  166 us
    pallas_call x13, Pallas kernels, mix(): pl.pallas_call(functools.partial(mix_kernel, plan, len(lhs), len(ws)), gr...  97.3 us
    pallas_call x4, Pallas kernels, glu(): pl.pallas_call(glu_kernel, grid=(tokens // blk,), in_specs=[pl.BlockSpec(...  52.8 us
    pallas_call x1, Pallas kernels, attention(): pl.pallas_call(attn_kernel, grid_spec=pltpu.PrefetchScalarGridSpec(num_sc...  46 us
    ppermute x44, starting transfers between devices, swap(): return lambda a: lax.ppermute(a, axis, pairs)  32.8 us
    pallas_call x1, Pallas kernels, layer_norm(): pl.pallas_call(norm_kernel, grid_spec=pltpu.PrefetchScalarGridSpec(num_sc...  13 us
    unnamed x77, local copies, waits for them, and re-layouts  13 us
  transfers between devices with their start and end apart: 44, of which 15 were waited for; matrix products, arithmetic and copies ran while one was open for 11% of the time, Pallas kernels for 41%

profile of v3, /device:TPU:0, one launch (start us, length us, event | category | flops | bytes accessed | tf_op | source)
XLA Modules:
  0.0 473.3 jit_solution(16706749474259247676)
XLA Ops:
  8.2 21.9 %collective-permute-done.refs_1_.refs_6_ = bf16[2048,256]{1,0:T(8,128)(2,1)} collective-permute-done((bf16[2048,256]{1,0:T(8,128)(2,1)}, bf16[2048,256]{1,0:T(8,128)(2,1)}, u32[]{:S(2)}, u32[]{:S(2)}) %collective-permute-start) | collective-permute-done | bytes 1048608 | tf_op jit(solution)/shard_map/ppermute | solution.py:17
  35.7 6.0 %slice_bitcast_fusion = (bf16[1,1024,512]{2,1,0:T(8,128)(2,1)S(1)}, bf16[1,1024,512]{2,1,0:T(8,128)(2,1)}, bf16[1,1024,512]{2,1,0:T(8,128)(2,1)}, bf16[1,1024,51...) fusion(bf16[1024,2048]{1,0:T(8,128)(2,1)} %param.21, ...), kind=kLoop, calls=%fused_computation.28 | loop fusion | bytes 16777216 | tf_op jit(solution)/shard_map/stack | solution.py:256
  41.7 13.0 %collective-permute-done.8 = f32[2,256]{1,0:T(2,128)S(1)} collective-permute-done((f32[2,256]{1,0:T(2,128)S(1)}, f32[2,256]{1,0:T(2,128)S(1)}, u32[]{:S(2)}, u32[]{:S(2)}) %collective-permute-start.8) | collective-permute-done | bytes 2080 | tf_op jit(solution)/shard_map/ppermute | solution.py:17
  72.6 13.0 %norm.1.h_ref.refs_0_ = bf16[2048,2048]{1,0:T(8,128)(2,1)} custom-call(s32[8]{0:T(128)} %stack.115.offs_ref, bf16[2048,256]{1,0:T(8,128)(2,1)} %copy-done.6, bf16[2048,256]{1,0:T(8,128)(2,1)} %collective-permute-done.refs_1_.refs_6_, bf16[2048,256]{1,0:T(8,128)(2,1)} %collective-permute-done.1.refs_2_, bf16[2048,256]{1,0:T(8,128)(2,1)} %collective-permute-done.2.refs_3_, ...), custom_call_target="tpu_custom_call" | custom-call | flops 83886080 | bytes 16777216 | tf_op jit(solution)/shard_map/norm/pallas_call | solution.py:47
  85.6 8.7 %mix.13 = bf16[2048,512]{1,0:T(8,128)(2,1)} custom-call(bf16[2048,2048]{1,0:T(8,128)(2,1)} %norm.1.h_ref.refs_0_, bf16[2048,512]{1,0:T(8,128)(2,1)} %pad_maximum_fusion.3.refs_1_), custom_call_target="tpu_custom_call" | custom-call | flops 4294967296 | bytes 10485760 | tf_op jit(solution)/shard_map/mix/pallas_call | solution.py:192
  97.3 23.0 %collective-permute-done.17 = bf16[512,256]{1,0:T(8,128)(2,1)} collective-permute-done((bf16[512,256]{1,0:T(8,128)(2,1)S(1)}, bf16[512,256]{1,0:T(8,128)(2,1)}, u32[]{:S(2)}, u32[]{:S(2)}) %collective-permute-start.17) | collective-permute-done | bytes 262176 | tf_op jit(solution)/shard_map/ppermute | solution.py:17
  127.9 13.2 %glu.4.refs_0_ = bf16[2048,512]{1,0:T(8,128)(2,1)} custom-call(bf16[2048,2048]{1,0:T(8,128)(2,1)} %norm.1.h_ref.refs_0_, bf16[2,1024,512]{2,1,0:T(8,128)(2,1)} %pad_maximum_fusion.1.near_w, bf16[2,1024,512]{2,1,0:T(8,128)(2,1)} %collective-permute-done.11.far_w), custom_call_target="tpu_custom_call" | custom-call | flops 8589934592 | bytes 14680064 | tf_op jit(solution)/shard_map/glu/pallas_call | solution.py:155
  145.2 46.0 %attn.1 = (bf16[512,512]{1,0:T(8,128)(2,1)}, bf16[512,512]{1,0:T(8,128)(2,1)}, bf16[512,512]{1,0:T(8,128)(2,1)}, bf16[512,512]{1,0:T(8,128)(2,1)}, bf16[8,2048,1...) custom-call(s32[8]{0:T(128)} %len_ref.1, bf16[512,512]{1,0:T(8,128)(2,1)} %get-tuple-element.24.q0, ...), custom_call_target="tpu_custom_call" | custom-call | flops 17179869184 | bytes 16777216 | tf_op jit(solution)/shard_map/attn/pallas_call | solution.py:125
  191.4 3.9 constant_dynamic-slice_fusion.1
  201.1 13.2 %glu.5.refs_1_ = bf16[2048,512]{1,0:T(8,128)(2,1)} custom-call(bf16[2048,2048]{1,0:T(8,128)(2,1)} %norm.1.h_ref.refs_0_, bf16[2,1024,512]{2,1,0:T(8,128)(2,1)} %pad_maximum_fusion.2.near_w, bf16[2,1024,512]{2,1,0:T(8,128)(2,1)} %collective-permute-done.12.far_w), custom_call_target="tpu_custom_call" | custom-call | flops 8589934592 | bytes 14680064 | tf_op jit(solution)/shard_map/glu/pallas_call | solution.py:155
  214.2 13.2 %glu.6.refs_2_ = bf16[2048,512]{1,0:T(8,128)(2,1)} custom-call(bf16[2048,2048]{1,0:T(8,128)(2,1)} %norm.1.h_ref.refs_0_, bf16[2,1024,512]{2,1,0:T(8,128)(2,1)} %pad_maximum_fusion.4.near_w, bf16[2,1024,512]{2,1,0:T(8,128)(2,1)} %collective-permute-done.19.far_w), custom_call_target="tpu_custom_call" | custom-call | flops 8589934592 | bytes 14680064 | tf_op jit(solution)/shard_map/glu/pallas_call | solution.py:155
  238.2 10.7 %mix.14.refs_4_ = f32[2048,256]{1,0:T(8,128)} custom-call(bf16[2048,512]{1,0:T(8,128)(2,1)} %glu.4.refs_0_, bf16[2048,512]{1,0:T(8,128)(2,1)} %glu.5.refs_1_, bf16[2048,512]{1,0:T(8,128)(2,1)} %glu.6.refs_2_, bf16[2048,512]{1,0:T(8,128)(2,1)} %bitcast.63, bf16[2048,512]{1,0:T(8,128)(2,1)} %collective-permute-done.23.refs_4_.refs_0_, ...), custom_call_target="tpu_custom_call" | custom-call | flops 4294967296 | bytes 18874368 | tf_op jit(solution)/shard_map/mix/pallas_call | solution.py:192
  250.0 11.1 %mix.15.refs_4_ = f32[2048,256]{1,0:T(8,128)} custom-call(bf16[2048,512]{1,0:T(8,128)(2,1)} %glu.4.refs_0_, bf16[2048,512]{1,0:T(8,128)(2,1)} %glu.5.refs_1_, bf16[2048,512]{1,0:T(8,128)(2,1)} %glu.6.refs_2_, bf16[2048,512]{1,0:T(8,128)(2,1)} %bitcast.64, bf16[2048,512]{1,0:T(8,128)(2,1)} %collective-permute-done.23.refs_4_.refs_0_, ...), custom_call_target="tpu_custom_call" | custom-call | flops 4294967296 | bytes 18874368 | tf_op jit(solution)/shard_map/mix/pallas_call | solution.py:192
  261.1 20.3 %collective-permute-done.10.far_w = bf16[2,1024,512]{2,1,0:T(8,128)(2,1)} collective-permute-done((bf16[2,1024,512]{2,1,0:T(8,128)(2,1)}, bf16[2,1024,512]{2,1,0:T(8,128)(2,1)}, u32[]{:S(2)}, u32[]{:S(2)}) %collective-permute-start.10) | collective-permute-done | bytes 2097184 | tf_op jit(solution)/shard_map/ppermute | solution.py:17
  281.4 13.2 %glu.7.refs_0_.refs_3_ = bf16[2048,512]{1,0:T(8,128)(2,1)} custom-call(bf16[2048,2048]{1,0:T(8,128)(2,1)} %norm.1.h_ref.refs_0_, bf16[2,1024,512]{2,1,0:T(8,128)(2,1)} %pad_maximum_fusion.near_w, bf16[2,1024,512]{2,1,0:T(8,128)(2,1)} %collective-permute-done.10.far_w), custom_call_target="tpu_custom_call" | custom-call | flops 8589934592 | bytes 14680064 | tf_op jit(solution)/shard_map/glu/pallas_call | solution.py:155
  300.3 3.4 mix.17
  303.7 5.9 %mix.16 = f32[1536,256]{1,0:T(8,128)} custom-call(bf16[2048,512]{1,0:T(8,128)(2,1)} %glu.7.refs_0_.refs_3_, bf16[2048,512]{1,0:T(8,128)(2,1)} %copy-done.3, bf16[2560,256]{1,0:T(8,128)(2,1)} %pad_maximum_fusion.6.refs_8_.refs_2_, bf16[2560,256]{1,0:T(8,128)(2,1)} %copy-done.5, f32[2048,256]{1,0:T(8,128)} %mix.14.refs_4_), custom_call_target="tpu_custom_call" | custom-call | flops 805306368 | bytes 3670016 | tf_op jit(solution)/shard_map/mix/pallas_call | solution.py:192
  309.6 16.5 %collective-permute-done.33 = bf16[2560,256]{1,0:T(8,128)(2,1)} collective-permute-done((bf16[2560,256]{1,0:T(8,128)(2,1)}, bf16[2560,256]{1,0:T(8,128)(2,1)}, u32[]{:S(2)}, u32[]{:S(2)}) %collective-permute-start.33) | collective-permute-done | bytes 1310752 | tf_op jit(solution)/shard_map/ppermute | solution.py:17
  333.1 7.9 %mix.18.refs_6_ = f32[2048,256]{1,0:T(8,128)} custom-call(bf16[2048,512]{1,0:T(8,128)(2,1)} %collective-permute-done.23.refs_4_.refs_0_, bf16[2048,512]{1,0:T(8,128)(2,1)} %collective-permute-done.24.refs_5_.refs_1_, bf16[2048,512]{1,0:T(8,128)(2,1)} %collective-permute-done.25.refs_6_.refs_2_, bf16[2048,512]{1,0:T(8,128)(2,1)} %copy-done.3, ...), custom_call_target="tpu_custom_call" | custom-call | flops 2684354560 | bytes 11796480 | tf_op jit(solution)/shard_map/mix/pallas_call | solution.py:192
  341.1 32.4 %collective-permute-done.32.refs_5_ = bf16[2560,128]{1,0:T(8,128)(2,1)S(1)} collective-permute-done((bf16[2560,128]{1,0:T(8,128)(2,1)}, bf16[2560,128]{1,0:T(8,128)(2,1)S(1)}, u32[]{:S(2)}, u32[]{:S(2)}) %collective-permute-start.32) | collective-permute-done | bytes 655392 | tf_op jit(solution)/shard_map/ppermute | solution.py:17
  374.3 7.7 %mix.19 = f32[2048,128]{1,0:T(8,128)} custom-call(bf16[2048,512]{1,0:T(8,128)(2,1)} %glu.4.refs_0_, bf16[2048,512]{1,0:T(8,128)(2,1)} %glu.5.refs_1_, bf16[2048,512]{1,0:T(8,128)(2,1)} %glu.6.refs_2_, bf16[2048,512]{1,0:T(8,128)(2,1)} %glu.7.refs_0_.refs_3_, bf16[2048,512]{1,0:T(8,128)(2,1)} %bitcast.65, bf16[2560,128]{1,0:T(8,128)(2,1)} %copy-done.29, ...), custom_call_target="tpu_custom_call" | custom-call | flops 1342177280 | bytes 11141120 | tf_op jit(solution)/shard_map/mix/pallas_call | solution.py:192
  382.0 4.8 %collective-permute-done.31.refs_5_ = bf16[2560,128]{1,0:T(8,128)(2,1)S(1)} collective-permute-done((bf16[2560,128]{1,0:T(8,128)(2,1)S(1)}, bf16[2560,128]{1,0:T(8,128)(2,1)S(1)}, u32[]{:S(2)}, u32[]{:S(2)}) %collective-permute-start.31) | collective-permute-done | bytes 655392 | tf_op jit(solution)/shard_map/ppermute | solution.py:17
  387.6 7.7 %mix.20 = f32[2048,128]{1,0:T(8,128)} custom-call(bf16[2048,512]{1,0:T(8,128)(2,1)} %glu.4.refs_0_, bf16[2048,512]{1,0:T(8,128)(2,1)} %glu.5.refs_1_, bf16[2048,512]{1,0:T(8,128)(2,1)} %glu.6.refs_2_, bf16[2048,512]{1,0:T(8,128)(2,1)} %glu.7.refs_0_.refs_3_, bf16[2048,512]{1,0:T(8,128)(2,1)} %bitcast.66, bf16[2560,128]{1,0:T(8,128)(2,1)} %copy-done.28, ...), custom_call_target="tpu_custom_call" | custom-call | flops 1342177280 | bytes 11141120 | tf_op jit(solution)/shard_map/mix/pallas_call | solution.py:192
  395.3 6.2 %mix.21 = bf16[1536,256]{1,0:T(8,128)(2,1)} custom-call(bf16[2048,512]{1,0:T(8,128)(2,1)} %glu.7.refs_0_.refs_3_, bf16[2048,512]{1,0:T(8,128)(2,1)} %copy-done.3, bf16[2560,256]{1,0:T(8,128)(2,1)} %pad_maximum_fusion.5.refs_8_.refs_2_, bf16[2560,256]{1,0:T(8,128)(2,1)} %copy-done.4, f32[2048,256]{1,0:T(8,128)} %mix.15.refs_4_, ...), custom_call_target="tpu_custom_call" | custom-call | flops 805306368 | bytes 3670016 | tf_op jit(solution)/shard_map/mix/pallas_call | solution.py:192
  407.9 8.3 %mix.22.refs_6_ = f32[2048,256]{1,0:T(8,128)} custom-call(bf16[2048,512]{1,0:T(8,128)(2,1)} %collective-permute-done.23.refs_4_.refs_0_, bf16[2048,512]{1,0:T(8,128)(2,1)} %collective-permute-done.24.refs_5_.refs_1_, bf16[2048,512]{1,0:T(8,128)(2,1)} %collective-permute-done.25.refs_6_.refs_2_, bf16[2048,512]{1,0:T(8,128)(2,1)} %copy-done.3, ...), custom_call_target="tpu_custom_call" | custom-call | flops 2684354560 | bytes 11796480 | tf_op jit(solution)/shard_map/mix/pallas_call | solution.py:192
  416.2 5.0 %collective-permute-done.37.refs_5_ = bf16[2560,128]{1,0:T(8,128)(2,1)S(1)} collective-permute-done((bf16[2560,128]{1,0:T(8,128)(2,1)}, bf16[2560,128]{1,0:T(8,128)(2,1)S(1)}, u32[]{:S(2)}, u32[]{:S(2)}) %collective-permute-start.37) | collective-permute-done | bytes 655392 | tf_op jit(solution)/shard_map/ppermute | solution.py:17
  421.2 6.7 %collective-permute-done.40.refs_7_ = f32[2048,128]{1,0:T(8,128)} collective-permute-done((f32[2048,128]{1,0:T(8,128)}, f32[2048,128]{1,0:T(8,128)}, u32[]{:S(2)}, u32[]{:S(2)}) %collective-permute-start.40) | collective-permute-done | bytes 1048608 | tf_op jit(solution)/shard_map/ppermute | solution.py:17
  427.9 8.0 %mix.23 = bf16[2048,128]{1,0:T(8,128)(2,1)} custom-call(bf16[2048,512]{1,0:T(8,128)(2,1)} %glu.4.refs_0_, bf16[2048,512]{1,0:T(8,128)(2,1)} %glu.5.refs_1_, bf16[2048,512]{1,0:T(8,128)(2,1)} %glu.6.refs_2_, bf16[2048,512]{1,0:T(8,128)(2,1)} %glu.7.refs_0_.refs_3_, bf16[2048,512]{1,0:T(8,128)(2,1)} %bitcast.67, bf16[2560,128]{1,0:T(8,128)(2,1)} %copy-done.30, ...), custom_call_target="tpu_custom_call" | custom-call | flops 1342177280 | bytes 11141120 | tf_op jit(solution)/shard_map/mix/pallas_call | solution.py:192
  439.0 11.3 %collective-permute-done.41.refs_7_ = f32[2048,128]{1,0:T(8,128)S(1)} collective-permute-done((f32[2048,128]{1,0:T(8,128)}, f32[2048,128]{1,0:T(8,128)S(1)}, u32[]{:S(2)}, u32[]{:S(2)}) %collective-permute-start.41) | collective-permute-done | bytes 1048608 | tf_op jit(solution)/shard_map/ppermute | solution.py:17
  451.2 8.0 %mix.24 = bf16[2048,128]{1,0:T(8,128)(2,1)} custom-call(bf16[2048,512]{1,0:T(8,128)(2,1)} %glu.4.refs_0_, bf16[2048,512]{1,0:T(8,128)(2,1)} %glu.5.refs_1_, bf16[2048,512]{1,0:T(8,128)(2,1)} %glu.6.refs_2_, bf16[2048,512]{1,0:T(8,128)(2,1)} %glu.7.refs_0_.refs_3_, bf16[2048,512]{1,0:T(8,128)(2,1)} %bitcast.68, ...), custom_call_target="tpu_custom_call" | custom-call | flops 1342177280 | bytes 11141120 | tf_op jit(solution)/shard_map/mix/pallas_call | solution.py:192
  461.1 3.6 mix.25
  467.3 5.2 %collective-permute-done.43 = bf16[2048,128]{1,0:T(8,128)(2,1)S(1)} collective-permute-done((bf16[2048,128]{1,0:T(8,128)(2,1)}, bf16[2048,128]{1,0:T(8,128)(2,1)S(1)}, u32[]{:S(2)}, u32[]{:S(2)}) %collective-permute-start.43) | collective-permute-done | bytes 524320 | tf_op jit(solution)/shard_map/ppermute | solution.py:17
  (194 shorter events, 93.1 us)
Async XLA Ops:
  3.3 26.8 %collective-permute-start = (bf16[2048,256]{1,0:T(8,128)(2,1)}, bf16[2048,256]{1,0:T(8,128)(2,1)}, u32[]{:S(2)}, u32[]{:S(2)}) collective-permute-start(bf16[2048,256]{1,0:T(8,128)(2,1)} %dynamic-slice_bitcast_fusion.2), channel_id=1, source_target_pairs={{0,4},{4,0},{1,5},{5,1},{2,6},{6,2},{3,7},{7,3}} | collective-permute-start | bytes 3145736 | tf_op jit(solution)/shard_map/ppermute | solution.py:17
  6.7 49.4 %collective-permute-start.1 = (bf16[2048,256]{1,0:T(8,128)(2,1)S(1)}, bf16[2048,256]{1,0:T(8,128)(2,1)}, u32[]{:S(2)}, u32[]{:S(2)}) collective-permute-start(bf16[2048,256]{1,0:T(8,128)(2,1)S(1)} %dynamic-slice_bitcast_fusion.1.refs_0_.refs_10_), channel_id=1, source_target_pairs={{0,2},{2,0},{1,3},{3,1},{4,6},{6,4},{5,7},{7,5}} | collective-permute-start | bytes 3145736 | tf_op jit(solution)/shard_map/ppermute | solution.py:17
  30.1 26.4 %collective-permute-start.2 = (bf16[2048,256]{1,0:T(8,128)(2,1)}, bf16[2048,256]{1,0:T(8,128)(2,1)}, u32[]{:S(2)}, u32[]{:S(2)}) collective-permute-start(bf16[2048,256]{1,0:T(8,128)(2,1)} %collective-permute-done.refs_1_.refs_6_), channel_id=1, source_target_pairs={{0,2},{2,0},{1,3},{3,1},{4,6},{6,4},{5,7},{7,5}} | collective-permute-start | bytes 3145736 | tf_op jit(solution)/shard_map/ppermute | solution.py:17
  33.3 36.7 %collective-permute-start.3 = (bf16[2048,256]{1,0:T(8,128)(2,1)S(1)}, bf16[2048,256]{1,0:T(8,128)(2,1)}, u32[]{:S(2)}, u32[]{:S(2)}) collective-permute-start(bf16[2048,256]{1,0:T(8,128)(2,1)S(1)} %dynamic-slice_bitcast_fusion.1.refs_0_.refs_10_), channel_id=1, source_target_pairs={{0,1},{1,0},{2,3},{3,2},{4,5},{5,4},{6,7},{7,6}} | collective-permute-start | bytes 3145736 | tf_op jit(solution)/shard_map/ppermute | solution.py:17
  33.3 32.5 %collective-permute-start.13 = (bf16[1024,512]{1,0:T(8,128)(2,1)}, bf16[1024,512]{1,0:T(8,128)(2,1)}, u32[]{:S(2)}, u32[]{:S(2)}) collective-permute-start(bf16[1024,512]{1,0:T(8,128)(2,1)} %param.17), channel_id=1, source_target_pairs={{0,4},{4,0},{1,5},{5,1},{2,6},{6,2},{3,7},{7,3}} | collective-permute-start | bytes 3145736 | tf_op jit(solution)/shard_map/ppermute | solution.py:17
  35.4 19.3 %collective-permute-start.8 = (f32[2,256]{1,0:T(2,128)S(1)}, f32[2,256]{1,0:T(2,128)S(1)}, u32[]{:S(2)}, u32[]{:S(2)}) collective-permute-start(f32[2,256]{1,0:T(2,128)S(1)} %pad_maximum_fusion.15), channel_id=1, source_target_pairs={{0,2},{2,0},{1,3},{3,1},{4,6},{6,4},{5,7},{7,5}} | collective-permute-start | bytes 6152 | tf_op jit(solution)/shard_map/ppermute | solution.py:17
  55.9 16.1 %collective-permute-start.4 = (bf16[2048,256]{1,0:T(8,128)(2,1)}, bf16[2048,256]{1,0:T(8,128)(2,1)}, u32[]{:S(2)}, u32[]{:S(2)}) collective-permute-start(bf16[2048,256]{1,0:T(8,128)(2,1)} %collective-permute-done.refs_1_.refs_6_), channel_id=1, source_target_pairs={{0,1},{1,0},{2,3},{3,2},{4,5},{5,4},{6,7},{7,6}} | collective-permute-start | bytes 3145736 | tf_op jit(solution)/shard_map/ppermute | solution.py:17
  56.5 16.1 %collective-permute-start.6 = (bf16[2048,256]{1,0:T(8,128)(2,1)}, bf16[2048,256]{1,0:T(8,128)(2,1)}, u32[]{:S(2)}, u32[]{:S(2)}) collective-permute-start(bf16[2048,256]{1,0:T(8,128)(2,1)} %collective-permute-done.2.refs_3_), channel_id=1, source_target_pairs={{0,1},{1,0},{2,3},{3,2},{4,5},{5,4},{6,7},{7,6}} | collective-permute-start | bytes 3145736 | tf_op jit(solution)/shard_map/ppermute | solution.py:17
  65.8 62.0 %collective-permute-start.11 = (bf16[2,1024,512]{2,1,0:T(8,128)(2,1)}, bf16[2,1024,512]{2,1,0:T(8,128)(2,1)}, u32[]{:S(2)}, u32[]{:S(2)}) collective-permute-start(bf16[2,1024,512]{2,1,0:T(8,128)(2,1)} %pad_maximum_fusion.1.near_w), channel_id=1, source_target_pairs={{0,4},{4,0},{1,5},{5,1},{2,6},{6,2},{3,7},{7,3}} | collective-permute-start | bytes 6291464 | tf_op jit(solution)/shard_map/ppermute | solution.py:17
  70.0 50.3 %collective-permute-start.17 = (bf16[512,256]{1,0:T(8,128)(2,1)S(1)}, bf16[512,256]{1,0:T(8,128)(2,1)}, u32[]{:S(2)}, u32[]{:S(2)}) collective-permute-start(bf16[512,256]{1,0:T(8,128)(2,1)S(1)} %constant_dynamic-slice_fusion.8), channel_id=1, source_target_pairs={{0,4},{4,0},{1,5},{5,1},{2,6},{6,2},{3,7},{7,3}} | collective-permute-start | bytes 786440 | tf_op jit(solution)/shard_map/ppermute | solution.py:17
  70.6 127.3 %collective-permute-start.12 = (bf16[2,1024,512]{2,1,0:T(8,128)(2,1)}, bf16[2,1024,512]{2,1,0:T(8,128)(2,1)}, u32[]{:S(2)}, u32[]{:S(2)}) collective-permute-start(bf16[2,1024,512]{2,1,0:T(8,128)(2,1)} %pad_maximum_fusion.2.near_w), channel_id=1, source_target_pairs={{0,4},{4,0},{1,5},{5,1},{2,6},{6,2},{3,7},{7,3}} | collective-permute-start | bytes 6291464 | tf_op jit(solution)/shard_map/ppermute | solution.py:17
  72.0 142.2 %collective-permute-start.19 = (bf16[2,1024,512]{2,1,0:T(8,128)(2,1)}, bf16[2,1024,512]{2,1,0:T(8,128)(2,1)}, u32[]{:S(2)}, u32[]{:S(2)}) collective-permute-start(bf16[2,1024,512]{2,1,0:T(8,128)(2,1)} %pad_maximum_fusion.4.near_w), channel_id=1, source_target_pairs={{0,4},{4,0},{1,5},{5,1},{2,6},{6,2},{3,7},{7,3}} | collective-permute-start | bytes 6291464 | tf_op jit(solution)/shard_map/ppermute | solution.py:17
  95.6 30.1 %collective-permute-start.14 = (bf16[2,512,512]{2,1,0:T(8,128)(2,1)S(1)}, bf16[2,512,512]{2,1,0:T(8,128)(2,1)}, u32[]{:S(2)}, u32[]{:S(2)}) collective-permute-start(bf16[2,512,512]{2,1,0:T(8,128)(2,1)S(1)} %dynamic-slice_bitcast_fusion), channel_id=1, source_target_pairs={{0,2},{2,0},{1,3},{3,1},{4,6},{6,4},{5,7},{7,5}} | collective-permute-start | bytes 3145736 | tf_op jit(solution)/shard_map/ppermute | solution.py:17
  125.3 18.9 %collective-permute-start.15 = (bf16[512,512]{1,0:T(8,128)(2,1)}, bf16[512,512]{1,0:T(8,128)(2,1)S(1)}, u32[]{:S(2)}, u32[]{:S(2)}) collective-permute-start(bf16[512,512]{1,0:T(8,128)(2,1)} %get-tuple-element.55), channel_id=1, source_target_pairs={{0,1},{1,0},{2,3},{3,2},{4,5},{5,4},{6,7},{7,6}} | collective-permute-start | bytes 1572872 | tf_op jit(solution)/shard_map/ppermute | solution.py:17
  127.8 16.3 %collective-permute-start.16 = (bf16[512,512]{1,0:T(8,128)(2,1)S(1)}, bf16[512,512]{1,0:T(8,128)(2,1)S(1)}, u32[]{:S(2)}, u32[]{:S(2)}) collective-permute-start(bf16[512,512]{1,0:T(8,128)(2,1)S(1)} %get-tuple-element.65), channel_id=1, source_target_pairs={{0,1},{1,0},{2,3},{3,2},{4,5},{5,4},{6,7},{7,6}} | collective-permute-start | bytes 1572872 | tf_op jit(solution)/shard_map/ppermute | solution.py:17
  197.4 36.2 %collective-permute-start.27 = (bf16[2560,256]{1,0:T(8,128)(2,1)}, bf16[2560,256]{1,0:T(8,128)(2,1)S(1)}, u32[]{:S(2)}, u32[]{:S(2)}) collective-permute-start(bf16[2560,256]{1,0:T(8,128)(2,1)} %pad_maximum_fusion.7), channel_id=1, source_target_pairs={{0,1},{1,0},{2,3},{3,2},{4,5},{5,4},{6,7},{7,6}} | collective-permute-start | bytes 3932168 | tf_op jit(solution)/shard_map/ppermute | solution.py:17
  197.7 38.1 %collective-permute-start.23 = (bf16[2048,512]{1,0:T(8,128)(2,1)}, bf16[2048,512]{1,0:T(8,128)(2,1)}, u32[]{:S(2)}, u32[]{:S(2)}) collective-permute-start(bf16[2048,512]{1,0:T(8,128)(2,1)} %glu.4.refs_0_), channel_id=1, source_target_pairs={{0,1},{1,0},{2,3},{3,2},{4,5},{5,4},{6,7},{7,6}} | collective-permute-start | bytes 6291464 | tf_op jit(solution)/shard_map/ppermute | solution.py:17
  197.9 29.6 %collective-permute-start.20 = (bf16[512,512]{1,0:T(8,128)(2,1)}, bf16[512,512]{1,0:T(8,128)(2,1)}, u32[]{:S(2)}, u32[]{:S(2)}) collective-permute-start(bf16[512,512]{1,0:T(8,128)(2,1)} %get-tuple-element.28), channel_id=1, source_target_pairs={{0,1},{1,0},{2,3},{3,2},{4,5},{5,4},{6,7},{7,6}} | collective-permute-start | bytes 1572872 | tf_op jit(solution)/shard_map/ppermute | solution.py:17
  200.4 29.2 %collective-permute-start.22 = (bf16[2,512,512]{2,1,0:T(8,128)(2,1)}, bf16[2,512,512]{2,1,0:T(8,128)(2,1)S(1)}, u32[]{:S(2)}, u32[]{:S(2)}) collective-permute-start(bf16[2,512,512]{2,1,0:T(8,128)(2,1)} %pad_maximum_fusion.9), channel_id=1, source_target_pairs={{0,2},{2,0},{1,3},{3,1},{4,6},{6,4},{5,7},{7,5}} | collective-permute-start | bytes 3145736 | tf_op jit(solution)/shard_map/ppermute | solution.py:17
  214.2 23.9 %collective-permute-start.24 = (bf16[2048,512]{1,0:T(8,128)(2,1)}, bf16[2048,512]{1,0:T(8,128)(2,1)}, u32[]{:S(2)}, u32[]{:S(2)}) collective-permute-start(bf16[2048,512]{1,0:T(8,128)(2,1)} %glu.5.refs_1_), channel_id=1, source_target_pairs={{0,1},{1,0},{2,3},{3,2},{4,5},{5,4},{6,7},{7,6}} | collective-permute-start | bytes 6291464 | tf_op jit(solution)/shard_map/ppermute | solution.py:17
  233.5 47.9 %collective-permute-start.10 = (bf16[2,1024,512]{2,1,0:T(8,128)(2,1)}, bf16[2,1024,512]{2,1,0:T(8,128)(2,1)}, u32[]{:S(2)}, u32[]{:S(2)}) collective-permute-start(bf16[2,1024,512]{2,1,0:T(8,128)(2,1)} %pad_maximum_fusion.near_w), channel_id=1, source_target_pairs={{0,4},{4,0},{1,5},{5,1},{2,6},{6,2},{3,7},{7,3}} | collective-permute-start | bytes 6291464 | tf_op jit(solution)/shard_map/ppermute | solution.py:17
  294.6 31.5 %collective-permute-start.33 = (bf16[2560,256]{1,0:T(8,128)(2,1)}, bf16[2560,256]{1,0:T(8,128)(2,1)}, u32[]{:S(2)}, u32[]{:S(2)}) collective-permute-start(bf16[2560,256]{1,0:T(8,128)(2,1)} %pad_maximum_fusion.7), channel_id=1, source_target_pairs={{0,4},{4,0},{1,5},{5,1},{2,6},{6,2},{3,7},{7,3}} | collective-permute-start | bytes 3932168 | tf_op jit(solution)/shard_map/ppermute | solution.py:17
  326.1 69.2 %collective-permute-start.30 = (f32[1536,256]{1,0:T(8,128)}, f32[1536,256]{1,0:T(8,128)}, u32[]{:S(2)}, u32[]{:S(2)}) collective-permute-start(f32[1536,256]{1,0:T(8,128)} %mix.16), channel_id=1, source_target_pairs={{0,2},{2,0},{1,3},{3,1},{4,6},{6,4},{5,7},{7,5}} | collective-permute-start | bytes 4718600 | tf_op jit(solution)/shard_map/ppermute | solution.py:17
  327.5 74.0 %collective-permute-start.38 = (bf16[2560,256]{1,0:T(8,128)(2,1)}, bf16[2560,256]{1,0:T(8,128)(2,1)}, u32[]{:S(2)}, u32[]{:S(2)}) collective-permute-start(bf16[2560,256]{1,0:T(8,128)(2,1)} %pad_maximum_fusion.8), channel_id=1, source_target_pairs={{0,4},{4,0},{1,5},{5,1},{2,6},{6,2},{3,7},{7,3}} | collective-permute-start | bytes 3932168 | tf_op jit(solution)/shard_map/ppermute | solution.py:17
  330.0 43.4 %collective-permute-start.32 = (bf16[2560,128]{1,0:T(8,128)(2,1)}, bf16[2560,128]{1,0:T(8,128)(2,1)S(1)}, u32[]{:S(2)}, u32[]{:S(2)}) collective-permute-start(bf16[2560,128]{1,0:T(8,128)(2,1)} %get-tuple-element.59), channel_id=1, source_target_pairs={{0,4},{4,0},{1,5},{5,1},{2,6},{6,2},{3,7},{7,3}} | collective-permute-start | bytes 1966088 | tf_op jit(solution)/shard_map/ppermute | solution.py:17
  330.5 56.2 %collective-permute-start.31 = (bf16[2560,128]{1,0:T(8,128)(2,1)S(1)}, bf16[2560,128]{1,0:T(8,128)(2,1)S(1)}, u32[]{:S(2)}, u32[]{:S(2)}) collective-permute-start(bf16[2560,128]{1,0:T(8,128)(2,1)S(1)} %get-tuple-element.60), channel_id=1, source_target_pairs={{0,4},{4,0},{1,5},{5,1},{2,6},{6,2},{3,7},{7,3}} | collective-permute-start | bytes 1966088 | tf_op jit(solution)/shard_map/ppermute | solution.py:17
  401.5 26.4 %collective-permute-start.40 = (f32[2048,128]{1,0:T(8,128)}, f32[2048,128]{1,0:T(8,128)}, u32[]{:S(2)}, u32[]{:S(2)}) collective-permute-start(f32[2048,128]{1,0:T(8,128)} %mix.19), channel_id=1, source_target_pairs={{0,2},{2,0},{1,3},{3,1},{4,6},{6,4},{5,7},{7,5}} | collective-permute-start | bytes 3145736 | tf_op jit(solution)/shard_map/ppermute | solution.py:17
  403.4 17.8 %collective-permute-start.37 = (bf16[2560,128]{1,0:T(8,128)(2,1)}, bf16[2560,128]{1,0:T(8,128)(2,1)S(1)}, u32[]{:S(2)}, u32[]{:S(2)}) collective-permute-start(bf16[2560,128]{1,0:T(8,128)(2,1)} %get-tuple-element.57), channel_id=1, source_target_pairs={{0,4},{4,0},{1,5},{5,1},{2,6},{6,2},{3,7},{7,3}} | collective-permute-start | bytes 1966088 | tf_op jit(solution)/shard_map/ppermute | solution.py:17
  404.6 45.7 %collective-permute-start.41 = (f32[2048,128]{1,0:T(8,128)}, f32[2048,128]{1,0:T(8,128)S(1)}, u32[]{:S(2)}, u32[]{:S(2)}) collective-permute-start(f32[2048,128]{1,0:T(8,128)} %mix.20), channel_id=1, source_target_pairs={{0,2},{2,0},{1,3},{3,1},{4,6},{6,4},{5,7},{7,5}} | collective-permute-start | bytes 3145736 | tf_op jit(solution)/shard_map/ppermute | solution.py:17
  406.3 32.7 %collective-permute-start.36 = (bf16[2560,128]{1,0:T(8,128)(2,1)}, bf16[2560,128]{1,0:T(8,128)(2,1)}, u32[]{:S(2)}, u32[]{:S(2)}) collective-permute-start(bf16[2560,128]{1,0:T(8,128)(2,1)} %get-tuple-element.58), channel_id=1, source_target_pairs={{0,4},{4,0},{1,5},{5,1},{2,6},{6,2},{3,7},{7,3}} | collective-permute-start | bytes 1966088 | tf_op jit(solution)/shard_map/ppermute | solution.py:17
  406.8 54.3 %collective-permute-start.35 = (f32[512,256]{1,0:T(8,128)}, f32[512,256]{1,0:T(8,128)}, u32[]{:S(2)}, u32[]{:S(2)}) collective-permute-start(f32[512,256]{1,0:T(8,128)} %mix.17), channel_id=1, source_target_pairs={{0,2},{2,0},{1,3},{3,1},{4,6},{6,4},{5,7},{7,5}} | collective-permute-start | bytes 1572872 | tf_op jit(solution)/shard_map/ppermute | solution.py:17
  435.9 30.5 %collective-permute-start.42 = (bf16[2048,128]{1,0:T(8,128)(2,1)}, bf16[2048,128]{1,0:T(8,128)(2,1)S(1)}, u32[]{:S(2)}, u32[]{:S(2)}) collective-permute-start(bf16[2048,128]{1,0:T(8,128)(2,1)} %mix.23), channel_id=1, source_target_pairs={{0,4},{4,0},{1,5},{5,1},{2,6},{6,2},{3,7},{7,3}} | collective-permute-start | bytes 1572872 | tf_op jit(solution)/shard_map/ppermute | solution.py:17
  (50 other events, 368.8 us)

commit v4 on v3

--- a/solution.py
+++ b/solution.py
@@ -228,7 +228,7 @@
         mine_x = swap_x(mine)
         from_yx = swap_x(from_y)
         near = [mine, from_y, mine_x, from_yx]
-        far = [swap_c(p) for p in near]
+        far = [swap_c(near[0])] + [swap_c(p) for p in near[1:]]
         offs = []
         for cr in range(2):
             for xr in range(2):
@@ -236,11 +236,12 @@
                     offs.append(width * (4 * yr + 2 * (xr ^ xi) + (cr ^ ci)))
         h = layer_norm(near + far, g, jnp.stack(offs).astype(jnp.int32))
 
-        kv_rows = w_key.shape[0] // 2
+        kv_rows = w_key.shape[0] // 4
         w_kv = jnp.concatenate([w_key, w_value], axis=1)
-        kv_part = swap_y(lax.dynamic_slice_in_dim(w_kv, ci * kv_rows, kv_rows, 0))
-        kv_pair = jnp.stack([kv_part, swap_c(kv_part)])
-        kv_far = jnp.where(ci == 0, kv_pair, kv_pair[::-1]).reshape(w_kv.shape)
+        ordered = lambda pair, i, axis: jnp.where(i == 0, jnp.stack(pair, axis), jnp.stack(pair[::-1], axis))
+        kv_part = swap_y(lax.dynamic_slice_in_dim(w_kv, ti * kv_rows, kv_rows, 0))
+        kv_pair = ordered([kv_part, swap_x(kv_part)], xi, 0)
+        kv_far = ordered([kv_pair, swap_c(kv_pair)], ci, 1).reshape(w_kv.shape)
         q_far = swap_y(w_query)
 
         q = mix([(h, jnp.concatenate([w_query, q_far], 0), 0)], dtype=BF16)
@@ -248,14 +249,17 @@
         kv = jnp.dot(h_own, jnp.concatenate([w_kv, kv_far], 0), preferred_element_type=F32).astype(BF16)
 
         q4 = q.reshape(2, 2, own_tok, q.shape[1])
-        q_x = [pick(q4, xi), swap_x(pick(q4, 1 - xi))]
-        q_c = [pick(v, ci) for v in q_x] + [swap_c(pick(v, 1 - ci)) for v in q_x]
+        q_back = swap_x(pick(q4, 1 - xi))
 
         chunks = 4
         cw = w_gate.shape[1] // chunks
         near_ws = [jnp.stack([w[:, j * cw : (j + 1) * cw] for w in (w_gate, w_up)]) for j in range(chunks)]
         far_ws = [swap_y(w) for w in near_ws]
         a_own = [glu(h, near_ws[0], far_ws[0])]
+        q_back = tie(q_back, a_own[0])
+        q_x = [pick(q4, xi), q_back]
+        q_c = [pick(v, ci) for v in q_x] + [swap_c(pick(v, 1 - ci)) for v in q_x]
+
         half_dim = dim // 2
         inv_freq = ROPE_BASE ** (-2.0 * jnp.arange(half_dim, dtype=F32) / dim)
         positions = (lengths[:, None] + jnp.arange(new, dtype=jnp.int32)[None, :]).reshape(own_tok)
@@ -263,7 +267,7 @@
         cos_t, sin_t = jnp.cos(angles), jnp.sin(angles)
         cos_t = jnp.concatenate([cos_t, cos_t], -1)
         sin_t = jnp.concatenate([-sin_t, sin_t], -1)
-        o0, o1, o2, o3, k_next, v_next = attention(lengths, [tie(q_c[0], a_own[0]), *q_c[1:]], kv, cos_t, sin_t, k_cache, v_cache)
+        o0, o1, o2, o3, k_next, v_next = attention(lengths, q_c, kv, cos_t, sin_t, k_cache, v_cache)
 
         keep = [o0, swap_c(o2)]
         send = swap_x(jnp.stack([o1, swap_c(o3)]))

time: 474 us -> 499 us (1.053)
  waiting for transfers between devices: 166 us -> 188 us
    ppermute x44 -> x45, waiting for transfers between devices: 166 us -> 188 us  [swap(): return lambda a: lax.ppermute(a, axis, pairs)]
    ppermute x44 -> x45, starting transfers between devices: 32.8 us -> 36.1 us  [swap(): return lambda a: lax.ppermute(a, axis, pairs)]
    unnamed x77 -> x73, local copies, waits for them, and re-layouts: 13 us -> 13.1 us
  transfers between devices with their start and end apart: 44 -> 45, of which waited for: 15 -> 15; matrix products, arithmetic and copies ran while one was open for 11% -> 10% of each run, Pallas kernels for 41% -> 39%
where the time goes in v4:
time: 499 us; the launch traced here: 498 us
  Pallas kernels  209 us (42%)
  waiting for transfers between devices  188 us (38%)
  starting transfers between devices  36.1 us (7%)
  local copies, waits for them, and re-layouts  35.2 us (7%)
  other arithmetic  24.9 us (5%)
    ppermute x45, waiting for transfers between devices, swap(): return lambda a: lax.ppermute(a, axis, pairs)  188 us
    pallas_call x13, Pallas kernels, mix(): pl.pallas_call(functools.partial(mix_kernel, plan, len(lhs), len(ws)), gr...  97.1 us
    pallas_call x4, Pallas kernels, glu(): pl.pallas_call(glu_kernel, grid=(tokens // blk,), in_specs=[pl.BlockSpec(...  52.7 us
    pallas_call x1, Pallas kernels, attention(): pl.pallas_call(attn_kernel, grid_spec=pltpu.PrefetchScalarGridSpec(num_sc...  46.2 us
    ppermute x45, starting transfers between devices, swap(): return lambda a: lax.ppermute(a, axis, pairs)  36.1 us
    unnamed x73, local copies, waits for them, and re-layouts  13.1 us
    pallas_call x1, Pallas kernels, layer_norm(): pl.pallas_call(norm_kernel, grid_spec=pltpu.PrefetchScalarGridSpec(num_sc...  13 us
  transfers between devices with their start and end apart: 45, of which 15 were waited for; matrix products, arithmetic and copies ran while one was open for 10% of the time, Pallas kernels for 39%

profile of v4, /device:TPU:0, one launch (start us, length us, event | category | flops | bytes accessed | tf_op | source)
XLA Modules:
  0.0 497.6 jit_solution(7317735036788805448)
XLA Ops:
  10.2 20.7 %collective-permute-done.refs_1_.refs_6_ = bf16[2048,256]{1,0:T(8,128)(2,1)} collective-permute-done((bf16[2048,256]{1,0:T(8,128)(2,1)}, bf16[2048,256]{1,0:T(8,128)(2,1)}, u32[]{:S(2)}, u32[]{:S(2)}) %collective-permute-start) | collective-permute-done | bytes 1048608 | tf_op jit(solution)/shard_map/ppermute | solution.py:17
  32.9 5.5 %slice_bitcast_fusion = (bf16[1,1024,512]{2,1,0:T(8,128)(2,1)S(1)}, bf16[1,1024,512]{2,1,0:T(8,128)(2,1)S(1)}, bf16[1,1024,512]{2,1,0:T(8,128)(2,1)}, bf16[1,102...) fusion(bf16[1024,2048]{1,0:T(8,128)(2,1)} %param.21, ...), kind=kLoop, calls=%fused_computation.28 | loop fusion | bytes 16777216 | tf_op jit(solution)/shard_map/stack | solution.py:256
  43.5 11.2 %collective-permute-done.8 = f32[2,256]{1,0:T(2,128)S(1)} collective-permute-done((f32[2,256]{1,0:T(2,128)S(1)}, f32[2,256]{1,0:T(2,128)S(1)}, u32[]{:S(2)}, u32[]{:S(2)}) %collective-permute-start.8) | collective-permute-done | bytes 2080 | tf_op jit(solution)/shard_map/ppermute | solution.py:17
  57.4 42.8 %collective-permute-done.17 = bf16[256,256]{1,0:T(8,128)(2,1)S(1)} collective-permute-done((bf16[256,256]{1,0:T(8,128)(2,1)S(1)}, bf16[256,256]{1,0:T(8,128)(2,1)S(1)}, u32[]{:S(2)}, u32[]{:S(2)}) %collective-permute-start.17) | collective-permute-done | bytes 131104 | tf_op jit(solution)/shard_map/ppermute | solution.py:17
  113.7 13.0 %norm.1.h_ref.refs_0_ = bf16[2048,2048]{1,0:T(8,128)(2,1)} custom-call(s32[8]{0:T(128)} %stack.140.offs_ref, bf16[2048,256]{1,0:T(8,128)(2,1)} %copy-done.6, bf16[2048,256]{1,0:T(8,128)(2,1)} %collective-permute-done.refs_1_.refs_6_, bf16[2048,256]{1,0:T(8,128)(2,1)} %collective-permute-done.1.refs_2_, bf16[2048,256]{1,0:T(8,128)(2,1)} %collective-permute-done.2.refs_3_, ...), custom_call_target="tpu_custom_call" | custom-call | flops 83886080 | bytes 16777216 | tf_op jit(solution)/shard_map/norm/pallas_call | solution.py:47
  126.8 8.7 %mix.13 = bf16[2048,512]{1,0:T(8,128)(2,1)} custom-call(bf16[2048,2048]{1,0:T(8,128)(2,1)} %norm.1.h_ref.refs_0_, bf16[2048,512]{1,0:T(8,128)(2,1)} %pad_maximum_fusion.3.refs_1_), custom_call_target="tpu_custom_call" | custom-call | flops 4294967296 | bytes 10485760 | tf_op jit(solution)/shard_map/mix/pallas_call | solution.py:192
  139.6 13.2 %glu.4.refs_0_ = bf16[2048,512]{1,0:T(8,128)(2,1)} custom-call(bf16[2048,2048]{1,0:T(8,128)(2,1)} %norm.1.h_ref.refs_0_, bf16[2,1024,512]{2,1,0:T(8,128)(2,1)} %pad_maximum_fusion.1.near_w, bf16[2,1024,512]{2,1,0:T(8,128)(2,1)} %collective-permute-done.11.far_w), custom_call_target="tpu_custom_call" | custom-call | flops 8589934592 | bytes 14680064 | tf_op jit(solution)/shard_map/glu/pallas_call | solution.py:155
  152.7 8.6 %collective-permute-done.14 = bf16[2,512,512]{2,1,0:T(8,128)(2,1)} collective-permute-done((bf16[2,512,512]{2,1,0:T(8,128)(2,1)S(1)}, bf16[2,512,512]{2,1,0:T(8,128)(2,1)}, u32[]{:S(2)}, u32[]{:S(2)}) %collective-permute-start.14) | collective-permute-done | bytes 1048608 | tf_op jit(solution)/shard_map/ppermute | solution.py:17
  170.8 46.2 %attn.1 = (bf16[512,512]{1,0:T(8,128)(2,1)}, bf16[512,512]{1,0:T(8,128)(2,1)}, bf16[512,512]{1,0:T(8,128)(2,1)}, bf16[512,512]{1,0:T(8,128)(2,1)}, bf16[8,2048,1...) custom-call(s32[8]{0:T(128)} %len_ref.1, bf16[512,512]{1,0:T(8,128)(2,1)} %get-tuple-element.56.q0, ...), custom_call_target="tpu_custom_call" | custom-call | flops 17179869184 | bytes 16777216 | tf_op jit(solution)/shard_map/attn/pallas_call | solution.py:125
  217.2 4.0 constant_dynamic-slice_fusion.1
  225.0 13.2 %glu.5.refs_1_ = bf16[2048,512]{1,0:T(8,128)(2,1)} custom-call(bf16[2048,2048]{1,0:T(8,128)(2,1)} %norm.1.h_ref.refs_0_, bf16[2,1024,512]{2,1,0:T(8,128)(2,1)} %pad_maximum_fusion.2.near_w, bf16[2,1024,512]{2,1,0:T(8,128)(2,1)} %collective-permute-done.12.far_w), custom_call_target="tpu_custom_call" | custom-call | flops 8589934592 | bytes 14680064 | tf_op jit(solution)/shard_map/glu/pallas_call | solution.py:155
  238.4 13.2 %glu.6.refs_2_ = bf16[2048,512]{1,0:T(8,128)(2,1)} custom-call(bf16[2048,2048]{1,0:T(8,128)(2,1)} %norm.1.h_ref.refs_0_, bf16[2,1024,512]{2,1,0:T(8,128)(2,1)} %pad_maximum_fusion.4.near_w, bf16[2,1024,512]{2,1,0:T(8,128)(2,1)} %collective-permute-done.20.far_w), custom_call_target="tpu_custom_call" | custom-call | flops 8589934592 | bytes 14680064 | tf_op jit(solution)/shard_map/glu/pallas_call | solution.py:155
  262.7 10.8 %mix.14.refs_4_ = f32[2048,256]{1,0:T(8,128)} custom-call(bf16[2048,512]{1,0:T(8,128)(2,1)} %glu.4.refs_0_, bf16[2048,512]{1,0:T(8,128)(2,1)} %glu.5.refs_1_, bf16[2048,512]{1,0:T(8,128)(2,1)} %glu.6.refs_2_, bf16[2048,512]{1,0:T(8,128)(2,1)} %bitcast.66, bf16[2048,512]{1,0:T(8,128)(2,1)} %collective-permute-done.24.refs_4_.refs_0_, ...), custom_call_target="tpu_custom_call" | custom-call | flops 4294967296 | bytes 18874368 | tf_op jit(solution)/shard_map/mix/pallas_call | solution.py:192
  274.5 11.1 %mix.15.refs_4_ = f32[2048,256]{1,0:T(8,128)} custom-call(bf16[2048,512]{1,0:T(8,128)(2,1)} %glu.4.refs_0_, bf16[2048,512]{1,0:T(8,128)(2,1)} %glu.5.refs_1_, bf16[2048,512]{1,0:T(8,128)(2,1)} %glu.6.refs_2_, bf16[2048,512]{1,0:T(8,128)(2,1)} %bitcast.67, bf16[2048,512]{1,0:T(8,128)(2,1)} %collective-permute-done.24.refs_4_.refs_0_, ...), custom_call_target="tpu_custom_call" | custom-call | flops 4294967296 | bytes 18874368 | tf_op jit(solution)/shard_map/mix/pallas_call | solution.py:192
  285.6 20.0 %collective-permute-done.10.far_w = bf16[2,1024,512]{2,1,0:T(8,128)(2,1)} collective-permute-done((bf16[2,1024,512]{2,1,0:T(8,128)(2,1)}, bf16[2,1024,512]{2,1,0:T(8,128)(2,1)}, u32[]{:S(2)}, u32[]{:S(2)}) %collective-permute-start.10) | collective-permute-done | bytes 2097184 | tf_op jit(solution)/shard_map/ppermute | solution.py:17
  305.6 13.2 %glu.7.refs_0_.refs_3_ = bf16[2048,512]{1,0:T(8,128)(2,1)} custom-call(bf16[2048,2048]{1,0:T(8,128)(2,1)} %norm.1.h_ref.refs_0_, bf16[2,1024,512]{2,1,0:T(8,128)(2,1)} %pad_maximum_fusion.near_w, bf16[2,1024,512]{2,1,0:T(8,128)(2,1)} %collective-permute-done.10.far_w), custom_call_target="tpu_custom_call" | custom-call | flops 8589934592 | bytes 14680064 | tf_op jit(solution)/shard_map/glu/pallas_call | solution.py:155
  327.9 5.9 %mix.16 = f32[1536,256]{1,0:T(8,128)} custom-call(bf16[2048,512]{1,0:T(8,128)(2,1)} %glu.7.refs_0_.refs_3_, bf16[2048,512]{1,0:T(8,128)(2,1)} %copy-done.3, bf16[2560,256]{1,0:T(8,128)(2,1)} %pad_maximum_fusion.6.refs_8_.refs_2_, bf16[2560,256]{1,0:T(8,128)(2,1)} %copy-done.5, f32[2048,256]{1,0:T(8,128)} %mix.14.refs_4_), custom_call_target="tpu_custom_call" | custom-call | flops 805306368 | bytes 3670016 | tf_op jit(solution)/shard_map/mix/pallas_call | solution.py:192
  333.8 16.5 %collective-permute-done.34 = bf16[2560,256]{1,0:T(8,128)(2,1)} collective-permute-done((bf16[2560,256]{1,0:T(8,128)(2,1)}, bf16[2560,256]{1,0:T(8,128)(2,1)}, u32[]{:S(2)}, u32[]{:S(2)}) %collective-permute-start.34) | collective-permute-done | bytes 1310752 | tf_op jit(solution)/shard_map/ppermute | solution.py:17
  357.8 7.9 %mix.18.refs_6_ = f32[2048,256]{1,0:T(8,128)} custom-call(bf16[2048,512]{1,0:T(8,128)(2,1)} %collective-permute-done.24.refs_4_.refs_0_, bf16[2048,512]{1,0:T(8,128)(2,1)} %collective-permute-done.25.refs_5_.refs_1_, bf16[2048,512]{1,0:T(8,128)(2,1)} %collective-permute-done.26.refs_6_.refs_2_, bf16[2048,512]{1,0:T(8,128)(2,1)} %copy-done.3, ...), custom_call_target="tpu_custom_call" | custom-call | flops 2684354560 | bytes 11796480 | tf_op jit(solution)/shard_map/mix/pallas_call | solution.py:192
  365.7 32.3 %collective-permute-done.33.refs_5_ = bf16[2560,128]{1,0:T(8,128)(2,1)S(1)} collective-permute-done((bf16[2560,128]{1,0:T(8,128)(2,1)}, bf16[2560,128]{1,0:T(8,128)(2,1)S(1)}, u32[]{:S(2)}, u32[]{:S(2)}) %collective-permute-start.33) | collective-permute-done | bytes 655392 | tf_op jit(solution)/shard_map/ppermute | solution.py:17
  398.9 7.7 %mix.19 = f32[2048,128]{1,0:T(8,128)} custom-call(bf16[2048,512]{1,0:T(8,128)(2,1)} %glu.4.refs_0_, bf16[2048,512]{1,0:T(8,128)(2,1)} %glu.5.refs_1_, bf16[2048,512]{1,0:T(8,128)(2,1)} %glu.6.refs_2_, bf16[2048,512]{1,0:T(8,128)(2,1)} %glu.7.refs_0_.refs_3_, bf16[2048,512]{1,0:T(8,128)(2,1)} %bitcast.68, bf16[2560,128]{1,0:T(8,128)(2,1)} %copy-done.27, ...), custom_call_target="tpu_custom_call" | custom-call | flops 1342177280 | bytes 11141120 | tf_op jit(solution)/shard_map/mix/pallas_call | solution.py:192
  406.6 4.8 collective-permute-done.32.refs_5_
  412.2 7.7 %mix.20 = f32[2048,128]{1,0:T(8,128)} custom-call(bf16[2048,512]{1,0:T(8,128)(2,1)} %glu.4.refs_0_, bf16[2048,512]{1,0:T(8,128)(2,1)} %glu.5.refs_1_, bf16[2048,512]{1,0:T(8,128)(2,1)} %glu.6.refs_2_, bf16[2048,512]{1,0:T(8,128)(2,1)} %glu.7.refs_0_.refs_3_, bf16[2048,512]{1,0:T(8,128)(2,1)} %bitcast.69, bf16[2560,128]{1,0:T(8,128)(2,1)} %copy-done.26, ...), custom_call_target="tpu_custom_call" | custom-call | flops 1342177280 | bytes 11141120 | tf_op jit(solution)/shard_map/mix/pallas_call | solution.py:192
  419.9 5.9 %mix.21 = bf16[1536,256]{1,0:T(8,128)(2,1)} custom-call(bf16[2048,512]{1,0:T(8,128)(2,1)} %glu.7.refs_0_.refs_3_, bf16[2048,512]{1,0:T(8,128)(2,1)} %copy-done.3, bf16[2560,256]{1,0:T(8,128)(2,1)} %pad_maximum_fusion.5.refs_8_.refs_2_, bf16[2560,256]{1,0:T(8,128)(2,1)} %copy-done.4, f32[2048,256]{1,0:T(8,128)} %mix.15.refs_4_, ...), custom_call_target="tpu_custom_call" | custom-call | flops 805306368 | bytes 3670016 | tf_op jit(solution)/shard_map/mix/pallas_call | solution.py:192
  432.1 8.3 %mix.22.refs_6_ = f32[2048,256]{1,0:T(8,128)} custom-call(bf16[2048,512]{1,0:T(8,128)(2,1)} %collective-permute-done.24.refs_4_.refs_0_, bf16[2048,512]{1,0:T(8,128)(2,1)} %collective-permute-done.25.refs_5_.refs_1_, bf16[2048,512]{1,0:T(8,128)(2,1)} %collective-permute-done.26.refs_6_.refs_2_, bf16[2048,512]{1,0:T(8,128)(2,1)} %copy-done.3, ...), custom_call_target="tpu_custom_call" | custom-call | flops 2684354560 | bytes 11796480 | tf_op jit(solution)/shard_map/mix/pallas_call | solution.py:192
  440.5 4.7 collective-permute-done.38.refs_5_
  445.1 7.1 %collective-permute-done.41.refs_7_ = f32[2048,128]{1,0:T(8,128)} collective-permute-done((f32[2048,128]{1,0:T(8,128)}, f32[2048,128]{1,0:T(8,128)}, u32[]{:S(2)}, u32[]{:S(2)}) %collective-permute-start.41) | collective-permute-done | bytes 1048608 | tf_op jit(solution)/shard_map/ppermute | solution.py:17
  452.2 8.0 %mix.23 = bf16[2048,128]{1,0:T(8,128)(2,1)} custom-call(bf16[2048,512]{1,0:T(8,128)(2,1)} %glu.4.refs_0_, bf16[2048,512]{1,0:T(8,128)(2,1)} %glu.5.refs_1_, bf16[2048,512]{1,0:T(8,128)(2,1)} %glu.6.refs_2_, bf16[2048,512]{1,0:T(8,128)(2,1)} %glu.7.refs_0_.refs_3_, bf16[2048,512]{1,0:T(8,128)(2,1)} %bitcast.70, bf16[2560,128]{1,0:T(8,128)(2,1)} %copy-done.28, ...), custom_call_target="tpu_custom_call" | custom-call | flops 1342177280 | bytes 11141120 | tf_op jit(solution)/shard_map/mix/pallas_call | solution.py:192
  463.4 11.2 %collective-permute-done.42.refs_7_ = f32[2048,128]{1,0:T(8,128)S(1)} collective-permute-done((f32[2048,128]{1,0:T(8,128)}, f32[2048,128]{1,0:T(8,128)S(1)}, u32[]{:S(2)}, u32[]{:S(2)}) %collective-permute-start.42) | collective-permute-done | bytes 1048608 | tf_op jit(solution)/shard_map/ppermute | solution.py:17
  475.5 8.0 %mix.24 = bf16[2048,128]{1,0:T(8,128)(2,1)} custom-call(bf16[2048,512]{1,0:T(8,128)(2,1)} %glu.4.refs_0_, bf16[2048,512]{1,0:T(8,128)(2,1)} %glu.5.refs_1_, bf16[2048,512]{1,0:T(8,128)(2,1)} %glu.6.refs_2_, bf16[2048,512]{1,0:T(8,128)(2,1)} %glu.7.refs_0_.refs_3_, bf16[2048,512]{1,0:T(8,128)(2,1)} %bitcast.71, ...), custom_call_target="tpu_custom_call" | custom-call | flops 1342177280 | bytes 11141120 | tf_op jit(solution)/shard_map/mix/pallas_call | solution.py:192
  485.4 3.6 mix.25
  491.5 5.2 %collective-permute-done.44 = bf16[2048,128]{1,0:T(8,128)(2,1)S(1)} collective-permute-done((bf16[2048,128]{1,0:T(8,128)(2,1)}, bf16[2048,128]{1,0:T(8,128)(2,1)S(1)}, u32[]{:S(2)}, u32[]{:S(2)}) %collective-permute-start.44) | collective-permute-done | bytes 524320 | tf_op jit(solution)/shard_map/ppermute | solution.py:17
  (194 shorter events, 96.5 us)
Async XLA Ops:
  3.3 27.7 %collective-permute-start = (bf16[2048,256]{1,0:T(8,128)(2,1)}, bf16[2048,256]{1,0:T(8,128)(2,1)}, u32[]{:S(2)}, u32[]{:S(2)}) collective-permute-start(bf16[2048,256]{1,0:T(8,128)(2,1)} %dynamic-slice_bitcast_fusion.2), channel_id=1, source_target_pairs={{0,4},{4,0},{1,5},{5,1},{2,6},{6,2},{3,7},{7,3}} | collective-permute-start | bytes 3145736 | tf_op jit(solution)/shard_map/ppermute | solution.py:17
  6.7 93.5 %collective-permute-start.1 = (bf16[2048,256]{1,0:T(8,128)(2,1)S(1)}, bf16[2048,256]{1,0:T(8,128)(2,1)}, u32[]{:S(2)}, u32[]{:S(2)}) collective-permute-start(bf16[2048,256]{1,0:T(8,128)(2,1)S(1)} %dynamic-slice_bitcast_fusion.1.refs_0_.refs_10_), channel_id=1, source_target_pairs={{0,2},{2,0},{1,3},{3,1},{4,6},{6,4},{5,7},{7,5}} | collective-permute-start | bytes 3145736 | tf_op jit(solution)/shard_map/ppermute | solution.py:17
  8.2 34.0 %collective-permute-start.7 = (f32[1,256]{1,0:T(1,128)S(1)}, f32[1,256]{1,0:T(1,128)S(1)}, u32[]{:S(2)}, u32[]{:S(2)}) collective-permute-start(f32[1,256]{1,0:T(1,128)S(1)} %bitcast.83), channel_id=1, source_target_pairs={{0,4},{4,0},{1,5},{5,1},{2,6},{6,2},{3,7},{7,3}} | collective-permute-start | bytes 3080 | tf_op jit(solution)/shard_map/ppermute | solution.py:17
  8.7 92.0 %collective-permute-start.13 = (bf16[1024,512]{1,0:T(8,128)(2,1)}, bf16[1024,512]{1,0:T(8,128)(2,1)}, u32[]{:S(2)}, u32[]{:S(2)}) collective-permute-start(bf16[1024,512]{1,0:T(8,128)(2,1)} %param.17), channel_id=1, source_target_pairs={{0,4},{4,0},{1,5},{5,1},{2,6},{6,2},{3,7},{7,3}} | collective-permute-start | bytes 3145736 | tf_op jit(solution)/shard_map/ppermute | solution.py:17
  30.9 69.8 %collective-permute-start.2 = (bf16[2048,256]{1,0:T(8,128)(2,1)}, bf16[2048,256]{1,0:T(8,128)(2,1)}, u32[]{:S(2)}, u32[]{:S(2)}) collective-permute-start(bf16[2048,256]{1,0:T(8,128)(2,1)} %collective-permute-done.refs_1_.refs_6_), channel_id=1, source_target_pairs={{0,2},{2,0},{1,3},{3,1},{4,6},{6,4},{5,7},{7,5}} | collective-permute-start | bytes 3145736 | tf_op jit(solution)/shard_map/ppermute | solution.py:17
  39.9 99.1 %collective-permute-start.11 = (bf16[2,1024,512]{2,1,0:T(8,128)(2,1)}, bf16[2,1024,512]{2,1,0:T(8,128)(2,1)}, u32[]{:S(2)}, u32[]{:S(2)}) collective-permute-start(bf16[2,1024,512]{2,1,0:T(8,128)(2,1)} %pad_maximum_fusion.1.near_w), channel_id=1, source_target_pairs={{0,4},{4,0},{1,5},{5,1},{2,6},{6,2},{3,7},{7,3}} | collective-permute-start | bytes 6291464 | tf_op jit(solution)/shard_map/ppermute | solution.py:17
  55.9 44.3 %collective-permute-start.17 = (bf16[256,256]{1,0:T(8,128)(2,1)S(1)}, bf16[256,256]{1,0:T(8,128)(2,1)S(1)}, u32[]{:S(2)}, u32[]{:S(2)}) collective-permute-start(bf16[256,256]{1,0:T(8,128)(2,1)S(1)} %constant_dynamic-slice_fusion.8), channel_id=1, source_target_pairs={{0,4},{4,0},{1,5},{5,1},{2,6},{6,2},{3,7},{7,3}} | collective-permute-start | bytes 393224 | tf_op jit(solution)/shard_map/ppermute | solution.py:17
  110.0 113.7 %collective-permute-start.12 = (bf16[2,1024,512]{2,1,0:T(8,128)(2,1)}, bf16[2,1024,512]{2,1,0:T(8,128)(2,1)}, u32[]{:S(2)}, u32[]{:S(2)}) collective-permute-start(bf16[2,1024,512]{2,1,0:T(8,128)(2,1)} %pad_maximum_fusion.2.near_w), channel_id=1, source_target_pairs={{0,4},{4,0},{1,5},{5,1},{2,6},{6,2},{3,7},{7,3}} | collective-permute-start | bytes 6291464 | tf_op jit(solution)/shard_map/ppermute | solution.py:17
  111.7 126.5 %collective-permute-start.20 = (bf16[2,1024,512]{2,1,0:T(8,128)(2,1)}, bf16[2,1024,512]{2,1,0:T(8,128)(2,1)}, u32[]{:S(2)}, u32[]{:S(2)}) collective-permute-start(bf16[2,1024,512]{2,1,0:T(8,128)(2,1)} %pad_maximum_fusion.4.near_w), channel_id=1, source_target_pairs={{0,4},{4,0},{1,5},{5,1},{2,6},{6,2},{3,7},{7,3}} | collective-permute-start | bytes 6291464 | tf_op jit(solution)/shard_map/ppermute | solution.py:17
  112.0 25.2 %collective-permute-start.18 = (bf16[256,256]{1,0:T(8,128)(2,1)S(1)}, bf16[256,256]{1,0:T(8,128)(2,1)S(1)}, u32[]{:S(2)}, u32[]{:S(2)}) collective-permute-start(bf16[256,256]{1,0:T(8,128)(2,1)S(1)} %collective-permute-done.17), channel_id=1, source_target_pairs={{0,2},{2,0},{1,3},{3,1},{4,6},{6,4},{5,7},{7,5}} | collective-permute-start | bytes 393224 | tf_op jit(solution)/shard_map/ppermute | solution.py:17
  136.9 24.4 %collective-permute-start.14 = (bf16[2,512,512]{2,1,0:T(8,128)(2,1)S(1)}, bf16[2,512,512]{2,1,0:T(8,128)(2,1)}, u32[]{:S(2)}, u32[]{:S(2)}) collective-permute-start(bf16[2,512,512]{2,1,0:T(8,128)(2,1)S(1)} %dynamic-slice_bitcast_fusion), channel_id=1, source_target_pairs={{0,2},{2,0},{1,3},{3,1},{4,6},{6,4},{5,7},{7,5}} | collective-permute-start | bytes 3145736 | tf_op jit(solution)/shard_map/ppermute | solution.py:17
  138.0 27.5 %collective-permute-start.19 = (bf16[2,256,256]{2,1,0:T(8,128)(2,1)}, bf16[2,256,256]{2,1,0:T(8,128)(2,1)}, u32[]{:S(2)}, u32[]{:S(2)}) collective-permute-start(bf16[2,256,256]{2,1,0:T(8,128)(2,1)} %maximum_select_fusion.4), channel_id=1, source_target_pairs={{0,1},{1,0},{2,3},{3,2},{4,5},{5,4},{6,7},{7,6}} | collective-permute-start | bytes 786440 | tf_op jit(solution)/shard_map/ppermute | solution.py:17
  139.1 30.7 %collective-permute-start.15 = (bf16[512,512]{1,0:T(8,128)(2,1)}, bf16[512,512]{1,0:T(8,128)(2,1)S(1)}, u32[]{:S(2)}, u32[]{:S(2)}) collective-permute-start(bf16[512,512]{1,0:T(8,128)(2,1)} %get-tuple-element.55), channel_id=1, source_target_pairs={{0,1},{1,0},{2,3},{3,2},{4,5},{5,4},{6,7},{7,6}} | collective-permute-start | bytes 1572872 | tf_op jit(solution)/shard_map/ppermute | solution.py:17
  223.2 34.3 %collective-permute-start.28 = (bf16[2560,256]{1,0:T(8,128)(2,1)}, bf16[2560,256]{1,0:T(8,128)(2,1)S(1)}, u32[]{:S(2)}, u32[]{:S(2)}) collective-permute-start(bf16[2560,256]{1,0:T(8,128)(2,1)} %pad_maximum_fusion.7), channel_id=1, source_target_pairs={{0,1},{1,0},{2,3},{3,2},{4,5},{5,4},{6,7},{7,6}} | collective-permute-start | bytes 3932168 | tf_op jit(solution)/shard_map/ppermute | solution.py:17
  223.5 36.7 %collective-permute-start.24 = (bf16[2048,512]{1,0:T(8,128)(2,1)}, bf16[2048,512]{1,0:T(8,128)(2,1)}, u32[]{:S(2)}, u32[]{:S(2)}) collective-permute-start(bf16[2048,512]{1,0:T(8,128)(2,1)} %glu.4.refs_0_), channel_id=1, source_target_pairs={{0,1},{1,0},{2,3},{3,2},{4,5},{5,4},{6,7},{7,6}} | collective-permute-start | bytes 6291464 | tf_op jit(solution)/shard_map/ppermute | solution.py:17
  223.7 27.9 %collective-permute-start.21 = (bf16[512,512]{1,0:T(8,128)(2,1)}, bf16[512,512]{1,0:T(8,128)(2,1)}, u32[]{:S(2)}, u32[]{:S(2)}) collective-permute-start(bf16[512,512]{1,0:T(8,128)(2,1)} %get-tuple-element.28), channel_id=1, source_target_pairs={{0,1},{1,0},{2,3},{3,2},{4,5},{5,4},{6,7},{7,6}} | collective-permute-start | bytes 1572872 | tf_op jit(solution)/shard_map/ppermute | solution.py:17
  225.0 28.6 %collective-permute-start.23 = (bf16[2,512,512]{2,1,0:T(8,128)(2,1)}, bf16[2,512,512]{2,1,0:T(8,128)(2,1)S(1)}, u32[]{:S(2)}, u32[]{:S(2)}) collective-permute-start(bf16[2,512,512]{2,1,0:T(8,128)(2,1)} %pad_maximum_fusion.9), channel_id=1, source_target_pairs={{0,2},{2,0},{1,3},{3,1},{4,6},{6,4},{5,7},{7,5}} | collective-permute-start | bytes 3145736 | tf_op jit(solution)/shard_map/ppermute | solution.py:17
  238.2 24.4 %collective-permute-start.25 = (bf16[2048,512]{1,0:T(8,128)(2,1)}, bf16[2048,512]{1,0:T(8,128)(2,1)}, u32[]{:S(2)}, u32[]{:S(2)}) collective-permute-start(bf16[2048,512]{1,0:T(8,128)(2,1)} %glu.5.refs_1_), channel_id=1, source_target_pairs={{0,1},{1,0},{2,3},{3,2},{4,5},{5,4},{6,7},{7,6}} | collective-permute-start | bytes 6291464 | tf_op jit(solution)/shard_map/ppermute | solution.py:17
  257.5 48.1 %collective-permute-start.10 = (bf16[2,1024,512]{2,1,0:T(8,128)(2,1)}, bf16[2,1024,512]{2,1,0:T(8,128)(2,1)}, u32[]{:S(2)}, u32[]{:S(2)}) collective-permute-start(bf16[2,1024,512]{2,1,0:T(8,128)(2,1)} %pad_maximum_fusion.near_w), channel_id=1, source_target_pairs={{0,4},{4,0},{1,5},{5,1},{2,6},{6,2},{3,7},{7,3}} | collective-permute-start | bytes 6291464 | tf_op jit(solution)/shard_map/ppermute | solution.py:17
  260.2 13.2 %collective-permute-start.29 = (bf16[2560,256]{1,0:T(8,128)(2,1)}, bf16[2560,256]{1,0:T(8,128)(2,1)S(1)}, u32[]{:S(2)}, u32[]{:S(2)}) collective-permute-start(bf16[2560,256]{1,0:T(8,128)(2,1)} %pad_maximum_fusion.8), channel_id=1, source_target_pairs={{0,1},{1,0},{2,3},{3,2},{4,5},{5,4},{6,7},{7,6}} | collective-permute-start | bytes 3932168 | tf_op jit(solution)/shard_map/ppermute | solution.py:17
  318.8 31.5 %collective-permute-start.34 = (bf16[2560,256]{1,0:T(8,128)(2,1)}, bf16[2560,256]{1,0:T(8,128)(2,1)}, u32[]{:S(2)}, u32[]{:S(2)}) collective-permute-start(bf16[2560,256]{1,0:T(8,128)(2,1)} %pad_maximum_fusion.7), channel_id=1, source_target_pairs={{0,4},{4,0},{1,5},{5,1},{2,6},{6,2},{3,7},{7,3}} | collective-permute-start | bytes 3932168 | tf_op jit(solution)/shard_map/ppermute | solution.py:17
  350.3 69.6 %collective-permute-start.31 = (f32[1536,256]{1,0:T(8,128)}, f32[1536,256]{1,0:T(8,128)}, u32[]{:S(2)}, u32[]{:S(2)}) collective-permute-start(f32[1536,256]{1,0:T(8,128)} %mix.16), channel_id=1, source_target_pairs={{0,2},{2,0},{1,3},{3,1},{4,6},{6,4},{5,7},{7,5}} | collective-permute-start | bytes 4718600 | tf_op jit(solution)/shard_map/ppermute | solution.py:17
  352.1 73.7 %collective-permute-start.39 = (bf16[2560,256]{1,0:T(8,128)(2,1)}, bf16[2560,256]{1,0:T(8,128)(2,1)}, u32[]{:S(2)}, u32[]{:S(2)}) collective-permute-start(bf16[2560,256]{1,0:T(8,128)(2,1)} %pad_maximum_fusion.8), channel_id=1, source_target_pairs={{0,4},{4,0},{1,5},{5,1},{2,6},{6,2},{3,7},{7,3}} | collective-permute-start | bytes 3932168 | tf_op jit(solution)/shard_map/ppermute | solution.py:17
  354.7 43.4 %collective-permute-start.33 = (bf16[2560,128]{1,0:T(8,128)(2,1)}, bf16[2560,128]{1,0:T(8,128)(2,1)S(1)}, u32[]{:S(2)}, u32[]{:S(2)}) collective-permute-start(bf16[2560,128]{1,0:T(8,128)(2,1)} %get-tuple-element.59), channel_id=1, source_target_pairs={{0,4},{4,0},{1,5},{5,1},{2,6},{6,2},{3,7},{7,3}} | collective-permute-start | bytes 1966088 | tf_op jit(solution)/shard_map/ppermute | solution.py:17
  355.1 56.2 %collective-permute-start.32 = (bf16[2560,128]{1,0:T(8,128)(2,1)S(1)}, bf16[2560,128]{1,0:T(8,128)(2,1)S(1)}, u32[]{:S(2)}, u32[]{:S(2)}) collective-permute-start(bf16[2560,128]{1,0:T(8,128)(2,1)S(1)} %get-tuple-element.60), channel_id=1, source_target_pairs={{0,4},{4,0},{1,5},{5,1},{2,6},{6,2},{3,7},{7,3}} | collective-permute-start | bytes 1966088 | tf_op jit(solution)/shard_map/ppermute | solution.py:17
  425.8 26.4 %collective-permute-start.41 = (f32[2048,128]{1,0:T(8,128)}, f32[2048,128]{1,0:T(8,128)}, u32[]{:S(2)}, u32[]{:S(2)}) collective-permute-start(f32[2048,128]{1,0:T(8,128)} %mix.19), channel_id=1, source_target_pairs={{0,2},{2,0},{1,3},{3,1},{4,6},{6,4},{5,7},{7,5}} | collective-permute-start | bytes 3145736 | tf_op jit(solution)/shard_map/ppermute | solution.py:17
  427.3 17.8 %collective-permute-start.38 = (bf16[2560,128]{1,0:T(8,128)(2,1)}, bf16[2560,128]{1,0:T(8,128)(2,1)S(1)}, u32[]{:S(2)}, u32[]{:S(2)}) collective-permute-start(bf16[2560,128]{1,0:T(8,128)(2,1)} %get-tuple-element.57), channel_id=1, source_target_pairs={{0,4},{4,0},{1,5},{5,1},{2,6},{6,2},{3,7},{7,3}} | collective-permute-start | bytes 1966088 | tf_op jit(solution)/shard_map/ppermute | solution.py:17
  428.9 45.7 %collective-permute-start.42 = (f32[2048,128]{1,0:T(8,128)}, f32[2048,128]{1,0:T(8,128)S(1)}, u32[]{:S(2)}, u32[]{:S(2)}) collective-permute-start(f32[2048,128]{1,0:T(8,128)} %mix.20), channel_id=1, source_target_pairs={{0,2},{2,0},{1,3},{3,1},{4,6},{6,4},{5,7},{7,5}} | collective-permute-start | bytes 3145736 | tf_op jit(solution)/shard_map/ppermute | solution.py:17
  430.6 32.7 %collective-permute-start.37 = (bf16[2560,128]{1,0:T(8,128)(2,1)}, bf16[2560,128]{1,0:T(8,128)(2,1)}, u32[]{:S(2)}, u32[]{:S(2)}) collective-permute-start(bf16[2560,128]{1,0:T(8,128)(2,1)} %get-tuple-element.58), channel_id=1, source_target_pairs={{0,4},{4,0},{1,5},{5,1},{2,6},{6,2},{3,7},{7,3}} | collective-permute-start | bytes 1966088 | tf_op jit(solution)/shard_map/ppermute | solution.py:17
  431.1 54.3 %collective-permute-start.36 = (f32[512,256]{1,0:T(8,128)}, f32[512,256]{1,0:T(8,128)}, u32[]{:S(2)}, u32[]{:S(2)}) collective-permute-start(f32[512,256]{1,0:T(8,128)} %mix.17), channel_id=1, source_target_pairs={{0,2},{2,0},{1,3},{3,1},{4,6},{6,4},{5,7},{7,5}} | collective-permute-start | bytes 1572872 | tf_op jit(solution)/shard_map/ppermute | solution.py:17
  460.2 30.5 %collective-permute-start.43 = (bf16[2048,128]{1,0:T(8,128)(2,1)}, bf16[2048,128]{1,0:T(8,128)(2,1)S(1)}, u32[]{:S(2)}, u32[]{:S(2)}) collective-permute-start(bf16[2048,128]{1,0:T(8,128)(2,1)} %mix.23), channel_id=1, source_target_pairs={{0,4},{4,0},{1,5},{5,1},{2,6},{6,2},{3,7},{7,3}} | collective-permute-start | bytes 1572872 | tf_op jit(solution)/shard_map/ppermute | solution.py:17
  483.6 13.2 %collective-permute-start.44 = (bf16[2048,128]{1,0:T(8,128)(2,1)}, bf16[2048,128]{1,0:T(8,128)(2,1)S(1)}, u32[]{:S(2)}, u32[]{:S(2)}) collective-permute-start(bf16[2048,128]{1,0:T(8,128)(2,1)} %mix.24), channel_id=1, source_target_pairs={{0,4},{4,0},{1,5},{5,1},{2,6},{6,2},{3,7},{7,3}} | collective-permute-start | bytes 1572872 | tf_op jit(solution)/shard_map/ppermute | solution.py:17
  (49 other events, 409.6 us)

commit v5 on v4

--- a/solution.py
+++ b/solution.py
@@ -163,6 +163,30 @@
     )(h, near_w, far_w)
 
 
+def project_kernel(h_ref, *refs):
+    total, row = None, 0
+    for w in refs[:-1]:
+        part = jnp.dot(h_ref[:, row : row + w.shape[0]], w[...], preferred_element_type=F32)
+        total = part if total is None else total + part
+        row += w.shape[0]
+    refs[-1][...] = total.astype(BF16)
+
+
+def project(h, ws):
+    tokens, depth = h.shape
+    cols = ws[0].shape[1]
+    blk = 512
+    return pl.pallas_call(
+        project_kernel,
+        grid=(tokens // blk,),
+        in_specs=[pl.BlockSpec((blk, depth), lambda i: (i, 0))] + [pl.BlockSpec(w.shape, lambda i: (0, 0)) for w in ws],
+        out_specs=pl.BlockSpec((blk, cols), lambda i: (i, 0)),
+        out_shape=jax.ShapeDtypeStruct((tokens, cols), BF16),
+        cost_estimate=pl.CostEstimate(flops=2 * tokens * depth * cols, bytes_accessed=2 * depth * (tokens + cols), transcendentals=0),
+        name="project",
+    )(h, *ws)
+
+
 def mix_kernel(plan, n_lhs, n_w, *refs):
     lhs, ws, adds, out_ref = refs[:n_lhs], refs[n_lhs : n_lhs + n_w], refs[n_lhs + n_w : -1], refs[-1]
     total = None
@@ -242,9 +266,10 @@
         kv_part = swap_y(lax.dynamic_slice_in_dim(w_kv, ti * kv_rows, kv_rows, 0))
         kv_pair = ordered([kv_part, swap_x(kv_part)], xi, 0)
         kv_far = ordered([kv_pair, swap_c(kv_pair)], ci, 1).reshape(w_kv.shape)
-        q_far = swap_y(w_query)
-
-        q = mix([(h, jnp.concatenate([w_query, q_far], 0), 0)], dtype=BF16)
+        lead = 256
+        q_far = [swap_y(w_query[:lead]), swap_y(w_query[lead:])]
+
+        q = project(h, [w_query, *q_far])
         h_own = lax.dynamic_slice_in_dim(h, ti * own_tok, own_tok, 0)
         kv = jnp.dot(h_own, jnp.concatenate([w_kv, kv_far], 0), preferred_element_type=F32).astype(BF16)
 

time: 499 us -> 487 us (0.976)
  waiting for transfers between devices: 188 us -> 179 us
    ppermute x45 -> x46, waiting for transfers between devices: 188 us -> 179 us  [swap(): return lambda a: lax.ppermute(a, axis, pairs)]
    pallas_call x13 -> x12, Pallas kernels: 97.1 us -> 88.3 us  [mix(): pl.pallas_call(functools.partial(mix_kernel, plan, len(lhs), len(ws)), gr...]
    pallas_call x0 -> x1, Pallas kernels: none -> 8.65 us  [project(): pl.pallas_call(project_kernel, grid=(tokens // blk,), in_specs=[pl.BlockS...]
    ppermute x45 -> x46, starting transfers between devices: 36.1 us -> 34.7 us  [swap(): return lambda a: lax.ppermute(a, axis, pairs)]
  transfers between devices with their start and end apart: 45 -> 46, of which waited for: 15 -> 15; matrix products, arithmetic and copies ran while one was open for 10% -> 10% of each run, Pallas kernels for 39% -> 40%
where the time goes in v5:
time: 487 us; the launch traced here: 486 us
  Pallas kernels  209 us (43%)
  waiting for transfers between devices  179 us (37%)
  local copies, waits for them, and re-layouts  35.8 us (7%)
  starting transfers between devices  34.7 us (7%)
  other arithmetic  23.4 us (5%)
    ppermute x46, waiting for transfers between devices, swap(): return lambda a: lax.ppermute(a, axis, pairs)  179 us
    pallas_call x12, Pallas kernels, mix(): pl.pallas_call(functools.partial(mix_kernel, plan, len(lhs), len(ws)), gr...  88.3 us
    pallas_call x4, Pallas kernels, glu(): pl.pallas_call(glu_kernel, grid=(tokens // blk,), in_specs=[pl.BlockSpec(...  52.7 us
    pallas_call x1, Pallas kernels, attention(): pl.pallas_call(attn_kernel, grid_spec=pltpu.PrefetchScalarGridSpec(num_sc...  46.2 us
    ppermute x46, starting transfers between devices, swap(): return lambda a: lax.ppermute(a, axis, pairs)  34.7 us
    pallas_call x1, Pallas kernels, layer_norm(): pl.pallas_call(norm_kernel, grid_spec=pltpu.PrefetchScalarGridSpec(num_sc...  13 us
    unnamed x73, local copies, waits for them, and re-layouts  12.1 us
  transfers between devices with their start and end apart: 46, of which 15 were waited for; matrix products, arithmetic and copies ran while one was open for 10% of the time, Pallas kernels for 40%

profile of v5, /device:TPU:0, one launch (start us, length us, event | category | flops | bytes accessed | tf_op | source)
XLA Modules:
  0.0 486.0 jit_solution(17045608712395437989)
XLA Ops:
  8.2 21.8 %collective-permute-done.refs_1_.refs_6_ = bf16[2048,256]{1,0:T(8,128)(2,1)S(1)} collective-permute-done((bf16[2048,256]{1,0:T(8,128)(2,1)}, bf16[2048,256]{1,0:T(8,128)(2,1)S(1)}, u32[]{:S(2)}, u32[]{:S(2)}) %collective-permute-start) | collective-permute-done | bytes 1048608 | tf_op jit(solution)/shard_map/ppermute | solution.py:17
  33.2 4.9 %slice_bitcast_fusion = (bf16[1,1024,512]{2,1,0:T(8,128)(2,1)S(1)}, bf16[1,1024,512]{2,1,0:T(8,128)(2,1)S(1)}, bf16[1,1024,512]{2,1,0:T(8,128)(2,1)}, bf16[1,102...) fusion(bf16[1024,2048]{1,0:T(8,128)(2,1)} %param.21, ...), kind=kLoop, calls=%fused_computation.27 | loop fusion | bytes 16777216 | tf_op jit(solution)/shard_map/stack | solution.py:281
  40.5 14.0 %collective-permute-done.8 = f32[2,256]{1,0:T(2,128)S(1)} collective-permute-done((f32[2,256]{1,0:T(2,128)S(1)}, f32[2,256]{1,0:T(2,128)S(1)}, u32[]{:S(2)}, u32[]{:S(2)}) %collective-permute-start.8) | collective-permute-done | bytes 2080 | tf_op jit(solution)/shard_map/ppermute | solution.py:17
  70.4 13.0 %norm.1.h_ref = bf16[2048,2048]{1,0:T(8,128)(2,1)} custom-call(s32[8]{0:T(128)} %stack.140.offs_ref, bf16[2048,256]{1,0:T(8,128)(2,1)} %copy-done.6, bf16[2048,256]{1,0:T(8,128)(2,1)} %copy-done.11, bf16[2048,256]{1,0:T(8,128)(2,1)} %collective-permute-done.1.refs_2_, bf16[2048,256]{1,0:T(8,128)(2,1)} %collective-permute-done.2.refs_3_, ...), custom_call_target="tpu_custom_call" | custom-call | flops 83886080 | bytes 16777216 | tf_op jit(solution)/shard_map/norm/pallas_call | solution.py:47
  83.4 30.8 %collective-permute-done.18 = bf16[256,256]{1,0:T(8,128)(2,1)S(1)} collective-permute-done((bf16[256,256]{1,0:T(8,128)(2,1)S(1)}, bf16[256,256]{1,0:T(8,128)(2,1)S(1)}, u32[]{:S(2)}, u32[]{:S(2)}) %collective-permute-start.18) | collective-permute-done | bytes 131104 | tf_op jit(solution)/shard_map/ppermute | solution.py:17
  116.2 8.7 %project.1 = bf16[2048,512]{1,0:T(8,128)(2,1)} custom-call(bf16[2048,2048]{1,0:T(8,128)(2,1)} %norm.1.h_ref, bf16[1024,512]{1,0:T(8,128)(2,1)} %refs_0_.1, bf16[256,512]{1,0:T(8,128)(2,1)} %copy-done.35, bf16[768,512]{1,0:T(8,128)(2,1)} %collective-permute-done.14.refs_2_), custom_call_target="tpu_custom_call" | custom-call | flops 4294967296 | bytes 10485760 | tf_op jit(solution)/shard_map/project/pallas_call | solution.py:179
  129.3 13.2 %glu.4.refs_0_ = bf16[2048,512]{1,0:T(8,128)(2,1)} custom-call(bf16[2048,2048]{1,0:T(8,128)(2,1)} %norm.1.h_ref, bf16[2,1024,512]{2,1,0:T(8,128)(2,1)} %pad_maximum_fusion.1.near_w, bf16[2,1024,512]{2,1,0:T(8,128)(2,1)} %collective-permute-done.11.far_w), custom_call_target="tpu_custom_call" | custom-call | flops 8589934592 | bytes 14680064 | tf_op jit(solution)/shard_map/glu/pallas_call | solution.py:155
  142.5 6.5 %collective-permute-done.15 = bf16[2,512,512]{2,1,0:T(8,128)(2,1)} collective-permute-done((bf16[2,512,512]{2,1,0:T(8,128)(2,1)S(1)}, bf16[2,512,512]{2,1,0:T(8,128)(2,1)}, u32[]{:S(2)}, u32[]{:S(2)}) %collective-permute-start.15) | collective-permute-done | bytes 1048608 | tf_op jit(solution)/shard_map/ppermute | solution.py:17
  158.4 46.2 %attn.1 = (bf16[512,512]{1,0:T(8,128)(2,1)}, bf16[512,512]{1,0:T(8,128)(2,1)}, bf16[512,512]{1,0:T(8,128)(2,1)}, bf16[512,512]{1,0:T(8,128)(2,1)}, bf16[8,2048,1...) custom-call(s32[8]{0:T(128)} %len_ref.1, bf16[512,512]{1,0:T(8,128)(2,1)} %get-tuple-element.56.q0, ...), custom_call_target="tpu_custom_call" | custom-call | flops 17179869184 | bytes 16777216 | tf_op jit(solution)/shard_map/attn/pallas_call | solution.py:125
  204.8 3.9 constant_dynamic-slice_fusion.1
  212.0 13.2 %glu.5.refs_1_ = bf16[2048,512]{1,0:T(8,128)(2,1)} custom-call(bf16[2048,2048]{1,0:T(8,128)(2,1)} %norm.1.h_ref, bf16[2,1024,512]{2,1,0:T(8,128)(2,1)} %pad_maximum_fusion.2.near_w, bf16[2,1024,512]{2,1,0:T(8,128)(2,1)} %collective-permute-done.12.far_w), custom_call_target="tpu_custom_call" | custom-call | flops 8589934592 | bytes 14680064 | tf_op jit(solution)/shard_map/glu/pallas_call | solution.py:155
  225.3 13.2 %glu.6.refs_2_ = bf16[2048,512]{1,0:T(8,128)(2,1)} custom-call(bf16[2048,2048]{1,0:T(8,128)(2,1)} %norm.1.h_ref, bf16[2,1024,512]{2,1,0:T(8,128)(2,1)} %pad_maximum_fusion.3.near_w, bf16[2,1024,512]{2,1,0:T(8,128)(2,1)} %collective-permute-done.21.far_w), custom_call_target="tpu_custom_call" | custom-call | flops 8589934592 | bytes 14680064 | tf_op jit(solution)/shard_map/glu/pallas_call | solution.py:155
  251.1 10.7 %mix.12.refs_4_ = f32[2048,256]{1,0:T(8,128)} custom-call(bf16[2048,512]{1,0:T(8,128)(2,1)} %glu.4.refs_0_, bf16[2048,512]{1,0:T(8,128)(2,1)} %glu.5.refs_1_, bf16[2048,512]{1,0:T(8,128)(2,1)} %glu.6.refs_2_, bf16[2048,512]{1,0:T(8,128)(2,1)} %bitcast.66, bf16[2048,512]{1,0:T(8,128)(2,1)} %collective-permute-done.25.refs_4_.refs_0_, ...), custom_call_target="tpu_custom_call" | custom-call | flops 4294967296 | bytes 18874368 | tf_op jit(solution)/shard_map/mix/pallas_call | solution.py:216
  263.0 11.1 %mix.13.refs_4_ = f32[2048,256]{1,0:T(8,128)} custom-call(bf16[2048,512]{1,0:T(8,128)(2,1)} %glu.4.refs_0_, bf16[2048,512]{1,0:T(8,128)(2,1)} %glu.5.refs_1_, bf16[2048,512]{1,0:T(8,128)(2,1)} %glu.6.refs_2_, bf16[2048,512]{1,0:T(8,128)(2,1)} %bitcast.67, bf16[2048,512]{1,0:T(8,128)(2,1)} %collective-permute-done.25.refs_4_.refs_0_, ...), custom_call_target="tpu_custom_call" | custom-call | flops 4294967296 | bytes 18874368 | tf_op jit(solution)/shard_map/mix/pallas_call | solution.py:216
  274.1 20.0 %collective-permute-done.10.far_w = bf16[2,1024,512]{2,1,0:T(8,128)(2,1)} collective-permute-done((bf16[2,1024,512]{2,1,0:T(8,128)(2,1)}, bf16[2,1024,512]{2,1,0:T(8,128)(2,1)}, u32[]{:S(2)}, u32[]{:S(2)}) %collective-permute-start.10) | collective-permute-done | bytes 2097184 | tf_op jit(solution)/shard_map/ppermute | solution.py:17
  294.1 13.2 %glu.7.refs_0_.refs_3_ = bf16[2048,512]{1,0:T(8,128)(2,1)} custom-call(bf16[2048,2048]{1,0:T(8,128)(2,1)} %norm.1.h_ref, bf16[2,1024,512]{2,1,0:T(8,128)(2,1)} %pad_maximum_fusion.near_w, bf16[2,1024,512]{2,1,0:T(8,128)(2,1)} %collective-permute-done.10.far_w), custom_call_target="tpu_custom_call" | custom-call | flops 8589934592 | bytes 14680064 | tf_op jit(solution)/shard_map/glu/pallas_call | solution.py:155
  316.4 5.9 %mix.14 = f32[1536,256]{1,0:T(8,128)} custom-call(bf16[2048,512]{1,0:T(8,128)(2,1)} %glu.7.refs_0_.refs_3_, bf16[2048,512]{1,0:T(8,128)(2,1)} %copy-done.3, bf16[2560,256]{1,0:T(8,128)(2,1)} %pad_maximum_fusion.5.refs_8_.refs_2_, bf16[2560,256]{1,0:T(8,128)(2,1)} %copy-done.5, f32[2048,256]{1,0:T(8,128)} %mix.12.refs_4_), custom_call_target="tpu_custom_call" | custom-call | flops 805306368 | bytes 3670016 | tf_op jit(solution)/shard_map/mix/pallas_call | solution.py:216
  322.3 16.5 %collective-permute-done.35 = bf16[2560,256]{1,0:T(8,128)(2,1)} collective-permute-done((bf16[2560,256]{1,0:T(8,128)(2,1)}, bf16[2560,256]{1,0:T(8,128)(2,1)}, u32[]{:S(2)}, u32[]{:S(2)}) %collective-permute-start.35) | collective-permute-done | bytes 1310752 | tf_op jit(solution)/shard_map/ppermute | solution.py:17
  345.2 7.9 %mix.16.refs_6_ = f32[2048,256]{1,0:T(8,128)} custom-call(bf16[2048,512]{1,0:T(8,128)(2,1)} %collective-permute-done.25.refs_4_.refs_0_, bf16[2048,512]{1,0:T(8,128)(2,1)} %collective-permute-done.26.refs_5_.refs_1_, bf16[2048,512]{1,0:T(8,128)(2,1)} %collective-permute-done.27.refs_6_.refs_2_, bf16[2048,512]{1,0:T(8,128)(2,1)} %copy-done.3, ...), custom_call_target="tpu_custom_call" | custom-call | flops 2684354560 | bytes 11796480 | tf_op jit(solution)/shard_map/mix/pallas_call | solution.py:216
  353.1 33.4 %collective-permute-done.34.refs_5_ = bf16[2560,128]{1,0:T(8,128)(2,1)S(1)} collective-permute-done((bf16[2560,128]{1,0:T(8,128)(2,1)}, bf16[2560,128]{1,0:T(8,128)(2,1)S(1)}, u32[]{:S(2)}, u32[]{:S(2)}) %collective-permute-start.34) | collective-permute-done | bytes 655392 | tf_op jit(solution)/shard_map/ppermute | solution.py:17
  387.3 7.7 %mix.17 = f32[2048,128]{1,0:T(8,128)} custom-call(bf16[2048,512]{1,0:T(8,128)(2,1)} %glu.4.refs_0_, bf16[2048,512]{1,0:T(8,128)(2,1)} %glu.5.refs_1_, bf16[2048,512]{1,0:T(8,128)(2,1)} %glu.6.refs_2_, bf16[2048,512]{1,0:T(8,128)(2,1)} %glu.7.refs_0_.refs_3_, bf16[2048,512]{1,0:T(8,128)(2,1)} %bitcast.68, bf16[2560,128]{1,0:T(8,128)(2,1)} %copy-done.24, ...), custom_call_target="tpu_custom_call" | custom-call | flops 1342177280 | bytes 11141120 | tf_op jit(solution)/shard_map/mix/pallas_call | solution.py:216
  395.0 4.8 collective-permute-done.33.refs_5_
  400.7 7.7 %mix.18 = f32[2048,128]{1,0:T(8,128)} custom-call(bf16[2048,512]{1,0:T(8,128)(2,1)} %glu.4.refs_0_, bf16[2048,512]{1,0:T(8,128)(2,1)} %glu.5.refs_1_, bf16[2048,512]{1,0:T(8,128)(2,1)} %glu.6.refs_2_, bf16[2048,512]{1,0:T(8,128)(2,1)} %glu.7.refs_0_.refs_3_, bf16[2048,512]{1,0:T(8,128)(2,1)} %bitcast.69, bf16[2560,128]{1,0:T(8,128)(2,1)} %copy-done.23, ...), custom_call_target="tpu_custom_call" | custom-call | flops 1342177280 | bytes 11141120 | tf_op jit(solution)/shard_map/mix/pallas_call | solution.py:216
  408.4 5.9 %mix.19 = bf16[1536,256]{1,0:T(8,128)(2,1)} custom-call(bf16[2048,512]{1,0:T(8,128)(2,1)} %glu.7.refs_0_.refs_3_, bf16[2048,512]{1,0:T(8,128)(2,1)} %copy-done.3, bf16[2560,256]{1,0:T(8,128)(2,1)} %pad_maximum_fusion.4.refs_8_.refs_2_, bf16[2560,256]{1,0:T(8,128)(2,1)} %copy-done.4, f32[2048,256]{1,0:T(8,128)} %mix.13.refs_4_, ...), custom_call_target="tpu_custom_call" | custom-call | flops 805306368 | bytes 3670016 | tf_op jit(solution)/shard_map/mix/pallas_call | solution.py:216
  419.8 8.3 %mix.20.refs_6_ = f32[2048,256]{1,0:T(8,128)} custom-call(bf16[2048,512]{1,0:T(8,128)(2,1)} %collective-permute-done.25.refs_4_.refs_0_, bf16[2048,512]{1,0:T(8,128)(2,1)} %collective-permute-done.26.refs_5_.refs_1_, bf16[2048,512]{1,0:T(8,128)(2,1)} %collective-permute-done.27.refs_6_.refs_2_, bf16[2048,512]{1,0:T(8,128)(2,1)} %copy-done.3, ...), custom_call_target="tpu_custom_call" | custom-call | flops 2684354560 | bytes 11796480 | tf_op jit(solution)/shard_map/mix/pallas_call | solution.py:216
  428.2 5.4 %collective-permute-done.39.refs_5_ = bf16[2560,128]{1,0:T(8,128)(2,1)S(1)} collective-permute-done((bf16[2560,128]{1,0:T(8,128)(2,1)}, bf16[2560,128]{1,0:T(8,128)(2,1)S(1)}, u32[]{:S(2)}, u32[]{:S(2)}) %collective-permute-start.39) | collective-permute-done | bytes 655392 | tf_op jit(solution)/shard_map/ppermute | solution.py:17
  433.6 7.0 %collective-permute-done.42.refs_7_ = f32[2048,128]{1,0:T(8,128)S(1)} collective-permute-done((f32[2048,128]{1,0:T(8,128)}, f32[2048,128]{1,0:T(8,128)S(1)}, u32[]{:S(2)}, u32[]{:S(2)}) %collective-permute-start.42) | collective-permute-done | bytes 1048608 | tf_op jit(solution)/shard_map/ppermute | solution.py:17
  441.6 8.0 %mix.21 = bf16[2048,128]{1,0:T(8,128)(2,1)} custom-call(bf16[2048,512]{1,0:T(8,128)(2,1)} %glu.4.refs_0_, bf16[2048,512]{1,0:T(8,128)(2,1)} %glu.5.refs_1_, bf16[2048,512]{1,0:T(8,128)(2,1)} %glu.6.refs_2_, bf16[2048,512]{1,0:T(8,128)(2,1)} %glu.7.refs_0_.refs_3_, bf16[2048,512]{1,0:T(8,128)(2,1)} %bitcast.70, bf16[2560,128]{1,0:T(8,128)(2,1)} %copy-done.25, ...), custom_call_target="tpu_custom_call" | custom-call | flops 1342177280 | bytes 11141120 | tf_op jit(solution)/shard_map/mix/pallas_call | solution.py:216
  453.6 9.5 %collective-permute-done.43.refs_7_ = f32[2048,128]{1,0:T(8,128)S(1)} collective-permute-done((f32[2048,128]{1,0:T(8,128)}, f32[2048,128]{1,0:T(8,128)S(1)}, u32[]{:S(2)}, u32[]{:S(2)}) %collective-permute-start.43) | collective-permute-done | bytes 1048608 | tf_op jit(solution)/shard_map/ppermute | solution.py:17
  464.0 8.0 %mix.22 = bf16[2048,128]{1,0:T(8,128)(2,1)} custom-call(bf16[2048,512]{1,0:T(8,128)(2,1)} %glu.4.refs_0_, bf16[2048,512]{1,0:T(8,128)(2,1)} %glu.5.refs_1_, bf16[2048,512]{1,0:T(8,128)(2,1)} %glu.6.refs_2_, bf16[2048,512]{1,0:T(8,128)(2,1)} %glu.7.refs_0_.refs_3_, bf16[2048,512]{1,0:T(8,128)(2,1)} %bitcast.71, ...), custom_call_target="tpu_custom_call" | custom-call | flops 1342177280 | bytes 11141120 | tf_op jit(solution)/shard_map/mix/pallas_call | solution.py:216
  473.9 3.6 mix.23
  480.0 5.2 %collective-permute-done.45 = bf16[2048,128]{1,0:T(8,128)(2,1)S(1)} collective-permute-done((bf16[2048,128]{1,0:T(8,128)(2,1)}, bf16[2048,128]{1,0:T(8,128)(2,1)S(1)}, u32[]{:S(2)}, u32[]{:S(2)}) %collective-permute-start.45) | collective-permute-done | bytes 524320 | tf_op jit(solution)/shard_map/ppermute | solution.py:17
  (197 shorter events, 95.8 us)
Async XLA Ops:
  3.3 26.7 %collective-permute-start = (bf16[2048,256]{1,0:T(8,128)(2,1)}, bf16[2048,256]{1,0:T(8,128)(2,1)S(1)}, u32[]{:S(2)}, u32[]{:S(2)}) collective-permute-start(bf16[2048,256]{1,0:T(8,128)(2,1)} %dynamic-slice_bitcast_fusion.2), channel_id=1, source_target_pairs={{0,4},{4,0},{1,5},{5,1},{2,6},{6,2},{3,7},{7,3}} | collective-permute-start | bytes 3145736 | tf_op jit(solution)/shard_map/ppermute | solution.py:17
  6.7 33.8 %collective-permute-start.1 = (bf16[2048,256]{1,0:T(8,128)(2,1)S(1)}, bf16[2048,256]{1,0:T(8,128)(2,1)}, u32[]{:S(2)}, u32[]{:S(2)}) collective-permute-start(bf16[2048,256]{1,0:T(8,128)(2,1)S(1)} %dynamic-slice_bitcast_fusion.1.refs_0_.refs_10_), channel_id=1, source_target_pairs={{0,2},{2,0},{1,3},{3,1},{4,6},{6,4},{5,7},{7,5}} | collective-permute-start | bytes 3145736 | tf_op jit(solution)/shard_map/ppermute | solution.py:17
  30.0 25.9 %collective-permute-start.2 = (bf16[2048,256]{1,0:T(8,128)(2,1)S(1)}, bf16[2048,256]{1,0:T(8,128)(2,1)}, u32[]{:S(2)}, u32[]{:S(2)}) collective-permute-start(bf16[2048,256]{1,0:T(8,128)(2,1)S(1)} %collective-permute-done.refs_1_.refs_6_), channel_id=1, source_target_pairs={{0,2},{2,0},{1,3},{3,1},{4,6},{6,4},{5,7},{7,5}} | collective-permute-start | bytes 3145736 | tf_op jit(solution)/shard_map/ppermute | solution.py:17
  31.7 27.8 %collective-permute-start.3 = (bf16[2048,256]{1,0:T(8,128)(2,1)S(1)}, bf16[2048,256]{1,0:T(8,128)(2,1)S(1)}, u32[]{:S(2)}, u32[]{:S(2)}) collective-permute-start(bf16[2048,256]{1,0:T(8,128)(2,1)S(1)} %dynamic-slice_bitcast_fusion.1.refs_0_.refs_10_), channel_id=1, source_target_pairs={{0,1},{1,0},{2,3},{3,2},{4,5},{5,4},{6,7},{7,6}} | collective-permute-start | bytes 3145736 | tf_op jit(solution)/shard_map/ppermute | solution.py:17
  38.1 16.4 %collective-permute-start.8 = (f32[2,256]{1,0:T(2,128)S(1)}, f32[2,256]{1,0:T(2,128)S(1)}, u32[]{:S(2)}, u32[]{:S(2)}) collective-permute-start(f32[2,256]{1,0:T(2,128)S(1)} %pad_maximum_fusion.13), channel_id=1, source_target_pairs={{0,2},{2,0},{1,3},{3,1},{4,6},{6,4},{5,7},{7,5}} | collective-permute-start | bytes 6152 | tf_op jit(solution)/shard_map/ppermute | solution.py:17
  40.2 88.6 %collective-permute-start.11 = (bf16[2,1024,512]{2,1,0:T(8,128)(2,1)}, bf16[2,1024,512]{2,1,0:T(8,128)(2,1)}, u32[]{:S(2)}, u32[]{:S(2)}) collective-permute-start(bf16[2,1024,512]{2,1,0:T(8,128)(2,1)} %pad_maximum_fusion.1.near_w), channel_id=1, source_target_pairs={{0,4},{4,0},{1,5},{5,1},{2,6},{6,2},{3,7},{7,3}} | collective-permute-start | bytes 6291464 | tf_op jit(solution)/shard_map/ppermute | solution.py:17
  40.5 23.8 %collective-permute-start.5 = (bf16[2048,256]{1,0:T(8,128)(2,1)}, bf16[2048,256]{1,0:T(8,128)(2,1)}, u32[]{:S(2)}, u32[]{:S(2)}) collective-permute-start(bf16[2048,256]{1,0:T(8,128)(2,1)} %collective-permute-done.1.refs_2_), channel_id=1, source_target_pairs={{0,1},{1,0},{2,3},{3,2},{4,5},{5,4},{6,7},{7,6}} | collective-permute-start | bytes 3145736 | tf_op jit(solution)/shard_map/ppermute | solution.py:17
  60.4 55.7 %collective-permute-start.14 = (bf16[768,512]{1,0:T(8,128)(2,1)}, bf16[768,512]{1,0:T(8,128)(2,1)}, u32[]{:S(2)}, u32[]{:S(2)}) collective-permute-start(bf16[768,512]{1,0:T(8,128)(2,1)} %slice.49), channel_id=1, source_target_pairs={{0,4},{4,0},{1,5},{5,1},{2,6},{6,2},{3,7},{7,3}} | collective-permute-start | bytes 2359304 | tf_op jit(solution)/shard_map/ppermute | solution.py:17
  64.3 50.2 %collective-permute-start.13 = (bf16[256,512]{1,0:T(8,128)(2,1)S(1)}, bf16[256,512]{1,0:T(8,128)(2,1)S(1)}, u32[]{:S(2)}, u32[]{:S(2)}) collective-permute-start(bf16[256,512]{1,0:T(8,128)(2,1)S(1)} %slice.48), channel_id=1, source_target_pairs={{0,4},{4,0},{1,5},{5,1},{2,6},{6,2},{3,7},{7,3}} | collective-permute-start | bytes 786440 | tf_op jit(solution)/shard_map/ppermute | solution.py:17
  65.8 48.4 %collective-permute-start.18 = (bf16[256,256]{1,0:T(8,128)(2,1)S(1)}, bf16[256,256]{1,0:T(8,128)(2,1)S(1)}, u32[]{:S(2)}, u32[]{:S(2)}) collective-permute-start(bf16[256,256]{1,0:T(8,128)(2,1)S(1)} %constant_dynamic-slice_fusion.8), channel_id=1, source_target_pairs={{0,4},{4,0},{1,5},{5,1},{2,6},{6,2},{3,7},{7,3}} | collective-permute-start | bytes 393224 | tf_op jit(solution)/shard_map/ppermute | solution.py:17
  69.8 140.7 %collective-permute-start.12 = (bf16[2,1024,512]{2,1,0:T(8,128)(2,1)}, bf16[2,1024,512]{2,1,0:T(8,128)(2,1)}, u32[]{:S(2)}, u32[]{:S(2)}) collective-permute-start(bf16[2,1024,512]{2,1,0:T(8,128)(2,1)} %pad_maximum_fusion.2.near_w), channel_id=1, source_target_pairs={{0,4},{4,0},{1,5},{5,1},{2,6},{6,2},{3,7},{7,3}} | collective-permute-start | bytes 6291464 | tf_op jit(solution)/shard_map/ppermute | solution.py:17
  114.2 111.0 %collective-permute-start.21 = (bf16[2,1024,512]{2,1,0:T(8,128)(2,1)}, bf16[2,1024,512]{2,1,0:T(8,128)(2,1)}, u32[]{:S(2)}, u32[]{:S(2)}) collective-permute-start(bf16[2,1024,512]{2,1,0:T(8,128)(2,1)} %pad_maximum_fusion.3.near_w), channel_id=1, source_target_pairs={{0,4},{4,0},{1,5},{5,1},{2,6},{6,2},{3,7},{7,3}} | collective-permute-start | bytes 6291464 | tf_op jit(solution)/shard_map/ppermute | solution.py:17
  126.3 22.7 %collective-permute-start.15 = (bf16[2,512,512]{2,1,0:T(8,128)(2,1)S(1)}, bf16[2,512,512]{2,1,0:T(8,128)(2,1)}, u32[]{:S(2)}, u32[]{:S(2)}) collective-permute-start(bf16[2,512,512]{2,1,0:T(8,128)(2,1)S(1)} %dynamic-slice_bitcast_fusion), channel_id=1, source_target_pairs={{0,2},{2,0},{1,3},{3,1},{4,6},{6,4},{5,7},{7,5}} | collective-permute-start | bytes 3145736 | tf_op jit(solution)/shard_map/ppermute | solution.py:17
  127.7 25.4 %collective-permute-start.20 = (bf16[2,256,256]{2,1,0:T(8,128)(2,1)}, bf16[2,256,256]{2,1,0:T(8,128)(2,1)}, u32[]{:S(2)}, u32[]{:S(2)}) collective-permute-start(bf16[2,256,256]{2,1,0:T(8,128)(2,1)} %maximum_select_fusion.4), channel_id=1, source_target_pairs={{0,1},{1,0},{2,3},{3,2},{4,5},{5,4},{6,7},{7,6}} | collective-permute-start | bytes 786440 | tf_op jit(solution)/shard_map/ppermute | solution.py:17
  128.8 28.6 %collective-permute-start.16 = (bf16[512,512]{1,0:T(8,128)(2,1)}, bf16[512,512]{1,0:T(8,128)(2,1)S(1)}, u32[]{:S(2)}, u32[]{:S(2)}) collective-permute-start(bf16[512,512]{1,0:T(8,128)(2,1)} %get-tuple-element.55), channel_id=1, source_target_pairs={{0,1},{1,0},{2,3},{3,2},{4,5},{5,4},{6,7},{7,6}} | collective-permute-start | bytes 1572872 | tf_op jit(solution)/shard_map/ppermute | solution.py:17
  210.0 36.1 %collective-permute-start.29 = (bf16[2560,256]{1,0:T(8,128)(2,1)}, bf16[2560,256]{1,0:T(8,128)(2,1)S(1)}, u32[]{:S(2)}, u32[]{:S(2)}) collective-permute-start(bf16[2560,256]{1,0:T(8,128)(2,1)} %pad_maximum_fusion.6), channel_id=1, source_target_pairs={{0,1},{1,0},{2,3},{3,2},{4,5},{5,4},{6,7},{7,6}} | collective-permute-start | bytes 3932168 | tf_op jit(solution)/shard_map/ppermute | solution.py:17
  210.3 38.4 %collective-permute-start.25 = (bf16[2048,512]{1,0:T(8,128)(2,1)}, bf16[2048,512]{1,0:T(8,128)(2,1)}, u32[]{:S(2)}, u32[]{:S(2)}) collective-permute-start(bf16[2048,512]{1,0:T(8,128)(2,1)} %glu.4.refs_0_), channel_id=1, source_target_pairs={{0,1},{1,0},{2,3},{3,2},{4,5},{5,4},{6,7},{7,6}} | collective-permute-start | bytes 6291464 | tf_op jit(solution)/shard_map/ppermute | solution.py:17
  210.5 28.0 %collective-permute-start.22 = (bf16[512,512]{1,0:T(8,128)(2,1)}, bf16[512,512]{1,0:T(8,128)(2,1)}, u32[]{:S(2)}, u32[]{:S(2)}) collective-permute-start(bf16[512,512]{1,0:T(8,128)(2,1)} %get-tuple-element.28), channel_id=1, source_target_pairs={{0,1},{1,0},{2,3},{3,2},{4,5},{5,4},{6,7},{7,6}} | collective-permute-start | bytes 1572872 | tf_op jit(solution)/shard_map/ppermute | solution.py:17
  211.9 28.7 %collective-permute-start.24 = (bf16[2,512,512]{2,1,0:T(8,128)(2,1)}, bf16[2,512,512]{2,1,0:T(8,128)(2,1)}, u32[]{:S(2)}, u32[]{:S(2)}) collective-permute-start(bf16[2,512,512]{2,1,0:T(8,128)(2,1)} %pad_maximum_fusion.8), channel_id=1, source_target_pairs={{0,2},{2,0},{1,3},{3,1},{4,6},{6,4},{5,7},{7,5}} | collective-permute-start | bytes 3145736 | tf_op jit(solution)/shard_map/ppermute | solution.py:17
  225.2 25.9 %collective-permute-start.26 = (bf16[2048,512]{1,0:T(8,128)(2,1)}, bf16[2048,512]{1,0:T(8,128)(2,1)}, u32[]{:S(2)}, u32[]{:S(2)}) collective-permute-start(bf16[2048,512]{1,0:T(8,128)(2,1)} %glu.5.refs_1_), channel_id=1, source_target_pairs={{0,1},{1,0},{2,3},{3,2},{4,5},{5,4},{6,7},{7,6}} | collective-permute-start | bytes 6291464 | tf_op jit(solution)/shard_map/ppermute | solution.py:17
  246.1 48.0 %collective-permute-start.10 = (bf16[2,1024,512]{2,1,0:T(8,128)(2,1)}, bf16[2,1024,512]{2,1,0:T(8,128)(2,1)}, u32[]{:S(2)}, u32[]{:S(2)}) collective-permute-start(bf16[2,1024,512]{2,1,0:T(8,128)(2,1)} %pad_maximum_fusion.near_w), channel_id=1, source_target_pairs={{0,4},{4,0},{1,5},{5,1},{2,6},{6,2},{3,7},{7,3}} | collective-permute-start | bytes 6291464 | tf_op jit(solution)/shard_map/ppermute | solution.py:17
  307.3 31.5 %collective-permute-start.35 = (bf16[2560,256]{1,0:T(8,128)(2,1)}, bf16[2560,256]{1,0:T(8,128)(2,1)}, u32[]{:S(2)}, u32[]{:S(2)}) collective-permute-start(bf16[2560,256]{1,0:T(8,128)(2,1)} %pad_maximum_fusion.6), channel_id=1, source_target_pairs={{0,4},{4,0},{1,5},{5,1},{2,6},{6,2},{3,7},{7,3}} | collective-permute-start | bytes 3932168 | tf_op jit(solution)/shard_map/ppermute | solution.py:17
  338.8 69.6 %collective-permute-start.32 = (f32[1536,256]{1,0:T(8,128)}, f32[1536,256]{1,0:T(8,128)}, u32[]{:S(2)}, u32[]{:S(2)}) collective-permute-start(f32[1536,256]{1,0:T(8,128)} %mix.14), channel_id=1, source_target_pairs={{0,2},{2,0},{1,3},{3,1},{4,6},{6,4},{5,7},{7,5}} | collective-permute-start | bytes 4718600 | tf_op jit(solution)/shard_map/ppermute | solution.py:17
  340.6 73.7 %collective-permute-start.40 = (bf16[2560,256]{1,0:T(8,128)(2,1)}, bf16[2560,256]{1,0:T(8,128)(2,1)}, u32[]{:S(2)}, u32[]{:S(2)}) collective-permute-start(bf16[2560,256]{1,0:T(8,128)(2,1)} %pad_maximum_fusion.7), channel_id=1, source_target_pairs={{0,4},{4,0},{1,5},{5,1},{2,6},{6,2},{3,7},{7,3}} | collective-permute-start | bytes 3932168 | tf_op jit(solution)/shard_map/ppermute | solution.py:17
  343.2 43.3 %collective-permute-start.34 = (bf16[2560,128]{1,0:T(8,128)(2,1)}, bf16[2560,128]{1,0:T(8,128)(2,1)S(1)}, u32[]{:S(2)}, u32[]{:S(2)}) collective-permute-start(bf16[2560,128]{1,0:T(8,128)(2,1)} %get-tuple-element.59), channel_id=1, source_target_pairs={{0,4},{4,0},{1,5},{5,1},{2,6},{6,2},{3,7},{7,3}} | collective-permute-start | bytes 1966088 | tf_op jit(solution)/shard_map/ppermute | solution.py:17
  343.6 56.2 %collective-permute-start.33 = (bf16[2560,128]{1,0:T(8,128)(2,1)S(1)}, bf16[2560,128]{1,0:T(8,128)(2,1)S(1)}, u32[]{:S(2)}, u32[]{:S(2)}) collective-permute-start(bf16[2560,128]{1,0:T(8,128)(2,1)S(1)} %get-tuple-element.60), channel_id=1, source_target_pairs={{0,4},{4,0},{1,5},{5,1},{2,6},{6,2},{3,7},{7,3}} | collective-permute-start | bytes 1966088 | tf_op jit(solution)/shard_map/ppermute | solution.py:17
  414.3 26.3 %collective-permute-start.42 = (f32[2048,128]{1,0:T(8,128)}, f32[2048,128]{1,0:T(8,128)S(1)}, u32[]{:S(2)}, u32[]{:S(2)}) collective-permute-start(f32[2048,128]{1,0:T(8,128)} %mix.17), channel_id=1, source_target_pairs={{0,2},{2,0},{1,3},{3,1},{4,6},{6,4},{5,7},{7,5}} | collective-permute-start | bytes 3145736 | tf_op jit(solution)/shard_map/ppermute | solution.py:17
  415.8 17.8 %collective-permute-start.39 = (bf16[2560,128]{1,0:T(8,128)(2,1)}, bf16[2560,128]{1,0:T(8,128)(2,1)S(1)}, u32[]{:S(2)}, u32[]{:S(2)}) collective-permute-start(bf16[2560,128]{1,0:T(8,128)(2,1)} %get-tuple-element.57), channel_id=1, source_target_pairs={{0,4},{4,0},{1,5},{5,1},{2,6},{6,2},{3,7},{7,3}} | collective-permute-start | bytes 1966088 | tf_op jit(solution)/shard_map/ppermute | solution.py:17
  417.4 45.7 %collective-permute-start.43 = (f32[2048,128]{1,0:T(8,128)}, f32[2048,128]{1,0:T(8,128)S(1)}, u32[]{:S(2)}, u32[]{:S(2)}) collective-permute-start(f32[2048,128]{1,0:T(8,128)} %mix.18), channel_id=1, source_target_pairs={{0,2},{2,0},{1,3},{3,1},{4,6},{6,4},{5,7},{7,5}} | collective-permute-start | bytes 3145736 | tf_op jit(solution)/shard_map/ppermute | solution.py:17
  419.1 34.5 %collective-permute-start.38 = (bf16[2560,128]{1,0:T(8,128)(2,1)}, bf16[2560,128]{1,0:T(8,128)(2,1)}, u32[]{:S(2)}, u32[]{:S(2)}) collective-permute-start(bf16[2560,128]{1,0:T(8,128)(2,1)} %get-tuple-element.58), channel_id=1, source_target_pairs={{0,4},{4,0},{1,5},{5,1},{2,6},{6,2},{3,7},{7,3}} | collective-permute-start | bytes 1966088 | tf_op jit(solution)/shard_map/ppermute | solution.py:17
  419.5 54.4 %collective-permute-start.37 = (f32[512,256]{1,0:T(8,128)}, f32[512,256]{1,0:T(8,128)}, u32[]{:S(2)}, u32[]{:S(2)}) collective-permute-start(f32[512,256]{1,0:T(8,128)} %mix.15), channel_id=1, source_target_pairs={{0,2},{2,0},{1,3},{3,1},{4,6},{6,4},{5,7},{7,5}} | collective-permute-start | bytes 1572872 | tf_op jit(solution)/shard_map/ppermute | solution.py:17
  449.6 29.6 %collective-permute-start.44 = (bf16[2048,128]{1,0:T(8,128)(2,1)}, bf16[2048,128]{1,0:T(8,128)(2,1)S(1)}, u32[]{:S(2)}, u32[]{:S(2)}) collective-permute-start(bf16[2048,128]{1,0:T(8,128)(2,1)} %mix.21), channel_id=1, source_target_pairs={{0,4},{4,0},{1,5},{5,1},{2,6},{6,2},{3,7},{7,3}} | collective-permute-start | bytes 1572872 | tf_op jit(solution)/shard_map/ppermute | solution.py:17
  (50 other events, 415.9 us)

commit v6 on v5

--- a/solution.py
+++ b/solution.py
@@ -266,10 +266,9 @@
         kv_part = swap_y(lax.dynamic_slice_in_dim(w_kv, ti * kv_rows, kv_rows, 0))
         kv_pair = ordered([kv_part, swap_x(kv_part)], xi, 0)
         kv_far = ordered([kv_pair, swap_c(kv_pair)], ci, 1).reshape(w_kv.shape)
-        lead = 256
-        q_far = [swap_y(w_query[:lead]), swap_y(w_query[lead:])]
-
-        q = project(h, [w_query, *q_far])
+        q_far = swap_y(w_query)
+
+        q = project(h, [w_query, q_far])
         h_own = lax.dynamic_slice_in_dim(h, ti * own_tok, own_tok, 0)
         kv = jnp.dot(h_own, jnp.concatenate([w_kv, kv_far], 0), preferred_element_type=F32).astype(BF16)
 
@@ -308,7 +307,8 @@
 
         def block(xr, cr):
             col = (2 * (xi ^ xr) + (ci ^ cr)) * width
-            return jnp.concatenate([lax.dynamic_slice_in_dim(w, col, width, 1) for w in (w_down, w_out)], 0)
+            pair = (w_down, w_out) if xr and cr else (tie(w_down, h), tie(w_out, h))
+            return jnp.concatenate([lax.dynamic_slice_in_dim(w, col, width, 1) for w in pair], 0)
 
         blocks = [[block(xr, cr) for cr in range(2)] for xr in range(2)]
         narrow = width // 2

time: 487 us -> 483 us (level)
    ppermute x46 -> x45, waiting for transfers between devices: 179 us -> 180 us  [swap(): return lambda a: lax.ppermute(a, axis, pairs)]
    unnamed x73 -> x67, local copies, waits for them, and re-layouts: 12.1 us -> 11.6 us
    ppermute x46 -> x45, starting transfers between devices: 34.7 us -> 34.6 us  [swap(): return lambda a: lax.ppermute(a, axis, pairs)]
  transfers between devices with their start and end apart: 46 -> 45, of which waited for: 15 -> 16; matrix products, arithmetic and copies ran while one was open for 10% -> 9% of each run, Pallas kernels for 40% -> 41%
where the time goes in v6:
time: 483 us; the launch traced here: 482 us
  Pallas kernels  209 us (43%)
  waiting for transfers between devices  180 us (37%)
  starting transfers between devices  34.6 us (7%)
  local copies, waits for them, and re-layouts  31.5 us (7%)
  other arithmetic  23.5 us (5%)
    ppermute x45, waiting for transfers between devices, swap(): return lambda a: lax.ppermute(a, axis, pairs)  180 us
    pallas_call x12, Pallas kernels, mix(): pl.pallas_call(functools.partial(mix_kernel, plan, len(lhs), len(ws)), gr...  88.3 us
    pallas_call x4, Pallas kernels, glu(): pl.pallas_call(glu_kernel, grid=(tokens // blk,), in_specs=[pl.BlockSpec(...  52.7 us
    pallas_call x1, Pallas kernels, attention(): pl.pallas_call(attn_kernel, grid_spec=pltpu.PrefetchScalarGridSpec(num_sc...  46 us
    ppermute x45, starting transfers between devices, swap(): return lambda a: lax.ppermute(a, axis, pairs)  34.6 us
    pallas_call x1, Pallas kernels, layer_norm(): pl.pallas_call(norm_kernel, grid_spec=pltpu.PrefetchScalarGridSpec(num_sc...  13 us
    unnamed x67, local copies, waits for them, and re-layouts  11.6 us
    another operation x4, other arithmetic, local_layer(): jnp.stack([w[:, j * cw:(j + 1) * cw] for w in (w_gate, w_up)])  9.73 us
  transfers between devices with their start and end apart: 45, of which 16 were waited for; matrix products, arithmetic and copies ran while one was open for 9% of the time, Pallas kernels for 41%

profile of v6, /device:TPU:0, one launch (start us, length us, event | category | flops | bytes accessed | tf_op | source)
XLA Modules:
  0.0 482.0 jit_solution(9583396073883939321)
XLA Ops:
  8.7 21.4 %collective-permute-done.refs_1_.refs_6_ = bf16[2048,256]{1,0:T(8,128)(2,1)} collective-permute-done((bf16[2048,256]{1,0:T(8,128)(2,1)}, bf16[2048,256]{1,0:T(8,128)(2,1)}, u32[]{:S(2)}, u32[]{:S(2)}) %collective-permute-start) | collective-permute-done | bytes 1048608 | tf_op jit(solution)/shard_map/ppermute | solution.py:17
  31.8 5.5 %slice_bitcast_fusion = (bf16[1,1024,512]{2,1,0:T(8,128)(2,1)S(1)}, bf16[1,1024,512]{2,1,0:T(8,128)(2,1)S(1)}, bf16[1,1024,512]{2,1,0:T(8,128)(2,1)}, bf16[1,102...) fusion(bf16[1024,2048]{1,0:T(8,128)(2,1)} %param.21, ...), kind=kLoop, calls=%fused_computation.27 | loop fusion | bytes 16777216 | tf_op jit(solution)/shard_map/stack | solution.py:280
  42.4 12.3 %collective-permute-done.8 = f32[2,256]{1,0:T(2,128)S(1)} collective-permute-done((f32[2,256]{1,0:T(2,128)S(1)}, f32[2,256]{1,0:T(2,128)S(1)}, u32[]{:S(2)}, u32[]{:S(2)}) %collective-permute-start.8) | collective-permute-done | bytes 2080 | tf_op jit(solution)/shard_map/ppermute | solution.py:17
  57.4 30.7 %collective-permute-done.17 = bf16[256,256]{1,0:T(8,128)(2,1)S(1)} collective-permute-done((bf16[256,256]{1,0:T(8,128)(2,1)S(1)}, bf16[256,256]{1,0:T(8,128)(2,1)S(1)}, u32[]{:S(2)}, u32[]{:S(2)}) %collective-permute-start.17) | collective-permute-done | bytes 131104 | tf_op jit(solution)/shard_map/ppermute | solution.py:17
  98.6 13.0 %norm.1.h_ref = bf16[2048,2048]{1,0:T(8,128)(2,1)} custom-call(s32[8]{0:T(128)} %stack.140.offs_ref, bf16[2048,256]{1,0:T(8,128)(2,1)} %copy-done.6, bf16[2048,256]{1,0:T(8,128)(2,1)} %collective-permute-done.refs_1_.refs_6_, bf16[2048,256]{1,0:T(8,128)(2,1)} %collective-permute-done.1.refs_2_, bf16[2048,256]{1,0:T(8,128)(2,1)} %collective-permute-done.2.refs_3_, ...), custom_call_target="tpu_custom_call" | custom-call | flops 83886080 | bytes 16777216 | tf_op jit(solution)/shard_map/norm/pallas_call | solution.py:47
  114.9 8.7 %project.1 = bf16[2048,512]{1,0:T(8,128)(2,1)} custom-call(bf16[2048,2048]{1,0:T(8,128)(2,1)} %norm.1.h_ref, bf16[1024,512]{1,0:T(8,128)(2,1)} %refs_0_.1, bf16[1024,512]{1,0:T(8,128)(2,1)} %collective-permute-done.13.refs_1_), custom_call_target="tpu_custom_call" | custom-call | flops 4294967296 | bytes 10485760 | tf_op jit(solution)/shard_map/project/pallas_call | solution.py:179
  127.9 13.2 %glu.4.refs_0_ = bf16[2048,512]{1,0:T(8,128)(2,1)} custom-call(bf16[2048,2048]{1,0:T(8,128)(2,1)} %norm.1.h_ref, bf16[2,1024,512]{2,1,0:T(8,128)(2,1)} %pad_maximum_fusion.1.near_w, bf16[2,1024,512]{2,1,0:T(8,128)(2,1)} %collective-permute-done.11.far_w), custom_call_target="tpu_custom_call" | custom-call | flops 8589934592 | bytes 14680064 | tf_op jit(solution)/shard_map/glu/pallas_call | solution.py:155
  141.1 7.3 %collective-permute-done.14 = bf16[2,512,512]{2,1,0:T(8,128)(2,1)} collective-permute-done((bf16[2,512,512]{2,1,0:T(8,128)(2,1)S(1)}, bf16[2,512,512]{2,1,0:T(8,128)(2,1)}, u32[]{:S(2)}, u32[]{:S(2)}) %collective-permute-start.14) | collective-permute-done | bytes 1048608 | tf_op jit(solution)/shard_map/ppermute | solution.py:17
  157.8 46.0 %attn.1 = (bf16[512,512]{1,0:T(8,128)(2,1)}, bf16[512,512]{1,0:T(8,128)(2,1)}, bf16[512,512]{1,0:T(8,128)(2,1)}, bf16[512,512]{1,0:T(8,128)(2,1)}, bf16[8,2048,1...) custom-call(s32[8]{0:T(128)} %len_ref.1, bf16[512,512]{1,0:T(8,128)(2,1)} %get-tuple-element.59.q0, ...), custom_call_target="tpu_custom_call" | custom-call | flops 17179869184 | bytes 16777216 | tf_op jit(solution)/shard_map/attn/pallas_call | solution.py:125
  208.5 13.2 %glu.5.refs_1_ = bf16[2048,512]{1,0:T(8,128)(2,1)} custom-call(bf16[2048,2048]{1,0:T(8,128)(2,1)} %norm.1.h_ref, bf16[2,1024,512]{2,1,0:T(8,128)(2,1)} %pad_maximum_fusion.2.near_w, bf16[2,1024,512]{2,1,0:T(8,128)(2,1)} %collective-permute-done.12.far_w), custom_call_target="tpu_custom_call" | custom-call | flops 8589934592 | bytes 14680064 | tf_op jit(solution)/shard_map/glu/pallas_call | solution.py:155
  221.8 13.2 %glu.6.refs_2_ = bf16[2048,512]{1,0:T(8,128)(2,1)} custom-call(bf16[2048,2048]{1,0:T(8,128)(2,1)} %norm.1.h_ref, bf16[2,1024,512]{2,1,0:T(8,128)(2,1)} %pad_maximum_fusion.3.near_w, bf16[2,1024,512]{2,1,0:T(8,128)(2,1)} %collective-permute-done.20.far_w), custom_call_target="tpu_custom_call" | custom-call | flops 8589934592 | bytes 14680064 | tf_op jit(solution)/shard_map/glu/pallas_call | solution.py:155
  237.8 3.7 pad_maximum_fusion.near_w
  247.3 10.8 %mix.12.refs_4_ = f32[2048,256]{1,0:T(8,128)} custom-call(bf16[2048,512]{1,0:T(8,128)(2,1)} %glu.4.refs_0_, bf16[2048,512]{1,0:T(8,128)(2,1)} %glu.5.refs_1_, bf16[2048,512]{1,0:T(8,128)(2,1)} %glu.6.refs_2_, bf16[2048,512]{1,0:T(8,128)(2,1)} %bitcast.66, bf16[2048,512]{1,0:T(8,128)(2,1)} %collective-permute-done.24.refs_4_.refs_0_, ...), custom_call_target="tpu_custom_call" | custom-call | flops 4294967296 | bytes 18874368 | tf_op jit(solution)/shard_map/mix/pallas_call | solution.py:216
  259.2 11.1 %mix.13.refs_4_ = f32[2048,256]{1,0:T(8,128)} custom-call(bf16[2048,512]{1,0:T(8,128)(2,1)} %glu.4.refs_0_, bf16[2048,512]{1,0:T(8,128)(2,1)} %glu.5.refs_1_, bf16[2048,512]{1,0:T(8,128)(2,1)} %glu.6.refs_2_, bf16[2048,512]{1,0:T(8,128)(2,1)} %bitcast.67, bf16[2048,512]{1,0:T(8,128)(2,1)} %collective-permute-done.24.refs_4_.refs_0_, ...), custom_call_target="tpu_custom_call" | custom-call | flops 4294967296 | bytes 18874368 | tf_op jit(solution)/shard_map/mix/pallas_call | solution.py:216
  270.3 19.8 %collective-permute-done.10.far_w = bf16[2,1024,512]{2,1,0:T(8,128)(2,1)} collective-permute-done((bf16[2,1024,512]{2,1,0:T(8,128)(2,1)}, bf16[2,1024,512]{2,1,0:T(8,128)(2,1)}, u32[]{:S(2)}, u32[]{:S(2)}) %collective-permute-start.10) | collective-permute-done | bytes 2097184 | tf_op jit(solution)/shard_map/ppermute | solution.py:17
  290.0 13.2 %glu.7.refs_0_.refs_3_ = bf16[2048,512]{1,0:T(8,128)(2,1)} custom-call(bf16[2048,2048]{1,0:T(8,128)(2,1)} %norm.1.h_ref, bf16[2,1024,512]{2,1,0:T(8,128)(2,1)} %pad_maximum_fusion.near_w, bf16[2,1024,512]{2,1,0:T(8,128)(2,1)} %collective-permute-done.10.far_w), custom_call_target="tpu_custom_call" | custom-call | flops 8589934592 | bytes 14680064 | tf_op jit(solution)/shard_map/glu/pallas_call | solution.py:155
  312.3 5.9 %mix.14 = f32[1536,256]{1,0:T(8,128)} custom-call(bf16[2048,512]{1,0:T(8,128)(2,1)} %glu.7.refs_0_.refs_3_, bf16[2048,512]{1,0:T(8,128)(2,1)} %copy-done.3, bf16[2560,256]{1,0:T(8,128)(2,1)} %pad_maximum_fusion.5.refs_8_.refs_2_, bf16[2560,256]{1,0:T(8,128)(2,1)} %copy-done.5, f32[2048,256]{1,0:T(8,128)} %mix.12.refs_4_), custom_call_target="tpu_custom_call" | custom-call | flops 805306368 | bytes 3670016 | tf_op jit(solution)/shard_map/mix/pallas_call | solution.py:216
  318.2 16.5 %collective-permute-done.34 = bf16[2560,256]{1,0:T(8,128)(2,1)} collective-permute-done((bf16[2560,256]{1,0:T(8,128)(2,1)}, bf16[2560,256]{1,0:T(8,128)(2,1)}, u32[]{:S(2)}, u32[]{:S(2)}) %collective-permute-start.34) | collective-permute-done | bytes 1310752 | tf_op jit(solution)/shard_map/ppermute | solution.py:17
  342.2 7.9 %mix.16.refs_6_ = f32[2048,256]{1,0:T(8,128)} custom-call(bf16[2048,512]{1,0:T(8,128)(2,1)} %collective-permute-done.24.refs_4_.refs_0_, bf16[2048,512]{1,0:T(8,128)(2,1)} %collective-permute-done.25.refs_5_.refs_1_, bf16[2048,512]{1,0:T(8,128)(2,1)} %collective-permute-done.26.refs_6_.refs_2_, bf16[2048,512]{1,0:T(8,128)(2,1)} %copy-done.3, ...), custom_call_target="tpu_custom_call" | custom-call | flops 2684354560 | bytes 11796480 | tf_op jit(solution)/shard_map/mix/pallas_call | solution.py:216
  350.1 32.3 %collective-permute-done.33.refs_5_ = bf16[2560,128]{1,0:T(8,128)(2,1)S(1)} collective-permute-done((bf16[2560,128]{1,0:T(8,128)(2,1)}, bf16[2560,128]{1,0:T(8,128)(2,1)S(1)}, u32[]{:S(2)}, u32[]{:S(2)}) %collective-permute-start.33) | collective-permute-done | bytes 655392 | tf_op jit(solution)/shard_map/ppermute | solution.py:17
  383.3 7.7 %mix.17 = f32[2048,128]{1,0:T(8,128)} custom-call(bf16[2048,512]{1,0:T(8,128)(2,1)} %glu.4.refs_0_, bf16[2048,512]{1,0:T(8,128)(2,1)} %glu.5.refs_1_, bf16[2048,512]{1,0:T(8,128)(2,1)} %glu.6.refs_2_, bf16[2048,512]{1,0:T(8,128)(2,1)} %glu.7.refs_0_.refs_3_, bf16[2048,512]{1,0:T(8,128)(2,1)} %bitcast.68, bf16[2560,128]{1,0:T(8,128)(2,1)} %copy-done.24, ...), custom_call_target="tpu_custom_call" | custom-call | flops 1342177280 | bytes 11141120 | tf_op jit(solution)/shard_map/mix/pallas_call | solution.py:216
  391.0 4.8 collective-permute-done.32.refs_5_
  396.6 7.7 %mix.18 = f32[2048,128]{1,0:T(8,128)} custom-call(bf16[2048,512]{1,0:T(8,128)(2,1)} %glu.4.refs_0_, bf16[2048,512]{1,0:T(8,128)(2,1)} %glu.5.refs_1_, bf16[2048,512]{1,0:T(8,128)(2,1)} %glu.6.refs_2_, bf16[2048,512]{1,0:T(8,128)(2,1)} %glu.7.refs_0_.refs_3_, bf16[2048,512]{1,0:T(8,128)(2,1)} %bitcast.69, bf16[2560,128]{1,0:T(8,128)(2,1)} %copy-done.23, ...), custom_call_target="tpu_custom_call" | custom-call | flops 1342177280 | bytes 11141120 | tf_op jit(solution)/shard_map/mix/pallas_call | solution.py:216
  404.3 5.9 %mix.19 = bf16[1536,256]{1,0:T(8,128)(2,1)} custom-call(bf16[2048,512]{1,0:T(8,128)(2,1)} %glu.7.refs_0_.refs_3_, bf16[2048,512]{1,0:T(8,128)(2,1)} %copy-done.3, bf16[2560,256]{1,0:T(8,128)(2,1)} %pad_maximum_fusion.4.refs_8_.refs_2_, bf16[2560,256]{1,0:T(8,128)(2,1)} %copy-done.4, f32[2048,256]{1,0:T(8,128)} %mix.13.refs_4_, ...), custom_call_target="tpu_custom_call" | custom-call | flops 805306368 | bytes 3670016 | tf_op jit(solution)/shard_map/mix/pallas_call | solution.py:216
  416.6 8.3 %mix.20.refs_6_ = f32[2048,256]{1,0:T(8,128)} custom-call(bf16[2048,512]{1,0:T(8,128)(2,1)} %collective-permute-done.24.refs_4_.refs_0_, bf16[2048,512]{1,0:T(8,128)(2,1)} %collective-permute-done.25.refs_5_.refs_1_, bf16[2048,512]{1,0:T(8,128)(2,1)} %collective-permute-done.26.refs_6_.refs_2_, bf16[2048,512]{1,0:T(8,128)(2,1)} %copy-done.3, ...), custom_call_target="tpu_custom_call" | custom-call | flops 2684354560 | bytes 11796480 | tf_op jit(solution)/shard_map/mix/pallas_call | solution.py:216
  424.9 4.7 collective-permute-done.38.refs_5_
  429.6 7.0 %collective-permute-done.41.refs_7_ = f32[2048,128]{1,0:T(8,128)} collective-permute-done((f32[2048,128]{1,0:T(8,128)}, f32[2048,128]{1,0:T(8,128)}, u32[]{:S(2)}, u32[]{:S(2)}) %collective-permute-start.41) | collective-permute-done | bytes 1048608 | tf_op jit(solution)/shard_map/ppermute | solution.py:17
  436.6 8.0 %mix.21 = bf16[2048,128]{1,0:T(8,128)(2,1)} custom-call(bf16[2048,512]{1,0:T(8,128)(2,1)} %glu.4.refs_0_, bf16[2048,512]{1,0:T(8,128)(2,1)} %glu.5.refs_1_, bf16[2048,512]{1,0:T(8,128)(2,1)} %glu.6.refs_2_, bf16[2048,512]{1,0:T(8,128)(2,1)} %glu.7.refs_0_.refs_3_, bf16[2048,512]{1,0:T(8,128)(2,1)} %bitcast.70, bf16[2560,128]{1,0:T(8,128)(2,1)} %copy-done.25, ...), custom_call_target="tpu_custom_call" | custom-call | flops 1342177280 | bytes 11141120 | tf_op jit(solution)/shard_map/mix/pallas_call | solution.py:216
  447.8 11.2 %collective-permute-done.42.refs_7_ = f32[2048,128]{1,0:T(8,128)S(1)} collective-permute-done((f32[2048,128]{1,0:T(8,128)}, f32[2048,128]{1,0:T(8,128)S(1)}, u32[]{:S(2)}, u32[]{:S(2)}) %collective-permute-start.42) | collective-permute-done | bytes 1048608 | tf_op jit(solution)/shard_map/ppermute | solution.py:17
  460.0 8.0 %mix.22 = bf16[2048,128]{1,0:T(8,128)(2,1)} custom-call(bf16[2048,512]{1,0:T(8,128)(2,1)} %glu.4.refs_0_, bf16[2048,512]{1,0:T(8,128)(2,1)} %glu.5.refs_1_, bf16[2048,512]{1,0:T(8,128)(2,1)} %glu.6.refs_2_, bf16[2048,512]{1,0:T(8,128)(2,1)} %glu.7.refs_0_.refs_3_, bf16[2048,512]{1,0:T(8,128)(2,1)} %bitcast.71, ...), custom_call_target="tpu_custom_call" | custom-call | flops 1342177280 | bytes 11141120 | tf_op jit(solution)/shard_map/mix/pallas_call | solution.py:216
  469.9 3.6 mix.23
  476.0 5.2 %collective-permute-done.44 = bf16[2048,128]{1,0:T(8,128)(2,1)S(1)} collective-permute-done((bf16[2048,128]{1,0:T(8,128)(2,1)}, bf16[2048,128]{1,0:T(8,128)(2,1)S(1)}, u32[]{:S(2)}, u32[]{:S(2)}) %collective-permute-start.44) | collective-permute-done | bytes 524320 | tf_op jit(solution)/shard_map/ppermute | solution.py:17
  (189 shorter events, 93.4 us)
Async XLA Ops:
  3.3 26.8 %collective-permute-start = (bf16[2048,256]{1,0:T(8,128)(2,1)}, bf16[2048,256]{1,0:T(8,128)(2,1)}, u32[]{:S(2)}, u32[]{:S(2)}) collective-permute-start(bf16[2048,256]{1,0:T(8,128)(2,1)} %dynamic-slice_bitcast_fusion.2), channel_id=1, source_target_pairs={{0,4},{4,0},{1,5},{5,1},{2,6},{6,2},{3,7},{7,3}} | collective-permute-start | bytes 3145736 | tf_op jit(solution)/shard_map/ppermute | solution.py:17
  6.7 50.7 %collective-permute-start.1 = (bf16[2048,256]{1,0:T(8,128)(2,1)S(1)}, bf16[2048,256]{1,0:T(8,128)(2,1)}, u32[]{:S(2)}, u32[]{:S(2)}) collective-permute-start(bf16[2048,256]{1,0:T(8,128)(2,1)S(1)} %dynamic-slice_bitcast_fusion.1.refs_0_.refs_10_), channel_id=1, source_target_pairs={{0,2},{2,0},{1,3},{3,1},{4,6},{6,4},{5,7},{7,5}} | collective-permute-start | bytes 3145736 | tf_op jit(solution)/shard_map/ppermute | solution.py:17
  8.2 80.4 %collective-permute-start.3 = (bf16[2048,256]{1,0:T(8,128)(2,1)S(1)}, bf16[2048,256]{1,0:T(8,128)(2,1)}, u32[]{:S(2)}, u32[]{:S(2)}) collective-permute-start(bf16[2048,256]{1,0:T(8,128)(2,1)S(1)} %dynamic-slice_bitcast_fusion.1.refs_0_.refs_10_), channel_id=1, source_target_pairs={{0,1},{1,0},{2,3},{3,2},{4,5},{5,4},{6,7},{7,6}} | collective-permute-start | bytes 3145736 | tf_op jit(solution)/shard_map/ppermute | solution.py:17
  8.2 32.9 %collective-permute-start.7 = (f32[1,256]{1,0:T(1,128)S(1)}, f32[1,256]{1,0:T(1,128)S(1)}, u32[]{:S(2)}, u32[]{:S(2)}) collective-permute-start(f32[1,256]{1,0:T(1,128)S(1)} %bitcast.83), channel_id=1, source_target_pairs={{0,4},{4,0},{1,5},{5,1},{2,6},{6,2},{3,7},{7,3}} | collective-permute-start | bytes 3080 | tf_op jit(solution)/shard_map/ppermute | solution.py:17
  30.1 58.0 %collective-permute-start.2 = (bf16[2048,256]{1,0:T(8,128)(2,1)}, bf16[2048,256]{1,0:T(8,128)(2,1)}, u32[]{:S(2)}, u32[]{:S(2)}) collective-permute-start(bf16[2048,256]{1,0:T(8,128)(2,1)} %collective-permute-done.refs_1_.refs_6_), channel_id=1, source_target_pairs={{0,2},{2,0},{1,3},{3,1},{4,6},{6,4},{5,7},{7,5}} | collective-permute-start | bytes 3145736 | tf_op jit(solution)/shard_map/ppermute | solution.py:17
  38.8 88.6 %collective-permute-start.11 = (bf16[2,1024,512]{2,1,0:T(8,128)(2,1)}, bf16[2,1024,512]{2,1,0:T(8,128)(2,1)}, u32[]{:S(2)}, u32[]{:S(2)}) collective-permute-start(bf16[2,1024,512]{2,1,0:T(8,128)(2,1)} %pad_maximum_fusion.1.near_w), channel_id=1, source_target_pairs={{0,4},{4,0},{1,5},{5,1},{2,6},{6,2},{3,7},{7,3}} | collective-permute-start | bytes 6291464 | tf_op jit(solution)/shard_map/ppermute | solution.py:17
  55.9 32.1 %collective-permute-start.17 = (bf16[256,256]{1,0:T(8,128)(2,1)S(1)}, bf16[256,256]{1,0:T(8,128)(2,1)S(1)}, u32[]{:S(2)}, u32[]{:S(2)}) collective-permute-start(bf16[256,256]{1,0:T(8,128)(2,1)S(1)} %constant_dynamic-slice_fusion.8), channel_id=1, source_target_pairs={{0,4},{4,0},{1,5},{5,1},{2,6},{6,2},{3,7},{7,3}} | collective-permute-start | bytes 393224 | tf_op jit(solution)/shard_map/ppermute | solution.py:17
  57.4 38.7 %collective-permute-start.5 = (bf16[2048,256]{1,0:T(8,128)(2,1)}, bf16[2048,256]{1,0:T(8,128)(2,1)}, u32[]{:S(2)}, u32[]{:S(2)}) collective-permute-start(bf16[2048,256]{1,0:T(8,128)(2,1)} %collective-permute-done.1.refs_2_), channel_id=1, source_target_pairs={{0,1},{1,0},{2,3},{3,2},{4,5},{5,4},{6,7},{7,6}} | collective-permute-start | bytes 3145736 | tf_op jit(solution)/shard_map/ppermute | solution.py:17
  88.6 26.3 %collective-permute-start.13 = (bf16[1024,512]{1,0:T(8,128)(2,1)}, bf16[1024,512]{1,0:T(8,128)(2,1)}, u32[]{:S(2)}, u32[]{:S(2)}) collective-permute-start(bf16[1024,512]{1,0:T(8,128)(2,1)} %refs_0_.1), channel_id=1, source_target_pairs={{0,4},{4,0},{1,5},{5,1},{2,6},{6,2},{3,7},{7,3}} | collective-permute-start | bytes 3145736 | tf_op jit(solution)/shard_map/ppermute | solution.py:17
  96.1 111.9 %collective-permute-start.12 = (bf16[2,1024,512]{2,1,0:T(8,128)(2,1)}, bf16[2,1024,512]{2,1,0:T(8,128)(2,1)}, u32[]{:S(2)}, u32[]{:S(2)}) collective-permute-start(bf16[2,1024,512]{2,1,0:T(8,128)(2,1)} %pad_maximum_fusion.2.near_w), channel_id=1, source_target_pairs={{0,4},{4,0},{1,5},{5,1},{2,6},{6,2},{3,7},{7,3}} | collective-permute-start | bytes 6291464 | tf_op jit(solution)/shard_map/ppermute | solution.py:17
  96.6 125.1 %collective-permute-start.20 = (bf16[2,1024,512]{2,1,0:T(8,128)(2,1)}, bf16[2,1024,512]{2,1,0:T(8,128)(2,1)}, u32[]{:S(2)}, u32[]{:S(2)}) collective-permute-start(bf16[2,1024,512]{2,1,0:T(8,128)(2,1)} %pad_maximum_fusion.3.near_w), channel_id=1, source_target_pairs={{0,4},{4,0},{1,5},{5,1},{2,6},{6,2},{3,7},{7,3}} | collective-permute-start | bytes 6291464 | tf_op jit(solution)/shard_map/ppermute | solution.py:17
  98.1 27.6 %collective-permute-start.18 = (bf16[256,256]{1,0:T(8,128)(2,1)S(1)}, bf16[256,256]{1,0:T(8,128)(2,1)S(1)}, u32[]{:S(2)}, u32[]{:S(2)}) collective-permute-start(bf16[256,256]{1,0:T(8,128)(2,1)S(1)} %collective-permute-done.17), channel_id=1, source_target_pairs={{0,2},{2,0},{1,3},{3,1},{4,6},{6,4},{5,7},{7,5}} | collective-permute-start | bytes 393224 | tf_op jit(solution)/shard_map/ppermute | solution.py:17
  125.0 23.4 %collective-permute-start.14 = (bf16[2,512,512]{2,1,0:T(8,128)(2,1)S(1)}, bf16[2,512,512]{2,1,0:T(8,128)(2,1)}, u32[]{:S(2)}, u32[]{:S(2)}) collective-permute-start(bf16[2,512,512]{2,1,0:T(8,128)(2,1)S(1)} %dynamic-slice_bitcast_fusion), channel_id=1, source_target_pairs={{0,2},{2,0},{1,3},{3,1},{4,6},{6,4},{5,7},{7,5}} | collective-permute-start | bytes 3145736 | tf_op jit(solution)/shard_map/ppermute | solution.py:17
  126.4 26.2 %collective-permute-start.19 = (bf16[2,256,256]{2,1,0:T(8,128)(2,1)}, bf16[2,256,256]{2,1,0:T(8,128)(2,1)}, u32[]{:S(2)}, u32[]{:S(2)}) collective-permute-start(bf16[2,256,256]{2,1,0:T(8,128)(2,1)} %maximum_select_fusion.4), channel_id=1, source_target_pairs={{0,1},{1,0},{2,3},{3,2},{4,5},{5,4},{6,7},{7,6}} | collective-permute-start | bytes 786440 | tf_op jit(solution)/shard_map/ppermute | solution.py:17
  127.4 29.4 %collective-permute-start.15 = (bf16[512,512]{1,0:T(8,128)(2,1)}, bf16[512,512]{1,0:T(8,128)(2,1)S(1)}, u32[]{:S(2)}, u32[]{:S(2)}) collective-permute-start(bf16[512,512]{1,0:T(8,128)(2,1)} %get-tuple-element.58), channel_id=1, source_target_pairs={{0,1},{1,0},{2,3},{3,2},{4,5},{5,4},{6,7},{7,6}} | collective-permute-start | bytes 1572872 | tf_op jit(solution)/shard_map/ppermute | solution.py:17
  207.5 34.5 %collective-permute-start.28 = (bf16[2560,256]{1,0:T(8,128)(2,1)}, bf16[2560,256]{1,0:T(8,128)(2,1)S(1)}, u32[]{:S(2)}, u32[]{:S(2)}) collective-permute-start(bf16[2560,256]{1,0:T(8,128)(2,1)} %pad_maximum_fusion.6), channel_id=1, source_target_pairs={{0,1},{1,0},{2,3},{3,2},{4,5},{5,4},{6,7},{7,6}} | collective-permute-start | bytes 3932168 | tf_op jit(solution)/shard_map/ppermute | solution.py:17
  207.8 36.9 %collective-permute-start.24 = (bf16[2048,512]{1,0:T(8,128)(2,1)}, bf16[2048,512]{1,0:T(8,128)(2,1)}, u32[]{:S(2)}, u32[]{:S(2)}) collective-permute-start(bf16[2048,512]{1,0:T(8,128)(2,1)} %glu.4.refs_0_), channel_id=1, source_target_pairs={{0,1},{1,0},{2,3},{3,2},{4,5},{5,4},{6,7},{7,6}} | collective-permute-start | bytes 6291464 | tf_op jit(solution)/shard_map/ppermute | solution.py:17
  208.0 27.0 %collective-permute-start.21 = (bf16[512,512]{1,0:T(8,128)(2,1)}, bf16[512,512]{1,0:T(8,128)(2,1)}, u32[]{:S(2)}, u32[]{:S(2)}) collective-permute-start(bf16[512,512]{1,0:T(8,128)(2,1)} %get-tuple-element.30), channel_id=1, source_target_pairs={{0,1},{1,0},{2,3},{3,2},{4,5},{5,4},{6,7},{7,6}} | collective-permute-start | bytes 1572872 | tf_op jit(solution)/shard_map/ppermute | solution.py:17
  208.4 28.6 %collective-permute-start.23 = (bf16[2,512,512]{2,1,0:T(8,128)(2,1)S(1)}, bf16[2,512,512]{2,1,0:T(8,128)(2,1)S(1)}, u32[]{:S(2)}, u32[]{:S(2)}) collective-permute-start(bf16[2,512,512]{2,1,0:T(8,128)(2,1)S(1)} %pad_maximum_fusion.8), channel_id=1, source_target_pairs={{0,2},{2,0},{1,3},{3,1},{4,6},{6,4},{5,7},{7,5}} | collective-permute-start | bytes 3145736 | tf_op jit(solution)/shard_map/ppermute | solution.py:17
  221.7 25.6 %collective-permute-start.25 = (bf16[2048,512]{1,0:T(8,128)(2,1)}, bf16[2048,512]{1,0:T(8,128)(2,1)}, u32[]{:S(2)}, u32[]{:S(2)}) collective-permute-start(bf16[2048,512]{1,0:T(8,128)(2,1)} %glu.5.refs_1_), channel_id=1, source_target_pairs={{0,1},{1,0},{2,3},{3,2},{4,5},{5,4},{6,7},{7,6}} | collective-permute-start | bytes 6291464 | tf_op jit(solution)/shard_map/ppermute | solution.py:17
  242.0 48.1 %collective-permute-start.10 = (bf16[2,1024,512]{2,1,0:T(8,128)(2,1)}, bf16[2,1024,512]{2,1,0:T(8,128)(2,1)}, u32[]{:S(2)}, u32[]{:S(2)}) collective-permute-start(bf16[2,1024,512]{2,1,0:T(8,128)(2,1)} %pad_maximum_fusion.near_w), channel_id=1, source_target_pairs={{0,4},{4,0},{1,5},{5,1},{2,6},{6,2},{3,7},{7,3}} | collective-permute-start | bytes 6291464 | tf_op jit(solution)/shard_map/ppermute | solution.py:17
  303.2 31.5 %collective-permute-start.34 = (bf16[2560,256]{1,0:T(8,128)(2,1)}, bf16[2560,256]{1,0:T(8,128)(2,1)}, u32[]{:S(2)}, u32[]{:S(2)}) collective-permute-start(bf16[2560,256]{1,0:T(8,128)(2,1)} %pad_maximum_fusion.6), channel_id=1, source_target_pairs={{0,4},{4,0},{1,5},{5,1},{2,6},{6,2},{3,7},{7,3}} | collective-permute-start | bytes 3932168 | tf_op jit(solution)/shard_map/ppermute | solution.py:17
  334.7 69.6 %collective-permute-start.31 = (f32[1536,256]{1,0:T(8,128)}, f32[1536,256]{1,0:T(8,128)}, u32[]{:S(2)}, u32[]{:S(2)}) collective-permute-start(f32[1536,256]{1,0:T(8,128)} %mix.14), channel_id=1, source_target_pairs={{0,2},{2,0},{1,3},{3,1},{4,6},{6,4},{5,7},{7,5}} | collective-permute-start | bytes 4718600 | tf_op jit(solution)/shard_map/ppermute | solution.py:17
  336.5 73.7 %collective-permute-start.39 = (bf16[2560,256]{1,0:T(8,128)(2,1)}, bf16[2560,256]{1,0:T(8,128)(2,1)}, u32[]{:S(2)}, u32[]{:S(2)}) collective-permute-start(bf16[2560,256]{1,0:T(8,128)(2,1)} %pad_maximum_fusion.7), channel_id=1, source_target_pairs={{0,4},{4,0},{1,5},{5,1},{2,6},{6,2},{3,7},{7,3}} | collective-permute-start | bytes 3932168 | tf_op jit(solution)/shard_map/ppermute | solution.py:17
  339.1 43.3 %collective-permute-start.33 = (bf16[2560,128]{1,0:T(8,128)(2,1)}, bf16[2560,128]{1,0:T(8,128)(2,1)S(1)}, u32[]{:S(2)}, u32[]{:S(2)}) collective-permute-start(bf16[2560,128]{1,0:T(8,128)(2,1)} %get-tuple-element.62), channel_id=1, source_target_pairs={{0,4},{4,0},{1,5},{5,1},{2,6},{6,2},{3,7},{7,3}} | collective-permute-start | bytes 1966088 | tf_op jit(solution)/shard_map/ppermute | solution.py:17
  339.5 56.2 %collective-permute-start.32 = (bf16[2560,128]{1,0:T(8,128)(2,1)S(1)}, bf16[2560,128]{1,0:T(8,128)(2,1)S(1)}, u32[]{:S(2)}, u32[]{:S(2)}) collective-permute-start(bf16[2560,128]{1,0:T(8,128)(2,1)S(1)} %get-tuple-element.63), channel_id=1, source_target_pairs={{0,4},{4,0},{1,5},{5,1},{2,6},{6,2},{3,7},{7,3}} | collective-permute-start | bytes 1966088 | tf_op jit(solution)/shard_map/ppermute | solution.py:17
  410.3 26.4 %collective-permute-start.41 = (f32[2048,128]{1,0:T(8,128)}, f32[2048,128]{1,0:T(8,128)}, u32[]{:S(2)}, u32[]{:S(2)}) collective-permute-start(f32[2048,128]{1,0:T(8,128)} %mix.17), channel_id=1, source_target_pairs={{0,2},{2,0},{1,3},{3,1},{4,6},{6,4},{5,7},{7,5}} | collective-permute-start | bytes 3145736 | tf_op jit(solution)/shard_map/ppermute | solution.py:17
  411.8 17.8 %collective-permute-start.38 = (bf16[2560,128]{1,0:T(8,128)(2,1)}, bf16[2560,128]{1,0:T(8,128)(2,1)S(1)}, u32[]{:S(2)}, u32[]{:S(2)}) collective-permute-start(bf16[2560,128]{1,0:T(8,128)(2,1)} %get-tuple-element.60), channel_id=1, source_target_pairs={{0,4},{4,0},{1,5},{5,1},{2,6},{6,2},{3,7},{7,3}} | collective-permute-start | bytes 1966088 | tf_op jit(solution)/shard_map/ppermute | solution.py:17
  413.5 45.5 %collective-permute-start.42 = (f32[2048,128]{1,0:T(8,128)}, f32[2048,128]{1,0:T(8,128)S(1)}, u32[]{:S(2)}, u32[]{:S(2)}) collective-permute-start(f32[2048,128]{1,0:T(8,128)} %mix.18), channel_id=1, source_target_pairs={{0,2},{2,0},{1,3},{3,1},{4,6},{6,4},{5,7},{7,5}} | collective-permute-start | bytes 3145736 | tf_op jit(solution)/shard_map/ppermute | solution.py:17
  415.2 32.7 %collective-permute-start.37 = (bf16[2560,128]{1,0:T(8,128)(2,1)}, bf16[2560,128]{1,0:T(8,128)(2,1)}, u32[]{:S(2)}, u32[]{:S(2)}) collective-permute-start(bf16[2560,128]{1,0:T(8,128)(2,1)} %get-tuple-element.61), channel_id=1, source_target_pairs={{0,4},{4,0},{1,5},{5,1},{2,6},{6,2},{3,7},{7,3}} | collective-permute-start | bytes 1966088 | tf_op jit(solution)/shard_map/ppermute | solution.py:17
  415.6 54.3 %collective-permute-start.36 = (f32[512,256]{1,0:T(8,128)}, f32[512,256]{1,0:T(8,128)}, u32[]{:S(2)}, u32[]{:S(2)}) collective-permute-start(f32[512,256]{1,0:T(8,128)} %mix.15), channel_id=1, source_target_pairs={{0,2},{2,0},{1,3},{3,1},{4,6},{6,4},{5,7},{7,5}} | collective-permute-start | bytes 1572872 | tf_op jit(solution)/shard_map/ppermute | solution.py:17
  444.7 30.5 %collective-permute-start.43 = (bf16[2048,128]{1,0:T(8,128)(2,1)}, bf16[2048,128]{1,0:T(8,128)(2,1)S(1)}, u32[]{:S(2)}, u32[]{:S(2)}) collective-permute-start(bf16[2048,128]{1,0:T(8,128)(2,1)} %mix.21), channel_id=1, source_target_pairs={{0,4},{4,0},{1,5},{5,1},{2,6},{6,2},{3,7},{7,3}} | collective-permute-start | bytes 1572872 | tf_op jit(solution)/shard_map/ppermute | solution.py:17
  (46 other events, 333.3 us)

commit v7 on v6

--- a/solution.py
+++ b/solution.py
@@ -90,26 +90,32 @@
         for h in range(hpg):
             qs[g * hpg * new + h * new : g * hpg * new + (h + 1) * new, :] = rope(q_refs[g][:, h * dim : (h + 1) * dim], cos_t, sin_t)
 
-    def attend(keys):
+    fold = dim ** -0.5 * 1.4426950408889634
+
+    def attend(keys, edge):
         @pl.loop(0, 4)
         def _(g):
             group = pl.ds(pl.multiple_of(g * hpg * new, hpg * new), hpg * new)
             q = qs[group, :]
-            s = lax.dot_general(q, kn_ref[0, :keys, :], (((1,), (1,)), ((), ())), preferred_element_type=F32)
-            s = s * (dim ** -0.5)
-            tok = lax.broadcasted_iota(jnp.int32, (hpg * new, keys), 0) % new
-            pos = lax.broadcasted_iota(jnp.int32, (hpg * new, keys), 1)
-            s = jnp.where(pos - tok <= length, s, -1e30)
-            e = jnp.exp(s - jnp.max(s, axis=-1, keepdims=True))
-            p = (e * (1.0 / jnp.sum(e, axis=-1, keepdims=True))).astype(BF16)
-            qs[group, :] = jnp.dot(p, vn_ref[0, :keys, :], preferred_element_type=F32).astype(BF16)
+            nt = (((1,), (1,)), ((), ()))
+            sure = lax.dot_general(q, kn_ref[0, :edge, :], nt, preferred_element_type=F32) * fold
+            rest = lax.dot_general(q, kn_ref[0, edge:keys, :], nt, preferred_element_type=F32) * fold
+            tok = lax.broadcasted_iota(jnp.int32, rest.shape, 0) % new
+            pos = lax.broadcasted_iota(jnp.int32, rest.shape, 1)
+            rest = jnp.where(pos - tok <= length - edge, rest, -1e30)
+            top = jnp.maximum(jnp.max(sure, axis=-1, keepdims=True), jnp.max(rest, axis=-1, keepdims=True))
+            sure, rest = jnp.exp2(sure - top), jnp.exp2(rest - top)
+            scale = 1.0 / (jnp.sum(sure, axis=-1, keepdims=True) + jnp.sum(rest, axis=-1, keepdims=True))
+            o = jnp.dot((sure * scale).astype(BF16), vn_ref[0, :edge, :], preferred_element_type=F32)
+            o = o + jnp.dot((rest * scale).astype(BF16), vn_ref[0, edge:keys, :], preferred_element_type=F32)
+            qs[group, :] = o.astype(BF16)
 
     step = 256
     need = (length + new + step - 1) // step
     sizes = list(range(5, cache // step + 1))
     for n in sizes:
         cond = need <= n if n == sizes[0] else need == n
-        pl.when(cond)(functools.partial(attend, n * step))
+        pl.when(cond)(functools.partial(attend, n * step, (n - 1) * step - 128))
     for g in range(4):
         for h in range(hpg):
             o_refs[g][:, h * dim : (h + 1) * dim] = qs[(g * hpg + h) * new : (g * hpg + h + 1) * new, :]
@@ -258,6 +264,14 @@
             for xr in range(2):
                 for yr in range(2):
                     offs.append(width * (4 * yr + 2 * (xr ^ xi) + (cr ^ ci)))
+        half_dim = dim // 2
+        inv_freq = ROPE_BASE ** (-2.0 * jnp.arange(half_dim, dtype=F32) / dim)
+        positions = (lengths[:, None] + jnp.arange(new, dtype=jnp.int32)[None, :]).reshape(own_tok)
+        angles = positions.astype(F32)[:, None] * inv_freq
+        cos_t, sin_t = jnp.cos(angles), jnp.sin(angles)
+        cos_t = jnp.concatenate([cos_t, cos_t], -1)
+        sin_t = jnp.concatenate([-sin_t, sin_t], -1)
+        g = tie(g, cos_t, sin_t)
         h = layer_norm(near + far, g, jnp.stack(offs).astype(jnp.int32))
 
         kv_rows = w_key.shape[0] // 4
@@ -284,13 +298,6 @@
         q_x = [pick(q4, xi), q_back]
         q_c = [pick(v, ci) for v in q_x] + [swap_c(pick(v, 1 - ci)) for v in q_x]
 
-        half_dim = dim // 2
-        inv_freq = ROPE_BASE ** (-2.0 * jnp.arange(half_dim, dtype=F32) / dim)
-        positions = (lengths[:, None] + jnp.arange(new, dtype=jnp.int32)[None, :]).reshape(own_tok)
-        angles = positions.astype(F32)[:, None] * inv_freq
-        cos_t, sin_t = jnp.cos(angles), jnp.sin(angles)
-        cos_t = jnp.concatenate([cos_t, cos_t], -1)
-        sin_t = jnp.concatenate([-sin_t, sin_t], -1)
         o0, o1, o2, o3, k_next, v_next = attention(lengths, q_c, kv, cos_t, sin_t, k_cache, v_cache)
 
         keep = [o0, swap_c(o2)]

time: 483 us -> 483 us (level)
  waiting for transfers between devices: 180 us -> 187 us
  starting transfers between devices: 34.6 us -> 28.1 us
    ppermute x45, waiting for transfers between devices: 180 us -> 187 us  [swap(): return lambda a: lax.ppermute(a, axis, pairs)]
    ppermute x45, starting transfers between devices: 34.6 us -> 28.1 us  [swap(): return lambda a: lax.ppermute(a, axis, pairs)]
    unnamed x67 -> x69, local copies, waits for them, and re-layouts: 11.6 us -> 12.8 us
  transfers between devices with their start and end apart: 45 -> 45, of which waited for: 16 -> 16; matrix products, arithmetic and copies ran while one was open for 9% -> 9% of each run, Pallas kernels for 41% -> 40%
where the time goes in v7:
time: 483 us; the launch traced here: 481 us
  Pallas kernels  207 us (43%)
  waiting for transfers between devices  187 us (39%)
  local copies, waits for them, and re-layouts  32.7 us (7%)
  starting transfers between devices  28.1 us (6%)
  other arithmetic  22.1 us (5%)
    ppermute x45, waiting for transfers between devices, swap(): return lambda a: lax.ppermute(a, axis, pairs)  187 us
    pallas_call x12, Pallas kernels, mix(): pl.pallas_call(functools.partial(mix_kernel, plan, len(lhs), len(ws)), gr...  88.4 us
    pallas_call x4, Pallas kernels, glu(): pl.pallas_call(glu_kernel, grid=(tokens // blk,), in_specs=[pl.BlockSpec(...  52.7 us
    pallas_call x1, Pallas kernels, attention(): pl.pallas_call(attn_kernel, grid_spec=pltpu.PrefetchScalarGridSpec(num_sc...  44.5 us
    ppermute x45, starting transfers between devices, swap(): return lambda a: lax.ppermute(a, axis, pairs)  28.1 us
    pallas_call x1, Pallas kernels, layer_norm(): pl.pallas_call(norm_kernel, grid_spec=pltpu.PrefetchScalarGridSpec(num_sc...  13 us
    unnamed x69, local copies, waits for them, and re-layouts  12.8 us
  transfers between devices with their start and end apart: 45, of which 16 were waited for; matrix products, arithmetic and copies ran while one was open for 9% of the time, Pallas kernels for 40%

profile of v7, /device:TPU:0, one launch (start us, length us, event | category | flops | bytes accessed | tf_op | source)
XLA Modules:
  0.0 481.5 jit_solution(788852433512340436)
XLA Ops:
  8.7 21.4 %collective-permute-done.refs_1_.refs_6_ = bf16[2048,256]{1,0:T(8,128)(2,1)} collective-permute-done((bf16[2048,256]{1,0:T(8,128)(2,1)}, bf16[2048,256]{1,0:T(8,128)(2,1)}, u32[]{:S(2)}, u32[]{:S(2)}) %collective-permute-start) | collective-permute-done | bytes 1048608 | tf_op jit(solution)/shard_map/ppermute | solution.py:17
  31.8 5.5 %slice_bitcast_fusion = (bf16[1,1024,512]{2,1,0:T(8,128)(2,1)S(1)}, bf16[1,1024,512]{2,1,0:T(8,128)(2,1)S(1)}, bf16[1,1024,512]{2,1,0:T(8,128)(2,1)}, bf16[1,102...) fusion(bf16[1024,2048]{1,0:T(8,128)(2,1)} %param.21, ...), kind=kLoop, calls=%fused_computation.27 | loop fusion | bytes 16777216 | tf_op jit(solution)/shard_map/stack | solution.py:294
  42.4 12.3 %collective-permute-done.8 = f32[2,256]{1,0:T(2,128)S(1)} collective-permute-done((f32[2,256]{1,0:T(2,128)S(1)}, f32[2,256]{1,0:T(2,128)S(1)}, u32[]{:S(2)}, u32[]{:S(2)}) %collective-permute-start.8) | collective-permute-done | bytes 2080 | tf_op jit(solution)/shard_map/ppermute | solution.py:17
  57.4 30.6 %collective-permute-done.17 = bf16[256,256]{1,0:T(8,128)(2,1)S(1)} collective-permute-done((bf16[256,256]{1,0:T(8,128)(2,1)S(1)}, bf16[256,256]{1,0:T(8,128)(2,1)S(1)}, u32[]{:S(2)}, u32[]{:S(2)}) %collective-permute-start.17) | collective-permute-done | bytes 131104 | tf_op jit(solution)/shard_map/ppermute | solution.py:17
  96.1 13.0 %norm.1.h_ref = bf16[2048,2048]{1,0:T(8,128)(2,1)} custom-call(s32[8]{0:T(128)} %stack.140.offs_ref, bf16[2048,256]{1,0:T(8,128)(2,1)} %copy-done.6, bf16[2048,256]{1,0:T(8,128)(2,1)} %collective-permute-done.refs_1_.refs_6_, bf16[2048,256]{1,0:T(8,128)(2,1)} %collective-permute-done.1.refs_2_, bf16[2048,256]{1,0:T(8,128)(2,1)} %collective-permute-done.2.refs_3_, ...), custom_call_target="tpu_custom_call" | custom-call | flops 83886080 | bytes 16777216 | tf_op jit(solution)/shard_map/norm/pallas_call | solution.py:47
  109.1 5.8 %collective-permute-done.13.refs_1_ = bf16[1024,512]{1,0:T(8,128)(2,1)} collective-permute-done((bf16[1024,512]{1,0:T(8,128)(2,1)}, bf16[1024,512]{1,0:T(8,128)(2,1)}, u32[]{:S(2)}, u32[]{:S(2)}) %collective-permute-start.13) | collective-permute-done | bytes 1048608 | tf_op jit(solution)/shard_map/ppermute | solution.py:17
  114.9 8.7 %project.1 = bf16[2048,512]{1,0:T(8,128)(2,1)} custom-call(bf16[2048,2048]{1,0:T(8,128)(2,1)} %norm.1.h_ref, bf16[1024,512]{1,0:T(8,128)(2,1)} %refs_0_.1, bf16[1024,512]{1,0:T(8,128)(2,1)} %collective-permute-done.13.refs_1_), custom_call_target="tpu_custom_call" | custom-call | flops 4294967296 | bytes 10485760 | tf_op jit(solution)/shard_map/project/pallas_call | solution.py:185
  127.9 13.2 %glu.4.refs_0_ = bf16[2048,512]{1,0:T(8,128)(2,1)} custom-call(bf16[2048,2048]{1,0:T(8,128)(2,1)} %norm.1.h_ref, bf16[2,1024,512]{2,1,0:T(8,128)(2,1)} %pad_maximum_fusion.1.near_w, bf16[2,1024,512]{2,1,0:T(8,128)(2,1)} %collective-permute-done.11.far_w), custom_call_target="tpu_custom_call" | custom-call | flops 8589934592 | bytes 14680064 | tf_op jit(solution)/shard_map/glu/pallas_call | solution.py:161
  141.1 7.4 %collective-permute-done.14 = bf16[2,512,512]{2,1,0:T(8,128)(2,1)} collective-permute-done((bf16[2,512,512]{2,1,0:T(8,128)(2,1)S(1)}, bf16[2,512,512]{2,1,0:T(8,128)(2,1)}, u32[]{:S(2)}, u32[]{:S(2)}) %collective-permute-start.14) | collective-permute-done | bytes 1048608 | tf_op jit(solution)/shard_map/ppermute | solution.py:17
  158.7 44.5 %attn.1 = (bf16[512,512]{1,0:T(8,128)(2,1)}, bf16[512,512]{1,0:T(8,128)(2,1)}, bf16[512,512]{1,0:T(8,128)(2,1)}, bf16[512,512]{1,0:T(8,128)(2,1)}, bf16[8,2048,1...) custom-call(s32[8]{0:T(128)} %len_ref.1, bf16[512,512]{1,0:T(8,128)(2,1)} %get-tuple-element.61.q0, ...), custom_call_target="tpu_custom_call" | custom-call | flops 17179869184 | bytes 16777216 | tf_op jit(solution)/shard_map/attn/pallas_call | solution.py:131
  207.9 13.2 %glu.5.refs_1_ = bf16[2048,512]{1,0:T(8,128)(2,1)} custom-call(bf16[2048,2048]{1,0:T(8,128)(2,1)} %norm.1.h_ref, bf16[2,1024,512]{2,1,0:T(8,128)(2,1)} %pad_maximum_fusion.2.near_w, bf16[2,1024,512]{2,1,0:T(8,128)(2,1)} %collective-permute-done.12.far_w), custom_call_target="tpu_custom_call" | custom-call | flops 8589934592 | bytes 14680064 | tf_op jit(solution)/shard_map/glu/pallas_call | solution.py:161
  221.1 13.2 %glu.6.refs_2_ = bf16[2048,512]{1,0:T(8,128)(2,1)} custom-call(bf16[2048,2048]{1,0:T(8,128)(2,1)} %norm.1.h_ref, bf16[2,1024,512]{2,1,0:T(8,128)(2,1)} %pad_maximum_fusion.3.near_w, bf16[2,1024,512]{2,1,0:T(8,128)(2,1)} %collective-permute-done.20.far_w), custom_call_target="tpu_custom_call" | custom-call | flops 8589934592 | bytes 14680064 | tf_op jit(solution)/shard_map/glu/pallas_call | solution.py:161
  237.2 3.8 pad_maximum_fusion.near_w
  246.0 10.8 %mix.12.refs_4_ = f32[2048,256]{1,0:T(8,128)} custom-call(bf16[2048,512]{1,0:T(8,128)(2,1)} %glu.4.refs_0_, bf16[2048,512]{1,0:T(8,128)(2,1)} %glu.5.refs_1_, bf16[2048,512]{1,0:T(8,128)(2,1)} %glu.6.refs_2_, bf16[2048,512]{1,0:T(8,128)(2,1)} %bitcast.66, bf16[2048,512]{1,0:T(8,128)(2,1)} %collective-permute-done.24.refs_4_.refs_0_, ...), custom_call_target="tpu_custom_call" | custom-call | flops 4294967296 | bytes 18874368 | tf_op jit(solution)/shard_map/mix/pallas_call | solution.py:222
  257.9 11.1 %mix.13.refs_4_ = f32[2048,256]{1,0:T(8,128)} custom-call(bf16[2048,512]{1,0:T(8,128)(2,1)} %glu.4.refs_0_, bf16[2048,512]{1,0:T(8,128)(2,1)} %glu.5.refs_1_, bf16[2048,512]{1,0:T(8,128)(2,1)} %glu.6.refs_2_, bf16[2048,512]{1,0:T(8,128)(2,1)} %bitcast.67, bf16[2048,512]{1,0:T(8,128)(2,1)} %collective-permute-done.24.refs_4_.refs_0_, ...), custom_call_target="tpu_custom_call" | custom-call | flops 4294967296 | bytes 18874368 | tf_op jit(solution)/shard_map/mix/pallas_call | solution.py:222
  269.0 20.3 %collective-permute-done.10.far_w = bf16[2,1024,512]{2,1,0:T(8,128)(2,1)} collective-permute-done((bf16[2,1024,512]{2,1,0:T(8,128)(2,1)}, bf16[2,1024,512]{2,1,0:T(8,128)(2,1)}, u32[]{:S(2)}, u32[]{:S(2)}) %collective-permute-start.10) | collective-permute-done | bytes 2097184 | tf_op jit(solution)/shard_map/ppermute | solution.py:17
  289.3 13.2 %glu.7.refs_0_.refs_3_ = bf16[2048,512]{1,0:T(8,128)(2,1)} custom-call(bf16[2048,2048]{1,0:T(8,128)(2,1)} %norm.1.h_ref, bf16[2,1024,512]{2,1,0:T(8,128)(2,1)} %pad_maximum_fusion.near_w, bf16[2,1024,512]{2,1,0:T(8,128)(2,1)} %collective-permute-done.10.far_w), custom_call_target="tpu_custom_call" | custom-call | flops 8589934592 | bytes 14680064 | tf_op jit(solution)/shard_map/glu/pallas_call | solution.py:161
  311.6 5.9 %mix.14 = f32[1536,256]{1,0:T(8,128)} custom-call(bf16[2048,512]{1,0:T(8,128)(2,1)} %glu.7.refs_0_.refs_3_, bf16[2048,512]{1,0:T(8,128)(2,1)} %copy-done.3, bf16[2560,256]{1,0:T(8,128)(2,1)} %pad_maximum_fusion.5.refs_8_.refs_2_, bf16[2560,256]{1,0:T(8,128)(2,1)} %copy-done.5, f32[2048,256]{1,0:T(8,128)} %mix.12.refs_4_), custom_call_target="tpu_custom_call" | custom-call | flops 805306368 | bytes 3670016 | tf_op jit(solution)/shard_map/mix/pallas_call | solution.py:222
  317.5 16.5 %collective-permute-done.34 = bf16[2560,256]{1,0:T(8,128)(2,1)} collective-permute-done((bf16[2560,256]{1,0:T(8,128)(2,1)}, bf16[2560,256]{1,0:T(8,128)(2,1)}, u32[]{:S(2)}, u32[]{:S(2)}) %collective-permute-start.34) | collective-permute-done | bytes 1310752 | tf_op jit(solution)/shard_map/ppermute | solution.py:17
  340.3 7.9 %mix.16.refs_6_ = f32[2048,256]{1,0:T(8,128)} custom-call(bf16[2048,512]{1,0:T(8,128)(2,1)} %collective-permute-done.24.refs_4_.refs_0_, bf16[2048,512]{1,0:T(8,128)(2,1)} %collective-permute-done.25.refs_5_.refs_1_, bf16[2048,512]{1,0:T(8,128)(2,1)} %collective-permute-done.26.refs_6_.refs_2_, bf16[2048,512]{1,0:T(8,128)(2,1)} %copy-done.3, ...), custom_call_target="tpu_custom_call" | custom-call | flops 2684354560 | bytes 11796480 | tf_op jit(solution)/shard_map/mix/pallas_call | solution.py:222
  348.3 33.6 %collective-permute-done.33.refs_5_ = bf16[2560,128]{1,0:T(8,128)(2,1)S(1)} collective-permute-done((bf16[2560,128]{1,0:T(8,128)(2,1)}, bf16[2560,128]{1,0:T(8,128)(2,1)S(1)}, u32[]{:S(2)}, u32[]{:S(2)}) %collective-permute-start.33) | collective-permute-done | bytes 655392 | tf_op jit(solution)/shard_map/ppermute | solution.py:17
  382.7 7.7 %mix.17 = f32[2048,128]{1,0:T(8,128)} custom-call(bf16[2048,512]{1,0:T(8,128)(2,1)} %glu.4.refs_0_, bf16[2048,512]{1,0:T(8,128)(2,1)} %glu.5.refs_1_, bf16[2048,512]{1,0:T(8,128)(2,1)} %glu.6.refs_2_, bf16[2048,512]{1,0:T(8,128)(2,1)} %glu.7.refs_0_.refs_3_, bf16[2048,512]{1,0:T(8,128)(2,1)} %bitcast.68, bf16[2560,128]{1,0:T(8,128)(2,1)} %copy-done.26, ...), custom_call_target="tpu_custom_call" | custom-call | flops 1342177280 | bytes 11141120 | tf_op jit(solution)/shard_map/mix/pallas_call | solution.py:222
  390.4 4.8 collective-permute-done.32.refs_5_
  396.0 7.7 %mix.18 = f32[2048,128]{1,0:T(8,128)} custom-call(bf16[2048,512]{1,0:T(8,128)(2,1)} %glu.4.refs_0_, bf16[2048,512]{1,0:T(8,128)(2,1)} %glu.5.refs_1_, bf16[2048,512]{1,0:T(8,128)(2,1)} %glu.6.refs_2_, bf16[2048,512]{1,0:T(8,128)(2,1)} %glu.7.refs_0_.refs_3_, bf16[2048,512]{1,0:T(8,128)(2,1)} %bitcast.69, bf16[2560,128]{1,0:T(8,128)(2,1)} %copy-done.25, ...), custom_call_target="tpu_custom_call" | custom-call | flops 1342177280 | bytes 11141120 | tf_op jit(solution)/shard_map/mix/pallas_call | solution.py:222
  403.7 5.9 %mix.19 = bf16[1536,256]{1,0:T(8,128)(2,1)} custom-call(bf16[2048,512]{1,0:T(8,128)(2,1)} %glu.7.refs_0_.refs_3_, bf16[2048,512]{1,0:T(8,128)(2,1)} %copy-done.3, bf16[2560,256]{1,0:T(8,128)(2,1)} %pad_maximum_fusion.4.refs_8_.refs_2_, bf16[2560,256]{1,0:T(8,128)(2,1)} %copy-done.4, f32[2048,256]{1,0:T(8,128)} %mix.13.refs_4_, ...), custom_call_target="tpu_custom_call" | custom-call | flops 805306368 | bytes 3670016 | tf_op jit(solution)/shard_map/mix/pallas_call | solution.py:222
  416.1 8.3 %mix.20.refs_6_ = f32[2048,256]{1,0:T(8,128)} custom-call(bf16[2048,512]{1,0:T(8,128)(2,1)} %collective-permute-done.24.refs_4_.refs_0_, bf16[2048,512]{1,0:T(8,128)(2,1)} %collective-permute-done.25.refs_5_.refs_1_, bf16[2048,512]{1,0:T(8,128)(2,1)} %collective-permute-done.26.refs_6_.refs_2_, bf16[2048,512]{1,0:T(8,128)(2,1)} %copy-done.3, ...), custom_call_target="tpu_custom_call" | custom-call | flops 2684354560 | bytes 11796480 | tf_op jit(solution)/shard_map/mix/pallas_call | solution.py:222
  424.4 4.6 collective-permute-done.38.refs_5_
  429.1 7.0 %collective-permute-done.41.refs_7_ = f32[2048,128]{1,0:T(8,128)} collective-permute-done((f32[2048,128]{1,0:T(8,128)}, f32[2048,128]{1,0:T(8,128)}, u32[]{:S(2)}, u32[]{:S(2)}) %collective-permute-start.41) | collective-permute-done | bytes 1048608 | tf_op jit(solution)/shard_map/ppermute | solution.py:17
  436.1 8.0 %mix.21 = bf16[2048,128]{1,0:T(8,128)(2,1)} custom-call(bf16[2048,512]{1,0:T(8,128)(2,1)} %glu.4.refs_0_, bf16[2048,512]{1,0:T(8,128)(2,1)} %glu.5.refs_1_, bf16[2048,512]{1,0:T(8,128)(2,1)} %glu.6.refs_2_, bf16[2048,512]{1,0:T(8,128)(2,1)} %glu.7.refs_0_.refs_3_, bf16[2048,512]{1,0:T(8,128)(2,1)} %bitcast.70, bf16[2560,128]{1,0:T(8,128)(2,1)} %copy-done.27, ...), custom_call_target="tpu_custom_call" | custom-call | flops 1342177280 | bytes 11141120 | tf_op jit(solution)/shard_map/mix/pallas_call | solution.py:222
  446.6 11.8 %collective-permute-done.42.refs_7_ = f32[2048,128]{1,0:T(8,128)S(1)} collective-permute-done((f32[2048,128]{1,0:T(8,128)}, f32[2048,128]{1,0:T(8,128)S(1)}, u32[]{:S(2)}, u32[]{:S(2)}) %collective-permute-start.42) | collective-permute-done | bytes 1048608 | tf_op jit(solution)/shard_map/ppermute | solution.py:17
  459.4 8.0 %mix.22 = bf16[2048,128]{1,0:T(8,128)(2,1)} custom-call(bf16[2048,512]{1,0:T(8,128)(2,1)} %glu.4.refs_0_, bf16[2048,512]{1,0:T(8,128)(2,1)} %glu.5.refs_1_, bf16[2048,512]{1,0:T(8,128)(2,1)} %glu.6.refs_2_, bf16[2048,512]{1,0:T(8,128)(2,1)} %glu.7.refs_0_.refs_3_, bf16[2048,512]{1,0:T(8,128)(2,1)} %bitcast.71, ...), custom_call_target="tpu_custom_call" | custom-call | flops 1342177280 | bytes 11141120 | tf_op jit(solution)/shard_map/mix/pallas_call | solution.py:222
  475.4 5.2 %collective-permute-done.44 = bf16[2048,128]{1,0:T(8,128)(2,1)S(1)} collective-permute-done((bf16[2048,128]{1,0:T(8,128)(2,1)}, bf16[2048,128]{1,0:T(8,128)(2,1)S(1)}, u32[]{:S(2)}, u32[]{:S(2)}) %collective-permute-start.44) | collective-permute-done | bytes 524320 | tf_op jit(solution)/shard_map/ppermute | solution.py:17
  (191 shorter events, 89.4 us)
Async XLA Ops:
  3.3 26.8 %collective-permute-start = (bf16[2048,256]{1,0:T(8,128)(2,1)}, bf16[2048,256]{1,0:T(8,128)(2,1)}, u32[]{:S(2)}, u32[]{:S(2)}) collective-permute-start(bf16[2048,256]{1,0:T(8,128)(2,1)} %dynamic-slice_bitcast_fusion.2), channel_id=1, source_target_pairs={{0,4},{4,0},{1,5},{5,1},{2,6},{6,2},{3,7},{7,3}} | collective-permute-start | bytes 3145736 | tf_op jit(solution)/shard_map/ppermute | solution.py:17
  6.7 50.7 %collective-permute-start.1 = (bf16[2048,256]{1,0:T(8,128)(2,1)S(1)}, bf16[2048,256]{1,0:T(8,128)(2,1)}, u32[]{:S(2)}, u32[]{:S(2)}) collective-permute-start(bf16[2048,256]{1,0:T(8,128)(2,1)S(1)} %dynamic-slice_bitcast_fusion.1.refs_0_.refs_10_), channel_id=1, source_target_pairs={{0,2},{2,0},{1,3},{3,1},{4,6},{6,4},{5,7},{7,5}} | collective-permute-start | bytes 3145736 | tf_op jit(solution)/shard_map/ppermute | solution.py:17
  8.2 80.4 %collective-permute-start.3 = (bf16[2048,256]{1,0:T(8,128)(2,1)S(1)}, bf16[2048,256]{1,0:T(8,128)(2,1)}, u32[]{:S(2)}, u32[]{:S(2)}) collective-permute-start(bf16[2048,256]{1,0:T(8,128)(2,1)S(1)} %dynamic-slice_bitcast_fusion.1.refs_0_.refs_10_), channel_id=1, source_target_pairs={{0,1},{1,0},{2,3},{3,2},{4,5},{5,4},{6,7},{7,6}} | collective-permute-start | bytes 3145736 | tf_op jit(solution)/shard_map/ppermute | solution.py:17
  8.2 32.9 %collective-permute-start.7 = (f32[1,256]{1,0:T(1,128)S(1)}, f32[1,256]{1,0:T(1,128)S(1)}, u32[]{:S(2)}, u32[]{:S(2)}) collective-permute-start(f32[1,256]{1,0:T(1,128)S(1)} %bitcast.83), channel_id=1, source_target_pairs={{0,4},{4,0},{1,5},{5,1},{2,6},{6,2},{3,7},{7,3}} | collective-permute-start | bytes 3080 | tf_op jit(solution)/shard_map/ppermute | solution.py:17
  30.1 58.0 %collective-permute-start.2 = (bf16[2048,256]{1,0:T(8,128)(2,1)}, bf16[2048,256]{1,0:T(8,128)(2,1)}, u32[]{:S(2)}, u32[]{:S(2)}) collective-permute-start(bf16[2048,256]{1,0:T(8,128)(2,1)} %collective-permute-done.refs_1_.refs_6_), channel_id=1, source_target_pairs={{0,2},{2,0},{1,3},{3,1},{4,6},{6,4},{5,7},{7,5}} | collective-permute-start | bytes 3145736 | tf_op jit(solution)/shard_map/ppermute | solution.py:17
  38.8 89.1 %collective-permute-start.11 = (bf16[2,1024,512]{2,1,0:T(8,128)(2,1)}, bf16[2,1024,512]{2,1,0:T(8,128)(2,1)}, u32[]{:S(2)}, u32[]{:S(2)}) collective-permute-start(bf16[2,1024,512]{2,1,0:T(8,128)(2,1)} %pad_maximum_fusion.1.near_w), channel_id=1, source_target_pairs={{0,4},{4,0},{1,5},{5,1},{2,6},{6,2},{3,7},{7,3}} | collective-permute-start | bytes 6291464 | tf_op jit(solution)/shard_map/ppermute | solution.py:17
  55.9 32.1 %collective-permute-start.17 = (bf16[256,256]{1,0:T(8,128)(2,1)S(1)}, bf16[256,256]{1,0:T(8,128)(2,1)S(1)}, u32[]{:S(2)}, u32[]{:S(2)}) collective-permute-start(bf16[256,256]{1,0:T(8,128)(2,1)S(1)} %constant_dynamic-slice_fusion.8), channel_id=1, source_target_pairs={{0,4},{4,0},{1,5},{5,1},{2,6},{6,2},{3,7},{7,3}} | collective-permute-start | bytes 393224 | tf_op jit(solution)/shard_map/ppermute | solution.py:17
  57.4 37.6 %collective-permute-start.5 = (bf16[2048,256]{1,0:T(8,128)(2,1)}, bf16[2048,256]{1,0:T(8,128)(2,1)}, u32[]{:S(2)}, u32[]{:S(2)}) collective-permute-start(bf16[2048,256]{1,0:T(8,128)(2,1)} %collective-permute-done.1.refs_2_), channel_id=1, source_target_pairs={{0,1},{1,0},{2,3},{3,2},{4,5},{5,4},{6,7},{7,6}} | collective-permute-start | bytes 3145736 | tf_op jit(solution)/shard_map/ppermute | solution.py:17
  88.6 26.3 %collective-permute-start.13 = (bf16[1024,512]{1,0:T(8,128)(2,1)}, bf16[1024,512]{1,0:T(8,128)(2,1)}, u32[]{:S(2)}, u32[]{:S(2)}) collective-permute-start(bf16[1024,512]{1,0:T(8,128)(2,1)} %refs_0_.1), channel_id=1, source_target_pairs={{0,4},{4,0},{1,5},{5,1},{2,6},{6,2},{3,7},{7,3}} | collective-permute-start | bytes 3145736 | tf_op jit(solution)/shard_map/ppermute | solution.py:17
  95.0 112.3 %collective-permute-start.12 = (bf16[2,1024,512]{2,1,0:T(8,128)(2,1)}, bf16[2,1024,512]{2,1,0:T(8,128)(2,1)}, u32[]{:S(2)}, u32[]{:S(2)}) collective-permute-start(bf16[2,1024,512]{2,1,0:T(8,128)(2,1)} %pad_maximum_fusion.2.near_w), channel_id=1, source_target_pairs={{0,4},{4,0},{1,5},{5,1},{2,6},{6,2},{3,7},{7,3}} | collective-permute-start | bytes 6291464 | tf_op jit(solution)/shard_map/ppermute | solution.py:17
  95.5 30.1 %collective-permute-start.18 = (bf16[256,256]{1,0:T(8,128)(2,1)S(1)}, bf16[256,256]{1,0:T(8,128)(2,1)S(1)}, u32[]{:S(2)}, u32[]{:S(2)}) collective-permute-start(bf16[256,256]{1,0:T(8,128)(2,1)S(1)} %collective-permute-done.17), channel_id=1, source_target_pairs={{0,2},{2,0},{1,3},{3,1},{4,6},{6,4},{5,7},{7,5}} | collective-permute-start | bytes 393224 | tf_op jit(solution)/shard_map/ppermute | solution.py:17
  125.0 23.4 %collective-permute-start.14 = (bf16[2,512,512]{2,1,0:T(8,128)(2,1)S(1)}, bf16[2,512,512]{2,1,0:T(8,128)(2,1)}, u32[]{:S(2)}, u32[]{:S(2)}) collective-permute-start(bf16[2,512,512]{2,1,0:T(8,128)(2,1)S(1)} %dynamic-slice_bitcast_fusion), channel_id=1, source_target_pairs={{0,2},{2,0},{1,3},{3,1},{4,6},{6,4},{5,7},{7,5}} | collective-permute-start | bytes 3145736 | tf_op jit(solution)/shard_map/ppermute | solution.py:17
  126.4 27.2 %collective-permute-start.19 = (bf16[2,256,256]{2,1,0:T(8,128)(2,1)}, bf16[2,256,256]{2,1,0:T(8,128)(2,1)}, u32[]{:S(2)}, u32[]{:S(2)}) collective-permute-start(bf16[2,256,256]{2,1,0:T(8,128)(2,1)} %maximum_select_fusion.4), channel_id=1, source_target_pairs={{0,1},{1,0},{2,3},{3,2},{4,5},{5,4},{6,7},{7,6}} | collective-permute-start | bytes 786440 | tf_op jit(solution)/shard_map/ppermute | solution.py:17
  127.4 30.5 %collective-permute-start.15 = (bf16[512,512]{1,0:T(8,128)(2,1)}, bf16[512,512]{1,0:T(8,128)(2,1)}, u32[]{:S(2)}, u32[]{:S(2)}) collective-permute-start(bf16[512,512]{1,0:T(8,128)(2,1)} %get-tuple-element.60), channel_id=1, source_target_pairs={{0,1},{1,0},{2,3},{3,2},{4,5},{5,4},{6,7},{7,6}} | collective-permute-start | bytes 1572872 | tf_op jit(solution)/shard_map/ppermute | solution.py:17
  152.1 69.1 %collective-permute-start.20 = (bf16[2,1024,512]{2,1,0:T(8,128)(2,1)}, bf16[2,1024,512]{2,1,0:T(8,128)(2,1)}, u32[]{:S(2)}, u32[]{:S(2)}) collective-permute-start(bf16[2,1024,512]{2,1,0:T(8,128)(2,1)} %pad_maximum_fusion.3.near_w), channel_id=1, source_target_pairs={{0,4},{4,0},{1,5},{5,1},{2,6},{6,2},{3,7},{7,3}} | collective-permute-start | bytes 6291464 | tf_op jit(solution)/shard_map/ppermute | solution.py:17
  206.8 34.6 %collective-permute-start.28 = (bf16[2560,256]{1,0:T(8,128)(2,1)}, bf16[2560,256]{1,0:T(8,128)(2,1)S(1)}, u32[]{:S(2)}, u32[]{:S(2)}) collective-permute-start(bf16[2560,256]{1,0:T(8,128)(2,1)} %pad_maximum_fusion.6), channel_id=1, source_target_pairs={{0,1},{1,0},{2,3},{3,2},{4,5},{5,4},{6,7},{7,6}} | collective-permute-start | bytes 3932168 | tf_op jit(solution)/shard_map/ppermute | solution.py:17
  207.3 36.4 %collective-permute-start.24 = (bf16[2048,512]{1,0:T(8,128)(2,1)}, bf16[2048,512]{1,0:T(8,128)(2,1)}, u32[]{:S(2)}, u32[]{:S(2)}) collective-permute-start(bf16[2048,512]{1,0:T(8,128)(2,1)} %glu.4.refs_0_), channel_id=1, source_target_pairs={{0,1},{1,0},{2,3},{3,2},{4,5},{5,4},{6,7},{7,6}} | collective-permute-start | bytes 6291464 | tf_op jit(solution)/shard_map/ppermute | solution.py:17
  207.3 27.0 %collective-permute-start.21 = (bf16[512,512]{1,0:T(8,128)(2,1)}, bf16[512,512]{1,0:T(8,128)(2,1)}, u32[]{:S(2)}, u32[]{:S(2)}) collective-permute-start(bf16[512,512]{1,0:T(8,128)(2,1)} %get-tuple-element.32), channel_id=1, source_target_pairs={{0,1},{1,0},{2,3},{3,2},{4,5},{5,4},{6,7},{7,6}} | collective-permute-start | bytes 1572872 | tf_op jit(solution)/shard_map/ppermute | solution.py:17
  207.9 28.6 %collective-permute-start.23 = (bf16[2,512,512]{2,1,0:T(8,128)(2,1)S(1)}, bf16[2,512,512]{2,1,0:T(8,128)(2,1)S(1)}, u32[]{:S(2)}, u32[]{:S(2)}) collective-permute-start(bf16[2,512,512]{2,1,0:T(8,128)(2,1)S(1)} %pad_maximum_fusion.8), channel_id=1, source_target_pairs={{0,2},{2,0},{1,3},{3,1},{4,6},{6,4},{5,7},{7,5}} | collective-permute-start | bytes 3145736 | tf_op jit(solution)/shard_map/ppermute | solution.py:17
  221.1 24.9 %collective-permute-start.25 = (bf16[2048,512]{1,0:T(8,128)(2,1)}, bf16[2048,512]{1,0:T(8,128)(2,1)}, u32[]{:S(2)}, u32[]{:S(2)}) collective-permute-start(bf16[2048,512]{1,0:T(8,128)(2,1)} %glu.5.refs_1_), channel_id=1, source_target_pairs={{0,1},{1,0},{2,3},{3,2},{4,5},{5,4},{6,7},{7,6}} | collective-permute-start | bytes 6291464 | tf_op jit(solution)/shard_map/ppermute | solution.py:17
  241.4 47.9 %collective-permute-start.10 = (bf16[2,1024,512]{2,1,0:T(8,128)(2,1)}, bf16[2,1024,512]{2,1,0:T(8,128)(2,1)}, u32[]{:S(2)}, u32[]{:S(2)}) collective-permute-start(bf16[2,1024,512]{2,1,0:T(8,128)(2,1)} %pad_maximum_fusion.near_w), channel_id=1, source_target_pairs={{0,4},{4,0},{1,5},{5,1},{2,6},{6,2},{3,7},{7,3}} | collective-permute-start | bytes 6291464 | tf_op jit(solution)/shard_map/ppermute | solution.py:17
  302.5 31.5 %collective-permute-start.34 = (bf16[2560,256]{1,0:T(8,128)(2,1)}, bf16[2560,256]{1,0:T(8,128)(2,1)}, u32[]{:S(2)}, u32[]{:S(2)}) collective-permute-start(bf16[2560,256]{1,0:T(8,128)(2,1)} %pad_maximum_fusion.6), channel_id=1, source_target_pairs={{0,4},{4,0},{1,5},{5,1},{2,6},{6,2},{3,7},{7,3}} | collective-permute-start | bytes 3932168 | tf_op jit(solution)/shard_map/ppermute | solution.py:17
  334.0 69.8 %collective-permute-start.31 = (f32[1536,256]{1,0:T(8,128)}, f32[1536,256]{1,0:T(8,128)}, u32[]{:S(2)}, u32[]{:S(2)}) collective-permute-start(f32[1536,256]{1,0:T(8,128)} %mix.14), channel_id=1, source_target_pairs={{0,2},{2,0},{1,3},{3,1},{4,6},{6,4},{5,7},{7,5}} | collective-permute-start | bytes 4718600 | tf_op jit(solution)/shard_map/ppermute | solution.py:17
  336.0 73.7 %collective-permute-start.39 = (bf16[2560,256]{1,0:T(8,128)(2,1)}, bf16[2560,256]{1,0:T(8,128)(2,1)}, u32[]{:S(2)}, u32[]{:S(2)}) collective-permute-start(bf16[2560,256]{1,0:T(8,128)(2,1)} %pad_maximum_fusion.7), channel_id=1, source_target_pairs={{0,4},{4,0},{1,5},{5,1},{2,6},{6,2},{3,7},{7,3}} | collective-permute-start | bytes 3932168 | tf_op jit(solution)/shard_map/ppermute | solution.py:17
  337.2 44.6 %collective-permute-start.33 = (bf16[2560,128]{1,0:T(8,128)(2,1)}, bf16[2560,128]{1,0:T(8,128)(2,1)S(1)}, u32[]{:S(2)}, u32[]{:S(2)}) collective-permute-start(bf16[2560,128]{1,0:T(8,128)(2,1)} %get-tuple-element.64), channel_id=1, source_target_pairs={{0,4},{4,0},{1,5},{5,1},{2,6},{6,2},{3,7},{7,3}} | collective-permute-start | bytes 1966088 | tf_op jit(solution)/shard_map/ppermute | solution.py:17
  339.0 56.2 %collective-permute-start.32 = (bf16[2560,128]{1,0:T(8,128)(2,1)S(1)}, bf16[2560,128]{1,0:T(8,128)(2,1)S(1)}, u32[]{:S(2)}, u32[]{:S(2)}) collective-permute-start(bf16[2560,128]{1,0:T(8,128)(2,1)S(1)} %get-tuple-element.65), channel_id=1, source_target_pairs={{0,4},{4,0},{1,5},{5,1},{2,6},{6,2},{3,7},{7,3}} | collective-permute-start | bytes 1966088 | tf_op jit(solution)/shard_map/ppermute | solution.py:17
  409.7 26.4 %collective-permute-start.41 = (f32[2048,128]{1,0:T(8,128)}, f32[2048,128]{1,0:T(8,128)}, u32[]{:S(2)}, u32[]{:S(2)}) collective-permute-start(f32[2048,128]{1,0:T(8,128)} %mix.17), channel_id=1, source_target_pairs={{0,2},{2,0},{1,3},{3,1},{4,6},{6,4},{5,7},{7,5}} | collective-permute-start | bytes 3145736 | tf_op jit(solution)/shard_map/ppermute | solution.py:17
  411.3 17.8 %collective-permute-start.38 = (bf16[2560,128]{1,0:T(8,128)(2,1)}, bf16[2560,128]{1,0:T(8,128)(2,1)S(1)}, u32[]{:S(2)}, u32[]{:S(2)}) collective-permute-start(bf16[2560,128]{1,0:T(8,128)(2,1)} %get-tuple-element.62), channel_id=1, source_target_pairs={{0,4},{4,0},{1,5},{5,1},{2,6},{6,2},{3,7},{7,3}} | collective-permute-start | bytes 1966088 | tf_op jit(solution)/shard_map/ppermute | solution.py:17
  411.6 46.8 %collective-permute-start.42 = (f32[2048,128]{1,0:T(8,128)}, f32[2048,128]{1,0:T(8,128)S(1)}, u32[]{:S(2)}, u32[]{:S(2)}) collective-permute-start(f32[2048,128]{1,0:T(8,128)} %mix.18), channel_id=1, source_target_pairs={{0,2},{2,0},{1,3},{3,1},{4,6},{6,4},{5,7},{7,5}} | collective-permute-start | bytes 3145736 | tf_op jit(solution)/shard_map/ppermute | solution.py:17
  413.3 33.3 %collective-permute-start.37 = (bf16[2560,128]{1,0:T(8,128)(2,1)}, bf16[2560,128]{1,0:T(8,128)(2,1)}, u32[]{:S(2)}, u32[]{:S(2)}) collective-permute-start(bf16[2560,128]{1,0:T(8,128)(2,1)} %get-tuple-element.63), channel_id=1, source_target_pairs={{0,4},{4,0},{1,5},{5,1},{2,6},{6,2},{3,7},{7,3}} | collective-permute-start | bytes 1966088 | tf_op jit(solution)/shard_map/ppermute | solution.py:17
  415.0 54.3 %collective-permute-start.36 = (f32[512,256]{1,0:T(8,128)}, f32[512,256]{1,0:T(8,128)}, u32[]{:S(2)}, u32[]{:S(2)}) collective-permute-start(f32[512,256]{1,0:T(8,128)} %mix.15), channel_id=1, source_target_pairs={{0,2},{2,0},{1,3},{3,1},{4,6},{6,4},{5,7},{7,5}} | collective-permute-start | bytes 1572872 | tf_op jit(solution)/shard_map/ppermute | solution.py:17
  444.1 30.5 %collective-permute-start.43 = (bf16[2048,128]{1,0:T(8,128)(2,1)}, bf16[2048,128]{1,0:T(8,128)(2,1)S(1)}, u32[]{:S(2)}, u32[]{:S(2)}) collective-permute-start(bf16[2048,128]{1,0:T(8,128)(2,1)} %mix.21), channel_id=1, source_target_pairs={{0,4},{4,0},{1,5},{5,1},{2,6},{6,2},{3,7},{7,3}} | collective-permute-start | bytes 1572872 | tf_op jit(solution)/shard_map/ppermute | solution.py:17
  (47 other events, 328.4 us)

commit v8 on v7

--- a/solution.py
+++ b/solution.py
@@ -226,6 +226,7 @@
         out_specs=pl.BlockSpec((blk, cols), lambda i: (i, 0)),
         out_shape=jax.ShapeDtypeStruct((tokens, cols), dtype),
         cost_estimate=pl.CostEstimate(flops=2 * tokens * depth * cols, bytes_accessed=2 * depth * (tokens + cols), transcendentals=0),
+        compiler_params=pltpu.CompilerParams(vmem_limit_bytes=67043328),
         name="mix",
     )(*lhs, *ws, *adds)
 
@@ -251,19 +252,12 @@
         g = jnp.concatenate([g, swap_y(g)], 0)
         g = jnp.concatenate([g, swap_x(g)], 0)
         g = jnp.concatenate([g, swap_c(g)], 0)
-        hid2 = hidden.reshape(2, half, width)
-        other = pick(hid2, 1 - yi)
-        mine = pick(tie(hid2, other), yi)
-        from_y = swap_y(other)
-        mine_x = swap_x(mine)
-        from_yx = swap_x(from_y)
-        near = [mine, from_y, mine_x, from_yx]
-        far = [swap_c(near[0])] + [swap_c(p) for p in near[1:]]
         offs = []
         for cr in range(2):
             for xr in range(2):
                 for yr in range(2):
                     offs.append(width * (4 * yr + 2 * (xr ^ xi) + (cr ^ ci)))
+        offs = jnp.stack(offs).astype(jnp.int32)
         half_dim = dim // 2
         inv_freq = ROPE_BASE ** (-2.0 * jnp.arange(half_dim, dtype=F32) / dim)
         positions = (lengths[:, None] + jnp.arange(new, dtype=jnp.int32)[None, :]).reshape(own_tok)
@@ -271,8 +265,6 @@
         cos_t, sin_t = jnp.cos(angles), jnp.sin(angles)
         cos_t = jnp.concatenate([cos_t, cos_t], -1)
         sin_t = jnp.concatenate([-sin_t, sin_t], -1)
-        g = tie(g, cos_t, sin_t)
-        h = layer_norm(near + far, g, jnp.stack(offs).astype(jnp.int32))
 
         kv_rows = w_key.shape[0] // 4
         w_kv = jnp.concatenate([w_key, w_value], axis=1)
@@ -280,6 +272,21 @@
         kv_part = swap_y(lax.dynamic_slice_in_dim(w_kv, ti * kv_rows, kv_rows, 0))
         kv_pair = ordered([kv_part, swap_x(kv_part)], xi, 0)
         kv_far = ordered([kv_pair, swap_c(kv_pair)], ci, 1).reshape(w_kv.shape)
+
+        hid2 = hidden.reshape(2, half, width)
+        other = pick(hid2, 1 - yi)
+        mine = pick(tie(hid2, other), yi)
+        mine_x = swap_x(mine)
+        over = [swap_y(other[i * half // 2 : (i + 1) * half // 2]) for i in range(2)]
+        over[0] = tie(over[0], cos_t, sin_t, offs)
+        forward = [swap_x(p) for p in over]
+        from_y = jnp.concatenate(over, 0)
+        far = [swap_c(mine), swap_c(from_y), swap_c(mine_x)]
+        from_yx = jnp.concatenate(forward, 0)
+        near = [mine, from_y, mine_x, from_yx]
+        far.append(swap_c(from_yx))
+        h = layer_norm(near + far, g, offs)
+
         q_far = swap_y(w_query)
 
         q = project(h, [w_query, q_far])
@@ -335,7 +342,7 @@
             return out
 
         early, late, every = [*range(chunks - 1), "o"], [chunks - 1], [*range(chunks), "o"]
-        split = (0, 3 * half // 4), (3 * half // 4, half // 4)
+        split = (0, half // 2), (half // 2, half // 2)
 
         cross_far, same_far = swap_c(blocks[1][1]), swap_c(blocks[0][1])
         pre_cross = mix(terms(blocks[1][0], cross_far, early))

time: 483 us -> 489 us (1.012)
  other arithmetic: 22.1 us -> 27.7 us
    unnamed x69 -> x45, local copies, waits for them, and re-layouts: 12.8 us -> 5.34 us
    ppermute x45 -> x47, starting transfers between devices: 28.1 us -> 31.2 us  [swap(): return lambda a: lax.ppermute(a, axis, pairs)]
    ppermute x45 -> x47, waiting for transfers between devices: 187 us -> 188 us  [swap(): return lambda a: lax.ppermute(a, axis, pairs)]
  transfers between devices with their start and end apart: 45 -> 47, of which waited for: 16 -> 16; matrix products, arithmetic and copies ran while one was open for 9% -> 12% of each run, Pallas kernels for 40% -> 39%
where the time goes in v8:
time: 489 us; the launch traced here: 488 us
  Pallas kernels  205 us (42%)
  waiting for transfers between devices  188 us (38%)
  local copies, waits for them, and re-layouts  32.3 us (7%)
  starting transfers between devices  31.2 us (6%)
  other arithmetic  27.7 us (6%)
    ppermute x47, waiting for transfers between devices, swap(): return lambda a: lax.ppermute(a, axis, pairs)  188 us
    pallas_call x12, Pallas kernels, mix(): pl.pallas_call(functools.partial(mix_kernel, plan, len(lhs), len(ws)), gr...  86.1 us
    pallas_call x4, Pallas kernels, glu(): pl.pallas_call(glu_kernel, grid=(tokens // blk,), in_specs=[pl.BlockSpec(...  52.8 us
    pallas_call x1, Pallas kernels, attention(): pl.pallas_call(attn_kernel, grid_spec=pltpu.PrefetchScalarGridSpec(num_sc...  44.5 us
    ppermute x47, starting transfers between devices, swap(): return lambda a: lax.ppermute(a, axis, pairs)  31.2 us
    pallas_call x1, Pallas kernels, layer_norm(): pl.pallas_call(norm_kernel, grid_spec=pltpu.PrefetchScalarGridSpec(num_sc...  13 us
    another operation x4, other arithmetic, local_layer(): jnp.stack([w[:, j * cw:(j + 1) * cw] for w in (w_gate, w_up)])  11.1 us
  transfers between devices with their start and end apart: 47, of which 16 were waited for; matrix products, arithmetic and copies ran while one was open for 12% of the time, Pallas kernels for 39%

profile of v8, /device:TPU:0, one launch (start us, length us, event | category | flops | bytes accessed | tf_op | source)
XLA Modules:
  0.0 488.1 jit_solution(9052471822875534214)
XLA Ops:
  11.2 6.1 %slice_bitcast_fusion = (bf16[1,1024,512]{2,1,0:T(8,128)(2,1)S(1)}, bf16[1,1024,512]{2,1,0:T(8,128)(2,1)S(1)}, bf16[1,1024,512]{2,1,0:T(8,128)(2,1)}, bf16[1,102...) fusion(bf16[1024,2048]{1,0:T(8,128)(2,1)} %param.21, ...), kind=kLoop, calls=%fused_computation.27 | loop fusion | bytes 16777216 | tf_op jit(solution)/shard_map/stack | solution.py:301
  23.8 8.6 %collective-permute-done.9 = f32[1,256]{1,0:T(1,128)S(1)} collective-permute-done((f32[1,256]{1,0:T(1,128)S(1)}, f32[1,256]{1,0:T(1,128)S(1)}, u32[]{:S(2)}, u32[]{:S(2)}) %collective-permute-start.9) | collective-permute-done | bytes 1056 | tf_op jit(solution)/shard_map/ppermute | solution.py:17
  35.4 5.4 %collective-permute-done.10 = f32[2,256]{1,0:T(2,128)S(1)} collective-permute-done((f32[2,256]{1,0:T(2,128)S(1)}, f32[2,256]{1,0:T(2,128)S(1)}, u32[]{:S(2)}, u32[]{:S(2)}) %collective-permute-start.10) | collective-permute-done | bytes 2080 | tf_op jit(solution)/shard_map/ppermute | solution.py:17
  45.9 5.2 %collective-permute-done.4 = bf16[1024,256]{1,0:T(8,128)(2,1)S(1)} collective-permute-done((bf16[1024,256]{1,0:T(8,128)(2,1)}, bf16[1024,256]{1,0:T(8,128)(2,1)S(1)}, u32[]{:S(2)}, u32[]{:S(2)}) %collective-permute-start.4) | collective-permute-done | bytes 524320 | tf_op jit(solution)/shard_map/ppermute | solution.py:17
  52.5 37.2 %collective-permute-done.19 = bf16[256,256]{1,0:T(8,128)(2,1)S(1)} collective-permute-done((bf16[256,256]{1,0:T(8,128)(2,1)S(1)}, bf16[256,256]{1,0:T(8,128)(2,1)S(1)}, u32[]{:S(2)}, u32[]{:S(2)}) %collective-permute-start.19) | collective-permute-done | bytes 131104 | tf_op jit(solution)/shard_map/ppermute | solution.py:17
  97.4 13.0 %norm.1.h_ref = bf16[2048,2048]{1,0:T(8,128)(2,1)} custom-call(s32[8]{0:T(128)} %stack.140.offs_ref, bf16[2048,256]{1,0:T(8,128)(2,1)} %copy-done.2, bf16[2048,256]{1,0:T(8,128)(2,1)} %copy-done.5, bf16[2048,256]{1,0:T(8,128)(2,1)} %collective-permute-done.2.refs_2_, bf16[2048,256]{1,0:T(8,128)(2,1)} %constant_dynamic-update-slice_fusion.2.refs_3_, ...), custom_call_target="tpu_custom_call" | custom-call | flops 83886080 | bytes 16777216 | tf_op jit(solution)/shard_map/norm/pallas_call | solution.py:47
  110.4 6.1 %collective-permute-done.15.refs_1_ = bf16[1024,512]{1,0:T(8,128)(2,1)S(1)} collective-permute-done((bf16[1024,512]{1,0:T(8,128)(2,1)}, bf16[1024,512]{1,0:T(8,128)(2,1)S(1)}, u32[]{:S(2)}, u32[]{:S(2)}) %collective-permute-start.15) | collective-permute-done | bytes 1048608 | tf_op jit(solution)/shard_map/ppermute | solution.py:17
  117.4 8.7 %project.1 = bf16[2048,512]{1,0:T(8,128)(2,1)} custom-call(bf16[2048,2048]{1,0:T(8,128)(2,1)} %norm.1.h_ref, bf16[1024,512]{1,0:T(8,128)(2,1)} %refs_0_.1, bf16[1024,512]{1,0:T(8,128)(2,1)} %copy-done.19), custom_call_target="tpu_custom_call" | custom-call | flops 4294967296 | bytes 10485760 | tf_op jit(solution)/shard_map/project/pallas_call | solution.py:185
  131.3 13.2 %glu.4.refs_0_ = bf16[2048,512]{1,0:T(8,128)(2,1)} custom-call(bf16[2048,2048]{1,0:T(8,128)(2,1)} %norm.1.h_ref, bf16[2,1024,512]{2,1,0:T(8,128)(2,1)} %pad_maximum_fusion.1.near_w, bf16[2,1024,512]{2,1,0:T(8,128)(2,1)} %collective-permute-done.13.far_w), custom_call_target="tpu_custom_call" | custom-call | flops 8589934592 | bytes 14680064 | tf_op jit(solution)/shard_map/glu/pallas_call | solution.py:161
  144.5 6.4 %collective-permute-done.16 = bf16[2,512,512]{2,1,0:T(8,128)(2,1)S(1)} collective-permute-done((bf16[2,512,512]{2,1,0:T(8,128)(2,1)S(1)}, bf16[2,512,512]{2,1,0:T(8,128)(2,1)S(1)}, u32[]{:S(2)}, u32[]{:S(2)}) %collective-permute-start.16) | collective-permute-done | bytes 1048608 | tf_op jit(solution)/shard_map/ppermute | solution.py:17
  159.9 44.5 %attn.1 = (bf16[512,512]{1,0:T(8,128)(2,1)}, bf16[512,512]{1,0:T(8,128)(2,1)}, bf16[512,512]{1,0:T(8,128)(2,1)}, bf16[512,512]{1,0:T(8,128)(2,1)}, bf16[8,2048,1...) custom-call(s32[8]{0:T(128)} %len_ref.1, bf16[512,512]{1,0:T(8,128)(2,1)} %get-tuple-element.59.q0, ...), custom_call_target="tpu_custom_call" | custom-call | flops 17179869184 | bytes 16777216 | tf_op jit(solution)/shard_map/attn/pallas_call | solution.py:131
  210.0 13.2 %glu.5.refs_1_ = bf16[2048,512]{1,0:T(8,128)(2,1)} custom-call(bf16[2048,2048]{1,0:T(8,128)(2,1)} %norm.1.h_ref, bf16[2,1024,512]{2,1,0:T(8,128)(2,1)} %pad_maximum_fusion.2.near_w, bf16[2,1024,512]{2,1,0:T(8,128)(2,1)} %collective-permute-done.14.far_w), custom_call_target="tpu_custom_call" | custom-call | flops 8589934592 | bytes 14680064 | tf_op jit(solution)/shard_map/glu/pallas_call | solution.py:161
  223.2 13.2 %glu.6.refs_2_ = bf16[2048,512]{1,0:T(8,128)(2,1)} custom-call(bf16[2048,2048]{1,0:T(8,128)(2,1)} %norm.1.h_ref, bf16[2,1024,512]{2,1,0:T(8,128)(2,1)} %pad_maximum_fusion.3.near_w, bf16[2,1024,512]{2,1,0:T(8,128)(2,1)} %collective-permute-done.22.far_w), custom_call_target="tpu_custom_call" | custom-call | flops 8589934592 | bytes 14680064 | tf_op jit(solution)/shard_map/glu/pallas_call | solution.py:161
  248.1 10.8 %mix.12.refs_4_ = f32[2048,256]{1,0:T(8,128)} custom-call(bf16[2048,512]{1,0:T(8,128)(2,1)} %glu.4.refs_0_, bf16[2048,512]{1,0:T(8,128)(2,1)} %glu.5.refs_1_, bf16[2048,512]{1,0:T(8,128)(2,1)} %glu.6.refs_2_, bf16[2048,512]{1,0:T(8,128)(2,1)} %bitcast.66, bf16[2048,512]{1,0:T(8,128)(2,1)} %collective-permute-done.26.refs_4_.refs_0_, ...), custom_call_target="tpu_custom_call" | custom-call | flops 4294967296 | bytes 18874368 | tf_op jit(solution)/shard_map/mix/pallas_call | solution.py:222
  258.9 11.1 %mix.13.refs_4_ = f32[2048,256]{1,0:T(8,128)} custom-call(bf16[2048,512]{1,0:T(8,128)(2,1)} %glu.4.refs_0_, bf16[2048,512]{1,0:T(8,128)(2,1)} %glu.5.refs_1_, bf16[2048,512]{1,0:T(8,128)(2,1)} %glu.6.refs_2_, bf16[2048,512]{1,0:T(8,128)(2,1)} %bitcast.67, bf16[2048,512]{1,0:T(8,128)(2,1)} %collective-permute-done.26.refs_4_.refs_0_, ...), custom_call_target="tpu_custom_call" | custom-call | flops 4294967296 | bytes 18874368 | tf_op jit(solution)/shard_map/mix/pallas_call | solution.py:222
  270.0 21.3 %collective-permute-done.12.far_w = bf16[2,1024,512]{2,1,0:T(8,128)(2,1)} collective-permute-done((bf16[2,1024,512]{2,1,0:T(8,128)(2,1)}, bf16[2,1024,512]{2,1,0:T(8,128)(2,1)}, u32[]{:S(2)}, u32[]{:S(2)}) %collective-permute-start.12) | collective-permute-done | bytes 2097184 | tf_op jit(solution)/shard_map/ppermute | solution.py:17
  291.3 13.2 %glu.7.refs_0_.refs_3_ = bf16[2048,512]{1,0:T(8,128)(2,1)} custom-call(bf16[2048,2048]{1,0:T(8,128)(2,1)} %norm.1.h_ref, bf16[2,1024,512]{2,1,0:T(8,128)(2,1)} %pad_maximum_fusion.near_w, bf16[2,1024,512]{2,1,0:T(8,128)(2,1)} %collective-permute-done.12.far_w), custom_call_target="tpu_custom_call" | custom-call | flops 8589934592 | bytes 14680064 | tf_op jit(solution)/shard_map/glu/pallas_call | solution.py:161
  304.8 4.2 collective-permute-done.32.refs_1_.refs_3_
  317.3 18.8 %collective-permute-done.36 = bf16[2560,256]{1,0:T(8,128)(2,1)} collective-permute-done((bf16[2560,256]{1,0:T(8,128)(2,1)}, bf16[2560,256]{1,0:T(8,128)(2,1)}, u32[]{:S(2)}, u32[]{:S(2)}) %collective-permute-start.36) | collective-permute-done | bytes 1310752 | tf_op jit(solution)/shard_map/ppermute | solution.py:17
  342.0 7.9 %mix.16.refs_6_ = f32[2048,256]{1,0:T(8,128)} custom-call(bf16[2048,512]{1,0:T(8,128)(2,1)} %collective-permute-done.26.refs_4_.refs_0_, bf16[2048,512]{1,0:T(8,128)(2,1)} %collective-permute-done.27.refs_5_.refs_1_, bf16[2048,512]{1,0:T(8,128)(2,1)} %collective-permute-done.28.refs_6_.refs_2_, bf16[2048,512]{1,0:T(8,128)(2,1)} %collective-permute-done.32.refs_1_.refs_3_, ...), custom_call_target="tpu_custom_call" | custom-call | flops 2684354560 | bytes 11796480 | tf_op jit(solution)/shard_map/mix/pallas_call | solution.py:222
  349.9 32.1 %collective-permute-done.35.refs_5_ = bf16[2560,128]{1,0:T(8,128)(2,1)} collective-permute-done((bf16[2560,128]{1,0:T(8,128)(2,1)}, bf16[2560,128]{1,0:T(8,128)(2,1)}, u32[]{:S(2)}, u32[]{:S(2)}) %collective-permute-start.35) | collective-permute-done | bytes 655392 | tf_op jit(solution)/shard_map/ppermute | solution.py:17
  382.1 7.7 %mix.17 = f32[2048,128]{1,0:T(8,128)} custom-call(bf16[2048,512]{1,0:T(8,128)(2,1)} %glu.4.refs_0_, bf16[2048,512]{1,0:T(8,128)(2,1)} %glu.5.refs_1_, bf16[2048,512]{1,0:T(8,128)(2,1)} %glu.6.refs_2_, bf16[2048,512]{1,0:T(8,128)(2,1)} %glu.7.refs_0_.refs_3_, bf16[2048,512]{1,0:T(8,128)(2,1)} %bitcast.68, bf16[2560,128]{1,0:T(8,128)(2,1)} %collective-permute-done.35.refs_5_, ...), custom_call_target="tpu_custom_call" | custom-call | flops 1342177280 | bytes 11141120 | tf_op jit(solution)/shard_map/mix/pallas_call | solution.py:222
  389.8 5.9 %collective-permute-done.34.refs_5_ = bf16[2560,128]{1,0:T(8,128)(2,1)} collective-permute-done((bf16[2560,128]{1,0:T(8,128)(2,1)}, bf16[2560,128]{1,0:T(8,128)(2,1)}, u32[]{:S(2)}, u32[]{:S(2)}) %collective-permute-start.34) | collective-permute-done | bytes 655392 | tf_op jit(solution)/shard_map/ppermute | solution.py:17
  395.6 7.7 %mix.18 = f32[2048,128]{1,0:T(8,128)} custom-call(bf16[2048,512]{1,0:T(8,128)(2,1)} %glu.4.refs_0_, bf16[2048,512]{1,0:T(8,128)(2,1)} %glu.5.refs_1_, bf16[2048,512]{1,0:T(8,128)(2,1)} %glu.6.refs_2_, bf16[2048,512]{1,0:T(8,128)(2,1)} %glu.7.refs_0_.refs_3_, bf16[2048,512]{1,0:T(8,128)(2,1)} %bitcast.69, bf16[2560,128]{1,0:T(8,128)(2,1)} %collective-permute-done.34.refs_5_, ...), custom_call_target="tpu_custom_call" | custom-call | flops 1342177280 | bytes 11141120 | tf_op jit(solution)/shard_map/mix/pallas_call | solution.py:222
  403.3 4.2 mix.19
  415.1 8.3 %mix.20.refs_6_ = f32[2048,256]{1,0:T(8,128)} custom-call(bf16[2048,512]{1,0:T(8,128)(2,1)} %collective-permute-done.26.refs_4_.refs_0_, bf16[2048,512]{1,0:T(8,128)(2,1)} %collective-permute-done.27.refs_5_.refs_1_, bf16[2048,512]{1,0:T(8,128)(2,1)} %collective-permute-done.28.refs_6_.refs_2_, bf16[2048,512]{1,0:T(8,128)(2,1)} %collective-permute-done.32.refs_1_.refs_3_, ...), custom_call_target="tpu_custom_call" | custom-call | flops 2684354560 | bytes 11796480 | tf_op jit(solution)/shard_map/mix/pallas_call | solution.py:222
  423.5 6.5 %collective-permute-done.40.refs_5_ = bf16[2560,128]{1,0:T(8,128)(2,1)} collective-permute-done((bf16[2560,128]{1,0:T(8,128)(2,1)}, bf16[2560,128]{1,0:T(8,128)(2,1)}, u32[]{:S(2)}, u32[]{:S(2)}) %collective-permute-start.40) | collective-permute-done | bytes 655392 | tf_op jit(solution)/shard_map/ppermute | solution.py:17
  433.9 8.0 %mix.21 = bf16[2048,128]{1,0:T(8,128)(2,1)} custom-call(bf16[2048,512]{1,0:T(8,128)(2,1)} %glu.4.refs_0_, bf16[2048,512]{1,0:T(8,128)(2,1)} %glu.5.refs_1_, bf16[2048,512]{1,0:T(8,128)(2,1)} %glu.6.refs_2_, bf16[2048,512]{1,0:T(8,128)(2,1)} %glu.7.refs_0_.refs_3_, bf16[2048,512]{1,0:T(8,128)(2,1)} %bitcast.70, ...), custom_call_target="tpu_custom_call" | custom-call | flops 1342177280 | bytes 11141120 | tf_op jit(solution)/shard_map/mix/pallas_call | solution.py:222
  444.5 11.9 %collective-permute-done.44.refs_7_ = f32[2048,128]{1,0:T(8,128)} collective-permute-done((f32[2048,128]{1,0:T(8,128)}, f32[2048,128]{1,0:T(8,128)}, u32[]{:S(2)}, u32[]{:S(2)}) %collective-permute-start.44) | collective-permute-done | bytes 1048608 | tf_op jit(solution)/shard_map/ppermute | solution.py:17
  456.4 8.0 %mix.22 = bf16[2048,128]{1,0:T(8,128)(2,1)} custom-call(bf16[2048,512]{1,0:T(8,128)(2,1)} %glu.4.refs_0_, bf16[2048,512]{1,0:T(8,128)(2,1)} %glu.5.refs_1_, bf16[2048,512]{1,0:T(8,128)(2,1)} %glu.6.refs_2_, bf16[2048,512]{1,0:T(8,128)(2,1)} %glu.7.refs_0_.refs_3_, bf16[2048,512]{1,0:T(8,128)(2,1)} %bitcast.71, ...), custom_call_target="tpu_custom_call" | custom-call | flops 1342177280 | bytes 11141120 | tf_op jit(solution)/shard_map/mix/pallas_call | solution.py:222
  464.7 13.7 %collective-permute-done.38.refs_5_ = f32[1024,256]{1,0:T(8,128)} collective-permute-done((f32[1024,256]{1,0:T(8,128)}, f32[1024,256]{1,0:T(8,128)}, u32[]{:S(2)}, u32[]{:S(2)}) %collective-permute-start.38) | collective-permute-done | bytes 1048608 | tf_op jit(solution)/shard_map/ppermute | solution.py:17
  478.4 4.2 mix.23
  (173 shorter events, 100.9 us)
Async XLA Ops:
  2.1 87.6 %collective-permute-start.2 = (bf16[2048,256]{1,0:T(8,128)(2,1)S(1)}, bf16[2048,256]{1,0:T(8,128)(2,1)}, u32[]{:S(2)}, u32[]{:S(2)}) collective-permute-start(bf16[2048,256]{1,0:T(8,128)(2,1)S(1)} %dynamic-slice_bitcast_fusion.1.refs_0_.refs_10_), channel_id=1, source_target_pairs={{0,2},{2,0},{1,3},{3,1},{4,6},{6,4},{5,7},{7,5}} | collective-permute-start | bytes 3145736 | tf_op jit(solution)/shard_map/ppermute | solution.py:17
  5.4 84.8 %collective-permute-start.5 = (bf16[2048,256]{1,0:T(8,128)(2,1)S(1)}, bf16[2048,256]{1,0:T(8,128)(2,1)}, u32[]{:S(2)}, u32[]{:S(2)}) collective-permute-start(bf16[2048,256]{1,0:T(8,128)(2,1)S(1)} %dynamic-slice_bitcast_fusion.1.refs_0_.refs_10_), channel_id=1, source_target_pairs={{0,1},{1,0},{2,3},{3,2},{4,5},{5,4},{6,7},{7,6}} | collective-permute-start | bytes 3145736 | tf_op jit(solution)/shard_map/ppermute | solution.py:17
  8.0 24.7 %collective-permute-start.1 = (bf16[1024,256]{1,0:T(8,128)(2,1)}, bf16[1024,256]{1,0:T(8,128)(2,1)}, u32[]{:S(2)}, u32[]{:S(2)}) collective-permute-start(bf16[1024,256]{1,0:T(8,128)(2,1)} %get-tuple-element.60), channel_id=1, source_target_pairs={{0,4},{4,0},{1,5},{5,1},{2,6},{6,2},{3,7},{7,3}} | collective-permute-start | bytes 1572872 | tf_op jit(solution)/shard_map/ppermute | solution.py:17
  8.5 23.9 %collective-permute-start.9 = (f32[1,256]{1,0:T(1,128)S(1)}, f32[1,256]{1,0:T(1,128)S(1)}, u32[]{:S(2)}, u32[]{:S(2)}) collective-permute-start(f32[1,256]{1,0:T(1,128)S(1)} %bitcast.84), channel_id=1, source_target_pairs={{0,4},{4,0},{1,5},{5,1},{2,6},{6,2},{3,7},{7,3}} | collective-permute-start | bytes 3080 | tf_op jit(solution)/shard_map/ppermute | solution.py:17
  23.2 21.8 %collective-permute-start.3 = (bf16[1024,256]{1,0:T(8,128)(2,1)}, bf16[1024,256]{1,0:T(8,128)(2,1)S(1)}, u32[]{:S(2)}, u32[]{:S(2)}) collective-permute-start(bf16[1024,256]{1,0:T(8,128)(2,1)} %collective-permute-done), channel_id=1, source_target_pairs={{0,2},{2,0},{1,3},{3,1},{4,6},{6,4},{5,7},{7,5}} | collective-permute-start | bytes 1572872 | tf_op jit(solution)/shard_map/ppermute | solution.py:17
  40.7 90.6 %collective-permute-start.13 = (bf16[2,1024,512]{2,1,0:T(8,128)(2,1)}, bf16[2,1024,512]{2,1,0:T(8,128)(2,1)}, u32[]{:S(2)}, u32[]{:S(2)}) collective-permute-start(bf16[2,1024,512]{2,1,0:T(8,128)(2,1)} %pad_maximum_fusion.1.near_w), channel_id=1, source_target_pairs={{0,4},{4,0},{1,5},{5,1},{2,6},{6,2},{3,7},{7,3}} | collective-permute-start | bytes 6291464 | tf_op jit(solution)/shard_map/ppermute | solution.py:17
  45.0 44.7 %collective-permute-start.19 = (bf16[256,256]{1,0:T(8,128)(2,1)S(1)}, bf16[256,256]{1,0:T(8,128)(2,1)S(1)}, u32[]{:S(2)}, u32[]{:S(2)}) collective-permute-start(bf16[256,256]{1,0:T(8,128)(2,1)S(1)} %constant_dynamic-slice_fusion.8), channel_id=1, source_target_pairs={{0,4},{4,0},{1,5},{5,1},{2,6},{6,2},{3,7},{7,3}} | collective-permute-start | bytes 393224 | tf_op jit(solution)/shard_map/ppermute | solution.py:17
  52.3 43.1 %collective-permute-start.6 = (bf16[2048,256]{1,0:T(8,128)(2,1)S(1)}, bf16[2048,256]{1,0:T(8,128)(2,1)}, u32[]{:S(2)}, u32[]{:S(2)}) collective-permute-start(bf16[2048,256]{1,0:T(8,128)(2,1)S(1)} %constant_dynamic-update-slice_fusion.refs_1_.refs_6_), channel_id=1, source_target_pairs={{0,1},{1,0},{2,3},{3,2},{4,5},{5,4},{6,7},{7,6}} | collective-permute-start | bytes 3145736 | tf_op jit(solution)/shard_map/ppermute | solution.py:17
  90.2 26.2 %collective-permute-start.15 = (bf16[1024,512]{1,0:T(8,128)(2,1)}, bf16[1024,512]{1,0:T(8,128)(2,1)S(1)}, u32[]{:S(2)}, u32[]{:S(2)}) collective-permute-start(bf16[1024,512]{1,0:T(8,128)(2,1)} %refs_0_.1), channel_id=1, source_target_pairs={{0,4},{4,0},{1,5},{5,1},{2,6},{6,2},{3,7},{7,3}} | collective-permute-start | bytes 3145736 | tf_op jit(solution)/shard_map/ppermute | solution.py:17
  95.4 113.1 %collective-permute-start.14 = (bf16[2,1024,512]{2,1,0:T(8,128)(2,1)}, bf16[2,1024,512]{2,1,0:T(8,128)(2,1)}, u32[]{:S(2)}, u32[]{:S(2)}) collective-permute-start(bf16[2,1024,512]{2,1,0:T(8,128)(2,1)} %pad_maximum_fusion.2.near_w), channel_id=1, source_target_pairs={{0,4},{4,0},{1,5},{5,1},{2,6},{6,2},{3,7},{7,3}} | collective-permute-start | bytes 6291464 | tf_op jit(solution)/shard_map/ppermute | solution.py:17
  95.9 33.1 %collective-permute-start.20 = (bf16[256,256]{1,0:T(8,128)(2,1)S(1)}, bf16[256,256]{1,0:T(8,128)(2,1)S(1)}, u32[]{:S(2)}, u32[]{:S(2)}) collective-permute-start(bf16[256,256]{1,0:T(8,128)(2,1)S(1)} %collective-permute-done.19), channel_id=1, source_target_pairs={{0,2},{2,0},{1,3},{3,1},{4,6},{6,4},{5,7},{7,5}} | collective-permute-start | bytes 393224 | tf_op jit(solution)/shard_map/ppermute | solution.py:17
  127.5 23.3 %collective-permute-start.16 = (bf16[2,512,512]{2,1,0:T(8,128)(2,1)S(1)}, bf16[2,512,512]{2,1,0:T(8,128)(2,1)S(1)}, u32[]{:S(2)}, u32[]{:S(2)}) collective-permute-start(bf16[2,512,512]{2,1,0:T(8,128)(2,1)S(1)} %dynamic-slice_bitcast_fusion), channel_id=1, source_target_pairs={{0,2},{2,0},{1,3},{3,1},{4,6},{6,4},{5,7},{7,5}} | collective-permute-start | bytes 3145736 | tf_op jit(solution)/shard_map/ppermute | solution.py:17
  129.7 25.0 %collective-permute-start.21 = (bf16[2,256,256]{2,1,0:T(8,128)(2,1)}, bf16[2,256,256]{2,1,0:T(8,128)(2,1)}, u32[]{:S(2)}, u32[]{:S(2)}) collective-permute-start(bf16[2,256,256]{2,1,0:T(8,128)(2,1)} %maximum_select_fusion.4), channel_id=1, source_target_pairs={{0,1},{1,0},{2,3},{3,2},{4,5},{5,4},{6,7},{7,6}} | collective-permute-start | bytes 786440 | tf_op jit(solution)/shard_map/ppermute | solution.py:17
  130.8 28.3 %collective-permute-start.17 = (bf16[512,512]{1,0:T(8,128)(2,1)}, bf16[512,512]{1,0:T(8,128)(2,1)}, u32[]{:S(2)}, u32[]{:S(2)}) collective-permute-start(bf16[512,512]{1,0:T(8,128)(2,1)} %get-tuple-element.58), channel_id=1, source_target_pairs={{0,1},{1,0},{2,3},{3,2},{4,5},{5,4},{6,7},{7,6}} | collective-permute-start | bytes 1572872 | tf_op jit(solution)/shard_map/ppermute | solution.py:17
  153.2 69.9 %collective-permute-start.22 = (bf16[2,1024,512]{2,1,0:T(8,128)(2,1)}, bf16[2,1024,512]{2,1,0:T(8,128)(2,1)}, u32[]{:S(2)}, u32[]{:S(2)}) collective-permute-start(bf16[2,1024,512]{2,1,0:T(8,128)(2,1)} %pad_maximum_fusion.3.near_w), channel_id=1, source_target_pairs={{0,4},{4,0},{1,5},{5,1},{2,6},{6,2},{3,7},{7,3}} | collective-permute-start | bytes 6291464 | tf_op jit(solution)/shard_map/ppermute | solution.py:17
  207.9 35.5 %collective-permute-start.30 = (bf16[2560,256]{1,0:T(8,128)(2,1)}, bf16[2560,256]{1,0:T(8,128)(2,1)S(1)}, u32[]{:S(2)}, u32[]{:S(2)}) collective-permute-start(bf16[2560,256]{1,0:T(8,128)(2,1)} %pad_maximum_fusion.6), channel_id=1, source_target_pairs={{0,1},{1,0},{2,3},{3,2},{4,5},{5,4},{6,7},{7,6}} | collective-permute-start | bytes 3932168 | tf_op jit(solution)/shard_map/ppermute | solution.py:17
  208.4 37.3 %collective-permute-start.26 = (bf16[2048,512]{1,0:T(8,128)(2,1)}, bf16[2048,512]{1,0:T(8,128)(2,1)}, u32[]{:S(2)}, u32[]{:S(2)}) collective-permute-start(bf16[2048,512]{1,0:T(8,128)(2,1)} %glu.4.refs_0_), channel_id=1, source_target_pairs={{0,1},{1,0},{2,3},{3,2},{4,5},{5,4},{6,7},{7,6}} | collective-permute-start | bytes 6291464 | tf_op jit(solution)/shard_map/ppermute | solution.py:17
  208.4 27.9 %collective-permute-start.23 = (bf16[512,512]{1,0:T(8,128)(2,1)}, bf16[512,512]{1,0:T(8,128)(2,1)}, u32[]{:S(2)}, u32[]{:S(2)}) collective-permute-start(bf16[512,512]{1,0:T(8,128)(2,1)} %get-tuple-element.30), channel_id=1, source_target_pairs={{0,1},{1,0},{2,3},{3,2},{4,5},{5,4},{6,7},{7,6}} | collective-permute-start | bytes 1572872 | tf_op jit(solution)/shard_map/ppermute | solution.py:17
  209.0 29.5 %collective-permute-start.25 = (bf16[2,512,512]{2,1,0:T(8,128)(2,1)S(1)}, bf16[2,512,512]{2,1,0:T(8,128)(2,1)S(1)}, u32[]{:S(2)}, u32[]{:S(2)}) collective-permute-start(bf16[2,512,512]{2,1,0:T(8,128)(2,1)S(1)} %pad_maximum_fusion.8), channel_id=1, source_target_pairs={{0,2},{2,0},{1,3},{3,1},{4,6},{6,4},{5,7},{7,5}} | collective-permute-start | bytes 3145736 | tf_op jit(solution)/shard_map/ppermute | solution.py:17
  223.2 25.0 %collective-permute-start.27 = (bf16[2048,512]{1,0:T(8,128)(2,1)}, bf16[2048,512]{1,0:T(8,128)(2,1)}, u32[]{:S(2)}, u32[]{:S(2)}) collective-permute-start(bf16[2048,512]{1,0:T(8,128)(2,1)} %glu.5.refs_1_), channel_id=1, source_target_pairs={{0,1},{1,0},{2,3},{3,2},{4,5},{5,4},{6,7},{7,6}} | collective-permute-start | bytes 6291464 | tf_op jit(solution)/shard_map/ppermute | solution.py:17
  243.5 47.9 %collective-permute-start.12 = (bf16[2,1024,512]{2,1,0:T(8,128)(2,1)}, bf16[2,1024,512]{2,1,0:T(8,128)(2,1)}, u32[]{:S(2)}, u32[]{:S(2)}) collective-permute-start(bf16[2,1024,512]{2,1,0:T(8,128)(2,1)} %pad_maximum_fusion.near_w), channel_id=1, source_target_pairs={{0,4},{4,0},{1,5},{5,1},{2,6},{6,2},{3,7},{7,3}} | collective-permute-start | bytes 6291464 | tf_op jit(solution)/shard_map/ppermute | solution.py:17
  304.5 31.5 %collective-permute-start.36 = (bf16[2560,256]{1,0:T(8,128)(2,1)}, bf16[2560,256]{1,0:T(8,128)(2,1)}, u32[]{:S(2)}, u32[]{:S(2)}) collective-permute-start(bf16[2560,256]{1,0:T(8,128)(2,1)} %pad_maximum_fusion.6), channel_id=1, source_target_pairs={{0,4},{4,0},{1,5},{5,1},{2,6},{6,2},{3,7},{7,3}} | collective-permute-start | bytes 3932168 | tf_op jit(solution)/shard_map/ppermute | solution.py:17
  336.1 71.5 %collective-permute-start.41 = (bf16[2560,256]{1,0:T(8,128)(2,1)}, bf16[2560,256]{1,0:T(8,128)(2,1)}, u32[]{:S(2)}, u32[]{:S(2)}) collective-permute-start(bf16[2560,256]{1,0:T(8,128)(2,1)} %pad_maximum_fusion.7), channel_id=1, source_target_pairs={{0,4},{4,0},{1,5},{5,1},{2,6},{6,2},{3,7},{7,3}} | collective-permute-start | bytes 3932168 | tf_op jit(solution)/shard_map/ppermute | solution.py:17
  336.3 67.0 %collective-permute-start.33 = (f32[1024,256]{1,0:T(8,128)}, f32[1024,256]{1,0:T(8,128)}, u32[]{:S(2)}, u32[]{:S(2)}) collective-permute-start(f32[1024,256]{1,0:T(8,128)} %mix.14), channel_id=1, source_target_pairs={{0,2},{2,0},{1,3},{3,1},{4,6},{6,4},{5,7},{7,5}} | collective-permute-start | bytes 3145736 | tf_op jit(solution)/shard_map/ppermute | solution.py:17
  340.0 42.1 %collective-permute-start.35 = (bf16[2560,128]{1,0:T(8,128)(2,1)}, bf16[2560,128]{1,0:T(8,128)(2,1)}, u32[]{:S(2)}, u32[]{:S(2)}) collective-permute-start(bf16[2560,128]{1,0:T(8,128)(2,1)} %get-tuple-element.64), channel_id=1, source_target_pairs={{0,4},{4,0},{1,5},{5,1},{2,6},{6,2},{3,7},{7,3}} | collective-permute-start | bytes 1966088 | tf_op jit(solution)/shard_map/ppermute | solution.py:17
  341.7 54.0 %collective-permute-start.34 = (bf16[2560,128]{1,0:T(8,128)(2,1)}, bf16[2560,128]{1,0:T(8,128)(2,1)}, u32[]{:S(2)}, u32[]{:S(2)}) collective-permute-start(bf16[2560,128]{1,0:T(8,128)(2,1)} %get-tuple-element.65), channel_id=1, source_target_pairs={{0,4},{4,0},{1,5},{5,1},{2,6},{6,2},{3,7},{7,3}} | collective-permute-start | bytes 1966088 | tf_op jit(solution)/shard_map/ppermute | solution.py:17
  407.5 26.4 %collective-permute-start.43 = (f32[2048,128]{1,0:T(8,128)}, f32[2048,128]{1,0:T(8,128)}, u32[]{:S(2)}, u32[]{:S(2)}) collective-permute-start(f32[2048,128]{1,0:T(8,128)} %mix.17), channel_id=1, source_target_pairs={{0,2},{2,0},{1,3},{3,1},{4,6},{6,4},{5,7},{7,5}} | collective-permute-start | bytes 3145736 | tf_op jit(solution)/shard_map/ppermute | solution.py:17
  408.7 47.7 %collective-permute-start.44 = (f32[2048,128]{1,0:T(8,128)}, f32[2048,128]{1,0:T(8,128)}, u32[]{:S(2)}, u32[]{:S(2)}) collective-permute-start(f32[2048,128]{1,0:T(8,128)} %mix.18), channel_id=1, source_target_pairs={{0,2},{2,0},{1,3},{3,1},{4,6},{6,4},{5,7},{7,5}} | collective-permute-start | bytes 3145736 | tf_op jit(solution)/shard_map/ppermute | solution.py:17
  412.3 66.1 %collective-permute-start.38 = (f32[1024,256]{1,0:T(8,128)}, f32[1024,256]{1,0:T(8,128)}, u32[]{:S(2)}, u32[]{:S(2)}) collective-permute-start(f32[1024,256]{1,0:T(8,128)} %mix.15), channel_id=1, source_target_pairs={{0,2},{2,0},{1,3},{3,1},{4,6},{6,4},{5,7},{7,5}} | collective-permute-start | bytes 3145736 | tf_op jit(solution)/shard_map/ppermute | solution.py:17
  413.4 31.1 %collective-permute-start.39 = (bf16[2560,128]{1,0:T(8,128)(2,1)}, bf16[2560,128]{1,0:T(8,128)(2,1)}, u32[]{:S(2)}, u32[]{:S(2)}) collective-permute-start(bf16[2560,128]{1,0:T(8,128)(2,1)} %get-tuple-element.63), channel_id=1, source_target_pairs={{0,4},{4,0},{1,5},{5,1},{2,6},{6,2},{3,7},{7,3}} | collective-permute-start | bytes 1966088 | tf_op jit(solution)/shard_map/ppermute | solution.py:17
  442.0 42.4 %collective-permute-start.45 = (bf16[2048,128]{1,0:T(8,128)(2,1)}, bf16[2048,128]{1,0:T(8,128)(2,1)}, u32[]{:S(2)}, u32[]{:S(2)}) collective-permute-start(bf16[2048,128]{1,0:T(8,128)(2,1)} %mix.21), channel_id=1, source_target_pairs={{0,4},{4,0},{1,5},{5,1},{2,6},{6,2},{3,7},{7,3}} | collective-permute-start | bytes 1572872 | tf_op jit(solution)/shard_map/ppermute | solution.py:17
  464.4 21.9 %collective-permute-start.46 = (bf16[2048,128]{1,0:T(8,128)(2,1)}, bf16[2048,128]{1,0:T(8,128)(2,1)}, u32[]{:S(2)}, u32[]{:S(2)}) collective-permute-start(bf16[2048,128]{1,0:T(8,128)(2,1)} %mix.22), channel_id=1, source_target_pairs={{0,4},{4,0},{1,5},{5,1},{2,6},{6,2},{3,7},{7,3}} | collective-permute-start | bytes 1572872 | tf_op jit(solution)/shard_map/ppermute | solution.py:17
  (36 other events, 279.5 us)

commit v9 on v8

--- a/solution.py
+++ b/solution.py
@@ -204,7 +204,7 @@
     out_ref[...] = total.astype(out_ref.dtype)
 
 
-def mix(terms, adds=(), dtype=F32, start=0, tokens=None, col=0):
+def mix(terms, adds=(), dtype=F32, start=0, tokens=None, col=0, room=0):
     ws, plan = [], []
     for _, w, row in terms:
         found = [i for i, v in enumerate(ws) if v is w]
@@ -226,7 +226,7 @@
         out_specs=pl.BlockSpec((blk, cols), lambda i: (i, 0)),
         out_shape=jax.ShapeDtypeStruct((tokens, cols), dtype),
         cost_estimate=pl.CostEstimate(flops=2 * tokens * depth * cols, bytes_accessed=2 * depth * (tokens + cols), transcendentals=0),
-        compiler_params=pltpu.CompilerParams(vmem_limit_bytes=67043328),
+        compiler_params=pltpu.CompilerParams(vmem_limit_bytes=67043328 - room),
         name="mix",
     )(*lhs, *ws, *adds)
 
@@ -362,7 +362,7 @@
             r_far.append(swap_x(held))
 
         def finish_own(i):
-            return mix(terms(blocks[0][0], same_far, late), [pre_same, r_own[i]], BF16, *split[i])
+            return mix(terms(blocks[0][0], same_far, late), [pre_same, r_own[i]], BF16, *split[i], room=i * 640 * 1024)
 
         out = jnp.zeros((2, half, width), BF16)
         r_own[0] = tie(r_own[0], held)
@@ -375,9 +375,9 @@
             out_far.append(swap_y(held))
         r_own[1] = tie(r_own[1], held)
         held = finish_own(1)
+        out = lax.dynamic_update_slice(out, out_far[0][None], (1 - yi, 0, 0))
         out = lax.dynamic_update_slice(out, held[None], (yi, split[1][0], 0))
-        for i, part in enumerate(out_far):
-            out = lax.dynamic_update_slice(out, part[None], (1 - yi, 0, i * narrow))
+        out = lax.dynamic_update_slice(out, out_far[1][None], (1 - yi, 0, narrow))
         return out.reshape(batch, new, width), k_next, v_next
 
     row_spec = P("dp", None, ("tx", "tyz"))

time: 489 us -> 488 us (level)
  no operation moved by 1% of the time
where the time goes in v9:
time: 488 us; the launch traced here: 487 us
  Pallas kernels  205 us (42%)
  waiting for transfers between devices  188 us (39%)
  local copies, waits for them, and re-layouts  31.3 us (6%)
  starting transfers between devices  31.2 us (6%)
  other arithmetic  27.7 us (6%)
    ppermute x47, waiting for transfers between devices, swap(): return lambda a: lax.ppermute(a, axis, pairs)  188 us
    pallas_call x12, Pallas kernels, mix(): pl.pallas_call(functools.partial(mix_kernel, plan, len(lhs), len(ws)), gr...  86.1 us
    pallas_call x4, Pallas kernels, glu(): pl.pallas_call(glu_kernel, grid=(tokens // blk,), in_specs=[pl.BlockSpec(...  52.8 us
    pallas_call x1, Pallas kernels, attention(): pl.pallas_call(attn_kernel, grid_spec=pltpu.PrefetchScalarGridSpec(num_sc...  44.5 us
    ppermute x47, starting transfers between devices, swap(): return lambda a: lax.ppermute(a, axis, pairs)  31.2 us
    pallas_call x1, Pallas kernels, layer_norm(): pl.pallas_call(norm_kernel, grid_spec=pltpu.PrefetchScalarGridSpec(num_sc...  13 us
    another operation x4, other arithmetic, local_layer(): jnp.stack([w[:, j * cw:(j + 1) * cw] for w in (w_gate, w_up)])  11.1 us
  transfers between devices with their start and end apart: 47, of which 16 were waited for; matrix products, arithmetic and copies ran while one was open for 12% of the time, Pallas kernels for 39%

profile of v9, /device:TPU:0, one launch (start us, length us, event | category | flops | bytes accessed | tf_op | source)
XLA Modules:
  0.0 487.1 jit_solution(1565588250376406636)
XLA Ops:
  11.2 6.1 %slice_bitcast_fusion = (bf16[1,1024,512]{2,1,0:T(8,128)(2,1)S(1)}, bf16[1,1024,512]{2,1,0:T(8,128)(2,1)S(1)}, bf16[1,1024,512]{2,1,0:T(8,128)(2,1)}, bf16[1,102...) fusion(bf16[1024,2048]{1,0:T(8,128)(2,1)} %param.21, ...), kind=kLoop, calls=%fused_computation.27 | loop fusion | bytes 16777216 | tf_op jit(solution)/shard_map/stack | solution.py:301
  23.8 8.6 %collective-permute-done.9 = f32[1,256]{1,0:T(1,128)S(1)} collective-permute-done((f32[1,256]{1,0:T(1,128)S(1)}, f32[1,256]{1,0:T(1,128)S(1)}, u32[]{:S(2)}, u32[]{:S(2)}) %collective-permute-start.9) | collective-permute-done | bytes 1056 | tf_op jit(solution)/shard_map/ppermute | solution.py:17
  35.4 5.4 %collective-permute-done.10 = f32[2,256]{1,0:T(2,128)S(1)} collective-permute-done((f32[2,256]{1,0:T(2,128)S(1)}, f32[2,256]{1,0:T(2,128)S(1)}, u32[]{:S(2)}, u32[]{:S(2)}) %collective-permute-start.10) | collective-permute-done | bytes 2080 | tf_op jit(solution)/shard_map/ppermute | solution.py:17
  45.9 5.2 %collective-permute-done.4 = bf16[1024,256]{1,0:T(8,128)(2,1)S(1)} collective-permute-done((bf16[1024,256]{1,0:T(8,128)(2,1)}, bf16[1024,256]{1,0:T(8,128)(2,1)S(1)}, u32[]{:S(2)}, u32[]{:S(2)}) %collective-permute-start.4) | collective-permute-done | bytes 524320 | tf_op jit(solution)/shard_map/ppermute | solution.py:17
  52.5 37.2 %collective-permute-done.19 = bf16[256,256]{1,0:T(8,128)(2,1)S(1)} collective-permute-done((bf16[256,256]{1,0:T(8,128)(2,1)S(1)}, bf16[256,256]{1,0:T(8,128)(2,1)S(1)}, u32[]{:S(2)}, u32[]{:S(2)}) %collective-permute-start.19) | collective-permute-done | bytes 131104 | tf_op jit(solution)/shard_map/ppermute | solution.py:17
  97.4 13.0 %norm.1.h_ref = bf16[2048,2048]{1,0:T(8,128)(2,1)} custom-call(s32[8]{0:T(128)} %stack.140.offs_ref, bf16[2048,256]{1,0:T(8,128)(2,1)} %copy-done.2, bf16[2048,256]{1,0:T(8,128)(2,1)} %copy-done.5, bf16[2048,256]{1,0:T(8,128)(2,1)} %collective-permute-done.2.refs_2_, bf16[2048,256]{1,0:T(8,128)(2,1)} %constant_dynamic-update-slice_fusion.2.refs_3_, ...), custom_call_target="tpu_custom_call" | custom-call | flops 83886080 | bytes 16777216 | tf_op jit(solution)/shard_map/norm/pallas_call | solution.py:47
  110.4 6.1 %collective-permute-done.15.refs_1_ = bf16[1024,512]{1,0:T(8,128)(2,1)S(1)} collective-permute-done((bf16[1024,512]{1,0:T(8,128)(2,1)}, bf16[1024,512]{1,0:T(8,128)(2,1)S(1)}, u32[]{:S(2)}, u32[]{:S(2)}) %collective-permute-start.15) | collective-permute-done | bytes 1048608 | tf_op jit(solution)/shard_map/ppermute | solution.py:17
  117.4 8.7 %project.1 = bf16[2048,512]{1,0:T(8,128)(2,1)} custom-call(bf16[2048,2048]{1,0:T(8,128)(2,1)} %norm.1.h_ref, bf16[1024,512]{1,0:T(8,128)(2,1)} %refs_0_.1, bf16[1024,512]{1,0:T(8,128)(2,1)} %copy-done.19), custom_call_target="tpu_custom_call" | custom-call | flops 4294967296 | bytes 10485760 | tf_op jit(solution)/shard_map/project/pallas_call | solution.py:185
  131.3 13.2 %glu.4.refs_0_ = bf16[2048,512]{1,0:T(8,128)(2,1)} custom-call(bf16[2048,2048]{1,0:T(8,128)(2,1)} %norm.1.h_ref, bf16[2,1024,512]{2,1,0:T(8,128)(2,1)} %pad_maximum_fusion.1.near_w, bf16[2,1024,512]{2,1,0:T(8,128)(2,1)} %collective-permute-done.13.far_w), custom_call_target="tpu_custom_call" | custom-call | flops 8589934592 | bytes 14680064 | tf_op jit(solution)/shard_map/glu/pallas_call | solution.py:161
  144.5 6.4 %collective-permute-done.16 = bf16[2,512,512]{2,1,0:T(8,128)(2,1)S(1)} collective-permute-done((bf16[2,512,512]{2,1,0:T(8,128)(2,1)S(1)}, bf16[2,512,512]{2,1,0:T(8,128)(2,1)S(1)}, u32[]{:S(2)}, u32[]{:S(2)}) %collective-permute-start.16) | collective-permute-done | bytes 1048608 | tf_op jit(solution)/shard_map/ppermute | solution.py:17
  159.9 44.5 %attn.1 = (bf16[512,512]{1,0:T(8,128)(2,1)}, bf16[512,512]{1,0:T(8,128)(2,1)}, bf16[512,512]{1,0:T(8,128)(2,1)}, bf16[512,512]{1,0:T(8,128)(2,1)}, bf16[8,2048,1...) custom-call(s32[8]{0:T(128)} %len_ref.1, bf16[512,512]{1,0:T(8,128)(2,1)} %get-tuple-element.59.q0, ...), custom_call_target="tpu_custom_call" | custom-call | flops 17179869184 | bytes 16777216 | tf_op jit(solution)/shard_map/attn/pallas_call | solution.py:131
  210.0 13.2 %glu.5.refs_1_ = bf16[2048,512]{1,0:T(8,128)(2,1)} custom-call(bf16[2048,2048]{1,0:T(8,128)(2,1)} %norm.1.h_ref, bf16[2,1024,512]{2,1,0:T(8,128)(2,1)} %pad_maximum_fusion.2.near_w, bf16[2,1024,512]{2,1,0:T(8,128)(2,1)} %collective-permute-done.14.far_w), custom_call_target="tpu_custom_call" | custom-call | flops 8589934592 | bytes 14680064 | tf_op jit(solution)/shard_map/glu/pallas_call | solution.py:161
  223.2 13.2 %glu.6.refs_2_ = bf16[2048,512]{1,0:T(8,128)(2,1)} custom-call(bf16[2048,2048]{1,0:T(8,128)(2,1)} %norm.1.h_ref, bf16[2,1024,512]{2,1,0:T(8,128)(2,1)} %pad_maximum_fusion.3.near_w, bf16[2,1024,512]{2,1,0:T(8,128)(2,1)} %collective-permute-done.22.far_w), custom_call_target="tpu_custom_call" | custom-call | flops 8589934592 | bytes 14680064 | tf_op jit(solution)/shard_map/glu/pallas_call | solution.py:161
  248.1 10.8 %mix.12.refs_4_ = f32[2048,256]{1,0:T(8,128)} custom-call(bf16[2048,512]{1,0:T(8,128)(2,1)} %glu.4.refs_0_, bf16[2048,512]{1,0:T(8,128)(2,1)} %glu.5.refs_1_, bf16[2048,512]{1,0:T(8,128)(2,1)} %glu.6.refs_2_, bf16[2048,512]{1,0:T(8,128)(2,1)} %bitcast.66, bf16[2048,512]{1,0:T(8,128)(2,1)} %collective-permute-done.26.refs_4_.refs_0_, ...), custom_call_target="tpu_custom_call" | custom-call | flops 4294967296 | bytes 18874368 | tf_op jit(solution)/shard_map/mix/pallas_call | solution.py:222
  258.9 11.1 %mix.13.refs_4_ = f32[2048,256]{1,0:T(8,128)} custom-call(bf16[2048,512]{1,0:T(8,128)(2,1)} %glu.4.refs_0_, bf16[2048,512]{1,0:T(8,128)(2,1)} %glu.5.refs_1_, bf16[2048,512]{1,0:T(8,128)(2,1)} %glu.6.refs_2_, bf16[2048,512]{1,0:T(8,128)(2,1)} %bitcast.67, bf16[2048,512]{1,0:T(8,128)(2,1)} %collective-permute-done.26.refs_4_.refs_0_, ...), custom_call_target="tpu_custom_call" | custom-call | flops 4294967296 | bytes 18874368 | tf_op jit(solution)/shard_map/mix/pallas_call | solution.py:222
  270.0 21.3 %collective-permute-done.12.far_w = bf16[2,1024,512]{2,1,0:T(8,128)(2,1)} collective-permute-done((bf16[2,1024,512]{2,1,0:T(8,128)(2,1)}, bf16[2,1024,512]{2,1,0:T(8,128)(2,1)}, u32[]{:S(2)}, u32[]{:S(2)}) %collective-permute-start.12) | collective-permute-done | bytes 2097184 | tf_op jit(solution)/shard_map/ppermute | solution.py:17
  291.3 13.2 %glu.7.refs_0_.refs_3_ = bf16[2048,512]{1,0:T(8,128)(2,1)} custom-call(bf16[2048,2048]{1,0:T(8,128)(2,1)} %norm.1.h_ref, bf16[2,1024,512]{2,1,0:T(8,128)(2,1)} %pad_maximum_fusion.near_w, bf16[2,1024,512]{2,1,0:T(8,128)(2,1)} %collective-permute-done.12.far_w), custom_call_target="tpu_custom_call" | custom-call | flops 8589934592 | bytes 14680064 | tf_op jit(solution)/shard_map/glu/pallas_call | solution.py:161
  304.8 4.2 collective-permute-done.32.refs_1_.refs_3_
  317.3 18.8 %collective-permute-done.36 = bf16[2560,256]{1,0:T(8,128)(2,1)} collective-permute-done((bf16[2560,256]{1,0:T(8,128)(2,1)}, bf16[2560,256]{1,0:T(8,128)(2,1)}, u32[]{:S(2)}, u32[]{:S(2)}) %collective-permute-start.36) | collective-permute-done | bytes 1310752 | tf_op jit(solution)/shard_map/ppermute | solution.py:17
  342.0 7.9 %mix.16.refs_6_ = f32[2048,256]{1,0:T(8,128)} custom-call(bf16[2048,512]{1,0:T(8,128)(2,1)} %collective-permute-done.26.refs_4_.refs_0_, bf16[2048,512]{1,0:T(8,128)(2,1)} %collective-permute-done.27.refs_5_.refs_1_, bf16[2048,512]{1,0:T(8,128)(2,1)} %collective-permute-done.28.refs_6_.refs_2_, bf16[2048,512]{1,0:T(8,128)(2,1)} %collective-permute-done.32.refs_1_.refs_3_, ...), custom_call_target="tpu_custom_call" | custom-call | flops 2684354560 | bytes 11796480 | tf_op jit(solution)/shard_map/mix/pallas_call | solution.py:222
  349.9 32.1 %collective-permute-done.35.refs_5_ = bf16[2560,128]{1,0:T(8,128)(2,1)} collective-permute-done((bf16[2560,128]{1,0:T(8,128)(2,1)}, bf16[2560,128]{1,0:T(8,128)(2,1)}, u32[]{:S(2)}, u32[]{:S(2)}) %collective-permute-start.35) | collective-permute-done | bytes 655392 | tf_op jit(solution)/shard_map/ppermute | solution.py:17
  382.1 7.7 %mix.17 = f32[2048,128]{1,0:T(8,128)} custom-call(bf16[2048,512]{1,0:T(8,128)(2,1)} %glu.4.refs_0_, bf16[2048,512]{1,0:T(8,128)(2,1)} %glu.5.refs_1_, bf16[2048,512]{1,0:T(8,128)(2,1)} %glu.6.refs_2_, bf16[2048,512]{1,0:T(8,128)(2,1)} %glu.7.refs_0_.refs_3_, bf16[2048,512]{1,0:T(8,128)(2,1)} %bitcast.68, bf16[2560,128]{1,0:T(8,128)(2,1)} %collective-permute-done.35.refs_5_, ...), custom_call_target="tpu_custom_call" | custom-call | flops 1342177280 | bytes 11141120 | tf_op jit(solution)/shard_map/mix/pallas_call | solution.py:222
  389.8 5.9 %collective-permute-done.34.refs_5_ = bf16[2560,128]{1,0:T(8,128)(2,1)} collective-permute-done((bf16[2560,128]{1,0:T(8,128)(2,1)}, bf16[2560,128]{1,0:T(8,128)(2,1)}, u32[]{:S(2)}, u32[]{:S(2)}) %collective-permute-start.34) | collective-permute-done | bytes 655392 | tf_op jit(solution)/shard_map/ppermute | solution.py:17
  395.6 7.7 %mix.18 = f32[2048,128]{1,0:T(8,128)} custom-call(bf16[2048,512]{1,0:T(8,128)(2,1)} %glu.4.refs_0_, bf16[2048,512]{1,0:T(8,128)(2,1)} %glu.5.refs_1_, bf16[2048,512]{1,0:T(8,128)(2,1)} %glu.6.refs_2_, bf16[2048,512]{1,0:T(8,128)(2,1)} %glu.7.refs_0_.refs_3_, bf16[2048,512]{1,0:T(8,128)(2,1)} %bitcast.69, bf16[2560,128]{1,0:T(8,128)(2,1)} %collective-permute-done.34.refs_5_, ...), custom_call_target="tpu_custom_call" | custom-call | flops 1342177280 | bytes 11141120 | tf_op jit(solution)/shard_map/mix/pallas_call | solution.py:222
  403.3 4.2 mix.19
  415.1 8.3 %mix.20.refs_6_ = f32[2048,256]{1,0:T(8,128)} custom-call(bf16[2048,512]{1,0:T(8,128)(2,1)} %collective-permute-done.26.refs_4_.refs_0_, bf16[2048,512]{1,0:T(8,128)(2,1)} %collective-permute-done.27.refs_5_.refs_1_, bf16[2048,512]{1,0:T(8,128)(2,1)} %collective-permute-done.28.refs_6_.refs_2_, bf16[2048,512]{1,0:T(8,128)(2,1)} %collective-permute-done.32.refs_1_.refs_3_, ...), custom_call_target="tpu_custom_call" | custom-call | flops 2684354560 | bytes 11796480 | tf_op jit(solution)/shard_map/mix/pallas_call | solution.py:222
  423.5 5.5 %collective-permute-done.38.refs_5_ = bf16[2560,128]{1,0:T(8,128)(2,1)} collective-permute-done((bf16[2560,128]{1,0:T(8,128)(2,1)}, bf16[2560,128]{1,0:T(8,128)(2,1)}, u32[]{:S(2)}, u32[]{:S(2)}) %collective-permute-start.38) | collective-permute-done | bytes 655392 | tf_op jit(solution)/shard_map/ppermute | solution.py:17
  429.0 4.9 %collective-permute-done.41.refs_7_ = f32[2048,128]{1,0:T(8,128)} collective-permute-done((f32[2048,128]{1,0:T(8,128)}, f32[2048,128]{1,0:T(8,128)}, u32[]{:S(2)}, u32[]{:S(2)}) %collective-permute-start.41) | collective-permute-done | bytes 1048608 | tf_op jit(solution)/shard_map/ppermute | solution.py:17
  433.9 8.0 %mix.21 = bf16[2048,128]{1,0:T(8,128)(2,1)} custom-call(bf16[2048,512]{1,0:T(8,128)(2,1)} %glu.4.refs_0_, bf16[2048,512]{1,0:T(8,128)(2,1)} %glu.5.refs_1_, bf16[2048,512]{1,0:T(8,128)(2,1)} %glu.6.refs_2_, bf16[2048,512]{1,0:T(8,128)(2,1)} %glu.7.refs_0_.refs_3_, bf16[2048,512]{1,0:T(8,128)(2,1)} %bitcast.70, ...), custom_call_target="tpu_custom_call" | custom-call | flops 1342177280 | bytes 11141120 | tf_op jit(solution)/shard_map/mix/pallas_call | solution.py:222
  444.5 11.9 %collective-permute-done.45.refs_7_ = f32[2048,128]{1,0:T(8,128)} collective-permute-done((f32[2048,128]{1,0:T(8,128)}, f32[2048,128]{1,0:T(8,128)}, u32[]{:S(2)}, u32[]{:S(2)}) %collective-permute-start.45) | collective-permute-done | bytes 1048608 | tf_op jit(solution)/shard_map/ppermute | solution.py:17
  456.4 8.0 %mix.22 = bf16[2048,128]{1,0:T(8,128)(2,1)} custom-call(bf16[2048,512]{1,0:T(8,128)(2,1)} %glu.4.refs_0_, bf16[2048,512]{1,0:T(8,128)(2,1)} %glu.5.refs_1_, bf16[2048,512]{1,0:T(8,128)(2,1)} %glu.6.refs_2_, bf16[2048,512]{1,0:T(8,128)(2,1)} %glu.7.refs_0_.refs_3_, bf16[2048,512]{1,0:T(8,128)(2,1)} %bitcast.71, ...), custom_call_target="tpu_custom_call" | custom-call | flops 1342177280 | bytes 11141120 | tf_op jit(solution)/shard_map/mix/pallas_call | solution.py:222
  464.7 13.7 %collective-permute-done.43.refs_5_ = f32[1024,256]{1,0:T(8,128)} collective-permute-done((f32[1024,256]{1,0:T(8,128)}, f32[1024,256]{1,0:T(8,128)}, u32[]{:S(2)}, u32[]{:S(2)}) %collective-permute-start.43) | collective-permute-done | bytes 1048608 | tf_op jit(solution)/shard_map/ppermute | solution.py:17
  (173 shorter events, 100.0 us)
Async XLA Ops:
  2.1 87.6 %collective-permute-start.2 = (bf16[2048,256]{1,0:T(8,128)(2,1)S(1)}, bf16[2048,256]{1,0:T(8,128)(2,1)}, u32[]{:S(2)}, u32[]{:S(2)}) collective-permute-start(bf16[2048,256]{1,0:T(8,128)(2,1)S(1)} %dynamic-slice_bitcast_fusion.1.refs_0_.refs_10_), channel_id=1, source_target_pairs={{0,2},{2,0},{1,3},{3,1},{4,6},{6,4},{5,7},{7,5}} | collective-permute-start | bytes 3145736 | tf_op jit(solution)/shard_map/ppermute | solution.py:17
  5.4 84.8 %collective-permute-start.5 = (bf16[2048,256]{1,0:T(8,128)(2,1)S(1)}, bf16[2048,256]{1,0:T(8,128)(2,1)}, u32[]{:S(2)}, u32[]{:S(2)}) collective-permute-start(bf16[2048,256]{1,0:T(8,128)(2,1)S(1)} %dynamic-slice_bitcast_fusion.1.refs_0_.refs_10_), channel_id=1, source_target_pairs={{0,1},{1,0},{2,3},{3,2},{4,5},{5,4},{6,7},{7,6}} | collective-permute-start | bytes 3145736 | tf_op jit(solution)/shard_map/ppermute | solution.py:17
  8.0 24.7 %collective-permute-start.1 = (bf16[1024,256]{1,0:T(8,128)(2,1)}, bf16[1024,256]{1,0:T(8,128)(2,1)}, u32[]{:S(2)}, u32[]{:S(2)}) collective-permute-start(bf16[1024,256]{1,0:T(8,128)(2,1)} %get-tuple-element.60), channel_id=1, source_target_pairs={{0,4},{4,0},{1,5},{5,1},{2,6},{6,2},{3,7},{7,3}} | collective-permute-start | bytes 1572872 | tf_op jit(solution)/shard_map/ppermute | solution.py:17
  8.5 23.9 %collective-permute-start.9 = (f32[1,256]{1,0:T(1,128)S(1)}, f32[1,256]{1,0:T(1,128)S(1)}, u32[]{:S(2)}, u32[]{:S(2)}) collective-permute-start(f32[1,256]{1,0:T(1,128)S(1)} %bitcast.84), channel_id=1, source_target_pairs={{0,4},{4,0},{1,5},{5,1},{2,6},{6,2},{3,7},{7,3}} | collective-permute-start | bytes 3080 | tf_op jit(solution)/shard_map/ppermute | solution.py:17
  23.2 21.8 %collective-permute-start.3 = (bf16[1024,256]{1,0:T(8,128)(2,1)}, bf16[1024,256]{1,0:T(8,128)(2,1)S(1)}, u32[]{:S(2)}, u32[]{:S(2)}) collective-permute-start(bf16[1024,256]{1,0:T(8,128)(2,1)} %collective-permute-done), channel_id=1, source_target_pairs={{0,2},{2,0},{1,3},{3,1},{4,6},{6,4},{5,7},{7,5}} | collective-permute-start | bytes 1572872 | tf_op jit(solution)/shard_map/ppermute | solution.py:17
  40.7 90.6 %collective-permute-start.13 = (bf16[2,1024,512]{2,1,0:T(8,128)(2,1)}, bf16[2,1024,512]{2,1,0:T(8,128)(2,1)}, u32[]{:S(2)}, u32[]{:S(2)}) collective-permute-start(bf16[2,1024,512]{2,1,0:T(8,128)(2,1)} %pad_maximum_fusion.1.near_w), channel_id=1, source_target_pairs={{0,4},{4,0},{1,5},{5,1},{2,6},{6,2},{3,7},{7,3}} | collective-permute-start | bytes 6291464 | tf_op jit(solution)/shard_map/ppermute | solution.py:17
  45.0 44.7 %collective-permute-start.19 = (bf16[256,256]{1,0:T(8,128)(2,1)S(1)}, bf16[256,256]{1,0:T(8,128)(2,1)S(1)}, u32[]{:S(2)}, u32[]{:S(2)}) collective-permute-start(bf16[256,256]{1,0:T(8,128)(2,1)S(1)} %constant_dynamic-slice_fusion.8), channel_id=1, source_target_pairs={{0,4},{4,0},{1,5},{5,1},{2,6},{6,2},{3,7},{7,3}} | collective-permute-start | bytes 393224 | tf_op jit(solution)/shard_map/ppermute | solution.py:17
  52.3 43.1 %collective-permute-start.6 = (bf16[2048,256]{1,0:T(8,128)(2,1)S(1)}, bf16[2048,256]{1,0:T(8,128)(2,1)}, u32[]{:S(2)}, u32[]{:S(2)}) collective-permute-start(bf16[2048,256]{1,0:T(8,128)(2,1)S(1)} %constant_dynamic-update-slice_fusion.refs_1_.refs_6_), channel_id=1, source_target_pairs={{0,1},{1,0},{2,3},{3,2},{4,5},{5,4},{6,7},{7,6}} | collective-permute-start | bytes 3145736 | tf_op jit(solution)/shard_map/ppermute | solution.py:17
  90.2 26.2 %collective-permute-start.15 = (bf16[1024,512]{1,0:T(8,128)(2,1)}, bf16[1024,512]{1,0:T(8,128)(2,1)S(1)}, u32[]{:S(2)}, u32[]{:S(2)}) collective-permute-start(bf16[1024,512]{1,0:T(8,128)(2,1)} %refs_0_.1), channel_id=1, source_target_pairs={{0,4},{4,0},{1,5},{5,1},{2,6},{6,2},{3,7},{7,3}} | collective-permute-start | bytes 3145736 | tf_op jit(solution)/shard_map/ppermute | solution.py:17
  95.4 113.1 %collective-permute-start.14 = (bf16[2,1024,512]{2,1,0:T(8,128)(2,1)}, bf16[2,1024,512]{2,1,0:T(8,128)(2,1)}, u32[]{:S(2)}, u32[]{:S(2)}) collective-permute-start(bf16[2,1024,512]{2,1,0:T(8,128)(2,1)} %pad_maximum_fusion.2.near_w), channel_id=1, source_target_pairs={{0,4},{4,0},{1,5},{5,1},{2,6},{6,2},{3,7},{7,3}} | collective-permute-start | bytes 6291464 | tf_op jit(solution)/shard_map/ppermute | solution.py:17
  95.9 33.1 %collective-permute-start.20 = (bf16[256,256]{1,0:T(8,128)(2,1)S(1)}, bf16[256,256]{1,0:T(8,128)(2,1)S(1)}, u32[]{:S(2)}, u32[]{:S(2)}) collective-permute-start(bf16[256,256]{1,0:T(8,128)(2,1)S(1)} %collective-permute-done.19), channel_id=1, source_target_pairs={{0,2},{2,0},{1,3},{3,1},{4,6},{6,4},{5,7},{7,5}} | collective-permute-start | bytes 393224 | tf_op jit(solution)/shard_map/ppermute | solution.py:17
  127.5 23.3 %collective-permute-start.16 = (bf16[2,512,512]{2,1,0:T(8,128)(2,1)S(1)}, bf16[2,512,512]{2,1,0:T(8,128)(2,1)S(1)}, u32[]{:S(2)}, u32[]{:S(2)}) collective-permute-start(bf16[2,512,512]{2,1,0:T(8,128)(2,1)S(1)} %dynamic-slice_bitcast_fusion), channel_id=1, source_target_pairs={{0,2},{2,0},{1,3},{3,1},{4,6},{6,4},{5,7},{7,5}} | collective-permute-start | bytes 3145736 | tf_op jit(solution)/shard_map/ppermute | solution.py:17
  129.7 25.0 %collective-permute-start.21 = (bf16[2,256,256]{2,1,0:T(8,128)(2,1)}, bf16[2,256,256]{2,1,0:T(8,128)(2,1)}, u32[]{:S(2)}, u32[]{:S(2)}) collective-permute-start(bf16[2,256,256]{2,1,0:T(8,128)(2,1)} %maximum_select_fusion.4), channel_id=1, source_target_pairs={{0,1},{1,0},{2,3},{3,2},{4,5},{5,4},{6,7},{7,6}} | collective-permute-start | bytes 786440 | tf_op jit(solution)/shard_map/ppermute | solution.py:17
  130.8 28.3 %collective-permute-start.17 = (bf16[512,512]{1,0:T(8,128)(2,1)}, bf16[512,512]{1,0:T(8,128)(2,1)}, u32[]{:S(2)}, u32[]{:S(2)}) collective-permute-start(bf16[512,512]{1,0:T(8,128)(2,1)} %get-tuple-element.58), channel_id=1, source_target_pairs={{0,1},{1,0},{2,3},{3,2},{4,5},{5,4},{6,7},{7,6}} | collective-permute-start | bytes 1572872 | tf_op jit(solution)/shard_map/ppermute | solution.py:17
  153.2 69.9 %collective-permute-start.22 = (bf16[2,1024,512]{2,1,0:T(8,128)(2,1)}, bf16[2,1024,512]{2,1,0:T(8,128)(2,1)}, u32[]{:S(2)}, u32[]{:S(2)}) collective-permute-start(bf16[2,1024,512]{2,1,0:T(8,128)(2,1)} %pad_maximum_fusion.3.near_w), channel_id=1, source_target_pairs={{0,4},{4,0},{1,5},{5,1},{2,6},{6,2},{3,7},{7,3}} | collective-permute-start | bytes 6291464 | tf_op jit(solution)/shard_map/ppermute | solution.py:17
  207.9 35.5 %collective-permute-start.30 = (bf16[2560,256]{1,0:T(8,128)(2,1)}, bf16[2560,256]{1,0:T(8,128)(2,1)S(1)}, u32[]{:S(2)}, u32[]{:S(2)}) collective-permute-start(bf16[2560,256]{1,0:T(8,128)(2,1)} %pad_maximum_fusion.6), channel_id=1, source_target_pairs={{0,1},{1,0},{2,3},{3,2},{4,5},{5,4},{6,7},{7,6}} | collective-permute-start | bytes 3932168 | tf_op jit(solution)/shard_map/ppermute | solution.py:17
  208.4 37.3 %collective-permute-start.26 = (bf16[2048,512]{1,0:T(8,128)(2,1)}, bf16[2048,512]{1,0:T(8,128)(2,1)}, u32[]{:S(2)}, u32[]{:S(2)}) collective-permute-start(bf16[2048,512]{1,0:T(8,128)(2,1)} %glu.4.refs_0_), channel_id=1, source_target_pairs={{0,1},{1,0},{2,3},{3,2},{4,5},{5,4},{6,7},{7,6}} | collective-permute-start | bytes 6291464 | tf_op jit(solution)/shard_map/ppermute | solution.py:17
  208.4 27.9 %collective-permute-start.23 = (bf16[512,512]{1,0:T(8,128)(2,1)}, bf16[512,512]{1,0:T(8,128)(2,1)}, u32[]{:S(2)}, u32[]{:S(2)}) collective-permute-start(bf16[512,512]{1,0:T(8,128)(2,1)} %get-tuple-element.30), channel_id=1, source_target_pairs={{0,1},{1,0},{2,3},{3,2},{4,5},{5,4},{6,7},{7,6}} | collective-permute-start | bytes 1572872 | tf_op jit(solution)/shard_map/ppermute | solution.py:17
  209.0 29.5 %collective-permute-start.25 = (bf16[2,512,512]{2,1,0:T(8,128)(2,1)S(1)}, bf16[2,512,512]{2,1,0:T(8,128)(2,1)S(1)}, u32[]{:S(2)}, u32[]{:S(2)}) collective-permute-start(bf16[2,512,512]{2,1,0:T(8,128)(2,1)S(1)} %pad_maximum_fusion.8), channel_id=1, source_target_pairs={{0,2},{2,0},{1,3},{3,1},{4,6},{6,4},{5,7},{7,5}} | collective-permute-start | bytes 3145736 | tf_op jit(solution)/shard_map/ppermute | solution.py:17
  223.2 25.0 %collective-permute-start.27 = (bf16[2048,512]{1,0:T(8,128)(2,1)}, bf16[2048,512]{1,0:T(8,128)(2,1)}, u32[]{:S(2)}, u32[]{:S(2)}) collective-permute-start(bf16[2048,512]{1,0:T(8,128)(2,1)} %glu.5.refs_1_), channel_id=1, source_target_pairs={{0,1},{1,0},{2,3},{3,2},{4,5},{5,4},{6,7},{7,6}} | collective-permute-start | bytes 6291464 | tf_op jit(solution)/shard_map/ppermute | solution.py:17
  243.5 47.9 %collective-permute-start.12 = (bf16[2,1024,512]{2,1,0:T(8,128)(2,1)}, bf16[2,1024,512]{2,1,0:T(8,128)(2,1)}, u32[]{:S(2)}, u32[]{:S(2)}) collective-permute-start(bf16[2,1024,512]{2,1,0:T(8,128)(2,1)} %pad_maximum_fusion.near_w), channel_id=1, source_target_pairs={{0,4},{4,0},{1,5},{5,1},{2,6},{6,2},{3,7},{7,3}} | collective-permute-start | bytes 6291464 | tf_op jit(solution)/shard_map/ppermute | solution.py:17
  304.5 31.5 %collective-permute-start.36 = (bf16[2560,256]{1,0:T(8,128)(2,1)}, bf16[2560,256]{1,0:T(8,128)(2,1)}, u32[]{:S(2)}, u32[]{:S(2)}) collective-permute-start(bf16[2560,256]{1,0:T(8,128)(2,1)} %pad_maximum_fusion.6), channel_id=1, source_target_pairs={{0,4},{4,0},{1,5},{5,1},{2,6},{6,2},{3,7},{7,3}} | collective-permute-start | bytes 3932168 | tf_op jit(solution)/shard_map/ppermute | solution.py:17
  336.1 71.5 %collective-permute-start.39 = (bf16[2560,256]{1,0:T(8,128)(2,1)}, bf16[2560,256]{1,0:T(8,128)(2,1)}, u32[]{:S(2)}, u32[]{:S(2)}) collective-permute-start(bf16[2560,256]{1,0:T(8,128)(2,1)} %pad_maximum_fusion.7), channel_id=1, source_target_pairs={{0,4},{4,0},{1,5},{5,1},{2,6},{6,2},{3,7},{7,3}} | collective-permute-start | bytes 3932168 | tf_op jit(solution)/shard_map/ppermute | solution.py:17
  336.3 67.0 %collective-permute-start.33 = (f32[1024,256]{1,0:T(8,128)}, f32[1024,256]{1,0:T(8,128)}, u32[]{:S(2)}, u32[]{:S(2)}) collective-permute-start(f32[1024,256]{1,0:T(8,128)} %mix.14), channel_id=1, source_target_pairs={{0,2},{2,0},{1,3},{3,1},{4,6},{6,4},{5,7},{7,5}} | collective-permute-start | bytes 3145736 | tf_op jit(solution)/shard_map/ppermute | solution.py:17
  340.0 42.1 %collective-permute-start.35 = (bf16[2560,128]{1,0:T(8,128)(2,1)}, bf16[2560,128]{1,0:T(8,128)(2,1)}, u32[]{:S(2)}, u32[]{:S(2)}) collective-permute-start(bf16[2560,128]{1,0:T(8,128)(2,1)} %get-tuple-element.64), channel_id=1, source_target_pairs={{0,4},{4,0},{1,5},{5,1},{2,6},{6,2},{3,7},{7,3}} | collective-permute-start | bytes 1966088 | tf_op jit(solution)/shard_map/ppermute | solution.py:17
  341.7 54.0 %collective-permute-start.34 = (bf16[2560,128]{1,0:T(8,128)(2,1)}, bf16[2560,128]{1,0:T(8,128)(2,1)}, u32[]{:S(2)}, u32[]{:S(2)}) collective-permute-start(bf16[2560,128]{1,0:T(8,128)(2,1)} %get-tuple-element.65), channel_id=1, source_target_pairs={{0,4},{4,0},{1,5},{5,1},{2,6},{6,2},{3,7},{7,3}} | collective-permute-start | bytes 1966088 | tf_op jit(solution)/shard_map/ppermute | solution.py:17
  407.5 26.4 %collective-permute-start.41 = (f32[2048,128]{1,0:T(8,128)}, f32[2048,128]{1,0:T(8,128)}, u32[]{:S(2)}, u32[]{:S(2)}) collective-permute-start(f32[2048,128]{1,0:T(8,128)} %mix.17), channel_id=1, source_target_pairs={{0,2},{2,0},{1,3},{3,1},{4,6},{6,4},{5,7},{7,5}} | collective-permute-start | bytes 3145736 | tf_op jit(solution)/shard_map/ppermute | solution.py:17
  411.4 45.0 %collective-permute-start.45 = (f32[2048,128]{1,0:T(8,128)}, f32[2048,128]{1,0:T(8,128)}, u32[]{:S(2)}, u32[]{:S(2)}) collective-permute-start(f32[2048,128]{1,0:T(8,128)} %mix.18), channel_id=1, source_target_pairs={{0,2},{2,0},{1,3},{3,1},{4,6},{6,4},{5,7},{7,5}} | collective-permute-start | bytes 3145736 | tf_op jit(solution)/shard_map/ppermute | solution.py:17
  412.3 66.1 %collective-permute-start.43 = (f32[1024,256]{1,0:T(8,128)}, f32[1024,256]{1,0:T(8,128)}, u32[]{:S(2)}, u32[]{:S(2)}) collective-permute-start(f32[1024,256]{1,0:T(8,128)} %mix.15), channel_id=1, source_target_pairs={{0,2},{2,0},{1,3},{3,1},{4,6},{6,4},{5,7},{7,5}} | collective-permute-start | bytes 3145736 | tf_op jit(solution)/shard_map/ppermute | solution.py:17
  413.4 31.1 %collective-permute-start.44 = (bf16[2560,128]{1,0:T(8,128)(2,1)}, bf16[2560,128]{1,0:T(8,128)(2,1)}, u32[]{:S(2)}, u32[]{:S(2)}) collective-permute-start(bf16[2560,128]{1,0:T(8,128)(2,1)} %get-tuple-element.62), channel_id=1, source_target_pairs={{0,4},{4,0},{1,5},{5,1},{2,6},{6,2},{3,7},{7,3}} | collective-permute-start | bytes 1966088 | tf_op jit(solution)/shard_map/ppermute | solution.py:17
  442.0 40.6 %collective-permute-start.42 = (bf16[2048,128]{1,0:T(8,128)(2,1)}, bf16[2048,128]{1,0:T(8,128)(2,1)}, u32[]{:S(2)}, u32[]{:S(2)}) collective-permute-start(bf16[2048,128]{1,0:T(8,128)(2,1)} %mix.21), channel_id=1, source_target_pairs={{0,4},{4,0},{1,5},{5,1},{2,6},{6,2},{3,7},{7,3}} | collective-permute-start | bytes 1572872 | tf_op jit(solution)/shard_map/ppermute | solution.py:17
  464.4 21.9 %collective-permute-start.46 = (bf16[2048,128]{1,0:T(8,128)(2,1)}, bf16[2048,128]{1,0:T(8,128)(2,1)S(1)}, u32[]{:S(2)}, u32[]{:S(2)}) collective-permute-start(bf16[2048,128]{1,0:T(8,128)(2,1)} %mix.22), channel_id=1, source_target_pairs={{0,4},{4,0},{1,5},{5,1},{2,6},{6,2},{3,7},{7,3}} | collective-permute-start | bytes 1572872 | tf_op jit(solution)/shard_map/ppermute | solution.py:17
  (36 other events, 279.5 us)
